TPU v7x, 32 devices: a whole 2x2x4 slice. The times are simulated.
32 devices in a mesh: seq: 16 (over z, y, x), head: 2 (over core).
Axes of the slice: x: 2, y: 2, z: 4, core: 2. Of those that a mesh axis runs over, the one named last changes fastest.
Arguments:
- queries: bfloat16 [2048, 2048], P('seq', 'head'), may hold values from -6 to 6
- key_vectors: bfloat16 [2, 2048, 2048], P(None, 'seq', 'head'), may hold values from -6 to 6
- values: bfloat16 [2, 2048, 2048], P(None, 'seq', 'head'), may hold values from -6 to 6
- strengths: float32 [2, 16, 2048], P(None, 'head', 'seq'), may hold values from 0.05 to 1.95
- out_weight: bfloat16 [2048, 4096], P('head', 'seq'), may hold values from -0.1875 to 0.1875
Outputs:
- mixed: bfloat16 [2048, 4096], P('seq', 'head')
All inputs are finite; a program needn't handle non-finite values.
Results may differ from a plain program's by a relative error of at most 0.014.
Values may be sent and summed in bfloat16 or wider, within the bound.
No kernel may reach another device: no remote copies, remote signals or barrier semaphores. Data moves between devices by JAX's collectives and lax.ppermute only.
A program may use at most 64 MiB of HBM per device.

v0:
```python
import functools

import jax
import jax.numpy as jnp
from jax import lax
from jax.experimental import pallas as pl
from jax.experimental.pallas import tpu as pltpu
from jax.sharding import PartitionSpec as P


CHUNK = 128
EPS = 1e-06
F32 = jnp.float32
BF16 = jnp.bfloat16


def dot(a, b):
    return jnp.dot(a, b, preferred_element_type=F32)


def dot_t(a, b):
    return lax.dot_general(a, b, (((1,), (1,)), ((), ())), preferred_element_type=F32)


def split(x):
    high = x.astype(BF16)
    return high, (x - high.astype(F32)).astype(BF16)


def product3(left, right):
    left_high, left_low = split(left)
    right_high, right_low = split(right)
    lhs = jnp.concatenate([left_high, left_low], axis=1)
    rhs = jnp.concatenate(
        [
            jnp.concatenate([right_high, right_low], axis=1),
            jnp.concatenate([right_high, jnp.zeros_like(right_low)], axis=1),
        ],
        axis=0,
    )
    wide = dot(lhs, rhs)
    width = right.shape[1]
    return wide[:, :width] + wide[:, width:]


def iota(shape, axis):
    return lax.broadcasted_iota(jnp.int32, shape, axis)


def weave(first, second):
    half = first.shape[0] // 2
    return jnp.concatenate([first[:half], second[:half], first[half:], second[half:]], axis=0)


def weave_lanes(first, second):
    half = first.shape[1] // 2
    return jnp.concatenate(
        [first[:, :half], second[:, :half], first[:, half:], second[:, half:]], axis=1
    )


def place(position, offset):
    return jnp.bitwise_xor(position, offset)


VMEM = pl.BlockSpec(memory_space=pltpu.VMEM)
PARAMS = pltpu.CompilerParams(vmem_limit_bytes=12 * 2**20)


def held(*arrays):
    return [pltpu.with_memory_space_constraint(array, pltpu.VMEM) for array in arrays]


def times(chunk):
    half = chunk // 2
    row, col = iota((chunk, chunk), 0), iota((chunk, chunk), 1)
    return 2 * lax.rem(row, half) + row // half, 2 * lax.rem(col, half) + col // half


def beta_rows(tokens, width):
    return -(-4 * max(tokens // width, 1) // 16) * 16


def invert_kernel(heads, tokens, *refs):
    key_in, (inverse_ref, table_ref, a_buf) = refs[:-3], refs[-3:]
    width = key_in[0].shape[1] // heads
    chunk = min(CHUNK, tokens)
    per_source = tokens // chunk
    chunks = len(key_in) * per_source
    pieces = max(tokens // width, 1)
    row_time, col_time = times(chunk)
    levels = chunk.bit_length() - 1

    def joins(level):
        same = (row_time >> (level + 1)) == (col_time >> (level + 1))
        return same & (((row_time >> level) & 1) == 1) & (((col_time >> level) & 1) == 0)

    def one_head(head, carry):
        lanes = pl.ds(pl.multiple_of(head * width, width), width)
        for index in range(chunks):
            key_ref, first = key_in[index // per_source], (index % per_source) * chunk
            key = weave(
                key_ref[first : first + chunk, lanes],
                key_ref[tokens + first : tokens + first + chunk, lanes],
            )
            gram = dot_t(key, key)
            wide_row, wide_col = iota(gram.shape, 0), iota(gram.shape, 1)
            square = jnp.sum(jnp.where(wide_row == wide_col, gram, 0.0), axis=0, keepdims=True)
            scale_row = lax.rsqrt(square + EPS)
            halves = key_ref[2 * tokens :, lanes].astype(F32)
            piece, inside = first // width, first % width

            def strength(reflection):
                high = reflection * pieces + piece
                low = (2 + reflection) * pieces + piece
                both = halves[high : high + 1] + halves[low : low + 1]
                return both[:, inside : inside + chunk]

            beta_row = weave_lanes(strength(0), strength(1))
            both_row = beta_row * scale_row
            table = jnp.concatenate(
                [scale_row, beta_row, both_row, jnp.zeros((5, 2 * chunk), F32)], axis=0
            )
            table_ref[head, index] = table
            system = table.T[:, 2:3] * (gram * scale_row)
            for block in range(2):
                here = slice(block * chunk, (block + 1) * chunk)
                diagonal = system[here, here]
                a_buf[2 * index + block] = diagonal
                inverse_ref[head, index, block] = jnp.where(
                    row_time == col_time, 1.0, 0.0
                ) - jnp.where(joins(0), diagonal, 0.0)
            inverse_ref[head, index, 2] = system[chunk:, :chunk]
        every = [(index, block) for index in range(chunks) for block in range(2)]
        for level in range(1, levels):
            mask = joins(level)
            inner = [
                product3(
                    jnp.where(mask, a_buf[2 * index + block], 0.0),
                    inverse_ref[head, index, block],
                )
                for index, block in every
            ]
            for (index, block), value in zip(every, inner):
                held = inverse_ref[head, index, block]
                inverse_ref[head, index, block] = held - product3(held, value)
        inner = [
            product3(inverse_ref[head, index, 2], inverse_ref[head, index, 0])
            for index in range(chunks)
        ]
        for index in range(chunks):
            inverse_ref[head, index, 2] = -product3(inverse_ref[head, index, 1], inner[index])
        return carry

    lax.fori_loop(0, heads, one_head, 0)


def invert(keys, heads, tokens):
    chunk = min(CHUNK, tokens)
    chunks = len(keys) * tokens // chunk
    return pl.pallas_call(
        functools.partial(invert_kernel, heads, tokens),
        out_shape=(
            pltpu.VMEM((heads, chunks, 3, chunk, chunk), F32),
            pltpu.VMEM((heads, chunks, 8, 2 * chunk), F32),
        ),
        in_specs=[VMEM] * len(keys),
        out_specs=(VMEM, VMEM),
        scratch_shapes=[pltpu.VMEM((2 * chunks, chunk, chunk), F32)],
        compiler_params=PARAMS,
        name="invert",
    )(*held(*keys))


def slot_of(group, index, per_source):
    position = lax.rem(lax.axis_index("seq"), group)
    return place(position, index // per_source) * per_source + index % per_source


def state_kernel(group, *refs):
    key_in, rest_in = refs[:group], refs[group : 2 * group]
    inverse_ref, table_ref = refs[2 * group : 2 * group + 2]
    high_ref, low_ref, before_ref, state_ref, step_buf = refs[2 * group + 2 :]
    heads, chunks, _, chunk, _ = inverse_ref.shape
    tokens = rest_in[0].shape[1]
    width = rest_in[0].shape[2] // heads
    per_source = tokens // chunk

    def one_head(head, carry):
        lanes = pl.ds(pl.multiple_of(head * width, width), width)
        for index in range(chunks):
            source, first = index // per_source, (index % per_source) * chunk
            key_ref, rest_ref = key_in[source], rest_in[source]
            key = weave(
                key_ref[first : first + chunk, lanes],
                key_ref[tokens + first : tokens + first + chunk, lanes],
            ).astype(F32)
            rows = slice(first, first + chunk)
            value = weave(rest_ref[0, rows, lanes], rest_ref[1, rows, lanes]).astype(F32)
            table = table_ref[head, index].T
            inverse = jnp.concatenate(
                [
                    jnp.concatenate(
                        [inverse_ref[head, index, 0], jnp.zeros((chunk, chunk), F32)], axis=1
                    ),
                    jnp.concatenate(
                        [inverse_ref[head, index, 2], inverse_ref[head, index, 1]], axis=1
                    ),
                ],
                axis=0,
            )
            right = jnp.concatenate([table[:, 2:3] * key, table[:, 1:2] * value], axis=1)
            high, low = split(dot3(inverse, *split(right)))
            high_ref[head, index] = high
            low_ref[head, index] = low
            step_buf[slot_of(group, index, per_source)] = dot3(
                (table[:, 0:1] * key).T, high, low
            )
        before = jnp.zeros((width, 2 * width), F32)
        for slot in range(chunks):
            narrow = before.astype(BF16)
            before_ref[head, slot] = narrow
            step = step_buf[slot]
            if slot:
                step = step - dot(step[:, :width].astype(BF16), narrow)
            before = before + step
        state_ref[head] = before.astype(BF16)
        return carry

    lax.fori_loop(0, heads, one_head, 0)


def dot3(left, high, low):
    left_high, left_low = split(left)
    return dot(left_high, high) + dot(left_low, high) + dot(left_high, low)


def carry_state(keys, rests, inverse, table):
    group = len(keys)
    heads, chunks, _, chunk, _ = inverse.shape
    width = rests[0].shape[2] // heads
    solved = pltpu.VMEM((heads, chunks, 2 * chunk, 2 * width), BF16)
    return pl.pallas_call(
        functools.partial(state_kernel, group),
        out_shape=(
            solved,
            solved,
            pltpu.VMEM((heads, chunks, width, 2 * width), BF16),
            pltpu.VMEM((heads, width, 2 * width), BF16),
        ),
        in_specs=[VMEM] * (2 * group + 2),
        out_specs=(VMEM,) * 4,
        scratch_shapes=[pltpu.VMEM((chunks, width, 2 * width), F32)],
        compiler_params=PARAMS,
        name="carry_state",
    )(*held(*keys, *rests, inverse, table))


def read_kernel(group, *refs):
    key_in, rest_in = refs[:group], refs[group : 2 * group]
    table_ref, high_ref, low_ref, before_ref, out_ref, lift_ref = refs[2 * group :]
    heads, chunks, _, wide = table_ref.shape
    chunk = wide // 2
    half = chunk // 2
    tokens = rest_in[0].shape[1]
    width = rest_in[0].shape[2] // heads
    per_source = tokens // chunk
    token_row = iota((chunk, 2 * chunk), 0)
    token_col = iota((chunk, 2 * chunk), 1)
    token_col = (token_col // chunk) * half + lax.rem(token_col, half)

    def one_head(head, carry):
        lanes = pl.ds(pl.multiple_of(head * width, width), width)
        for index in range(chunks):
            source, first = index // per_source, (index % per_source) * chunk
            key_ref, rest_ref = key_in[source], rest_in[source]
            key = weave(
                key_ref[first : first + chunk, lanes],
                key_ref[tokens + first : tokens + first + chunk, lanes],
            )
            query = rest_ref[2, first : first + chunk, lanes]
            wide_query = query.astype(F32)
            scale = lax.rsqrt(jnp.sum(wide_query * wide_query, axis=1, keepdims=True) + EPS)
            scores = jnp.where(
                token_col <= token_row,
                dot_t(query, key) * (scale * table_ref[head, index, 0:1, :]),
                0.0,
            )
            applied = dot3(scores, high_ref[head, index], low_ref[head, index])
            lifted = scale * wide_query - applied[:, :width]
            slot = slot_of(group, index, per_source)
            moved = dot(lifted.astype(BF16), before_ref[head, slot])
            rows = pl.ds(pl.multiple_of(slot * chunk, chunk), chunk)
            out_ref[rows, lanes] = applied[:, width:] + moved[:, width:]
            lift_ref[rows, lanes] = (lifted - moved[:, :width]).astype(BF16)
        return carry

    lax.fori_loop(0, heads, one_head, 0)


def read(keys, rests, table, high, low, before):
    group = len(keys)
    _, tokens, wide = rests[0].shape
    return pl.pallas_call(
        functools.partial(read_kernel, group),
        out_shape=(
            pltpu.VMEM((group * tokens, wide), F32),
            pltpu.VMEM((group * tokens, wide), BF16),
        ),
        in_specs=[VMEM] * (2 * group + 4),
        out_specs=(VMEM, VMEM),
        compiler_params=PARAMS,
        name="read",
    )(*held(*keys, *rests, table, high, low, before))


def join_kernel(count, *refs):
    states, (local_ref, lift_ref, out_ref) = refs[:count], refs[count:]
    heads, width, _ = states[0].shape
    for head in range(heads):
        lanes = slice(head * width, (head + 1) * width)
        total = None
        for state in reversed(states):
            step = state[head].astype(F32)
            if total is None:
                total = step[:, width:]
            else:
                total = (
                    total + step[:, width:] - dot(state[head, :, :width], total.astype(BF16))
                )
        out_ref[:, lanes] = (
            local_ref[:, lanes] + dot(lift_ref[:, lanes], total.astype(BF16))
        ).astype(BF16)


def join(states, local, lifted):
    return pl.pallas_call(
        functools.partial(join_kernel, len(states)),
        out_shape=pltpu.VMEM(local.shape, BF16),
        in_specs=[VMEM] * (len(states) + 2),
        out_specs=VMEM,
        compiler_params=PARAMS,
        name="join",
    )(*held(*states, local, lifted))


def compose(earlier, later):
    width = earlier.shape[1]
    moved = jnp.einsum("hab,hbc->hac", later[:, :, :width], earlier, preferred_element_type=F32)
    return (earlier.astype(F32) + later.astype(F32) - moved).astype(BF16)


def project_kernel(group, planes, *refs):
    count = group + planes
    heads_in, weight_in = refs[:group], refs[group:count]
    send_ref, keep_ref = refs[count:]
    device = lax.axis_index("seq")
    core = lax.axis_index("head")
    position, plane = lax.rem(device, group), device // group
    wide = heads_in[0].shape[1]
    side = planes // 2
    for offset in range(planes):
        columns = weight_in[offset].shape[1]
        owner = lax.rem(plane + planes - offset, planes)
        total = None
        for other in range(group):
            first = pl.multiple_of(place(position, other) * wide, wide)
            part = dot(heads_in[other][...], weight_in[offset][pl.ds(first, wide), :])
            total = part if total is None else total + part
        result = total.astype(BF16)
        lanes = pl.ds(pl.multiple_of(lax.rem(owner, side) * columns, columns), columns)

        @pl.when(owner // side == core)
        def _():
            keep_ref[:, lanes] = result

        @pl.when(owner // side != core)
        def _():
            send_ref[:, lanes] = result


def project(heads, weights):
    group, planes = len(heads), len(weights)
    rows = heads[0].shape[0]
    columns = weights[0].shape[1]
    shape = pltpu.VMEM((rows, columns * planes // 2), BF16)
    return pl.pallas_call(
        functools.partial(project_kernel, group, planes),
        out_shape=(shape, shape),
        in_specs=[VMEM] * (group + planes),
        out_specs=(VMEM, VMEM),
        compiler_params=PARAMS,
        name="project",
    )(*held(*heads, *weights))


def sum_kernel(group, keep_ref, other_ref, *outs):
    position = lax.rem(lax.axis_index("seq"), group)
    tokens = outs[0].shape[0]
    for offset in range(group):
        rows = pl.ds(pl.multiple_of(place(position, offset) * tokens, tokens), tokens)
        outs[offset][...] = (
            keep_ref[rows, :].astype(F32) + other_ref[rows, :].astype(F32)
        ).astype(BF16)


def sum_parts(keep, other, group):
    rows, columns = keep.shape
    return pl.pallas_call(
        functools.partial(sum_kernel, group),
        out_shape=[pltpu.VMEM((rows // group, columns), BF16)] * group,
        in_specs=[VMEM, VMEM],
        out_specs=[VMEM] * group,
        compiler_params=PARAMS,
        name="sum_parts",
    )(*held(keep, other))


def lay_kernel(group, columns, *refs):
    parts, out_ref, sems = refs[:group], refs[group], refs[group + 1]
    position = lax.rem(lax.axis_index("seq"), group)
    copies = []
    for offset in range(group):
        for index in range(parts[0].shape[1] // columns):
            first = (index * group + place(position, offset)) * columns
            copies.append(
                pltpu.make_async_copy(
                    parts[offset].at[:, index * columns : (index + 1) * columns],
                    out_ref.at[:, pl.ds(pl.multiple_of(first, columns), columns)],
                    sems.at[len(copies)],
                )
            )
    for copy in copies:
        copy.start()
    for copy in copies:
        copy.wait()


def lay_out(parts, columns):
    group = len(parts)
    rows, wide = parts[0].shape
    return pl.pallas_call(
        functools.partial(lay_kernel, group, columns),
        out_shape=jax.ShapeDtypeStruct((rows, group * wide), BF16),
        in_specs=[VMEM] * group,
        out_specs=pl.BlockSpec(memory_space=pl.ANY),
        scratch_shapes=[pltpu.SemaphoreType.DMA((group * wide // columns,))],
        compiler_params=PARAMS,
        name="lay_out",
    )(*held(*parts))


def swap(value, group, offset, count):
    pairs = [(i, (i // group) * group + ((i % group) ^ offset)) for i in range(count)]
    return lax.ppermute(value, "seq", pairs)


def per_device(queries, key_vectors, values, strengths, out_weight):
    count = lax.axis_size("seq")
    sides = lax.axis_size("head")
    heads = strengths.shape[1]
    tokens = queries.shape[0]
    width = queries.shape[1] // heads
    group = 1
    while group < 4 and heads % (2 * group) == 0 and count % (2 * group) == 0:
        group *= 2
    planes = count // group
    position = lax.axis_index("seq") % group
    mine = heads // group
    pieces = max(tokens // width, 1)
    high = lax.reduce_precision(strengths, 8, 7)
    beta = jnp.stack([high, strengths - high]).astype(BF16)
    beta = beta.reshape(4, heads, pieces, tokens // pieces)
    beta = jnp.pad(beta, ((0, 0), (0, 0), (0, 0), (0, width - tokens // pieces)))
    beta = jnp.swapaxes(beta, 1, 2).reshape(4 * pieces, heads * width)
    beta = jnp.pad(beta, ((0, beta_rows(tokens, width) - 4 * pieces), (0, 0)))
    packed = jnp.concatenate([key_vectors[0], key_vectors[1], beta], axis=0)

    keys, rests = [], []
    for offset in range(group):
        lane = jnp.bitwise_xor(position, offset) * mine * width
        key = lax.dynamic_slice_in_dim(packed, lane, mine * width, 1)
        rest = jnp.concatenate(
            [
                lax.dynamic_slice_in_dim(values, lane, mine * width, 2),
                lax.dynamic_slice_in_dim(queries, lane, mine * width, 1)[None],
            ],
            axis=0,
        )
        if offset:
            key = swap(key, group, offset, count)
            rest = swap(rest, group, offset, count)
        keys.append(key)
        rests.append(rest)

    split_out = sides == 2 and planes % 2 == 0 and planes <= 4 and group > 1
    weights = [out_weight]
    if split_out:
        for offset in range(1, planes):
            pairs = [
                (i, ((i // group + offset) % planes) * group + i % group)
                for i in range(count)
            ]
            weights.append(lax.ppermute(out_weight, "seq", pairs))

    inverse, table = invert(keys, mine, tokens)
    high, low, before, state = carry_state(keys, rests, inverse, table)
    local, lifted = read(keys, rests, table, high, low, before)

    def from_earlier(value, distance):
        pairs = [(i, i + distance * group) for i in range(count - distance * group)]
        return lax.ppermute(value, "seq", pairs)

    if planes <= 4:
        states = [from_earlier(state, distance) for distance in range(1, planes)]
    else:
        total = from_earlier(state, 1)
        distance = 1
        while distance < planes - 1:
            total = compose(from_earlier(total, distance), total)
            distance *= 2
        states = [total]
    mixed_heads = join(states, local, lifted)

    if split_out:
        gathered = [mixed_heads] + [
            swap(mixed_heads, group, offset, count) for offset in range(1, group)
        ]
        send, keep = project(gathered, weights)
        other = lax.ppermute(send, "head", [(0, 1), (1, 0)])
        parts = sum_parts(keep, other, group)
        parts = [parts[0]] + [
            swap(parts[offset], group, offset, count) for offset in range(1, group)
        ]
        return lay_out(parts, out_weight.shape[1])

    if group > 1:
        position_rows = []
        for offset in range(group):
            first = jnp.bitwise_xor(position, offset) * tokens
            part = lax.dynamic_slice_in_dim(mixed_heads, first, tokens, 0)
            position_rows.append(swap(part, group, offset, count) if offset else part)
        stacked = jnp.stack(position_rows)
        order = jnp.bitwise_xor(position, jnp.arange(group))
        stacked = jnp.take(stacked, order, axis=0)
        mixed_heads = jnp.swapaxes(stacked, 0, 1).reshape(tokens, heads * width)
    partial_sums = jnp.dot(
        mixed_heads,
        lax.all_gather(out_weight, "seq", axis=1, tiled=True),
        preferred_element_type=F32,
    )
    return lax.psum_scatter(
        partial_sums.astype(BF16), "head", scatter_dimension=1, tiled=True
    )


def solution(mesh):
    return jax.shard_map(
        per_device,
        mesh=mesh,
        in_specs=(
            P("seq", "head"),
            P(None, "seq", "head"),
            P(None, "seq", "head"),
            P(None, "head", "seq"),
            P("head", "seq"),
        ),
        out_specs=P("seq", "head"),
        check_vma=False,
    )
```

profile of v0, /device:TPU:24, one launch (start us, length us, event | category | flops | bytes accessed | tf_op | source)
XLA Modules:
  0.0 109.2 jit_solution(2652838238274699318)
XLA Ops:
  0.7 1.1 slice_bitcast_fusion.1
  2.0 1.6 %collective-permute-start = (bf16[272,256]{1,0:T(8,128)(2,1)S(1)}, bf16[272,256]{1,0:T(8,128)(2,1)S(1)}, u32[]{:S(2)}, u32[]{:S(2)}) collective-permute-start(bf16[272,256]{1,0:T(8,128)(2,1)S(1)} %get-tuple-element.35), channel_id=1, source_target_pairs={{0,2},{2,0},{4,6},{6,4},{8,10},{10,8},{12,14},{14,12},{16,18},{18,... | collective-permute-start | bytes 417800 | tf_op jit(solution)/shard_map/ppermute | solution.py:455
  3.5 1.5 %collective-permute-start.1 = (bf16[272,256]{1,0:T(8,128)(2,1)S(1)}, bf16[272,256]{1,0:T(8,128)(2,1)S(1)}, u32[]{:S(2)}, u32[]{:S(2)}) collective-permute-start(bf16[272,256]{1,0:T(8,128)(2,1)S(1)} %get-tuple-element.34), channel_id=1, source_target_pairs={{0,4},{2,6},{4,0},{6,2},{8,12},{10,14},{12,8},{14,10},{16,20},{18,... | collective-permute-start | bytes 417800 | tf_op jit(solution)/shard_map/ppermute | solution.py:455
  6.4 1.3 %collective-permute-done.refs_1_ = bf16[272,256]{1,0:T(8,128)(2,1)S(1)} collective-permute-done((bf16[272,256]{1,0:T(8,128)(2,1)S(1)}, bf16[272,256]{1,0:T(8,128)(2,1)S(1)}, u32[]{:S(2)}, u32[]{:S(2)}) %collective-permute-start) | collective-permute-done | bytes 139296 | tf_op jit(solution)/shard_map/ppermute | solution.py:455
  7.7 3.3 %collective-permute-start.5 = (bf16[3,128,256]{2,1,0:T(8,128)(2,1)S(1)}, bf16[3,128,256]{2,1,0:T(8,128)(2,1)S(1)}, u32[]{:S(2)}, u32[]{:S(2)}) collective-permute-start(bf16[3,128,256]{2,1,0:T(8,128)(2,1)S(1)} %pad_maximum_fusion.3), channel_id=1, source_target_pairs={{0,6},{2,4},{4,2},{6,0},{8,14},{10,12},{12,10},{14,8},{16,22},{18,... | collective-permute-start | bytes 589832 | tf_op jit(solution)/shard_map/ppermute | solution.py:455
  11.4 8.5 %collective-permute-done.2.refs_3_ = bf16[272,256]{1,0:T(8,128)(2,1)S(1)} collective-permute-done((bf16[272,256]{1,0:T(8,128)(2,1)S(1)}, bf16[272,256]{1,0:T(8,128)(2,1)S(1)}, u32[]{:S(2)}, u32[]{:S(2)}) %collective-permute-start.2) | collective-permute-done | bytes 139296 | tf_op jit(solution)/shard_map/ppermute | solution.py:455
  19.9 6.5 %invert.1 = (f32[2,4,3,128,128]{4,3,2,1,0:T(8,128)S(1)}, f32[2,4,8,256]{3,2,1,0:T(8,128)S(1)}) custom-call(bf16[272,256]{1,0:T(8,128)(2,1)S(1)} %get-tuple-element.36.refs_0_, bf16[272,256]{1,0:T(8,128)(2,1)S(1)} %collective-permute-done.refs_1_, bf16[272,256]{1,0:T(8,128)(2,1)S(1)} %collective-permute-done.1.refs_2_, ...), custom_call_target="tpu_custom_call" | custom-call | tf_op jit(solution)/shard_map/invert/pallas_call | solution.py:161
  26.5 5.3 %carry_state.1 = (bf16[2,4,256,256]{3,2,1,0:T(8,128)(2,1)S(1)}, bf16[2,4,256,256]{3,2,1,0:T(8,128)(2,1)S(1)}, bf16[2,4,128,256]{3,2,1,0:T(8,128)(2,1)S(1)}, bf16[2,128,256]{2,1,0:T(8,128)(2,1)S(1)}) custom-call(bf16[272,256]{1,0:T(8,128)(2,1)S(1)} %get-tuple-element.36.refs_0_, bf16[272,256]{1,0:T(8,128)(2,1)S(1)} %collective-permute-done.refs_1_, ...), custom_call_target="tpu_custom_call" | custom-call | tf_op jit(solution)/shard_map/carry_state/pallas_call | solution.py:243
  31.8 1.3 %collective-permute-start.6 = (bf16[2,128,256]{2,1,0:T(8,128)(2,1)S(1)}, bf16[2,128,256]{2,1,0:T(8,128)(2,1)S(1)}, u32[]{:S(2)}, u32[]{:S(2)}) collective-permute-start(bf16[2,128,256]{2,1,0:T(8,128)(2,1)S(1)} %get-tuple-element.21), channel_id=1, source_target_pairs={{0,8},{2,10},{4,12},{6,14},{8,16},{10,18},{12,20},{14,22},{16,24},... | collective-permute-start | bytes 393224 | tf_op jit(solution)/shard_map/ppermute | solution.py:512
  33.1 2.6 %collective-permute-start.13 = (bf16[1024,256]{1,0:T(8,128)(2,1)S(1)}, bf16[1024,256]{1,0:T(8,128)(2,1)S(1)}, u32[]{:S(2)}, u32[]{:S(2)}) collective-permute-start(bf16[1024,256]{1,0:T(8,128)(2,1)S(1)} %copy-done), channel_id=1, source_target_pairs={{0,16},{2,18},{4,20},{6,22},{8,24},{10,26},{12,28},{14,30},{16,0},... | collective-permute-start | bytes 1572872 | tf_op jit(solution)/shard_map/ppermute | solution.py:504
  36.2 1.3 %collective-permute-start.7 = (bf16[2,128,256]{2,1,0:T(8,128)(2,1)S(1)}, bf16[2,128,256]{2,1,0:T(8,128)(2,1)S(1)}, u32[]{:S(2)}, u32[]{:S(2)}) collective-permute-start(bf16[2,128,256]{2,1,0:T(8,128)(2,1)S(1)} %get-tuple-element.21), channel_id=1, source_target_pairs={{0,16},{2,18},{4,20},{6,22},{8,24},{10,26},{12,28},{14,30},{1,17},... | collective-permute-start | bytes 393224 | tf_op jit(solution)/shard_map/ppermute | solution.py:512
  37.5 1.8 %collective-permute-done.6.refs_0_ = bf16[2,128,256]{2,1,0:T(8,128)(2,1)S(1)} collective-permute-done((bf16[2,128,256]{2,1,0:T(8,128)(2,1)S(1)}, bf16[2,128,256]{2,1,0:T(8,128)(2,1)S(1)}, u32[]{:S(2)}, u32[]{:S(2)}) %collective-permute-start.6) | collective-permute-done | bytes 131104 | tf_op jit(solution)/shard_map/ppermute | solution.py:512
  39.3 1.3 %collective-permute-start.8 = (bf16[2,128,256]{2,1,0:T(8,128)(2,1)S(1)}, bf16[2,128,256]{2,1,0:T(8,128)(2,1)S(1)}, u32[]{:S(2)}, u32[]{:S(2)}) collective-permute-start(bf16[2,128,256]{2,1,0:T(8,128)(2,1)S(1)} %get-tuple-element.21), channel_id=1, source_target_pairs={{0,24},{2,26},{4,28},{6,30},{1,25},{3,27},{5,29},{7,31}} | collective-permute-start | bytes 393224 | tf_op jit(solution)/shard_map/ppermute | solution.py:512
  40.6 3.1 %read.1 = (f32[512,256]{1,0:T(8,128)S(1)}, bf16[512,256]{1,0:T(8,128)(2,1)S(1)}) custom-call(bf16[272,256]{1,0:T(8,128)(2,1)S(1)} %get-tuple-element.36.refs_0_, bf16[272,256]{1,0:T(8,128)(2,1)S(1)} %collective-permute-done.refs_1_, bf16[272,256]{1,0:T(8,128)(2,1)S(1)} %collective-permute-done.1.refs_2_, ...), custom_call_target="tpu_custom_call" | custom-call | tf_op jit(solution)/shard_map/read/pallas_call | solution.py:304
  43.7 36.4 %collective-permute-done.7.refs_1_ = bf16[2,128,256]{2,1,0:T(8,128)(2,1)S(1)} collective-permute-done((bf16[2,128,256]{2,1,0:T(8,128)(2,1)S(1)}, bf16[2,128,256]{2,1,0:T(8,128)(2,1)S(1)}, u32[]{:S(2)}, u32[]{:S(2)}) %collective-permute-start.7) | collective-permute-done | bytes 131104 | tf_op jit(solution)/shard_map/ppermute | solution.py:512
  80.9 2.7 %collective-permute-start.11 = (bf16[512,256]{1,0:T(8,128)(2,1)S(1)}, bf16[512,256]{1,0:T(8,128)(2,1)S(1)}, u32[]{:S(2)}, u32[]{:S(2)}) collective-permute-start(bf16[512,256]{1,0:T(8,128)(2,1)S(1)} %join.1.refs_0_), channel_id=1, source_target_pairs={{0,6},{2,4},{4,2},{6,0},{8,14},{10,12},{12,10},{14,8},{16,22},{18,... | collective-permute-start | bytes 786440 | tf_op jit(solution)/shard_map/ppermute | solution.py:455
  84.2 8.4 %collective-permute-done.10.refs_2_ = bf16[512,256]{1,0:T(8,128)(2,1)S(1)} collective-permute-done((bf16[512,256]{1,0:T(8,128)(2,1)S(1)}, bf16[512,256]{1,0:T(8,128)(2,1)S(1)}, u32[]{:S(2)}, u32[]{:S(2)}) %collective-permute-start.10) | collective-permute-done | bytes 262176 | tf_op jit(solution)/shard_map/ppermute | solution.py:455
  92.6 1.2 %collective-permute-done.9.refs_1_ = bf16[512,256]{1,0:T(8,128)(2,1)S(1)} collective-permute-done((bf16[512,256]{1,0:T(8,128)(2,1)S(1)}, bf16[512,256]{1,0:T(8,128)(2,1)S(1)}, u32[]{:S(2)}, u32[]{:S(2)}) %collective-permute-start.9) | collective-permute-done | bytes 262176 | tf_op jit(solution)/shard_map/ppermute | solution.py:455
  93.8 2.8 %project.1 = (bf16[512,512]{1,0:T(8,128)(2,1)S(1)}, bf16[512,512]{1,0:T(8,128)(2,1)S(1)}) custom-call(bf16[512,256]{1,0:T(8,128)(2,1)S(1)} %join.1.refs_0_, bf16[512,256]{1,0:T(8,128)(2,1)S(1)} %collective-permute-done.9.refs_1_, bf16[512,256]{1,0:T(8,128)(2,1)S(1)} %collective-permute-done.10.refs_2_, bf16[512,256]{1,0:T(8,128)(2,1)S(1)} %collective-permute-done.11.refs_3_, ...), custom_call_target="tpu_custom_call" | custom-call | tf_op jit(solution)/shard_map/project/pallas_call | solution.py:387
  96.7 1.9 %collective-permute-done.15.other_ref = bf16[512,512]{1,0:T(8,128)(2,1)S(1)} collective-permute-done((bf16[512,512]{1,0:T(8,128)(2,1)S(1)}, bf16[512,512]{1,0:T(8,128)(2,1)S(1)}, u32[]{:S(2)}, u32[]{:S(2)}) %collective-permute-start.15) | collective-permute-done | bytes 524320 | tf_op jit(solution)/shard_map/ppermute | solution.py:530
  98.7 1.6 %collective-permute-start.16 = (bf16[128,512]{1,0:T(8,128)(2,1)S(1)}, bf16[128,512]{1,0:T(8,128)(2,1)S(1)}, u32[]{:S(2)}, u32[]{:S(2)}) collective-permute-start(bf16[128,512]{1,0:T(8,128)(2,1)S(1)} %get-tuple-element.30), channel_id=1, source_target_pairs={{0,2},{2,0},{4,6},{6,4},{8,10},{10,8},{12,14},{14,12},{16,18},{18,... | collective-permute-start | bytes 393224 | tf_op jit(solution)/shard_map/ppermute | solution.py:455
  100.7 1.6 %collective-permute-start.18 = (bf16[128,512]{1,0:T(8,128)(2,1)S(1)}, bf16[128,512]{1,0:T(8,128)(2,1)S(1)}, u32[]{:S(2)}, u32[]{:S(2)}) collective-permute-start(bf16[128,512]{1,0:T(8,128)(2,1)S(1)} %get-tuple-element.32), channel_id=1, source_target_pairs={{0,6},{2,4},{4,2},{6,0},{8,14},{10,12},{12,10},{14,8},{16,22},{18,... | collective-permute-start | bytes 393224 | tf_op jit(solution)/shard_map/ppermute | solution.py:455
  102.3 2.4 %collective-permute-done.16.refs_1_ = bf16[128,512]{1,0:T(8,128)(2,1)S(1)} collective-permute-done((bf16[128,512]{1,0:T(8,128)(2,1)S(1)}, bf16[128,512]{1,0:T(8,128)(2,1)S(1)}, u32[]{:S(2)}, u32[]{:S(2)}) %collective-permute-start.16) | collective-permute-done | bytes 131104 | tf_op jit(solution)/shard_map/ppermute | solution.py:455
  104.7 3.7 %collective-permute-done.17.refs_2_ = bf16[128,512]{1,0:T(8,128)(2,1)S(1)} collective-permute-done((bf16[128,512]{1,0:T(8,128)(2,1)S(1)}, bf16[128,512]{1,0:T(8,128)(2,1)S(1)}, u32[]{:S(2)}, u32[]{:S(2)}) %collective-permute-start.17) | collective-permute-done | bytes 131104 | tf_op jit(solution)/shard_map/ppermute | solution.py:455
  (39 shorter events, 5.8 us)
Async XLA Ops:
  1.8 3.3 %copy-start.1 = (bf16[2,128,1024]{2,1,0:T(8,128)(2,1)S(1)}, bf16[2,128,1024]{2,1,0:T(8,128)(2,1)}, u32[]{:S(2)}) copy-start(bf16[2,128,1024]{2,1,0:T(8,128)(2,1)} %param.7) | copy-start | bytes 1572868
  1.9 3.3 %copy-start.2 = (bf16[128,1024]{1,0:T(8,128)(2,1)S(1)}, bf16[128,1024]{1,0:T(8,128)(2,1)}, u32[]{:S(2)}) copy-start(bf16[128,1024]{1,0:T(8,128)(2,1)} %param.5) | copy-start | bytes 786436
  2.0 5.8 %collective-permute-start = (bf16[272,256]{1,0:T(8,128)(2,1)S(1)}, bf16[272,256]{1,0:T(8,128)(2,1)S(1)}, u32[]{:S(2)}, u32[]{:S(2)}) collective-permute-start(bf16[272,256]{1,0:T(8,128)(2,1)S(1)} %get-tuple-element.35), channel_id=1, source_target_pairs={{0,2},{2,0},{4,6},{6,4},{8,10},{10,8},{12,14},{14,12},{16,18},{18,... | collective-permute-start | bytes 417800 | tf_op jit(solution)/shard_map/ppermute | solution.py:455
  3.5 2.9 %copy-start = (bf16[1024,256]{1,0:T(8,128)(2,1)S(1)}, bf16[1024,256]{1,0:T(8,128)(2,1)}, u32[]{:S(2)}) copy-start(bf16[1024,256]{1,0:T(8,128)(2,1)} %refs_4_.1) | copy-start | bytes 1572868
  3.5 7.5 %collective-permute-start.1 = (bf16[272,256]{1,0:T(8,128)(2,1)S(1)}, bf16[272,256]{1,0:T(8,128)(2,1)S(1)}, u32[]{:S(2)}, u32[]{:S(2)}) collective-permute-start(bf16[272,256]{1,0:T(8,128)(2,1)S(1)} %get-tuple-element.34), channel_id=1, source_target_pairs={{0,4},{2,6},{4,0},{6,2},{8,12},{10,14},{12,8},{14,10},{16,20},{18,... | collective-permute-start | bytes 417800 | tf_op jit(solution)/shard_map/ppermute | solution.py:455
  5.2 21.3 %collective-permute-start.3 = (bf16[3,128,256]{2,1,0:T(8,128)(2,1)S(1)}, bf16[3,128,256]{2,1,0:T(8,128)(2,1)S(1)}, u32[]{:S(2)}, u32[]{:S(2)}) collective-permute-start(bf16[3,128,256]{2,1,0:T(8,128)(2,1)S(1)} %pad_maximum_fusion.1), channel_id=1, source_target_pairs={{0,2},{2,0},{4,6},{6,4},{8,10},{10,8},{12,14},{14,12},{16,18},{18,... | collective-permute-start | bytes 589832 | tf_op jit(solution)/shard_map/ppermute | solution.py:455
  5.8 20.6 %collective-permute-start.4 = (bf16[3,128,256]{2,1,0:T(8,128)(2,1)S(1)}, bf16[3,128,256]{2,1,0:T(8,128)(2,1)S(1)}, u32[]{:S(2)}, u32[]{:S(2)}) collective-permute-start(bf16[3,128,256]{2,1,0:T(8,128)(2,1)S(1)} %pad_maximum_fusion.2), channel_id=1, source_target_pairs={{0,4},{2,6},{4,0},{6,2},{8,12},{10,14},{12,8},{14,10},{16,20},{18,... | collective-permute-start | bytes 589832 | tf_op jit(solution)/shard_map/ppermute | solution.py:455
  6.4 77.2 %collective-permute-start.12 = (bf16[1024,256]{1,0:T(8,128)(2,1)S(1)}, bf16[1024,256]{1,0:T(8,128)(2,1)S(1)}, u32[]{:S(2)}, u32[]{:S(2)}) collective-permute-start(bf16[1024,256]{1,0:T(8,128)(2,1)S(1)} %copy-done), channel_id=1, source_target_pairs={{0,8},{2,10},{4,12},{6,14},{8,16},{10,18},{12,20},{14,22},{16,24},... | collective-permute-start | bytes 1572872 | tf_op jit(solution)/shard_map/ppermute | solution.py:504
  7.7 18.7 %collective-permute-start.5 = (bf16[3,128,256]{2,1,0:T(8,128)(2,1)S(1)}, bf16[3,128,256]{2,1,0:T(8,128)(2,1)S(1)}, u32[]{:S(2)}, u32[]{:S(2)}) collective-permute-start(bf16[3,128,256]{2,1,0:T(8,128)(2,1)S(1)} %pad_maximum_fusion.3), channel_id=1, source_target_pairs={{0,6},{2,4},{4,2},{6,0},{8,14},{10,12},{12,10},{14,8},{16,22},{18,... | collective-permute-start | bytes 589832 | tf_op jit(solution)/shard_map/ppermute | solution.py:455
  11.0 8.9 %collective-permute-start.2 = (bf16[272,256]{1,0:T(8,128)(2,1)S(1)}, bf16[272,256]{1,0:T(8,128)(2,1)S(1)}, u32[]{:S(2)}, u32[]{:S(2)}) collective-permute-start(bf16[272,256]{1,0:T(8,128)(2,1)S(1)} %get-tuple-element.33), channel_id=1, source_target_pairs={{0,6},{2,4},{4,2},{6,0},{8,14},{10,12},{12,10},{14,8},{16,22},{18,... | collective-permute-start | bytes 417800 | tf_op jit(solution)/shard_map/ppermute | solution.py:455
  31.8 7.4 %collective-permute-start.6 = (bf16[2,128,256]{2,1,0:T(8,128)(2,1)S(1)}, bf16[2,128,256]{2,1,0:T(8,128)(2,1)S(1)}, u32[]{:S(2)}, u32[]{:S(2)}) collective-permute-start(bf16[2,128,256]{2,1,0:T(8,128)(2,1)S(1)} %get-tuple-element.21), channel_id=1, source_target_pairs={{0,8},{2,10},{4,12},{6,14},{8,16},{10,18},{12,20},{14,22},{16,24},... | collective-permute-start | bytes 393224 | tf_op jit(solution)/shard_map/ppermute | solution.py:512
  33.1 51.0 %collective-permute-start.13 = (bf16[1024,256]{1,0:T(8,128)(2,1)S(1)}, bf16[1024,256]{1,0:T(8,128)(2,1)S(1)}, u32[]{:S(2)}, u32[]{:S(2)}) collective-permute-start(bf16[1024,256]{1,0:T(8,128)(2,1)S(1)} %copy-done), channel_id=1, source_target_pairs={{0,16},{2,18},{4,20},{6,22},{8,24},{10,26},{12,28},{14,30},{16,0},... | collective-permute-start | bytes 1572872 | tf_op jit(solution)/shard_map/ppermute | solution.py:504
  35.7 48.4 %collective-permute-start.14 = (bf16[1024,256]{1,0:T(8,128)(2,1)S(1)}, bf16[1024,256]{1,0:T(8,128)(2,1)S(1)}, u32[]{:S(2)}, u32[]{:S(2)}) collective-permute-start(bf16[1024,256]{1,0:T(8,128)(2,1)S(1)} %copy-done), channel_id=1, source_target_pairs={{0,24},{2,26},{4,28},{6,30},{8,0},{10,2},{12,4},{14,6},{16,8},{18,... | collective-permute-start | bytes 1572872 | tf_op jit(solution)/shard_map/ppermute | solution.py:504
  36.2 43.9 %collective-permute-start.7 = (bf16[2,128,256]{2,1,0:T(8,128)(2,1)S(1)}, bf16[2,128,256]{2,1,0:T(8,128)(2,1)S(1)}, u32[]{:S(2)}, u32[]{:S(2)}) collective-permute-start(bf16[2,128,256]{2,1,0:T(8,128)(2,1)S(1)} %get-tuple-element.21), channel_id=1, source_target_pairs={{0,16},{2,18},{4,20},{6,22},{8,24},{10,26},{12,28},{14,30},{1,17},... | collective-permute-start | bytes 393224 | tf_op jit(solution)/shard_map/ppermute | solution.py:512
  39.3 40.8 %collective-permute-start.8 = (bf16[2,128,256]{2,1,0:T(8,128)(2,1)S(1)}, bf16[2,128,256]{2,1,0:T(8,128)(2,1)S(1)}, u32[]{:S(2)}, u32[]{:S(2)}) collective-permute-start(bf16[2,128,256]{2,1,0:T(8,128)(2,1)S(1)} %get-tuple-element.21), channel_id=1, source_target_pairs={{0,24},{2,26},{4,28},{6,30},{1,25},{3,27},{5,29},{7,31}} | collective-permute-start | bytes 393224 | tf_op jit(solution)/shard_map/ppermute | solution.py:512
  80.6 12.0 %collective-permute-start.10 = (bf16[512,256]{1,0:T(8,128)(2,1)S(1)}, bf16[512,256]{1,0:T(8,128)(2,1)S(1)}, u32[]{:S(2)}, u32[]{:S(2)}) collective-permute-start(bf16[512,256]{1,0:T(8,128)(2,1)S(1)} %join.1.refs_0_), channel_id=1, source_target_pairs={{0,4},{2,6},{4,0},{6,2},{8,12},{10,14},{12,8},{14,10},{16,20},{18,... | collective-permute-start | bytes 786440 | tf_op jit(solution)/shard_map/ppermute | solution.py:455
  80.9 11.7 %collective-permute-start.11 = (bf16[512,256]{1,0:T(8,128)(2,1)S(1)}, bf16[512,256]{1,0:T(8,128)(2,1)S(1)}, u32[]{:S(2)}, u32[]{:S(2)}) collective-permute-start(bf16[512,256]{1,0:T(8,128)(2,1)S(1)} %join.1.refs_0_), channel_id=1, source_target_pairs={{0,6},{2,4},{4,2},{6,0},{8,14},{10,12},{12,10},{14,8},{16,22},{18,... | collective-permute-start | bytes 786440 | tf_op jit(solution)/shard_map/ppermute | solution.py:455
  83.6 10.2 %collective-permute-start.9 = (bf16[512,256]{1,0:T(8,128)(2,1)S(1)}, bf16[512,256]{1,0:T(8,128)(2,1)S(1)}, u32[]{:S(2)}, u32[]{:S(2)}) collective-permute-start(bf16[512,256]{1,0:T(8,128)(2,1)S(1)} %join.1.refs_0_), channel_id=1, source_target_pairs={{0,2},{2,0},{4,6},{6,4},{8,10},{10,8},{12,14},{14,12},{16,18},{18,... | collective-permute-start | bytes 786440 | tf_op jit(solution)/shard_map/ppermute | solution.py:455
  96.6 2.0 %collective-permute-start.15 = (bf16[512,512]{1,0:T(8,128)(2,1)S(1)}, bf16[512,512]{1,0:T(8,128)(2,1)S(1)}, u32[]{:S(2)}, u32[]{:S(2)}) collective-permute-start(bf16[512,512]{1,0:T(8,128)(2,1)S(1)} %get-tuple-element.28), channel_id=1, source_target_pairs={{0,1},{1,0},{2,3},{3,2},{4,5},{5,4},{6,7},{7,6},{8,9},{9,8},{10,11... | collective-permute-start | bytes 1572872 | tf_op jit(solution)/shard_map/ppermute | solution.py:530
  98.7 6.0 %collective-permute-start.16 = (bf16[128,512]{1,0:T(8,128)(2,1)S(1)}, bf16[128,512]{1,0:T(8,128)(2,1)S(1)}, u32[]{:S(2)}, u32[]{:S(2)}) collective-permute-start(bf16[128,512]{1,0:T(8,128)(2,1)S(1)} %get-tuple-element.30), channel_id=1, source_target_pairs={{0,2},{2,0},{4,6},{6,4},{8,10},{10,8},{12,14},{14,12},{16,18},{18,... | collective-permute-start | bytes 393224 | tf_op jit(solution)/shard_map/ppermute | solution.py:455
  100.3 8.1 %collective-permute-start.17 = (bf16[128,512]{1,0:T(8,128)(2,1)S(1)}, bf16[128,512]{1,0:T(8,128)(2,1)S(1)}, u32[]{:S(2)}, u32[]{:S(2)}) collective-permute-start(bf16[128,512]{1,0:T(8,128)(2,1)S(1)} %get-tuple-element.31), channel_id=1, source_target_pairs={{0,4},{2,6},{4,0},{6,2},{8,12},{10,14},{12,8},{14,10},{16,20},{18,... | collective-permute-start | bytes 393224 | tf_op jit(solution)/shard_map/ppermute | solution.py:455
  100.7 7.7 %collective-permute-start.18 = (bf16[128,512]{1,0:T(8,128)(2,1)S(1)}, bf16[128,512]{1,0:T(8,128)(2,1)S(1)}, u32[]{:S(2)}, u32[]{:S(2)}) collective-permute-start(bf16[128,512]{1,0:T(8,128)(2,1)S(1)} %get-tuple-element.32), channel_id=1, source_target_pairs={{0,6},{2,4},{4,2},{6,0},{8,14},{10,12},{12,10},{14,8},{16,22},{18,... | collective-permute-start | bytes 393224 | tf_op jit(solution)/shard_map/ppermute | solution.py:455
where the time goes:
time: 109 us
  waiting for transfers between devices  65.7 us (60%)
  starting transfers between devices  22 us (20%)
  Pallas kernels  19.3 us (18%)
  local copies, waits for them, and re-layouts  1.29 us (1%)
    ppermute x3, waiting for transfers between devices, from_earlier(): return lax.ppermute(value, 'seq', pairs)  38.2 us
    ppermute x12, waiting for transfers between devices, swap(): return lax.ppermute(value, 'seq', pairs)  25.5 us
    ppermute x12, starting transfers between devices, swap(): return lax.ppermute(value, 'seq', pairs)  15 us
    pallas_call x1, Pallas kernels, invert(): pl.pallas_call(functools.partial(invert_kernel, heads, tokens), out_shape...  6.55 us
    pallas_call x1, Pallas kernels, carry_state(): pl.pallas_call(functools.partial(state_kernel, group), out_shape=(solved,...  5.34 us
    ppermute x3, starting transfers between devices, from_earlier(): return lax.ppermute(value, 'seq', pairs)  3.85 us
    pallas_call x1, Pallas kernels, read(): pl.pallas_call(functools.partial(read_kernel, group), out_shape=(pltpu.VM...  3.09 us
    ppermute x3, starting transfers between devices, per_device(): weights.append(lax.ppermute(out_weight, 'seq', pairs))  3.05 us
  transfers between devices with their start and end apart: 19, of which 9 were waited for; matrix products, arithmetic and copies ran while one was open for 0% of the time, Pallas kernels for 14%

commit v1 on v0

--- a/solution.py
+++ b/solution.py
@@ -180,7 +180,7 @@
 def state_kernel(group, *refs):
     key_in, rest_in = refs[:group], refs[group : 2 * group]
     inverse_ref, table_ref = refs[2 * group : 2 * group + 2]
-    high_ref, low_ref, before_ref, state_ref, step_buf = refs[2 * group + 2 :]
+    high_ref, low_ref, before_ref, state_ref, local_ref, step_buf = refs[2 * group + 2 :]
     heads, chunks, _, chunk, _ = inverse_ref.shape
     tokens = rest_in[0].shape[1]
     width = rest_in[0].shape[2] // heads
@@ -225,6 +225,7 @@
                 step = step - dot(step[:, :width].astype(BF16), narrow)
             before = before + step
         state_ref[head] = before.astype(BF16)
+        local_ref[head] = before[:, width:].astype(BF16)
         return carry
 
     lax.fori_loop(0, heads, one_head, 0)
@@ -247,9 +248,10 @@
             solved,
             pltpu.VMEM((heads, chunks, width, 2 * width), BF16),
             pltpu.VMEM((heads, width, 2 * width), BF16),
+            pltpu.VMEM((heads, width, width), BF16),
         ),
         in_specs=[VMEM] * (2 * group + 2),
-        out_specs=(VMEM,) * 4,
+        out_specs=(VMEM,) * 5,
         scratch_shapes=[pltpu.VMEM((chunks, width, 2 * width), F32)],
         compiler_params=PARAMS,
         name="carry_state",
@@ -321,10 +323,10 @@
         lanes = slice(head * width, (head + 1) * width)
         total = None
         for state in reversed(states):
-            step = state[head].astype(F32)
             if total is None:
-                total = step[:, width:]
+                total = state[head].astype(F32)
             else:
+                step = state[head].astype(F32)
                 total = (
                     total + step[:, width:] - dot(state[head, :, :width], total.astype(BF16))
                 )
@@ -350,22 +352,31 @@
     return (earlier.astype(F32) + later.astype(F32) - moved).astype(BF16)
 
 
-def project_kernel(group, planes, *refs):
-    count = group + planes
-    heads_in, weight_in = refs[:group], refs[group:count]
-    send_ref, keep_ref = refs[count:]
+def project_kernel(group, *refs):
+    heads_in, weight_in, (send_ref, keep_ref) = refs[:group], refs[group:-2], refs[-2:]
     device = lax.axis_index("seq")
     core = lax.axis_index("head")
     position, plane = lax.rem(device, group), device // group
     wide = heads_in[0].shape[1]
-    side = planes // 2
-    for offset in range(planes):
-        columns = weight_in[offset].shape[1]
-        owner = lax.rem(plane + planes - offset, planes)
+    columns = weight_in[0].shape[1]
+    side = keep_ref.shape[1] // columns
+    inner = (plane == 1) | (plane == 2)
+    lanes_of = {0: weight_in[0], 1: weight_in[1]}
+    if len(weight_in) > 2:
+        lanes_of[3] = weight_in[2]
+        lanes_of[2] = weight_in[3:]
+    for offset, source in lanes_of.items():
+        owner = jnp.bitwise_xor(plane, offset)
         total = None
         for other in range(group):
             first = pl.multiple_of(place(position, other) * wide, wide)
-            part = dot(heads_in[other][...], weight_in[offset][pl.ds(first, wide), :])
+            if offset == 2:
+                weight = jnp.where(
+                    inner, source[0][pl.ds(first, wide), :], source[1][pl.ds(first, wide), :]
+                )
+            else:
+                weight = source[pl.ds(first, wide), :]
+            part = dot(heads_in[other][...], weight)
             total = part if total is None else total + part
         result = total.astype(BF16)
         lanes = pl.ds(pl.multiple_of(lax.rem(owner, side) * columns, columns), columns)
@@ -379,15 +390,15 @@
             send_ref[:, lanes] = result
 
 
-def project(heads, weights):
-    group, planes = len(heads), len(weights)
+def project(heads, weights, planes):
+    group = len(heads)
     rows = heads[0].shape[0]
     columns = weights[0].shape[1]
     shape = pltpu.VMEM((rows, columns * planes // 2), BF16)
     return pl.pallas_call(
-        functools.partial(project_kernel, group, planes),
+        functools.partial(project_kernel, group),
         out_shape=(shape, shape),
-        in_specs=[VMEM] * (group + planes),
+        in_specs=[VMEM] * (group + len(weights)),
         out_specs=(VMEM, VMEM),
         compiler_params=PARAMS,
         name="project",
@@ -493,18 +504,15 @@
         keys.append(key)
         rests.append(rest)
 
-    split_out = sides == 2 and planes % 2 == 0 and planes <= 4 and group > 1
+    split_out = sides == 2 and planes in (2, 4) and group > 1
     weights = [out_weight]
     if split_out:
-        for offset in range(1, planes):
-            pairs = [
-                (i, ((i // group + offset) % planes) * group + i % group)
-                for i in range(count)
-            ]
+        for offset in range(1, planes, 2):
+            pairs = [(i, ((i // group) ^ offset) * group + i % group) for i in range(count)]
             weights.append(lax.ppermute(out_weight, "seq", pairs))
 
     inverse, table = invert(keys, mine, tokens)
-    high, low, before, state = carry_state(keys, rests, inverse, table)
+    high, low, before, state, local_state = carry_state(keys, rests, inverse, table)
     local, lifted = read(keys, rests, table, high, low, before)
 
     def from_earlier(value, distance):
@@ -512,21 +520,33 @@
         return lax.ppermute(value, "seq", pairs)
 
     if planes <= 4:
-        states = [from_earlier(state, distance) for distance in range(1, planes)]
+        states = []
+        for distance in range(1, planes):
+            sent = state if distance + 1 < planes else local_state
+            states.append(from_earlier(sent, distance))
     else:
         total = from_earlier(state, 1)
         distance = 1
         while distance < planes - 1:
             total = compose(from_earlier(total, distance), total)
             distance *= 2
-        states = [total]
+        states = [total[:, :, width:]]
+    if split_out and planes == 4:
+        for held_weight, hops in ((weights[1], ((1, 2), (2, 1))), (weights[2], ((1, 0), (2, 3)))):
+            pairs = [
+                (source * group + i, target * group + i)
+                for source, target in hops
+                for i in range(group)
+            ]
+            weights.append(lax.ppermute(held_weight, "seq", pairs))
+
     mixed_heads = join(states, local, lifted)
 
     if split_out:
         gathered = [mixed_heads] + [
             swap(mixed_heads, group, offset, count) for offset in range(1, group)
         ]
-        send, keep = project(gathered, weights)
+        send, keep = project(gathered, weights, planes)
         other = lax.ppermute(send, "head", [(0, 1), (1, 0)])
         parts = sum_parts(keep, other, group)
         parts = [parts[0]] + [

time: 109 us -> 82.5 us (0.76)
  the two profiles are of different devices: /device:TPU:24 before, /device:TPU:0 now
where the time goes in v1:
time: 82.5 us; the launch traced here: 82.3 us
  starting transfers between devices  31.4 us (38%)
  waiting for transfers between devices  29.2 us (35%)
  Pallas kernels  19.3 us (23%)
  local copies, waits for them, and re-layouts  1.29 us (2%)
  other arithmetic  0.83 us (1%)
    ppermute x12, waiting for transfers between devices, swap(): return lax.ppermute(value, 'seq', pairs)  18.7 us
    ppermute x12, starting transfers between devices, swap(): return lax.ppermute(value, 'seq', pairs)  15.3 us
    ppermute x2, waiting for transfers between devices, per_device(): weights.append(lax.ppermute(out_weight, 'seq', pairs))  8.53 us
    ppermute x3, starting transfers between devices, from_earlier(): return lax.ppermute(value, 'seq', pairs)  8.52 us
    pallas_call x1, Pallas kernels, invert(): pl.pallas_call(functools.partial(invert_kernel, heads, tokens), out_shape...  6.55 us
    ppermute x2, starting transfers between devices, per_device(): weights.append(lax.ppermute(out_weight, 'seq', pairs))  5.53 us
    pallas_call x1, Pallas kernels, carry_state(): pl.pallas_call(functools.partial(state_kernel, group), out_shape=(solved,...  5.34 us
    pallas_call x1, Pallas kernels, read(): pl.pallas_call(functools.partial(read_kernel, group), out_shape=(pltpu.VM...  3.09 us
  transfers between devices with their start and end apart: 20, of which 8 were waited for; matrix products, arithmetic and copies ran while one was open for 3% of the time, Pallas kernels for 19%

profile of v1, /device:TPU:0, one launch (start us, length us, event | category | flops | bytes accessed | tf_op | source)
XLA Modules:
  0.0 82.3 jit_solution(17359986630521066645)
XLA Ops:
  0.0 3.1 %collective-permute-start.12 = (bf16[1024,256]{1,0:T(8,128)(2,1)}, bf16[1024,256]{1,0:T(8,128)(2,1)S(1)}, u32[]{:S(2)}, u32[]{:S(2)}) collective-permute-start(bf16[1024,256]{1,0:T(8,128)(2,1)} %refs_4_.1), channel_id=1, source_target_pairs={{0,8},{2,10},{4,12},{6,14},{8,0},{10,2},{12,4},{14,6},{16,24},{18,... | collective-permute-start | bytes 1572872 | tf_op jit(solution)/shard_map/ppermute | solution.py:512
  3.1 2.5 %collective-permute-start.13 = (bf16[1024,256]{1,0:T(8,128)(2,1)}, bf16[1024,256]{1,0:T(8,128)(2,1)S(1)}, u32[]{:S(2)}, u32[]{:S(2)}) collective-permute-start(bf16[1024,256]{1,0:T(8,128)(2,1)} %refs_4_.1), channel_id=1, source_target_pairs={{0,24},{2,26},{4,28},{6,30},{8,16},{10,18},{12,20},{14,22},{16,8},... | collective-permute-start | bytes 1572872 | tf_op jit(solution)/shard_map/ppermute | solution.py:512
  7.5 1.6 %collective-permute-start = (bf16[272,256]{1,0:T(8,128)(2,1)S(1)}, bf16[272,256]{1,0:T(8,128)(2,1)S(1)}, u32[]{:S(2)}, u32[]{:S(2)}) collective-permute-start(bf16[272,256]{1,0:T(8,128)(2,1)S(1)} %get-tuple-element.37), channel_id=1, source_target_pairs={{0,2},{2,0},{4,6},{6,4},{8,10},{10,8},{12,14},{14,12},{16,18},{18,... | collective-permute-start | bytes 417800 | tf_op jit(solution)/shard_map/ppermute | solution.py:466
  9.1 1.5 %collective-permute-start.1 = (bf16[272,256]{1,0:T(8,128)(2,1)S(1)}, bf16[272,256]{1,0:T(8,128)(2,1)S(1)}, u32[]{:S(2)}, u32[]{:S(2)}) collective-permute-start(bf16[272,256]{1,0:T(8,128)(2,1)S(1)} %get-tuple-element.36), channel_id=1, source_target_pairs={{0,4},{2,6},{4,0},{6,2},{8,12},{10,14},{12,8},{14,10},{16,20},{18,... | collective-permute-start | bytes 417800 | tf_op jit(solution)/shard_map/ppermute | solution.py:466
  11.3 2.1 %collective-permute-done.refs_1_ = bf16[272,256]{1,0:T(8,128)(2,1)S(1)} collective-permute-done((bf16[272,256]{1,0:T(8,128)(2,1)S(1)}, bf16[272,256]{1,0:T(8,128)(2,1)S(1)}, u32[]{:S(2)}, u32[]{:S(2)}) %collective-permute-start) | collective-permute-done | bytes 139296 | tf_op jit(solution)/shard_map/ppermute | solution.py:466
  13.4 2.2 %collective-permute-start.3 = (bf16[3,128,256]{2,1,0:T(8,128)(2,1)S(1)}, bf16[3,128,256]{2,1,0:T(8,128)(2,1)S(1)}, u32[]{:S(2)}, u32[]{:S(2)}) collective-permute-start(bf16[3,128,256]{2,1,0:T(8,128)(2,1)S(1)} %pad_maximum_fusion.1), channel_id=1, source_target_pairs={{0,2},{2,0},{4,6},{6,4},{8,10},{10,8},{12,14},{14,12},{16,18},{18,... | collective-permute-start | bytes 589832 | tf_op jit(solution)/shard_map/ppermute | solution.py:466
  15.6 1.4 %collective-permute-done.1.refs_2_ = bf16[272,256]{1,0:T(8,128)(2,1)S(1)} collective-permute-done((bf16[272,256]{1,0:T(8,128)(2,1)S(1)}, bf16[272,256]{1,0:T(8,128)(2,1)S(1)}, u32[]{:S(2)}, u32[]{:S(2)}) %collective-permute-start.1) | collective-permute-done | bytes 139296 | tf_op jit(solution)/shard_map/ppermute | solution.py:466
  17.0 1.7 %collective-permute-start.4 = (bf16[3,128,256]{2,1,0:T(8,128)(2,1)S(1)}, bf16[3,128,256]{2,1,0:T(8,128)(2,1)S(1)}, u32[]{:S(2)}, u32[]{:S(2)}) collective-permute-start(bf16[3,128,256]{2,1,0:T(8,128)(2,1)S(1)} %pad_maximum_fusion.2), channel_id=1, source_target_pairs={{0,4},{2,6},{4,0},{6,2},{8,12},{10,14},{12,8},{14,10},{16,20},{18,... | collective-permute-start | bytes 589832 | tf_op jit(solution)/shard_map/ppermute | solution.py:466
  20.2 8.5 %collective-permute-done.13.refs_6_ = bf16[1024,256]{1,0:T(8,128)(2,1)S(1)} collective-permute-done((bf16[1024,256]{1,0:T(8,128)(2,1)}, bf16[1024,256]{1,0:T(8,128)(2,1)S(1)}, u32[]{:S(2)}, u32[]{:S(2)}) %collective-permute-start.13) | collective-permute-done | bytes 524320 | tf_op jit(solution)/shard_map/ppermute | solution.py:512
  30.0 6.6 %invert.1 = (f32[2,4,3,128,128]{4,3,2,1,0:T(8,128)S(1)}, f32[2,4,8,256]{3,2,1,0:T(8,128)S(1)}) custom-call(bf16[272,256]{1,0:T(8,128)(2,1)S(1)} %get-tuple-element.38.refs_0_, bf16[272,256]{1,0:T(8,128)(2,1)S(1)} %collective-permute-done.refs_1_, bf16[272,256]{1,0:T(8,128)(2,1)S(1)} %collective-permute-done.1.refs_2_, ...), custom_call_target="tpu_custom_call" | custom-call | tf_op jit(solution)/shard_map/invert/pallas_call | solution.py:161
  36.6 5.3 %carry_state.1 = (bf16[2,4,256,256]{3,2,1,0:T(8,128)(2,1)S(1)}, bf16[2,4,256,256]{3,2,1,0:T(8,128)(2,1)S(1)}, bf16[2,4,128,256]{3,2,1,0:T(8,128)(2,1)S(1)}, bf16...) custom-call(bf16[272,256]{1,0:T(8,128)(2,1)S(1)} %get-tuple-element.38.refs_0_, ...), custom_call_target="tpu_custom_call" | custom-call | tf_op jit(solution)/shard_map/carry_state/pallas_call | solution.py:244
  42.0 4.6 %collective-permute-start.6 = (bf16[2,128,256]{2,1,0:T(8,128)(2,1)S(1)}, bf16[2,128,256]{2,1,0:T(8,128)(2,1)S(1)}, u32[]{:S(2)}, u32[]{:S(2)}) collective-permute-start(bf16[2,128,256]{2,1,0:T(8,128)(2,1)S(1)} %get-tuple-element.22), channel_id=1, source_target_pairs={{0,8},{2,10},{4,12},{6,14},{8,16},{10,18},{12,20},{14,22},{16,24},... | collective-permute-start | bytes 393224 | tf_op jit(solution)/shard_map/ppermute | solution.py:520
  46.6 2.6 %collective-permute-start.7 = (bf16[2,128,256]{2,1,0:T(8,128)(2,1)S(1)}, bf16[2,128,256]{2,1,0:T(8,128)(2,1)S(1)}, u32[]{:S(2)}, u32[]{:S(2)}) collective-permute-start(bf16[2,128,256]{2,1,0:T(8,128)(2,1)S(1)} %get-tuple-element.22), channel_id=1, source_target_pairs={{0,16},{2,18},{4,20},{6,22},{8,24},{10,26},{12,28},{14,30},{1,17},... | collective-permute-start | bytes 393224 | tf_op jit(solution)/shard_map/ppermute | solution.py:520
  49.2 1.3 %collective-permute-start.8 = (bf16[2,128,128]{2,1,0:T(8,128)(2,1)S(1)}, bf16[2,128,128]{2,1,0:T(8,128)(2,1)S(1)}, u32[]{:S(2)}, u32[]{:S(2)}) collective-permute-start(bf16[2,128,128]{2,1,0:T(8,128)(2,1)S(1)} %get-tuple-element.23), channel_id=1, source_target_pairs={{0,24},{2,26},{4,28},{6,30},{1,25},{3,27},{5,29},{7,31}} | collective-permute-start | bytes 196616 | tf_op jit(solution)/shard_map/ppermute | solution.py:520
  50.5 3.1 %read.1 = (f32[512,256]{1,0:T(8,128)S(1)}, bf16[512,256]{1,0:T(8,128)(2,1)S(1)}) custom-call(bf16[272,256]{1,0:T(8,128)(2,1)S(1)} %get-tuple-element.38.refs_0_, bf16[272,256]{1,0:T(8,128)(2,1)S(1)} %collective-permute-done.refs_1_, bf16[272,256]{1,0:T(8,128)(2,1)S(1)} %collective-permute-done.1.refs_2_, ...), custom_call_target="tpu_custom_call" | custom-call | tf_op jit(solution)/shard_map/read/pallas_call | solution.py:306
  54.2 1.6 %collective-permute-start.10 = (bf16[512,256]{1,0:T(8,128)(2,1)S(1)}, bf16[512,256]{1,0:T(8,128)(2,1)S(1)}, u32[]{:S(2)}, u32[]{:S(2)}) collective-permute-start(bf16[512,256]{1,0:T(8,128)(2,1)S(1)} %join.1.refs_0_), channel_id=1, source_target_pairs={{0,4},{2,6},{4,0},{6,2},{8,12},{10,14},{12,8},{14,10},{16,20},{18,... | collective-permute-start | bytes 786440 | tf_op jit(solution)/shard_map/ppermute | solution.py:466
  55.7 1.4 %collective-permute-start.11 = (bf16[512,256]{1,0:T(8,128)(2,1)S(1)}, bf16[512,256]{1,0:T(8,128)(2,1)S(1)}, u32[]{:S(2)}, u32[]{:S(2)}) collective-permute-start(bf16[512,256]{1,0:T(8,128)(2,1)S(1)} %join.1.refs_0_), channel_id=1, source_target_pairs={{0,6},{2,4},{4,2},{6,0},{8,14},{10,12},{12,10},{14,8},{16,22},{18,... | collective-permute-start | bytes 786440 | tf_op jit(solution)/shard_map/ppermute | solution.py:466
  57.7 7.9 %collective-permute-done.10.refs_2_ = bf16[512,256]{1,0:T(8,128)(2,1)S(1)} collective-permute-done((bf16[512,256]{1,0:T(8,128)(2,1)S(1)}, bf16[512,256]{1,0:T(8,128)(2,1)S(1)}, u32[]{:S(2)}, u32[]{:S(2)}) %collective-permute-start.10) | collective-permute-done | bytes 262176 | tf_op jit(solution)/shard_map/ppermute | solution.py:466
  66.8 2.9 %project.1 = (bf16[512,512]{1,0:T(8,128)(2,1)S(1)}, bf16[512,512]{1,0:T(8,128)(2,1)S(1)}) custom-call(bf16[512,256]{1,0:T(8,128)(2,1)S(1)} %join.1.refs_0_, bf16[512,256]{1,0:T(8,128)(2,1)S(1)} %collective-permute-done.9.refs_1_, bf16[512,256]{1,0:T(8,128)(2,1)S(1)} %collective-permute-done.10.refs_2_, bf16[512,256]{1,0:T(8,128)(2,1)S(1)} %collective-permute-done.11.refs_3_, ...), custom_call_target="tpu_custom_call" | custom-call | tf_op jit(solution)/shard_map/project/pallas_call | solution.py:398
  69.8 1.9 %collective-permute-done.16.other_ref = bf16[512,512]{1,0:T(8,128)(2,1)S(1)} collective-permute-done((bf16[512,512]{1,0:T(8,128)(2,1)S(1)}, bf16[512,512]{1,0:T(8,128)(2,1)S(1)}, u32[]{:S(2)}, u32[]{:S(2)}) %collective-permute-start.16) | collective-permute-done | bytes 524320 | tf_op jit(solution)/shard_map/ppermute | solution.py:550
  71.8 1.6 %collective-permute-start.17 = (bf16[128,512]{1,0:T(8,128)(2,1)S(1)}, bf16[128,512]{1,0:T(8,128)(2,1)S(1)}, u32[]{:S(2)}, u32[]{:S(2)}) collective-permute-start(bf16[128,512]{1,0:T(8,128)(2,1)S(1)} %get-tuple-element.32), channel_id=1, source_target_pairs={{0,2},{2,0},{4,6},{6,4},{8,10},{10,8},{12,14},{14,12},{16,18},{18,... | collective-permute-start | bytes 393224 | tf_op jit(solution)/shard_map/ppermute | solution.py:466
  73.3 1.5 %collective-permute-start.18 = (bf16[128,512]{1,0:T(8,128)(2,1)S(1)}, bf16[128,512]{1,0:T(8,128)(2,1)S(1)}, u32[]{:S(2)}, u32[]{:S(2)}) collective-permute-start(bf16[128,512]{1,0:T(8,128)(2,1)S(1)} %get-tuple-element.33), channel_id=1, source_target_pairs={{0,4},{2,6},{4,0},{6,2},{8,12},{10,14},{12,8},{14,10},{16,20},{18,... | collective-permute-start | bytes 393224 | tf_op jit(solution)/shard_map/ppermute | solution.py:466
  75.3 2.5 %collective-permute-done.17.refs_1_ = bf16[128,512]{1,0:T(8,128)(2,1)S(1)} collective-permute-done((bf16[128,512]{1,0:T(8,128)(2,1)S(1)}, bf16[128,512]{1,0:T(8,128)(2,1)S(1)}, u32[]{:S(2)}, u32[]{:S(2)}) %collective-permute-start.17) | collective-permute-done | bytes 131104 | tf_op jit(solution)/shard_map/ppermute | solution.py:466
  77.8 3.6 %collective-permute-done.18.refs_2_ = bf16[128,512]{1,0:T(8,128)(2,1)S(1)} collective-permute-done((bf16[128,512]{1,0:T(8,128)(2,1)S(1)}, bf16[128,512]{1,0:T(8,128)(2,1)S(1)}, u32[]{:S(2)}, u32[]{:S(2)}) %collective-permute-start.18) | collective-permute-done | bytes 131104 | tf_op jit(solution)/shard_map/ppermute | solution.py:466
  (41 shorter events, 9.1 us)
Async XLA Ops:
  0.0 19.5 %collective-permute-start.12 = (bf16[1024,256]{1,0:T(8,128)(2,1)}, bf16[1024,256]{1,0:T(8,128)(2,1)S(1)}, u32[]{:S(2)}, u32[]{:S(2)}) collective-permute-start(bf16[1024,256]{1,0:T(8,128)(2,1)} %refs_4_.1), channel_id=1, source_target_pairs={{0,8},{2,10},{4,12},{6,14},{8,0},{10,2},{12,4},{14,6},{16,24},{18,... | collective-permute-start | bytes 1572872 | tf_op jit(solution)/shard_map/ppermute | solution.py:512
  3.1 25.7 %collective-permute-start.13 = (bf16[1024,256]{1,0:T(8,128)(2,1)}, bf16[1024,256]{1,0:T(8,128)(2,1)S(1)}, u32[]{:S(2)}, u32[]{:S(2)}) collective-permute-start(bf16[1024,256]{1,0:T(8,128)(2,1)} %refs_4_.1), channel_id=1, source_target_pairs={{0,24},{2,26},{4,28},{6,30},{8,16},{10,18},{12,20},{14,22},{16,8},... | collective-permute-start | bytes 1572872 | tf_op jit(solution)/shard_map/ppermute | solution.py:512
  7.3 3.7 %copy-start.1 = (bf16[2,128,1024]{2,1,0:T(8,128)(2,1)S(1)}, bf16[2,128,1024]{2,1,0:T(8,128)(2,1)}, u32[]{:S(2)}) copy-start(bf16[2,128,1024]{2,1,0:T(8,128)(2,1)} %param.7) | copy-start | bytes 1572868
  7.4 3.7 %copy-start.2 = (bf16[128,1024]{1,0:T(8,128)(2,1)S(1)}, bf16[128,1024]{1,0:T(8,128)(2,1)}, u32[]{:S(2)}) copy-start(bf16[128,1024]{1,0:T(8,128)(2,1)} %param.5) | copy-start | bytes 786436
  7.5 5.9 %collective-permute-start = (bf16[272,256]{1,0:T(8,128)(2,1)S(1)}, bf16[272,256]{1,0:T(8,128)(2,1)S(1)}, u32[]{:S(2)}, u32[]{:S(2)}) collective-permute-start(bf16[272,256]{1,0:T(8,128)(2,1)S(1)} %get-tuple-element.37), channel_id=1, source_target_pairs={{0,2},{2,0},{4,6},{6,4},{8,10},{10,8},{12,14},{14,12},{16,18},{18,... | collective-permute-start | bytes 417800 | tf_op jit(solution)/shard_map/ppermute | solution.py:466
  9.1 8.0 %collective-permute-start.1 = (bf16[272,256]{1,0:T(8,128)(2,1)S(1)}, bf16[272,256]{1,0:T(8,128)(2,1)S(1)}, u32[]{:S(2)}, u32[]{:S(2)}) collective-permute-start(bf16[272,256]{1,0:T(8,128)(2,1)S(1)} %get-tuple-element.36), channel_id=1, source_target_pairs={{0,4},{2,6},{4,0},{6,2},{8,12},{10,14},{12,8},{14,10},{16,20},{18,... | collective-permute-start | bytes 417800 | tf_op jit(solution)/shard_map/ppermute | solution.py:466
  10.6 8.2 %collective-permute-start.2 = (bf16[272,256]{1,0:T(8,128)(2,1)S(1)}, bf16[272,256]{1,0:T(8,128)(2,1)S(1)}, u32[]{:S(2)}, u32[]{:S(2)}) collective-permute-start(bf16[272,256]{1,0:T(8,128)(2,1)S(1)} %get-tuple-element.35), channel_id=1, source_target_pairs={{0,6},{2,4},{4,2},{6,0},{8,14},{10,12},{12,10},{14,8},{16,22},{18,... | collective-permute-start | bytes 417800 | tf_op jit(solution)/shard_map/ppermute | solution.py:466
  13.4 23.2 %collective-permute-start.3 = (bf16[3,128,256]{2,1,0:T(8,128)(2,1)S(1)}, bf16[3,128,256]{2,1,0:T(8,128)(2,1)S(1)}, u32[]{:S(2)}, u32[]{:S(2)}) collective-permute-start(bf16[3,128,256]{2,1,0:T(8,128)(2,1)S(1)} %pad_maximum_fusion.1), channel_id=1, source_target_pairs={{0,2},{2,0},{4,6},{6,4},{8,10},{10,8},{12,14},{14,12},{16,18},{18,... | collective-permute-start | bytes 589832 | tf_op jit(solution)/shard_map/ppermute | solution.py:466
  17.0 19.6 %collective-permute-start.4 = (bf16[3,128,256]{2,1,0:T(8,128)(2,1)S(1)}, bf16[3,128,256]{2,1,0:T(8,128)(2,1)S(1)}, u32[]{:S(2)}, u32[]{:S(2)}) collective-permute-start(bf16[3,128,256]{2,1,0:T(8,128)(2,1)S(1)} %pad_maximum_fusion.2), channel_id=1, source_target_pairs={{0,4},{2,6},{4,0},{6,2},{8,12},{10,14},{12,8},{14,10},{16,20},{18,... | collective-permute-start | bytes 589832 | tf_op jit(solution)/shard_map/ppermute | solution.py:466
  18.8 17.9 %collective-permute-start.5 = (bf16[3,128,256]{2,1,0:T(8,128)(2,1)S(1)}, bf16[3,128,256]{2,1,0:T(8,128)(2,1)S(1)}, u32[]{:S(2)}, u32[]{:S(2)}) collective-permute-start(bf16[3,128,256]{2,1,0:T(8,128)(2,1)S(1)} %pad_maximum_fusion.3), channel_id=1, source_target_pairs={{0,6},{2,4},{4,2},{6,0},{8,14},{10,12},{12,10},{14,8},{16,22},{18,... | collective-permute-start | bytes 589832 | tf_op jit(solution)/shard_map/ppermute | solution.py:466
  19.5 47.3 %collective-permute-start.14 = (bf16[1024,256]{1,0:T(8,128)(2,1)S(1)}, bf16[1024,256]{1,0:T(8,128)(2,1)S(1)}, u32[]{:S(2)}, u32[]{:S(2)}) collective-permute-start(bf16[1024,256]{1,0:T(8,128)(2,1)S(1)} %collective-permute-done.12.refs_5_), channel_id=1, source_target_pairs={{8,16},{10,18},{12,20},{14,22},{16,8},{18,10},{20,12},{22,14},{9,1... | collective-permute-start | bytes 1572872 | tf_op jit(solution)/shard_map/ppermute | solution.py:541
  28.7 38.1 %collective-permute-start.15 = (bf16[1024,256]{1,0:T(8,128)(2,1)S(1)}, bf16[1024,256]{1,0:T(8,128)(2,1)S(1)}, u32[]{:S(2)}, u32[]{:S(2)}) collective-permute-start(bf16[1024,256]{1,0:T(8,128)(2,1)S(1)} %collective-permute-done.13.refs_6_), channel_id=1, source_target_pairs={{8,0},{10,2},{12,4},{14,6},{16,24},{18,26},{20,28},{22,30},{9,1},{... | collective-permute-start | bytes 1572872 | tf_op jit(solution)/shard_map/ppermute | solution.py:541
  42.0 11.7 %collective-permute-start.6 = (bf16[2,128,256]{2,1,0:T(8,128)(2,1)S(1)}, bf16[2,128,256]{2,1,0:T(8,128)(2,1)S(1)}, u32[]{:S(2)}, u32[]{:S(2)}) collective-permute-start(bf16[2,128,256]{2,1,0:T(8,128)(2,1)S(1)} %get-tuple-element.22), channel_id=1, source_target_pairs={{0,8},{2,10},{4,12},{6,14},{8,16},{10,18},{12,20},{14,22},{16,24},... | collective-permute-start | bytes 393224 | tf_op jit(solution)/shard_map/ppermute | solution.py:520
  46.6 7.1 %collective-permute-start.7 = (bf16[2,128,256]{2,1,0:T(8,128)(2,1)S(1)}, bf16[2,128,256]{2,1,0:T(8,128)(2,1)S(1)}, u32[]{:S(2)}, u32[]{:S(2)}) collective-permute-start(bf16[2,128,256]{2,1,0:T(8,128)(2,1)S(1)} %get-tuple-element.22), channel_id=1, source_target_pairs={{0,16},{2,18},{4,20},{6,22},{8,24},{10,26},{12,28},{14,30},{1,17},... | collective-permute-start | bytes 393224 | tf_op jit(solution)/shard_map/ppermute | solution.py:520
  49.2 4.4 %collective-permute-start.8 = (bf16[2,128,128]{2,1,0:T(8,128)(2,1)S(1)}, bf16[2,128,128]{2,1,0:T(8,128)(2,1)S(1)}, u32[]{:S(2)}, u32[]{:S(2)}) collective-permute-start(bf16[2,128,128]{2,1,0:T(8,128)(2,1)S(1)} %get-tuple-element.23), channel_id=1, source_target_pairs={{0,24},{2,26},{4,28},{6,30},{1,25},{3,27},{5,29},{7,31}} | collective-permute-start | bytes 196616 | tf_op jit(solution)/shard_map/ppermute | solution.py:520
  53.6 13.2 %copy-start = (bf16[1024,256]{1,0:T(8,128)(2,1)S(1)}, bf16[1024,256]{1,0:T(8,128)(2,1)}, u32[]{:S(2)}) copy-start(bf16[1024,256]{1,0:T(8,128)(2,1)} %refs_4_.1) | copy-start | bytes 1572868
  54.2 11.4 %collective-permute-start.10 = (bf16[512,256]{1,0:T(8,128)(2,1)S(1)}, bf16[512,256]{1,0:T(8,128)(2,1)S(1)}, u32[]{:S(2)}, u32[]{:S(2)}) collective-permute-start(bf16[512,256]{1,0:T(8,128)(2,1)S(1)} %join.1.refs_0_), channel_id=1, source_target_pairs={{0,4},{2,6},{4,0},{6,2},{8,12},{10,14},{12,8},{14,10},{16,20},{18,... | collective-permute-start | bytes 786440 | tf_op jit(solution)/shard_map/ppermute | solution.py:466
  55.7 9.8 %collective-permute-start.11 = (bf16[512,256]{1,0:T(8,128)(2,1)S(1)}, bf16[512,256]{1,0:T(8,128)(2,1)S(1)}, u32[]{:S(2)}, u32[]{:S(2)}) collective-permute-start(bf16[512,256]{1,0:T(8,128)(2,1)S(1)} %join.1.refs_0_), channel_id=1, source_target_pairs={{0,6},{2,4},{4,2},{6,0},{8,14},{10,12},{12,10},{14,8},{16,22},{18,... | collective-permute-start | bytes 786440 | tf_op jit(solution)/shard_map/ppermute | solution.py:466
  57.2 9.6 %collective-permute-start.9 = (bf16[512,256]{1,0:T(8,128)(2,1)S(1)}, bf16[512,256]{1,0:T(8,128)(2,1)S(1)}, u32[]{:S(2)}, u32[]{:S(2)}) collective-permute-start(bf16[512,256]{1,0:T(8,128)(2,1)S(1)} %join.1.refs_0_), channel_id=1, source_target_pairs={{0,2},{2,0},{4,6},{6,4},{8,10},{10,8},{12,14},{14,12},{16,18},{18,... | collective-permute-start | bytes 786440 | tf_op jit(solution)/shard_map/ppermute | solution.py:466
  69.7 2.0 %collective-permute-start.16 = (bf16[512,512]{1,0:T(8,128)(2,1)S(1)}, bf16[512,512]{1,0:T(8,128)(2,1)S(1)}, u32[]{:S(2)}, u32[]{:S(2)}) collective-permute-start(bf16[512,512]{1,0:T(8,128)(2,1)S(1)} %get-tuple-element.30), channel_id=1, source_target_pairs={{0,1},{1,0},{2,3},{3,2},{4,5},{5,4},{6,7},{7,6},{8,9},{9,8},{10,11... | collective-permute-start | bytes 1572872 | tf_op jit(solution)/shard_map/ppermute | solution.py:550
  71.8 6.0 %collective-permute-start.17 = (bf16[128,512]{1,0:T(8,128)(2,1)S(1)}, bf16[128,512]{1,0:T(8,128)(2,1)S(1)}, u32[]{:S(2)}, u32[]{:S(2)}) collective-permute-start(bf16[128,512]{1,0:T(8,128)(2,1)S(1)} %get-tuple-element.32), channel_id=1, source_target_pairs={{0,2},{2,0},{4,6},{6,4},{8,10},{10,8},{12,14},{14,12},{16,18},{18,... | collective-permute-start | bytes 393224 | tf_op jit(solution)/shard_map/ppermute | solution.py:466
  73.3 8.1 %collective-permute-start.18 = (bf16[128,512]{1,0:T(8,128)(2,1)S(1)}, bf16[128,512]{1,0:T(8,128)(2,1)S(1)}, u32[]{:S(2)}, u32[]{:S(2)}) collective-permute-start(bf16[128,512]{1,0:T(8,128)(2,1)S(1)} %get-tuple-element.33), channel_id=1, source_target_pairs={{0,4},{2,6},{4,0},{6,2},{8,12},{10,14},{12,8},{14,10},{16,20},{18,... | collective-permute-start | bytes 393224 | tf_op jit(solution)/shard_map/ppermute | solution.py:466
  74.9 6.6 %collective-permute-start.19 = (bf16[128,512]{1,0:T(8,128)(2,1)S(1)}, bf16[128,512]{1,0:T(8,128)(2,1)S(1)}, u32[]{:S(2)}, u32[]{:S(2)}) collective-permute-start(bf16[128,512]{1,0:T(8,128)(2,1)S(1)} %get-tuple-element.34), channel_id=1, source_target_pairs={{0,6},{2,4},{4,2},{6,0},{8,14},{10,12},{12,10},{14,8},{16,22},{18,... | collective-permute-start | bytes 393224 | tf_op jit(solution)/shard_map/ppermute | solution.py:466

commit v2 on v1

--- a/solution.py
+++ b/solution.py
@@ -95,64 +95,76 @@
         same = (row_time >> (level + 1)) == (col_time >> (level + 1))
         return same & (((row_time >> level) & 1) == 1) & (((col_time >> level) & 1) == 0)
 
-    def one_head(head, carry):
-        lanes = pl.ds(pl.multiple_of(head * width, width), width)
-        for index in range(chunks):
-            key_ref, first = key_in[index // per_source], (index % per_source) * chunk
-            key = weave(
-                key_ref[first : first + chunk, lanes],
-                key_ref[tokens + first : tokens + first + chunk, lanes],
-            )
-            gram = dot_t(key, key)
-            wide_row, wide_col = iota(gram.shape, 0), iota(gram.shape, 1)
-            square = jnp.sum(jnp.where(wide_row == wide_col, gram, 0.0), axis=0, keepdims=True)
-            scale_row = lax.rsqrt(square + EPS)
-            halves = key_ref[2 * tokens :, lanes].astype(F32)
-            piece, inside = first // width, first % width
-
-            def strength(reflection):
-                high = reflection * pieces + piece
-                low = (2 + reflection) * pieces + piece
-                both = halves[high : high + 1] + halves[low : low + 1]
-                return both[:, inside : inside + chunk]
-
-            beta_row = weave_lanes(strength(0), strength(1))
-            both_row = beta_row * scale_row
-            table = jnp.concatenate(
-                [scale_row, beta_row, both_row, jnp.zeros((5, 2 * chunk), F32)], axis=0
-            )
-            table_ref[head, index] = table
-            system = table.T[:, 2:3] * (gram * scale_row)
-            for block in range(2):
-                here = slice(block * chunk, (block + 1) * chunk)
-                diagonal = system[here, here]
-                a_buf[2 * index + block] = diagonal
-                inverse_ref[head, index, block] = jnp.where(
-                    row_time == col_time, 1.0, 0.0
-                ) - jnp.where(joins(0), diagonal, 0.0)
-            inverse_ref[head, index, 2] = system[chunk:, :chunk]
-        every = [(index, block) for index in range(chunks) for block in range(2)]
+    def prepare(head, index):
+        lanes = lanes_of(head, width)
+        key_ref, first = key_in[index // per_source], (index % per_source) * chunk
+        key = weave(
+            key_ref[first : first + chunk, lanes],
+            key_ref[tokens + first : tokens + first + chunk, lanes],
+        )
+        gram = dot_t(key, key)
+        wide_row, wide_col = iota(gram.shape, 0), iota(gram.shape, 1)
+        square = jnp.sum(jnp.where(wide_row == wide_col, gram, 0.0), axis=0, keepdims=True)
+        scale_row = lax.rsqrt(square + EPS)
+        halves = key_ref[2 * tokens :, lanes].astype(F32)
+        piece, inside = first // width, first % width
+
+        def strength(reflection):
+            high = reflection * pieces + piece
+            low = (2 + reflection) * pieces + piece
+            both = halves[high : high + 1] + halves[low : low + 1]
+            return both[:, inside : inside + chunk]
+
+        beta_row = weave_lanes(strength(0), strength(1))
+        both_row = beta_row * scale_row
+        table = jnp.concatenate(
+            [scale_row, beta_row, both_row, jnp.zeros((5, 2 * chunk), F32)], axis=0
+        )
+        table_ref[head, index] = table
+        system = table.T[:, 2:3] * (gram * scale_row)
+        for block in range(2):
+            here = slice(block * chunk, (block + 1) * chunk)
+            diagonal = system[here, here]
+            a_buf[head, index, block] = diagonal
+            inverse_ref[head, index, block] = jnp.where(
+                row_time == col_time, 1.0, 0.0
+            ) - jnp.where(joins(0), diagonal, 0.0)
+        inverse_ref[head, index, 2] = system[chunk:, :chunk]
+
+    def solve(units):
+        for head, index in units:
+            prepare(head, index)
+        every = [(head, index, block) for head, index in units for block in range(2)]
         for level in range(1, levels):
             mask = joins(level)
             inner = [
-                product3(
-                    jnp.where(mask, a_buf[2 * index + block], 0.0),
-                    inverse_ref[head, index, block],
-                )
-                for index, block in every
+                product3(jnp.where(mask, a_buf[one], 0.0), inverse_ref[one]) for one in every
             ]
-            for (index, block), value in zip(every, inner):
-                held = inverse_ref[head, index, block]
-                inverse_ref[head, index, block] = held - product3(held, value)
+            for one, value in zip(every, inner):
+                known = inverse_ref[one]
+                inverse_ref[one] = known - product3(known, value)
         inner = [
             product3(inverse_ref[head, index, 2], inverse_ref[head, index, 0])
-            for index in range(chunks)
+            for head, index in units
         ]
-        for index in range(chunks):
-            inverse_ref[head, index, 2] = -product3(inverse_ref[head, index, 1], inner[index])
-        return carry
-
-    lax.fori_loop(0, heads, one_head, 0)
+        for (head, index), value in zip(units, inner):
+            inverse_ref[head, index, 2] = -product3(inverse_ref[head, index, 1], value)
+
+    if heads * chunks <= 8:
+        solve([(head, index) for head in range(heads) for index in range(chunks)])
+    else:
+
+        def one_head(head, carry):
+            solve([(head, index) for index in range(chunks)])
+            return carry
+
+        lax.fori_loop(0, heads, one_head, 0)
+
+
+def lanes_of(head, width):
+    if isinstance(head, int):
+        return slice(head * width, (head + 1) * width)
+    return pl.ds(pl.multiple_of(head * width, width), width)
 
 
 def invert(keys, heads, tokens):
@@ -166,7 +178,7 @@
         ),
         in_specs=[VMEM] * len(keys),
         out_specs=(VMEM, VMEM),
-        scratch_shapes=[pltpu.VMEM((2 * chunks, chunk, chunk), F32)],
+        scratch_shapes=[pltpu.VMEM((heads, chunks, 2, chunk, chunk), F32)],
         compiler_params=PARAMS,
         name="invert",
     )(*held(*keys))
@@ -180,7 +192,7 @@
 def state_kernel(group, *refs):
     key_in, rest_in = refs[:group], refs[group : 2 * group]
     inverse_ref, table_ref = refs[2 * group : 2 * group + 2]
-    high_ref, low_ref, before_ref, state_ref, local_ref, step_buf = refs[2 * group + 2 :]
+    high_ref, low_ref, step_ref, state_ref, local_ref = refs[2 * group + 2 :]
     heads, chunks, _, chunk, _ = inverse_ref.shape
     tokens = rest_in[0].shape[1]
     width = rest_in[0].shape[2] // heads
@@ -213,22 +225,27 @@
             high, low = split(dot3(inverse, *split(right)))
             high_ref[head, index] = high
             low_ref[head, index] = low
-            step_buf[slot_of(group, index, per_source)] = dot3(
+            step_ref[head, slot_of(group, index, per_source)] = dot3(
                 (table[:, 0:1] * key).T, high, low
             )
-        before = jnp.zeros((width, 2 * width), F32)
-        for slot in range(chunks):
-            narrow = before.astype(BF16)
-            before_ref[head, slot] = narrow
-            step = step_buf[slot]
-            if slot:
-                step = step - dot(step[:, :width].astype(BF16), narrow)
-            before = before + step
-        state_ref[head] = before.astype(BF16)
-        local_ref[head] = before[:, width:].astype(BF16)
         return carry
 
     lax.fori_loop(0, heads, one_head, 0)
+    totals = [[step_ref[head, slot] for slot in range(chunks)] for head in range(heads)]
+    while len(totals[0]) > 1:
+        totals = [
+            [after(one[i], one[i + 1]) for i in range(0, len(one) - 1, 2)]
+            + one[len(one) - len(one) % 2 :]
+            for one in totals
+        ]
+    for head, (total,) in enumerate(totals):
+        state_ref[head] = total.astype(BF16)
+        local_ref[head] = total[:, width:].astype(BF16)
+
+
+def after(earlier, later):
+    width = earlier.shape[0]
+    return earlier + later - dot(later[:, :width].astype(BF16), earlier.astype(BF16))
 
 
 def dot3(left, high, low):
@@ -246,13 +263,12 @@
         out_shape=(
             solved,
             solved,
-            pltpu.VMEM((heads, chunks, width, 2 * width), BF16),
+            pltpu.VMEM((heads, chunks, width, 2 * width), F32),
             pltpu.VMEM((heads, width, 2 * width), BF16),
             pltpu.VMEM((heads, width, width), BF16),
         ),
         in_specs=[VMEM] * (2 * group + 2),
         out_specs=(VMEM,) * 5,
-        scratch_shapes=[pltpu.VMEM((chunks, width, 2 * width), F32)],
         compiler_params=PARAMS,
         name="carry_state",
     )(*held(*keys, *rests, inverse, table))
@@ -260,7 +276,7 @@
 
 def read_kernel(group, *refs):
     key_in, rest_in = refs[:group], refs[group : 2 * group]
-    table_ref, high_ref, low_ref, before_ref, out_ref, lift_ref = refs[2 * group :]
+    table_ref, high_ref, low_ref, step_ref, out_ref, lift_ref, before_buf = refs[2 * group :]
     heads, chunks, _, wide = table_ref.shape
     chunk = wide // 2
     half = chunk // 2
@@ -270,6 +286,13 @@
     token_row = iota((chunk, 2 * chunk), 0)
     token_col = iota((chunk, 2 * chunk), 1)
     token_col = (token_col // chunk) * half + lax.rem(token_col, half)
+    totals = [step_ref[head, 0] for head in range(heads)]
+    for head in range(heads):
+        before_buf[head, 0] = jnp.zeros((width, 2 * width), BF16)
+    for slot in range(1, chunks):
+        for head in range(heads):
+            before_buf[head, slot] = totals[head].astype(BF16)
+        totals = [after(totals[head], step_ref[head, slot]) for head in range(heads)]
 
     def one_head(head, carry):
         lanes = pl.ds(pl.multiple_of(head * width, width), width)
@@ -291,7 +314,7 @@
             applied = dot3(scores, high_ref[head, index], low_ref[head, index])
             lifted = scale * wide_query - applied[:, :width]
             slot = slot_of(group, index, per_source)
-            moved = dot(lifted.astype(BF16), before_ref[head, slot])
+            moved = dot(lifted.astype(BF16), before_buf[head, slot])
             rows = pl.ds(pl.multiple_of(slot * chunk, chunk), chunk)
             out_ref[rows, lanes] = applied[:, width:] + moved[:, width:]
             lift_ref[rows, lanes] = (lifted - moved[:, :width]).astype(BF16)
@@ -300,7 +323,7 @@
     lax.fori_loop(0, heads, one_head, 0)
 
 
-def read(keys, rests, table, high, low, before):
+def read(keys, rests, table, high, low, steps):
     group = len(keys)
     _, tokens, wide = rests[0].shape
     return pl.pallas_call(
@@ -311,9 +334,10 @@
         ),
         in_specs=[VMEM] * (2 * group + 4),
         out_specs=(VMEM, VMEM),
+        scratch_shapes=[pltpu.VMEM(steps.shape, BF16)],
         compiler_params=PARAMS,
         name="read",
-    )(*held(*keys, *rests, table, high, low, before))
+    )(*held(*keys, *rests, table, high, low, steps))
 
 
 def join_kernel(count, *refs):
@@ -352,20 +376,26 @@
     return (earlier.astype(F32) + later.astype(F32) - moved).astype(BF16)
 
 
-def project_kernel(group, *refs):
+def project_kernel(group, targets, *refs):
     heads_in, weight_in, (send_ref, keep_ref) = refs[:group], refs[group:-2], refs[-2:]
     device = lax.axis_index("seq")
     core = lax.axis_index("head")
     position, plane = lax.rem(device, group), device // group
-    wide = heads_in[0].shape[1]
+    rows, wide = heads_in[0].shape
+    tokens = rows // group
     columns = weight_in[0].shape[1]
     side = keep_ref.shape[1] // columns
     inner = (plane == 1) | (plane == 2)
-    lanes_of = {0: weight_in[0], 1: weight_in[1]}
+    sources = {0: weight_in[0], 1: weight_in[1]}
     if len(weight_in) > 2:
-        lanes_of[3] = weight_in[2]
-        lanes_of[2] = weight_in[3:]
-    for offset, source in lanes_of.items():
+        sources[3] = weight_in[2]
+        sources[2] = weight_in[3:]
+
+    def rows_of(source):
+        firsts = [pl.multiple_of(place(position, t) * tokens, tokens) for t in targets]
+        return jnp.concatenate([source[pl.ds(first, tokens), :] for first in firsts], axis=0)
+
+    for offset, source in sources.items():
         owner = jnp.bitwise_xor(plane, offset)
         total = None
         for other in range(group):
@@ -376,7 +406,7 @@
                 )
             else:
                 weight = source[pl.ds(first, wide), :]
-            part = dot(heads_in[other][...], weight)
+            part = dot(rows_of(heads_in[other]), weight)
             total = part if total is None else total + part
         result = total.astype(BF16)
         lanes = pl.ds(pl.multiple_of(lax.rem(owner, side) * columns, columns), columns)
@@ -390,13 +420,13 @@
             send_ref[:, lanes] = result
 
 
-def project(heads, weights, planes):
+def project(heads, weights, planes, targets):
     group = len(heads)
-    rows = heads[0].shape[0]
+    rows = heads[0].shape[0] // group * len(targets)
     columns = weights[0].shape[1]
     shape = pltpu.VMEM((rows, columns * planes // 2), BF16)
     return pl.pallas_call(
-        functools.partial(project_kernel, group),
+        functools.partial(project_kernel, group, targets),
         out_shape=(shape, shape),
         in_specs=[VMEM] * (group + len(weights)),
         out_specs=(VMEM, VMEM),
@@ -405,23 +435,22 @@
     )(*held(*heads, *weights))
 
 
-def sum_kernel(group, keep_ref, other_ref, *outs):
-    position = lax.rem(lax.axis_index("seq"), group)
+def sum_kernel(keep_ref, other_ref, *outs):
     tokens = outs[0].shape[0]
-    for offset in range(group):
-        rows = pl.ds(pl.multiple_of(place(position, offset) * tokens, tokens), tokens)
-        outs[offset][...] = (
-            keep_ref[rows, :].astype(F32) + other_ref[rows, :].astype(F32)
-        ).astype(BF16)
-
-
-def sum_parts(keep, other, group):
+    for index, out_ref in enumerate(outs):
+        rows = slice(index * tokens, (index + 1) * tokens)
+        out_ref[...] = (keep_ref[rows, :].astype(F32) + other_ref[rows, :].astype(F32)).astype(
+            BF16
+        )
+
+
+def sum_parts(keep, other, count):
     rows, columns = keep.shape
     return pl.pallas_call(
-        functools.partial(sum_kernel, group),
-        out_shape=[pltpu.VMEM((rows // group, columns), BF16)] * group,
+        sum_kernel,
+        out_shape=[pltpu.VMEM((rows // count, columns), BF16)] * count,
         in_specs=[VMEM, VMEM],
-        out_specs=[VMEM] * group,
+        out_specs=[VMEM] * count,
         compiler_params=PARAMS,
         name="sum_parts",
     )(*held(keep, other))
@@ -512,8 +541,8 @@
             weights.append(lax.ppermute(out_weight, "seq", pairs))
 
     inverse, table = invert(keys, mine, tokens)
-    high, low, before, state, local_state = carry_state(keys, rests, inverse, table)
-    local, lifted = read(keys, rests, table, high, low, before)
+    high, low, steps, state, local_state = carry_state(keys, rests, inverse, table)
+    local, lifted = read(keys, rests, table, high, low, steps)
 
     def from_earlier(value, distance):
         pairs = [(i, i + distance * group) for i in range(count - distance * group)]
@@ -546,12 +575,17 @@
         gathered = [mixed_heads] + [
             swap(mixed_heads, group, offset, count) for offset in range(1, group)
         ]
-        send, keep = project(gathered, weights, planes)
-        other = lax.ppermute(send, "head", [(0, 1), (1, 0)])
-        parts = sum_parts(keep, other, group)
-        parts = [parts[0]] + [
-            swap(parts[offset], group, offset, count) for offset in range(1, group)
-        ]
+        order = tuple(reversed(range(group)))
+        order = order[:1] + order[2:-1] + order[1:2] + order[-1:] if group > 2 else order
+        parts = [None] * group
+        halves = []
+        for targets in (order[: group // 2], order[group // 2 :]):
+            send, keep = project(gathered, weights, planes, targets)
+            other = lax.ppermute(send, "head", [(0, 1), (1, 0)])
+            halves.append((targets, keep, other))
+        for targets, keep, other in halves:
+            for offset, part in zip(targets, sum_parts(keep, other, len(targets))):
+                parts[offset] = swap(part, group, offset, count) if offset else part
         return lay_out(parts, out_weight.shape[1])
 
     if group > 1:

time: 82.5 us -> 81.6 us (0.989)
    ppermute x1 -> x2, waiting for transfers between devices: 1.9 us -> 0.01 us  [per_device(): other = lax.ppermute(send, 'head', [(0, 1), (1, 0)])]
    pallas_call x1, Pallas kernels: 6.55 us -> 5.4 us  [invert(): pl.pallas_call(functools.partial(invert_kernel, heads, tokens), out_shape...]
    ppermute x12, waiting for transfers between devices: 18.7 us -> 19.8 us  [swap(): return lax.ppermute(value, 'seq', pairs)]
    pallas_call x2 -> x4, Pallas kernels: 2.98 us -> 3.59 us  [the longest x2 3.46 us: project(): pl.pallas_call(functools.partial(project_kernel, group, targets), out_sha...]
  transfers between devices with their start and end apart: 20 -> 21, of which waited for: 8 -> 8; matrix products, arithmetic and copies ran while one was open for 3% -> 3% of each run, Pallas kernels for 19% -> 20%
where the time goes in v2:
time: 81.6 us; the launch traced here: 81.3 us
  starting transfers between devices  32 us (39%)
  waiting for transfers between devices  28.4 us (35%)
  Pallas kernels  18.5 us (23%)
  local copies, waits for them, and re-layouts  1.29 us (2%)
  other arithmetic  0.83 us (1%)
    ppermute x12, waiting for transfers between devices, swap(): return lax.ppermute(value, 'seq', pairs)  19.8 us
    ppermute x12, starting transfers between devices, swap(): return lax.ppermute(value, 'seq', pairs)  15.4 us
    ppermute x2, waiting for transfers between devices, per_device(): weights.append(lax.ppermute(out_weight, 'seq', pairs))  8.53 us
    ppermute x3, starting transfers between devices, from_earlier(): return lax.ppermute(value, 'seq', pairs)  8.52 us
    ppermute x2, starting transfers between devices, per_device(): weights.append(lax.ppermute(out_weight, 'seq', pairs))  5.53 us
    pallas_call x1, Pallas kernels, invert(): pl.pallas_call(functools.partial(invert_kernel, heads, tokens), out_shape...  5.4 us
    pallas_call x1, Pallas kernels, carry_state(): pl.pallas_call(functools.partial(state_kernel, group), out_shape=(solved,...  4.78 us
    pallas_call x2, Pallas kernels, project(): pl.pallas_call(functools.partial(project_kernel, group, targets), out_sha...  3.46 us
  transfers between devices with their start and end apart: 21, of which 8 were waited for; matrix products, arithmetic and copies ran while one was open for 3% of the time, Pallas kernels for 20%

profile of v2, /device:TPU:0, one launch (start us, length us, event | category | flops | bytes accessed | tf_op | source)
XLA Modules:
  0.0 81.3 jit_solution(5262862173640668236)
XLA Ops:
  0.0 3.1 %collective-permute-start.12 = (bf16[1024,256]{1,0:T(8,128)(2,1)}, bf16[1024,256]{1,0:T(8,128)(2,1)S(1)}, u32[]{:S(2)}, u32[]{:S(2)}) collective-permute-start(bf16[1024,256]{1,0:T(8,128)(2,1)} %refs_4_.3), channel_id=1, source_target_pairs={{0,8},{2,10},{4,12},{6,14},{8,0},{10,2},{12,4},{14,6},{16,24},{18,... | collective-permute-start | bytes 1572872 | tf_op jit(solution)/shard_map/ppermute | solution.py:541
  3.1 2.5 %collective-permute-start.13 = (bf16[1024,256]{1,0:T(8,128)(2,1)}, bf16[1024,256]{1,0:T(8,128)(2,1)S(1)}, u32[]{:S(2)}, u32[]{:S(2)}) collective-permute-start(bf16[1024,256]{1,0:T(8,128)(2,1)} %refs_4_.3), channel_id=1, source_target_pairs={{0,24},{2,26},{4,28},{6,30},{8,16},{10,18},{12,20},{14,22},{16,8},... | collective-permute-start | bytes 1572872 | tf_op jit(solution)/shard_map/ppermute | solution.py:541
  7.5 1.6 %collective-permute-start = (bf16[272,256]{1,0:T(8,128)(2,1)S(1)}, bf16[272,256]{1,0:T(8,128)(2,1)S(1)}, u32[]{:S(2)}, u32[]{:S(2)}) collective-permute-start(bf16[272,256]{1,0:T(8,128)(2,1)S(1)} %get-tuple-element.41), channel_id=1, source_target_pairs={{0,2},{2,0},{4,6},{6,4},{8,10},{10,8},{12,14},{14,12},{16,18},{18,... | collective-permute-start | bytes 417800 | tf_op jit(solution)/shard_map/ppermute | solution.py:495
  9.1 1.5 %collective-permute-start.1 = (bf16[272,256]{1,0:T(8,128)(2,1)S(1)}, bf16[272,256]{1,0:T(8,128)(2,1)S(1)}, u32[]{:S(2)}, u32[]{:S(2)}) collective-permute-start(bf16[272,256]{1,0:T(8,128)(2,1)S(1)} %get-tuple-element.40), channel_id=1, source_target_pairs={{0,4},{2,6},{4,0},{6,2},{8,12},{10,14},{12,8},{14,10},{16,20},{18,... | collective-permute-start | bytes 417800 | tf_op jit(solution)/shard_map/ppermute | solution.py:495
  11.3 2.1 %collective-permute-done.refs_1_ = bf16[272,256]{1,0:T(8,128)(2,1)S(1)} collective-permute-done((bf16[272,256]{1,0:T(8,128)(2,1)S(1)}, bf16[272,256]{1,0:T(8,128)(2,1)S(1)}, u32[]{:S(2)}, u32[]{:S(2)}) %collective-permute-start) | collective-permute-done | bytes 139296 | tf_op jit(solution)/shard_map/ppermute | solution.py:495
  13.4 2.2 %collective-permute-start.3 = (bf16[3,128,256]{2,1,0:T(8,128)(2,1)S(1)}, bf16[3,128,256]{2,1,0:T(8,128)(2,1)S(1)}, u32[]{:S(2)}, u32[]{:S(2)}) collective-permute-start(bf16[3,128,256]{2,1,0:T(8,128)(2,1)S(1)} %pad_maximum_fusion.1), channel_id=1, source_target_pairs={{0,2},{2,0},{4,6},{6,4},{8,10},{10,8},{12,14},{14,12},{16,18},{18,... | collective-permute-start | bytes 589832 | tf_op jit(solution)/shard_map/ppermute | solution.py:495
  15.6 1.4 %collective-permute-done.1.refs_2_ = bf16[272,256]{1,0:T(8,128)(2,1)S(1)} collective-permute-done((bf16[272,256]{1,0:T(8,128)(2,1)S(1)}, bf16[272,256]{1,0:T(8,128)(2,1)S(1)}, u32[]{:S(2)}, u32[]{:S(2)}) %collective-permute-start.1) | collective-permute-done | bytes 139296 | tf_op jit(solution)/shard_map/ppermute | solution.py:495
  17.0 1.7 %collective-permute-start.4 = (bf16[3,128,256]{2,1,0:T(8,128)(2,1)S(1)}, bf16[3,128,256]{2,1,0:T(8,128)(2,1)S(1)}, u32[]{:S(2)}, u32[]{:S(2)}) collective-permute-start(bf16[3,128,256]{2,1,0:T(8,128)(2,1)S(1)} %pad_maximum_fusion.2), channel_id=1, source_target_pairs={{0,4},{2,6},{4,0},{6,2},{8,12},{10,14},{12,8},{14,10},{16,20},{18,... | collective-permute-start | bytes 589832 | tf_op jit(solution)/shard_map/ppermute | solution.py:495
  20.2 8.5 %collective-permute-done.13.refs_6_ = bf16[1024,256]{1,0:T(8,128)(2,1)S(1)} collective-permute-done((bf16[1024,256]{1,0:T(8,128)(2,1)}, bf16[1024,256]{1,0:T(8,128)(2,1)S(1)}, u32[]{:S(2)}, u32[]{:S(2)}) %collective-permute-start.13) | collective-permute-done | bytes 524320 | tf_op jit(solution)/shard_map/ppermute | solution.py:541
  30.0 5.4 %invert.1 = (f32[2,4,3,128,128]{4,3,2,1,0:T(8,128)S(1)}, f32[2,4,8,256]{3,2,1,0:T(8,128)S(1)}) custom-call(bf16[272,256]{1,0:T(8,128)(2,1)S(1)} %get-tuple-element.42.refs_0_, bf16[272,256]{1,0:T(8,128)(2,1)S(1)} %collective-permute-done.refs_1_, bf16[272,256]{1,0:T(8,128)(2,1)S(1)} %collective-permute-done.1.refs_2_, ...), custom_call_target="tpu_custom_call" | custom-call | tf_op jit(solution)/shard_map/invert/pallas_call | solution.py:173
  35.5 4.8 %carry_state.1 = (bf16[2,4,256,256]{3,2,1,0:T(8,128)(2,1)S(1)}, bf16[2,4,256,256]{3,2,1,0:T(8,128)(2,1)S(1)}, f32[2,4,128,256]{3,2,1,0:T(8,128)S(1)}, bf16[2,128...) custom-call(bf16[272,256]{1,0:T(8,128)(2,1)S(1)} %get-tuple-element.42.refs_0_, ...), custom_call_target="tpu_custom_call" | custom-call | tf_op jit(solution)/shard_map/carry_state/pallas_call | solution.py:261
  40.2 4.6 %collective-permute-start.6 = (bf16[2,128,256]{2,1,0:T(8,128)(2,1)S(1)}, bf16[2,128,256]{2,1,0:T(8,128)(2,1)S(1)}, u32[]{:S(2)}, u32[]{:S(2)}) collective-permute-start(bf16[2,128,256]{2,1,0:T(8,128)(2,1)S(1)} %get-tuple-element.24), channel_id=1, source_target_pairs={{0,8},{2,10},{4,12},{6,14},{8,16},{10,18},{12,20},{14,22},{16,24},... | collective-permute-start | bytes 393224 | tf_op jit(solution)/shard_map/ppermute | solution.py:549
  44.8 2.6 %collective-permute-start.7 = (bf16[2,128,256]{2,1,0:T(8,128)(2,1)S(1)}, bf16[2,128,256]{2,1,0:T(8,128)(2,1)S(1)}, u32[]{:S(2)}, u32[]{:S(2)}) collective-permute-start(bf16[2,128,256]{2,1,0:T(8,128)(2,1)S(1)} %get-tuple-element.24), channel_id=1, source_target_pairs={{0,16},{2,18},{4,20},{6,22},{8,24},{10,26},{12,28},{14,30},{1,17},... | collective-permute-start | bytes 393224 | tf_op jit(solution)/shard_map/ppermute | solution.py:549
  48.8 3.4 %read.1 = (f32[512,256]{1,0:T(8,128)S(1)}, bf16[512,256]{1,0:T(8,128)(2,1)S(1)}) custom-call(bf16[272,256]{1,0:T(8,128)(2,1)S(1)} %get-tuple-element.42.refs_0_, bf16[272,256]{1,0:T(8,128)(2,1)S(1)} %collective-permute-done.refs_1_, bf16[272,256]{1,0:T(8,128)(2,1)S(1)} %collective-permute-done.1.refs_2_, ...), custom_call_target="tpu_custom_call" | custom-call | tf_op jit(solution)/shard_map/read/pallas_call | solution.py:329
  52.8 1.6 %collective-permute-start.10 = (bf16[512,256]{1,0:T(8,128)(2,1)S(1)}, bf16[512,256]{1,0:T(8,128)(2,1)S(1)}, u32[]{:S(2)}, u32[]{:S(2)}) collective-permute-start(bf16[512,256]{1,0:T(8,128)(2,1)S(1)} %join.1.refs_0_), channel_id=1, source_target_pairs={{0,4},{2,6},{4,0},{6,2},{8,12},{10,14},{12,8},{14,10},{16,20},{18,... | collective-permute-start | bytes 786440 | tf_op jit(solution)/shard_map/ppermute | solution.py:495
  54.4 1.4 %collective-permute-start.11 = (bf16[512,256]{1,0:T(8,128)(2,1)S(1)}, bf16[512,256]{1,0:T(8,128)(2,1)S(1)}, u32[]{:S(2)}, u32[]{:S(2)}) collective-permute-start(bf16[512,256]{1,0:T(8,128)(2,1)S(1)} %join.1.refs_0_), channel_id=1, source_target_pairs={{0,6},{2,4},{4,2},{6,0},{8,14},{10,12},{12,10},{14,8},{16,22},{18,... | collective-permute-start | bytes 786440 | tf_op jit(solution)/shard_map/ppermute | solution.py:495
  56.3 7.9 %collective-permute-done.10.refs_2_ = bf16[512,256]{1,0:T(8,128)(2,1)S(1)} collective-permute-done((bf16[512,256]{1,0:T(8,128)(2,1)S(1)}, bf16[512,256]{1,0:T(8,128)(2,1)S(1)}, u32[]{:S(2)}, u32[]{:S(2)}) %collective-permute-start.10) | collective-permute-done | bytes 262176 | tf_op jit(solution)/shard_map/ppermute | solution.py:495
  65.4 1.7 %project.3 = (bf16[256,512]{1,0:T(8,128)(2,1)S(1)}, bf16[256,512]{1,0:T(8,128)(2,1)S(1)}) custom-call(bf16[512,256]{1,0:T(8,128)(2,1)S(1)} %join.1.refs_0_, bf16[512,256]{1,0:T(8,128)(2,1)S(1)} %collective-permute-done.9.refs_1_, bf16[512,256]{1,0:T(8,128)(2,1)S(1)} %collective-permute-done.10.refs_2_, bf16[512,256]{1,0:T(8,128)(2,1)S(1)} %collective-permute-done.11.refs_3_, ...), custom_call_target="tpu_custom_call" | custom-call | tf_op jit(solution)/shard_map/project/pallas_call | solution.py:428
  67.2 1.7 %project.2 = (bf16[256,512]{1,0:T(8,128)(2,1)S(1)}, bf16[256,512]{1,0:T(8,128)(2,1)S(1)}) custom-call(bf16[512,256]{1,0:T(8,128)(2,1)S(1)} %join.1.refs_0_, bf16[512,256]{1,0:T(8,128)(2,1)S(1)} %collective-permute-done.9.refs_1_, bf16[512,256]{1,0:T(8,128)(2,1)S(1)} %collective-permute-done.10.refs_2_, bf16[512,256]{1,0:T(8,128)(2,1)S(1)} %collective-permute-done.11.refs_3_, ...), custom_call_target="tpu_custom_call" | custom-call | tf_op jit(solution)/shard_map/project/pallas_call | solution.py:428
  69.6 1.5 %collective-permute-start.18 = (bf16[128,512]{1,0:T(8,128)(2,1)S(1)}, bf16[128,512]{1,0:T(8,128)(2,1)S(1)}, u32[]{:S(2)}, u32[]{:S(2)}) collective-permute-start(bf16[128,512]{1,0:T(8,128)(2,1)S(1)} %get-tuple-element.36), channel_id=1, source_target_pairs={{0,2},{2,0},{4,6},{6,4},{8,10},{10,8},{12,14},{14,12},{16,18},{18,... | collective-permute-start | bytes 393224 | tf_op jit(solution)/shard_map/ppermute | solution.py:495
  71.2 1.5 %collective-permute-start.20 = (bf16[128,512]{1,0:T(8,128)(2,1)S(1)}, bf16[128,512]{1,0:T(8,128)(2,1)S(1)}, u32[]{:S(2)}, u32[]{:S(2)}) collective-permute-start(bf16[128,512]{1,0:T(8,128)(2,1)S(1)} %get-tuple-element.38), channel_id=1, source_target_pairs={{0,6},{2,4},{4,2},{6,0},{8,14},{10,12},{12,10},{14,8},{16,22},{18,... | collective-permute-start | bytes 393224 | tf_op jit(solution)/shard_map/ppermute | solution.py:495
  73.3 2.4 %collective-permute-done.18.refs_1_ = bf16[128,512]{1,0:T(8,128)(2,1)S(1)} collective-permute-done((bf16[128,512]{1,0:T(8,128)(2,1)S(1)}, bf16[128,512]{1,0:T(8,128)(2,1)S(1)}, u32[]{:S(2)}, u32[]{:S(2)}) %collective-permute-start.18) | collective-permute-done | bytes 131104 | tf_op jit(solution)/shard_map/ppermute | solution.py:495
  75.7 3.2 %collective-permute-done.20.refs_3_ = bf16[128,512]{1,0:T(8,128)(2,1)S(1)} collective-permute-done((bf16[128,512]{1,0:T(8,128)(2,1)S(1)}, bf16[128,512]{1,0:T(8,128)(2,1)S(1)}, u32[]{:S(2)}, u32[]{:S(2)}) %collective-permute-start.20) | collective-permute-done | bytes 131104 | tf_op jit(solution)/shard_map/ppermute | solution.py:495
  79.0 1.5 %collective-permute-done.19.refs_2_ = bf16[128,512]{1,0:T(8,128)(2,1)S(1)} collective-permute-done((bf16[128,512]{1,0:T(8,128)(2,1)S(1)}, bf16[128,512]{1,0:T(8,128)(2,1)S(1)}, u32[]{:S(2)}, u32[]{:S(2)}) %collective-permute-start.19) | collective-permute-done | bytes 131104 | tf_op jit(solution)/shard_map/ppermute | solution.py:495
  (45 shorter events, 11.1 us)
Async XLA Ops:
  0.0 19.5 %collective-permute-start.12 = (bf16[1024,256]{1,0:T(8,128)(2,1)}, bf16[1024,256]{1,0:T(8,128)(2,1)S(1)}, u32[]{:S(2)}, u32[]{:S(2)}) collective-permute-start(bf16[1024,256]{1,0:T(8,128)(2,1)} %refs_4_.3), channel_id=1, source_target_pairs={{0,8},{2,10},{4,12},{6,14},{8,0},{10,2},{12,4},{14,6},{16,24},{18,... | collective-permute-start | bytes 1572872 | tf_op jit(solution)/shard_map/ppermute | solution.py:541
  3.1 25.7 %collective-permute-start.13 = (bf16[1024,256]{1,0:T(8,128)(2,1)}, bf16[1024,256]{1,0:T(8,128)(2,1)S(1)}, u32[]{:S(2)}, u32[]{:S(2)}) collective-permute-start(bf16[1024,256]{1,0:T(8,128)(2,1)} %refs_4_.3), channel_id=1, source_target_pairs={{0,24},{2,26},{4,28},{6,30},{8,16},{10,18},{12,20},{14,22},{16,8},... | collective-permute-start | bytes 1572872 | tf_op jit(solution)/shard_map/ppermute | solution.py:541
  7.3 3.7 %copy-start.1 = (bf16[2,128,1024]{2,1,0:T(8,128)(2,1)S(1)}, bf16[2,128,1024]{2,1,0:T(8,128)(2,1)}, u32[]{:S(2)}) copy-start(bf16[2,128,1024]{2,1,0:T(8,128)(2,1)} %param.7) | copy-start | bytes 1572868
  7.4 3.7 %copy-start.2 = (bf16[128,1024]{1,0:T(8,128)(2,1)S(1)}, bf16[128,1024]{1,0:T(8,128)(2,1)}, u32[]{:S(2)}) copy-start(bf16[128,1024]{1,0:T(8,128)(2,1)} %param.5) | copy-start | bytes 786436
  7.5 5.9 %collective-permute-start = (bf16[272,256]{1,0:T(8,128)(2,1)S(1)}, bf16[272,256]{1,0:T(8,128)(2,1)S(1)}, u32[]{:S(2)}, u32[]{:S(2)}) collective-permute-start(bf16[272,256]{1,0:T(8,128)(2,1)S(1)} %get-tuple-element.41), channel_id=1, source_target_pairs={{0,2},{2,0},{4,6},{6,4},{8,10},{10,8},{12,14},{14,12},{16,18},{18,... | collective-permute-start | bytes 417800 | tf_op jit(solution)/shard_map/ppermute | solution.py:495
  9.1 8.0 %collective-permute-start.1 = (bf16[272,256]{1,0:T(8,128)(2,1)S(1)}, bf16[272,256]{1,0:T(8,128)(2,1)S(1)}, u32[]{:S(2)}, u32[]{:S(2)}) collective-permute-start(bf16[272,256]{1,0:T(8,128)(2,1)S(1)} %get-tuple-element.40), channel_id=1, source_target_pairs={{0,4},{2,6},{4,0},{6,2},{8,12},{10,14},{12,8},{14,10},{16,20},{18,... | collective-permute-start | bytes 417800 | tf_op jit(solution)/shard_map/ppermute | solution.py:495
  10.6 8.2 %collective-permute-start.2 = (bf16[272,256]{1,0:T(8,128)(2,1)S(1)}, bf16[272,256]{1,0:T(8,128)(2,1)S(1)}, u32[]{:S(2)}, u32[]{:S(2)}) collective-permute-start(bf16[272,256]{1,0:T(8,128)(2,1)S(1)} %get-tuple-element.39), channel_id=1, source_target_pairs={{0,6},{2,4},{4,2},{6,0},{8,14},{10,12},{12,10},{14,8},{16,22},{18,... | collective-permute-start | bytes 417800 | tf_op jit(solution)/shard_map/ppermute | solution.py:495
  13.4 22.0 %collective-permute-start.3 = (bf16[3,128,256]{2,1,0:T(8,128)(2,1)S(1)}, bf16[3,128,256]{2,1,0:T(8,128)(2,1)S(1)}, u32[]{:S(2)}, u32[]{:S(2)}) collective-permute-start(bf16[3,128,256]{2,1,0:T(8,128)(2,1)S(1)} %pad_maximum_fusion.1), channel_id=1, source_target_pairs={{0,2},{2,0},{4,6},{6,4},{8,10},{10,8},{12,14},{14,12},{16,18},{18,... | collective-permute-start | bytes 589832 | tf_op jit(solution)/shard_map/ppermute | solution.py:495
  17.0 18.4 %collective-permute-start.4 = (bf16[3,128,256]{2,1,0:T(8,128)(2,1)S(1)}, bf16[3,128,256]{2,1,0:T(8,128)(2,1)S(1)}, u32[]{:S(2)}, u32[]{:S(2)}) collective-permute-start(bf16[3,128,256]{2,1,0:T(8,128)(2,1)S(1)} %pad_maximum_fusion.2), channel_id=1, source_target_pairs={{0,4},{2,6},{4,0},{6,2},{8,12},{10,14},{12,8},{14,10},{16,20},{18,... | collective-permute-start | bytes 589832 | tf_op jit(solution)/shard_map/ppermute | solution.py:495
  18.8 16.7 %collective-permute-start.5 = (bf16[3,128,256]{2,1,0:T(8,128)(2,1)S(1)}, bf16[3,128,256]{2,1,0:T(8,128)(2,1)S(1)}, u32[]{:S(2)}, u32[]{:S(2)}) collective-permute-start(bf16[3,128,256]{2,1,0:T(8,128)(2,1)S(1)} %pad_maximum_fusion.3), channel_id=1, source_target_pairs={{0,6},{2,4},{4,2},{6,0},{8,14},{10,12},{12,10},{14,8},{16,22},{18,... | collective-permute-start | bytes 589832 | tf_op jit(solution)/shard_map/ppermute | solution.py:495
  19.5 45.9 %collective-permute-start.14 = (bf16[1024,256]{1,0:T(8,128)(2,1)S(1)}, bf16[1024,256]{1,0:T(8,128)(2,1)S(1)}, u32[]{:S(2)}, u32[]{:S(2)}) collective-permute-start(bf16[1024,256]{1,0:T(8,128)(2,1)S(1)} %collective-permute-done.12.refs_5_), channel_id=1, source_target_pairs={{8,16},{10,18},{12,20},{14,22},{16,8},{18,10},{20,12},{22,14},{9,1... | collective-permute-start | bytes 1572872 | tf_op jit(solution)/shard_map/ppermute | solution.py:570
  28.7 36.7 %collective-permute-start.15 = (bf16[1024,256]{1,0:T(8,128)(2,1)S(1)}, bf16[1024,256]{1,0:T(8,128)(2,1)S(1)}, u32[]{:S(2)}, u32[]{:S(2)}) collective-permute-start(bf16[1024,256]{1,0:T(8,128)(2,1)S(1)} %collective-permute-done.13.refs_6_), channel_id=1, source_target_pairs={{8,0},{10,2},{12,4},{14,6},{16,24},{18,26},{20,28},{22,30},{9,1},{... | collective-permute-start | bytes 1572872 | tf_op jit(solution)/shard_map/ppermute | solution.py:570
  40.2 12.0 %collective-permute-start.6 = (bf16[2,128,256]{2,1,0:T(8,128)(2,1)S(1)}, bf16[2,128,256]{2,1,0:T(8,128)(2,1)S(1)}, u32[]{:S(2)}, u32[]{:S(2)}) collective-permute-start(bf16[2,128,256]{2,1,0:T(8,128)(2,1)S(1)} %get-tuple-element.24), channel_id=1, source_target_pairs={{0,8},{2,10},{4,12},{6,14},{8,16},{10,18},{12,20},{14,22},{16,24},... | collective-permute-start | bytes 393224 | tf_op jit(solution)/shard_map/ppermute | solution.py:549
  44.8 7.4 %collective-permute-start.7 = (bf16[2,128,256]{2,1,0:T(8,128)(2,1)S(1)}, bf16[2,128,256]{2,1,0:T(8,128)(2,1)S(1)}, u32[]{:S(2)}, u32[]{:S(2)}) collective-permute-start(bf16[2,128,256]{2,1,0:T(8,128)(2,1)S(1)} %get-tuple-element.24), channel_id=1, source_target_pairs={{0,16},{2,18},{4,20},{6,22},{8,24},{10,26},{12,28},{14,30},{1,17},... | collective-permute-start | bytes 393224 | tf_op jit(solution)/shard_map/ppermute | solution.py:549
  47.5 4.7 %collective-permute-start.8 = (bf16[2,128,128]{2,1,0:T(8,128)(2,1)S(1)}, bf16[2,128,128]{2,1,0:T(8,128)(2,1)S(1)}, u32[]{:S(2)}, u32[]{:S(2)}) collective-permute-start(bf16[2,128,128]{2,1,0:T(8,128)(2,1)S(1)} %get-tuple-element.25), channel_id=1, source_target_pairs={{0,24},{2,26},{4,28},{6,30},{1,25},{3,27},{5,29},{7,31}} | collective-permute-start | bytes 196616 | tf_op jit(solution)/shard_map/ppermute | solution.py:549
  52.2 13.2 %copy-start = (bf16[1024,256]{1,0:T(8,128)(2,1)S(1)}, bf16[1024,256]{1,0:T(8,128)(2,1)}, u32[]{:S(2)}) copy-start(bf16[1024,256]{1,0:T(8,128)(2,1)} %refs_4_.3) | copy-start | bytes 1572868
  52.8 11.4 %collective-permute-start.10 = (bf16[512,256]{1,0:T(8,128)(2,1)S(1)}, bf16[512,256]{1,0:T(8,128)(2,1)S(1)}, u32[]{:S(2)}, u32[]{:S(2)}) collective-permute-start(bf16[512,256]{1,0:T(8,128)(2,1)S(1)} %join.1.refs_0_), channel_id=1, source_target_pairs={{0,4},{2,6},{4,0},{6,2},{8,12},{10,14},{12,8},{14,10},{16,20},{18,... | collective-permute-start | bytes 786440 | tf_op jit(solution)/shard_map/ppermute | solution.py:495
  54.4 9.8 %collective-permute-start.11 = (bf16[512,256]{1,0:T(8,128)(2,1)S(1)}, bf16[512,256]{1,0:T(8,128)(2,1)S(1)}, u32[]{:S(2)}, u32[]{:S(2)}) collective-permute-start(bf16[512,256]{1,0:T(8,128)(2,1)S(1)} %join.1.refs_0_), channel_id=1, source_target_pairs={{0,6},{2,4},{4,2},{6,0},{8,14},{10,12},{12,10},{14,8},{16,22},{18,... | collective-permute-start | bytes 786440 | tf_op jit(solution)/shard_map/ppermute | solution.py:495
  55.8 9.6 %collective-permute-start.9 = (bf16[512,256]{1,0:T(8,128)(2,1)S(1)}, bf16[512,256]{1,0:T(8,128)(2,1)S(1)}, u32[]{:S(2)}, u32[]{:S(2)}) collective-permute-start(bf16[512,256]{1,0:T(8,128)(2,1)S(1)} %join.1.refs_0_), channel_id=1, source_target_pairs={{0,2},{2,0},{4,6},{6,4},{8,10},{10,8},{12,14},{14,12},{16,18},{18,... | collective-permute-start | bytes 786440 | tf_op jit(solution)/shard_map/ppermute | solution.py:495
  67.2 2.4 %collective-permute-start.17 = (bf16[256,512]{1,0:T(8,128)(2,1)S(1)}, bf16[256,512]{1,0:T(8,128)(2,1)S(1)}, u32[]{:S(2)}, u32[]{:S(2)}) collective-permute-start(bf16[256,512]{1,0:T(8,128)(2,1)S(1)} %get-tuple-element.35), channel_id=1, source_target_pairs={{0,1},{1,0},{2,3},{3,2},{4,5},{5,4},{6,7},{7,6},{8,9},{9,8},{10,11... | collective-permute-start | bytes 786440 | tf_op jit(solution)/shard_map/ppermute | solution.py:584
  69.0 3.7 %collective-permute-start.16 = (bf16[256,512]{1,0:T(8,128)(2,1)S(1)}, bf16[256,512]{1,0:T(8,128)(2,1)S(1)}, u32[]{:S(2)}, u32[]{:S(2)}) collective-permute-start(bf16[256,512]{1,0:T(8,128)(2,1)S(1)} %get-tuple-element.32), channel_id=1, source_target_pairs={{0,1},{1,0},{2,3},{3,2},{4,5},{5,4},{6,7},{7,6},{8,9},{9,8},{10,11... | collective-permute-start | bytes 786440 | tf_op jit(solution)/shard_map/ppermute | solution.py:584
  69.6 6.1 %collective-permute-start.18 = (bf16[128,512]{1,0:T(8,128)(2,1)S(1)}, bf16[128,512]{1,0:T(8,128)(2,1)S(1)}, u32[]{:S(2)}, u32[]{:S(2)}) collective-permute-start(bf16[128,512]{1,0:T(8,128)(2,1)S(1)} %get-tuple-element.36), channel_id=1, source_target_pairs={{0,2},{2,0},{4,6},{6,4},{8,10},{10,8},{12,14},{14,12},{16,18},{18,... | collective-permute-start | bytes 393224 | tf_op jit(solution)/shard_map/ppermute | solution.py:495
  71.2 7.8 %collective-permute-start.20 = (bf16[128,512]{1,0:T(8,128)(2,1)S(1)}, bf16[128,512]{1,0:T(8,128)(2,1)S(1)}, u32[]{:S(2)}, u32[]{:S(2)}) collective-permute-start(bf16[128,512]{1,0:T(8,128)(2,1)S(1)} %get-tuple-element.38), channel_id=1, source_target_pairs={{0,6},{2,4},{4,2},{6,0},{8,14},{10,12},{12,10},{14,8},{16,22},{18,... | collective-permute-start | bytes 393224 | tf_op jit(solution)/shard_map/ppermute | solution.py:495
  72.7 7.7 %collective-permute-start.19 = (bf16[128,512]{1,0:T(8,128)(2,1)S(1)}, bf16[128,512]{1,0:T(8,128)(2,1)S(1)}, u32[]{:S(2)}, u32[]{:S(2)}) collective-permute-start(bf16[128,512]{1,0:T(8,128)(2,1)S(1)} %get-tuple-element.37), channel_id=1, source_target_pairs={{0,4},{2,6},{4,0},{6,2},{8,12},{10,14},{12,8},{14,10},{16,20},{18,... | collective-permute-start | bytes 393224 | tf_op jit(solution)/shard_map/ppermute | solution.py:495

commit v3 on v2

--- a/solution.py
+++ b/solution.py
@@ -98,10 +98,7 @@
     def prepare(head, index):
         lanes = lanes_of(head, width)
         key_ref, first = key_in[index // per_source], (index % per_source) * chunk
-        key = weave(
-            key_ref[first : first + chunk, lanes],
-            key_ref[tokens + first : tokens + first + chunk, lanes],
-        )
+        key = woven_key(key_ref, tokens, first, chunk, lanes)
         gram = dot_t(key, key)
         wide_row, wide_col = iota(gram.shape, 0), iota(gram.shape, 1)
         square = jnp.sum(jnp.where(wide_row == wide_col, gram, 0.0), axis=0, keepdims=True)
@@ -150,15 +147,7 @@
         for (head, index), value in zip(units, inner):
             inverse_ref[head, index, 2] = -product3(inverse_ref[head, index, 1], value)
 
-    if heads * chunks <= 8:
-        solve([(head, index) for head in range(heads) for index in range(chunks)])
-    else:
-
-        def one_head(head, carry):
-            solve([(head, index) for index in range(chunks)])
-            return carry
-
-        lax.fori_loop(0, heads, one_head, 0)
+    every_unit(heads, chunks, solve)
 
 
 def lanes_of(head, width):
@@ -189,48 +178,71 @@
     return place(position, index // per_source) * per_source + index % per_source
 
 
-def state_kernel(group, *refs):
+def every_unit(heads, chunks, body):
+    if heads * chunks <= 8:
+        body([(head, index) for head in range(heads) for index in range(chunks)])
+    else:
+
+        def one_head(head, carry):
+            body([(head, index) for index in range(chunks)])
+            return carry
+
+        lax.fori_loop(0, heads, one_head, 0)
+
+
+def woven_key(key_ref, tokens, first, chunk, lanes):
+    return weave(
+        key_ref[first : first + chunk, lanes],
+        key_ref[tokens + first : tokens + first + chunk, lanes],
+    )
+
+
+def state_kernel(group, parts, *refs):
     key_in, rest_in = refs[:group], refs[group : 2 * group]
-    inverse_ref, table_ref = refs[2 * group : 2 * group + 2]
-    high_ref, low_ref, step_ref, state_ref, local_ref = refs[2 * group + 2 :]
-    heads, chunks, _, chunk, _ = inverse_ref.shape
+    inverse_in = refs[2 * group : 2 * group + parts]
+    table_in = refs[2 * group + parts : 2 * group + 2 * parts]
+    high_ref, low_ref, step_ref, state_ref, local_ref = refs[2 * group + 2 * parts :]
+    heads, per_part, _, chunk, _ = inverse_in[0].shape
+    chunks = parts * per_part
     tokens = rest_in[0].shape[1]
     width = rest_in[0].shape[2] // heads
     per_source = tokens // chunk
 
-    def one_head(head, carry):
-        lanes = pl.ds(pl.multiple_of(head * width, width), width)
-        for index in range(chunks):
+    def solve(units):
+        for head, index in units:
+            lanes = lanes_of(head, width)
+            part, inside = index // per_part, index % per_part
             source, first = index // per_source, (index % per_source) * chunk
             key_ref, rest_ref = key_in[source], rest_in[source]
-            key = weave(
-                key_ref[first : first + chunk, lanes],
-                key_ref[tokens + first : tokens + first + chunk, lanes],
-            ).astype(F32)
+            key = woven_key(key_ref, tokens, first, chunk, lanes).astype(F32)
             rows = slice(first, first + chunk)
             value = weave(rest_ref[0, rows, lanes], rest_ref[1, rows, lanes]).astype(F32)
-            table = table_ref[head, index].T
+            table = table_in[part][head, inside].T
             inverse = jnp.concatenate(
                 [
                     jnp.concatenate(
-                        [inverse_ref[head, index, 0], jnp.zeros((chunk, chunk), F32)], axis=1
+                        [inverse_in[part][head, inside, 0], jnp.zeros((chunk, chunk), F32)],
+                        axis=1,
                     ),
                     jnp.concatenate(
-                        [inverse_ref[head, index, 2], inverse_ref[head, index, 1]], axis=1
+                        [inverse_in[part][head, inside, 2], inverse_in[part][head, inside, 1]],
+                        axis=1,
                     ),
                 ],
                 axis=0,
             )
             right = jnp.concatenate([table[:, 2:3] * key, table[:, 1:2] * value], axis=1)
-            high, low = split(dot3(inverse, *split(right)))
+            high, low = split(table[:, 0:1] * dot3(inverse, *split(right)))
             high_ref[head, index] = high
             low_ref[head, index] = low
-            step_ref[head, slot_of(group, index, per_source)] = dot3(
-                (table[:, 0:1] * key).T, high, low
-            )
-        return carry
-
-    lax.fori_loop(0, heads, one_head, 0)
+        for head, index in units:
+            source, first = index // per_source, (index % per_source) * chunk
+            turned = woven_key(key_in[source], tokens, first, chunk, lanes_of(head, width)).T
+            step_ref[head, slot_of(group, index, per_source)] = dot(
+                turned, high_ref[head, index]
+            ) + dot(turned, low_ref[head, index])
+
+    every_unit(heads, chunks, solve)
     totals = [[step_ref[head, slot] for slot in range(chunks)] for head in range(heads)]
     while len(totals[0]) > 1:
         totals = [
@@ -253,13 +265,14 @@
     return dot(left_high, high) + dot(left_low, high) + dot(left_high, low)
 
 
-def carry_state(keys, rests, inverse, table):
-    group = len(keys)
-    heads, chunks, _, chunk, _ = inverse.shape
+def carry_state(keys, rests, inverses, tables):
+    group, parts = len(keys), len(inverses)
+    heads, per_part, _, chunk, _ = inverses[0].shape
+    chunks = parts * per_part
     width = rests[0].shape[2] // heads
     solved = pltpu.VMEM((heads, chunks, 2 * chunk, 2 * width), BF16)
     return pl.pallas_call(
-        functools.partial(state_kernel, group),
+        functools.partial(state_kernel, group, parts),
         out_shape=(
             solved,
             solved,
@@ -267,17 +280,17 @@
             pltpu.VMEM((heads, width, 2 * width), BF16),
             pltpu.VMEM((heads, width, width), BF16),
         ),
-        in_specs=[VMEM] * (2 * group + 2),
+        in_specs=[VMEM] * (2 * group + 2 * parts),
         out_specs=(VMEM,) * 5,
         compiler_params=PARAMS,
         name="carry_state",
-    )(*held(*keys, *rests, inverse, table))
+    )(*held(*keys, *rests, *inverses, *tables))
 
 
 def read_kernel(group, *refs):
     key_in, rest_in = refs[:group], refs[group : 2 * group]
-    table_ref, high_ref, low_ref, step_ref, out_ref, lift_ref, before_buf = refs[2 * group :]
-    heads, chunks, _, wide = table_ref.shape
+    high_ref, low_ref, step_ref, out_ref, lift_ref, before_buf = refs[2 * group :]
+    heads, chunks, wide, _ = high_ref.shape
     chunk = wide // 2
     half = chunk // 2
     tokens = rest_in[0].shape[1]
@@ -294,23 +307,15 @@
             before_buf[head, slot] = totals[head].astype(BF16)
         totals = [after(totals[head], step_ref[head, slot]) for head in range(heads)]
 
-    def one_head(head, carry):
-        lanes = pl.ds(pl.multiple_of(head * width, width), width)
-        for index in range(chunks):
+    def answer(units):
+        for head, index in units:
+            lanes = lanes_of(head, width)
             source, first = index // per_source, (index % per_source) * chunk
-            key_ref, rest_ref = key_in[source], rest_in[source]
-            key = weave(
-                key_ref[first : first + chunk, lanes],
-                key_ref[tokens + first : tokens + first + chunk, lanes],
-            )
-            query = rest_ref[2, first : first + chunk, lanes]
+            key = woven_key(key_in[source], tokens, first, chunk, lanes)
+            query = rest_in[source][2, first : first + chunk, lanes]
             wide_query = query.astype(F32)
             scale = lax.rsqrt(jnp.sum(wide_query * wide_query, axis=1, keepdims=True) + EPS)
-            scores = jnp.where(
-                token_col <= token_row,
-                dot_t(query, key) * (scale * table_ref[head, index, 0:1, :]),
-                0.0,
-            )
+            scores = jnp.where(token_col <= token_row, dot_t(query, key) * scale, 0.0)
             applied = dot3(scores, high_ref[head, index], low_ref[head, index])
             lifted = scale * wide_query - applied[:, :width]
             slot = slot_of(group, index, per_source)
@@ -318,12 +323,11 @@
             rows = pl.ds(pl.multiple_of(slot * chunk, chunk), chunk)
             out_ref[rows, lanes] = applied[:, width:] + moved[:, width:]
             lift_ref[rows, lanes] = (lifted - moved[:, :width]).astype(BF16)
-        return carry
-
-    lax.fori_loop(0, heads, one_head, 0)
-
-
-def read(keys, rests, table, high, low, steps):
+
+    every_unit(heads, chunks, answer)
+
+
+def read(keys, rests, high, low, steps):
     group = len(keys)
     _, tokens, wide = rests[0].shape
     return pl.pallas_call(
@@ -332,12 +336,12 @@
             pltpu.VMEM((group * tokens, wide), F32),
             pltpu.VMEM((group * tokens, wide), BF16),
         ),
-        in_specs=[VMEM] * (2 * group + 4),
+        in_specs=[VMEM] * (2 * group + 3),
         out_specs=(VMEM, VMEM),
         scratch_shapes=[pltpu.VMEM(steps.shape, BF16)],
         compiler_params=PARAMS,
         name="read",
-    )(*held(*keys, *rests, table, high, low, steps))
+    )(*held(*keys, *rests, high, low, steps))
 
 
 def join_kernel(count, *refs):
@@ -376,38 +380,68 @@
     return (earlier.astype(F32) + later.astype(F32) - moved).astype(BF16)
 
 
-def project_kernel(group, targets, *refs):
-    heads_in, weight_in, (send_ref, keep_ref) = refs[:group], refs[group:-2], refs[-2:]
+def weight_rows(weights, offset, inner, first, count):
+    rows = pl.ds(first, count)
+    if offset == 2:
+        return jnp.where(inner, weights[3][rows, :], weights[4][rows, :])
+    return weights[{0: 0, 1: 1, 3: 2}[offset]][rows, :]
+
+
+def where_am_i(group):
     device = lax.axis_index("seq")
+    return lax.rem(device, group), device // group
+
+
+def target_rows(source, group, targets):
+    position, _ = where_am_i(group)
+    tokens = source.shape[0] // group
+    firsts = [pl.multiple_of(place(position, t) * tokens, tokens) for t in targets]
+    return jnp.concatenate([source[pl.ds(first, tokens), :] for first in firsts], axis=0)
+
+
+def begin_kernel(group, halves, early, *refs):
+    heads_in, weight_in, totals = refs[: len(early[0])], refs[len(early[0]) : -2], refs[-2:]
+    position, _ = where_am_i(group)
+    wide = heads_in[0].shape[1]
+    columns = weight_in[0].shape[1]
+    for targets, total_ref in zip(halves, totals):
+        for number, offset in enumerate(early[1]):
+            total = None
+            for member, source in zip(early[0], heads_in):
+                first = pl.multiple_of(place(position, member) * wide, wide)
+                part = dot(
+                    target_rows(source, group, targets),
+                    weight_rows(weight_in, offset, None, first, wide),
+                )
+                total = part if total is None else total + part
+            total_ref[:, number * columns : (number + 1) * columns] = total
+
+
+def project_kernel(group, targets, early, offsets, *refs):
+    heads_in, weight_in = refs[:group], refs[group:-3]
+    total_ref, send_ref, keep_ref = refs[-3:]
     core = lax.axis_index("head")
-    position, plane = lax.rem(device, group), device // group
-    rows, wide = heads_in[0].shape
-    tokens = rows // group
+    position, plane = where_am_i(group)
+    wide = heads_in[0].shape[1]
     columns = weight_in[0].shape[1]
     side = keep_ref.shape[1] // columns
     inner = (plane == 1) | (plane == 2)
-    sources = {0: weight_in[0], 1: weight_in[1]}
-    if len(weight_in) > 2:
-        sources[3] = weight_in[2]
-        sources[2] = weight_in[3:]
-
-    def rows_of(source):
-        firsts = [pl.multiple_of(place(position, t) * tokens, tokens) for t in targets]
-        return jnp.concatenate([source[pl.ds(first, tokens), :] for first in firsts], axis=0)
-
-    for offset, source in sources.items():
+    for offset in offsets:
         owner = jnp.bitwise_xor(plane, offset)
         total = None
-        for other in range(group):
-            first = pl.multiple_of(place(position, other) * wide, wide)
-            if offset == 2:
-                weight = jnp.where(
-                    inner, source[0][pl.ds(first, wide), :], source[1][pl.ds(first, wide), :]
-                )
-            else:
-                weight = source[pl.ds(first, wide), :]
-            part = dot(rows_of(heads_in[other]), weight)
+        members = range(group)
+        if offset in early[1]:
+            number = early[1].index(offset)
+            members = [member for member in members if member not in early[0]]
+        for member in members:
+            first = pl.multiple_of(place(position, member) * wide, wide)
+            part = dot(
+                target_rows(heads_in[member], group, targets),
+                weight_rows(weight_in, offset, inner, first, wide),
+            )
             total = part if total is None else total + part
+        if offset in early[1]:
+            total = total + total_ref[:, number * columns : (number + 1) * columns]
         result = total.astype(BF16)
         lanes = pl.ds(pl.multiple_of(lax.rem(owner, side) * columns, columns), columns)
 
@@ -420,19 +454,38 @@
             send_ref[:, lanes] = result
 
 
-def project(heads, weights, planes, targets):
+def begin_projection(heads, weights, halves, early):
+    group = len(heads)
+    tokens = heads[0].shape[0] // group
+    columns = weights[0].shape[1]
+    here = [heads[member] for member in early[0]] + list(weights[: len(early[1])])
+    return pl.pallas_call(
+        functools.partial(begin_kernel, group, halves, early),
+        out_shape=[
+            pltpu.VMEM((tokens * len(targets), columns * len(early[1])), F32)
+            for targets in halves
+        ],
+        in_specs=[VMEM] * len(here),
+        out_specs=[VMEM] * 2,
+        compiler_params=PARAMS,
+        name="begin_projection",
+    )(*held(*here))
+
+
+def project(heads, weights, planes, targets, early, total):
     group = len(heads)
     rows = heads[0].shape[0] // group * len(targets)
     columns = weights[0].shape[1]
+    offsets = (0, 1, 3, 2) if planes == 4 else (0, 1)
     shape = pltpu.VMEM((rows, columns * planes // 2), BF16)
     return pl.pallas_call(
-        functools.partial(project_kernel, group, targets),
+        functools.partial(project_kernel, group, targets, early, offsets),
         out_shape=(shape, shape),
-        in_specs=[VMEM] * (group + len(weights)),
+        in_specs=[VMEM] * (group + len(weights) + 1),
         out_specs=(VMEM, VMEM),
         compiler_params=PARAMS,
         name="project",
-    )(*held(*heads, *weights))
+    )(*held(*heads, *weights, total))
 
 
 def sum_kernel(keep_ref, other_ref, *outs):
@@ -540,9 +593,14 @@
             pairs = [(i, ((i // group) ^ offset) * group + i % group) for i in range(count)]
             weights.append(lax.ppermute(out_weight, "seq", pairs))
 
-    inverse, table = invert(keys, mine, tokens)
-    high, low, steps, state, local_state = carry_state(keys, rests, inverse, table)
-    local, lifted = read(keys, rests, table, high, low, steps)
+    near = max(group // 2, 1)
+    solved = []
+    for part in (keys[:near], keys[near:]):
+        if part:
+            solved.append(invert(part, mine, tokens))
+    inverses, tables = zip(*solved)
+    high, low, steps, state, local_state = carry_state(keys, rests, inverses, tables)
+    local, lifted = read(keys, rests, high, low, steps)
 
     def from_earlier(value, distance):
         pairs = [(i, i + distance * group) for i in range(count - distance * group)]
@@ -572,15 +630,18 @@
     mixed_heads = join(states, local, lifted)
 
     if split_out:
-        gathered = [mixed_heads] + [
-            swap(mixed_heads, group, offset, count) for offset in range(1, group)
-        ]
         order = tuple(reversed(range(group)))
         order = order[:1] + order[2:-1] + order[1:2] + order[-1:] if group > 2 else order
+        row_halves = (order[: group // 2], order[group // 2 :])
+        early = (tuple(range(group - 1)), (0, 1, 3) if planes == 4 else (0, 1))
         parts = [None] * group
+        gathered = [mixed_heads]
+        for offset in range(1, group):
+            gathered.append(swap(mixed_heads, group, offset, count))
+        totals = begin_projection(gathered, weights, row_halves, early)
         halves = []
-        for targets in (order[: group // 2], order[group // 2 :]):
-            send, keep = project(gathered, weights, planes, targets)
+        for targets, total in zip(row_halves, totals):
+            send, keep = project(gathered, weights, planes, targets, early, total)
             other = lax.ppermute(send, "head", [(0, 1), (1, 0)])
             halves.append((targets, keep, other))
         for targets, keep, other in halves:

time: 81.6 us -> 79.2 us (0.971)
  Pallas kernels: 18.5 us -> 16.6 us
  waiting for transfers between devices: 28.4 us -> 27 us
    pallas_call x3 -> x4, Pallas kernels: 8.24 us -> 5.49 us  [the longest x1 2.55 us: carry_state(): pl.pallas_call(functools.partial(state_kernel, group, parts), out_shape=(...]
    pallas_call x1 -> x2, Pallas kernels: 5.4 us -> 6.54 us  [invert(): pl.pallas_call(functools.partial(invert_kernel, heads, tokens), out_shape...]
  transfers between devices with their start and end apart: 21 -> 21, of which waited for: 8 -> 9; matrix products, arithmetic and copies ran while one was open for 3% -> 3% of each run, Pallas kernels for 20% -> 19%
where the time goes in v3:
time: 79.2 us; the launch traced here: 78.9 us
  starting transfers between devices  32.8 us (41%)
  waiting for transfers between devices  27 us (34%)
  Pallas kernels  16.6 us (21%)
  local copies, waits for them, and re-layouts  1.29 us (2%)
  other arithmetic  0.83 us (1%)
    ppermute x12, waiting for transfers between devices, swap(): return lax.ppermute(value, 'seq', pairs)  19.1 us
    ppermute x12, starting transfers between devices, swap(): return lax.ppermute(value, 'seq', pairs)  16 us
    ppermute x3, starting transfers between devices, from_earlier(): return lax.ppermute(value, 'seq', pairs)  8.71 us
    ppermute x2, waiting for transfers between devices, per_device(): weights.append(lax.ppermute(out_weight, 'seq', pairs))  7.85 us
    pallas_call x2, Pallas kernels, invert(): pl.pallas_call(functools.partial(invert_kernel, heads, tokens), out_shape...  6.54 us
    ppermute x2, starting transfers between devices, per_device(): weights.append(lax.ppermute(out_weight, 'seq', pairs))  5.53 us
    pallas_call x1, Pallas kernels, read(): pl.pallas_call(functools.partial(read_kernel, group), out_shape=(pltpu.VM...  3.11 us
    pallas_call x1, Pallas kernels, carry_state(): pl.pallas_call(functools.partial(state_kernel, group, parts), out_shape=(...  2.55 us
  transfers between devices with their start and end apart: 21, of which 9 were waited for; matrix products, arithmetic and copies ran while one was open for 3% of the time, Pallas kernels for 19%

profile of v3, /device:TPU:0, one launch (start us, length us, event | category | flops | bytes accessed | tf_op | source)
XLA Modules:
  0.0 78.9 jit_solution(4865583758419551468)
XLA Ops:
  0.0 3.1 %collective-permute-start.12 = (bf16[1024,256]{1,0:T(8,128)(2,1)}, bf16[1024,256]{1,0:T(8,128)(2,1)S(1)}, u32[]{:S(2)}, u32[]{:S(2)}) collective-permute-start(bf16[1024,256]{1,0:T(8,128)(2,1)} %refs_4_.3), channel_id=1, source_target_pairs={{0,8},{2,10},{4,12},{6,14},{8,0},{10,2},{12,4},{14,6},{16,24},{18,... | collective-permute-start | bytes 1572872 | tf_op jit(solution)/shard_map/ppermute | solution.py:594
  3.1 2.5 %collective-permute-start.13 = (bf16[1024,256]{1,0:T(8,128)(2,1)}, bf16[1024,256]{1,0:T(8,128)(2,1)S(1)}, u32[]{:S(2)}, u32[]{:S(2)}) collective-permute-start(bf16[1024,256]{1,0:T(8,128)(2,1)} %refs_4_.3), channel_id=1, source_target_pairs={{0,24},{2,26},{4,28},{6,30},{8,16},{10,18},{12,20},{14,22},{16,8},... | collective-permute-start | bytes 1572872 | tf_op jit(solution)/shard_map/ppermute | solution.py:594
  7.5 1.6 %collective-permute-start.1 = (bf16[272,256]{1,0:T(8,128)(2,1)S(1)}, bf16[272,256]{1,0:T(8,128)(2,1)S(1)}, u32[]{:S(2)}, u32[]{:S(2)}) collective-permute-start(bf16[272,256]{1,0:T(8,128)(2,1)S(1)} %get-tuple-element.48), channel_id=1, source_target_pairs={{0,4},{2,6},{4,0},{6,2},{8,12},{10,14},{12,8},{14,10},{16,20},{18,... | collective-permute-start | bytes 417800 | tf_op jit(solution)/shard_map/ppermute | solution.py:548
  11.3 3.4 %collective-permute-done.1.refs_0_.refs_2_ = bf16[272,256]{1,0:T(8,128)(2,1)S(1)} collective-permute-done((bf16[272,256]{1,0:T(8,128)(2,1)S(1)}, bf16[272,256]{1,0:T(8,128)(2,1)S(1)}, u32[]{:S(2)}, u32[]{:S(2)}) %collective-permute-start.1) | collective-permute-done | bytes 139296 | tf_op jit(solution)/shard_map/ppermute | solution.py:548
  14.7 1.5 %collective-permute-start.3 = (bf16[3,128,256]{2,1,0:T(8,128)(2,1)S(1)}, bf16[3,128,256]{2,1,0:T(8,128)(2,1)S(1)}, u32[]{:S(2)}, u32[]{:S(2)}) collective-permute-start(bf16[3,128,256]{2,1,0:T(8,128)(2,1)S(1)} %pad_maximum_fusion.1), channel_id=1, source_target_pairs={{0,2},{2,0},{4,6},{6,4},{8,10},{10,8},{12,14},{14,12},{16,18},{18,... | collective-permute-start | bytes 589832 | tf_op jit(solution)/shard_map/ppermute | solution.py:548
  16.2 2.1 %collective-permute-start.4 = (bf16[3,128,256]{2,1,0:T(8,128)(2,1)S(1)}, bf16[3,128,256]{2,1,0:T(8,128)(2,1)S(1)}, u32[]{:S(2)}, u32[]{:S(2)}) collective-permute-start(bf16[3,128,256]{2,1,0:T(8,128)(2,1)S(1)} %pad_maximum_fusion.2), channel_id=1, source_target_pairs={{0,4},{2,6},{4,0},{6,2},{8,12},{10,14},{12,8},{14,10},{16,20},{18,... | collective-permute-start | bytes 589832 | tf_op jit(solution)/shard_map/ppermute | solution.py:548
  18.6 1.6 %collective-permute-start.5 = (bf16[3,128,256]{2,1,0:T(8,128)(2,1)S(1)}, bf16[3,128,256]{2,1,0:T(8,128)(2,1)S(1)}, u32[]{:S(2)}, u32[]{:S(2)}) collective-permute-start(bf16[3,128,256]{2,1,0:T(8,128)(2,1)S(1)} %pad_maximum_fusion.3), channel_id=1, source_target_pairs={{0,6},{2,4},{4,2},{6,0},{8,14},{10,12},{12,10},{14,8},{16,22},{18,... | collective-permute-start | bytes 589832 | tf_op jit(solution)/shard_map/ppermute | solution.py:548
  20.9 7.9 %collective-permute-done.13.refs_5_.refs_6_ = bf16[1024,256]{1,0:T(8,128)(2,1)S(1)} collective-permute-done((bf16[1024,256]{1,0:T(8,128)(2,1)}, bf16[1024,256]{1,0:T(8,128)(2,1)S(1)}, u32[]{:S(2)}, u32[]{:S(2)}) %collective-permute-start.13) | collective-permute-done | bytes 524320 | tf_op jit(solution)/shard_map/ppermute | solution.py:594
  30.0 3.3 %invert.3 = (f32[2,2,3,128,128]{4,3,2,1,0:T(8,128)S(1)}, f32[2,2,8,256]{3,2,1,0:T(8,128)S(1)}) custom-call(bf16[272,256]{1,0:T(8,128)(2,1)S(1)} %collective-permute-done.1.refs_0_.refs_2_, bf16[272,256]{1,0:T(8,128)(2,1)S(1)} %collective-permute-done.2.refs_1_.refs_3_), custom_call_target="tpu_custom_call" | custom-call | tf_op jit(solution)/shard_map/invert/pallas_call | solution.py:162
  33.3 3.3 %invert.2 = (f32[2,2,3,128,128]{4,3,2,1,0:T(8,128)S(1)}, f32[2,2,8,256]{3,2,1,0:T(8,128)S(1)}) custom-call(bf16[272,256]{1,0:T(8,128)(2,1)S(1)} %get-tuple-element.50.refs_0_, bf16[272,256]{1,0:T(8,128)(2,1)S(1)} %collective-permute-done.refs_1_), custom_call_target="tpu_custom_call" | custom-call | tf_op jit(solution)/shard_map/invert/pallas_call | solution.py:162
  36.6 2.5 %carry_state.1 = (bf16[2,4,256,256]{3,2,1,0:T(8,128)(2,1)S(1)}, bf16[2,4,256,256]{3,2,1,0:T(8,128)(2,1)S(1)}, f32[2,4,128,256]{3,2,1,0:T(8,128)S(1)}, bf16[2,128...) custom-call(bf16[272,256]{1,0:T(8,128)(2,1)S(1)} %get-tuple-element.50.refs_0_, ...), custom_call_target="tpu_custom_call" | custom-call | tf_op jit(solution)/shard_map/carry_state/pallas_call | solution.py:274
  39.2 4.6 %collective-permute-start.6 = (bf16[2,128,256]{2,1,0:T(8,128)(2,1)S(1)}, bf16[2,128,256]{2,1,0:T(8,128)(2,1)S(1)}, u32[]{:S(2)}, u32[]{:S(2)}) collective-permute-start(bf16[2,128,256]{2,1,0:T(8,128)(2,1)S(1)} %get-tuple-element.30), channel_id=1, source_target_pairs={{0,8},{2,10},{4,12},{6,14},{8,16},{10,18},{12,20},{14,22},{16,24},... | collective-permute-start | bytes 393224 | tf_op jit(solution)/shard_map/ppermute | solution.py:607
  43.8 2.6 %collective-permute-start.7 = (bf16[2,128,256]{2,1,0:T(8,128)(2,1)S(1)}, bf16[2,128,256]{2,1,0:T(8,128)(2,1)S(1)}, u32[]{:S(2)}, u32[]{:S(2)}) collective-permute-start(bf16[2,128,256]{2,1,0:T(8,128)(2,1)S(1)} %get-tuple-element.30), channel_id=1, source_target_pairs={{0,16},{2,18},{4,20},{6,22},{8,24},{10,26},{12,28},{14,30},{1,17},... | collective-permute-start | bytes 393224 | tf_op jit(solution)/shard_map/ppermute | solution.py:607
  46.4 1.5 %collective-permute-start.8 = (bf16[2,128,128]{2,1,0:T(8,128)(2,1)S(1)}, bf16[2,128,128]{2,1,0:T(8,128)(2,1)S(1)}, u32[]{:S(2)}, u32[]{:S(2)}) collective-permute-start(bf16[2,128,128]{2,1,0:T(8,128)(2,1)S(1)} %get-tuple-element.31), channel_id=1, source_target_pairs={{0,24},{2,26},{4,28},{6,30},{1,25},{3,27},{5,29},{7,31}} | collective-permute-start | bytes 196616 | tf_op jit(solution)/shard_map/ppermute | solution.py:607
  47.9 3.1 %read.1 = (f32[512,256]{1,0:T(8,128)S(1)}, bf16[512,256]{1,0:T(8,128)(2,1)S(1)}) custom-call(bf16[272,256]{1,0:T(8,128)(2,1)S(1)} %get-tuple-element.50.refs_0_, bf16[272,256]{1,0:T(8,128)(2,1)S(1)} %collective-permute-done.refs_1_, bf16[272,256]{1,0:T(8,128)(2,1)S(1)} %collective-permute-done.1.refs_0_.refs_2_, ...), custom_call_target="tpu_custom_call" | custom-call | tf_op jit(solution)/shard_map/read/pallas_call | solution.py:333
  51.6 1.6 %collective-permute-start.10 = (bf16[512,256]{1,0:T(8,128)(2,1)S(1)}, bf16[512,256]{1,0:T(8,128)(2,1)S(1)}, u32[]{:S(2)}, u32[]{:S(2)}) collective-permute-start(bf16[512,256]{1,0:T(8,128)(2,1)S(1)} %join.1.refs_0_), channel_id=1, source_target_pairs={{0,4},{2,6},{4,0},{6,2},{8,12},{10,14},{12,8},{14,10},{16,20},{18,... | collective-permute-start | bytes 786440 | tf_op jit(solution)/shard_map/ppermute | solution.py:548
  53.1 1.5 %collective-permute-start.9 = (bf16[512,256]{1,0:T(8,128)(2,1)S(1)}, bf16[512,256]{1,0:T(8,128)(2,1)S(1)}, u32[]{:S(2)}, u32[]{:S(2)}) collective-permute-start(bf16[512,256]{1,0:T(8,128)(2,1)S(1)} %join.1.refs_0_), channel_id=1, source_target_pairs={{0,2},{2,0},{4,6},{6,4},{8,10},{10,8},{12,14},{14,12},{16,18},{18,... | collective-permute-start | bytes 786440 | tf_op jit(solution)/shard_map/ppermute | solution.py:548
  55.1 5.7 %collective-permute-done.10.refs_2_ = bf16[512,256]{1,0:T(8,128)(2,1)S(1)} collective-permute-done((bf16[512,256]{1,0:T(8,128)(2,1)S(1)}, bf16[512,256]{1,0:T(8,128)(2,1)S(1)}, u32[]{:S(2)}, u32[]{:S(2)}) %collective-permute-start.10) | collective-permute-done | bytes 262176 | tf_op jit(solution)/shard_map/ppermute | solution.py:548
  62.2 2.0 %collective-permute-done.11.refs_3_ = bf16[512,256]{1,0:T(8,128)(2,1)S(1)} collective-permute-done((bf16[512,256]{1,0:T(8,128)(2,1)S(1)}, bf16[512,256]{1,0:T(8,128)(2,1)S(1)}, u32[]{:S(2)}, u32[]{:S(2)}) %collective-permute-start.11) | collective-permute-done | bytes 262176 | tf_op jit(solution)/shard_map/ppermute | solution.py:548
  67.1 1.5 %collective-permute-start.18 = (bf16[128,512]{1,0:T(8,128)(2,1)S(1)}, bf16[128,512]{1,0:T(8,128)(2,1)S(1)}, u32[]{:S(2)}, u32[]{:S(2)}) collective-permute-start(bf16[128,512]{1,0:T(8,128)(2,1)S(1)} %get-tuple-element.44), channel_id=1, source_target_pairs={{0,2},{2,0},{4,6},{6,4},{8,10},{10,8},{12,14},{14,12},{16,18},{18,... | collective-permute-start | bytes 393224 | tf_op jit(solution)/shard_map/ppermute | solution.py:548
  68.6 1.5 %collective-permute-start.20 = (bf16[128,512]{1,0:T(8,128)(2,1)S(1)}, bf16[128,512]{1,0:T(8,128)(2,1)S(1)}, u32[]{:S(2)}, u32[]{:S(2)}) collective-permute-start(bf16[128,512]{1,0:T(8,128)(2,1)S(1)} %get-tuple-element.46), channel_id=1, source_target_pairs={{0,6},{2,4},{4,2},{6,0},{8,14},{10,12},{12,10},{14,8},{16,22},{18,... | collective-permute-start | bytes 393224 | tf_op jit(solution)/shard_map/ppermute | solution.py:548
  70.8 2.5 %collective-permute-done.18.refs_1_ = bf16[128,512]{1,0:T(8,128)(2,1)S(1)} collective-permute-done((bf16[128,512]{1,0:T(8,128)(2,1)S(1)}, bf16[128,512]{1,0:T(8,128)(2,1)S(1)}, u32[]{:S(2)}, u32[]{:S(2)}) %collective-permute-start.18) | collective-permute-done | bytes 131104 | tf_op jit(solution)/shard_map/ppermute | solution.py:548
  73.2 3.2 %collective-permute-done.20.refs_3_ = bf16[128,512]{1,0:T(8,128)(2,1)S(1)} collective-permute-done((bf16[128,512]{1,0:T(8,128)(2,1)S(1)}, bf16[128,512]{1,0:T(8,128)(2,1)S(1)}, u32[]{:S(2)}, u32[]{:S(2)}) %collective-permute-start.20) | collective-permute-done | bytes 131104 | tf_op jit(solution)/shard_map/ppermute | solution.py:548
  76.4 1.5 %collective-permute-done.19.refs_2_ = bf16[128,512]{1,0:T(8,128)(2,1)S(1)} collective-permute-done((bf16[128,512]{1,0:T(8,128)(2,1)S(1)}, bf16[128,512]{1,0:T(8,128)(2,1)S(1)}, u32[]{:S(2)}, u32[]{:S(2)}) %collective-permute-start.19) | collective-permute-done | bytes 131104 | tf_op jit(solution)/shard_map/ppermute | solution.py:548
  (47 shorter events, 13.0 us)
Async XLA Ops:
  0.0 20.2 %collective-permute-start.12 = (bf16[1024,256]{1,0:T(8,128)(2,1)}, bf16[1024,256]{1,0:T(8,128)(2,1)S(1)}, u32[]{:S(2)}, u32[]{:S(2)}) collective-permute-start(bf16[1024,256]{1,0:T(8,128)(2,1)} %refs_4_.3), channel_id=1, source_target_pairs={{0,8},{2,10},{4,12},{6,14},{8,0},{10,2},{12,4},{14,6},{16,24},{18,... | collective-permute-start | bytes 1572872 | tf_op jit(solution)/shard_map/ppermute | solution.py:594
  3.1 25.7 %collective-permute-start.13 = (bf16[1024,256]{1,0:T(8,128)(2,1)}, bf16[1024,256]{1,0:T(8,128)(2,1)S(1)}, u32[]{:S(2)}, u32[]{:S(2)}) collective-permute-start(bf16[1024,256]{1,0:T(8,128)(2,1)} %refs_4_.3), channel_id=1, source_target_pairs={{0,24},{2,26},{4,28},{6,30},{8,16},{10,18},{12,20},{14,22},{16,8},... | collective-permute-start | bytes 1572872 | tf_op jit(solution)/shard_map/ppermute | solution.py:594
  7.3 3.7 %copy-start.1 = (bf16[2,128,1024]{2,1,0:T(8,128)(2,1)S(1)}, bf16[2,128,1024]{2,1,0:T(8,128)(2,1)}, u32[]{:S(2)}) copy-start(bf16[2,128,1024]{2,1,0:T(8,128)(2,1)} %param.7) | copy-start | bytes 1572868
  7.4 3.7 %copy-start.2 = (bf16[128,1024]{1,0:T(8,128)(2,1)S(1)}, bf16[128,1024]{1,0:T(8,128)(2,1)}, u32[]{:S(2)}) copy-start(bf16[128,1024]{1,0:T(8,128)(2,1)} %param.5) | copy-start | bytes 786436
  7.5 7.2 %collective-permute-start.1 = (bf16[272,256]{1,0:T(8,128)(2,1)S(1)}, bf16[272,256]{1,0:T(8,128)(2,1)S(1)}, u32[]{:S(2)}, u32[]{:S(2)}) collective-permute-start(bf16[272,256]{1,0:T(8,128)(2,1)S(1)} %get-tuple-element.48), channel_id=1, source_target_pairs={{0,4},{2,6},{4,0},{6,2},{8,12},{10,14},{12,8},{14,10},{16,20},{18,... | collective-permute-start | bytes 417800 | tf_op jit(solution)/shard_map/ppermute | solution.py:548
  9.1 7.1 %collective-permute-start.2 = (bf16[272,256]{1,0:T(8,128)(2,1)S(1)}, bf16[272,256]{1,0:T(8,128)(2,1)S(1)}, u32[]{:S(2)}, u32[]{:S(2)}) collective-permute-start(bf16[272,256]{1,0:T(8,128)(2,1)S(1)} %get-tuple-element.47), channel_id=1, source_target_pairs={{0,6},{2,4},{4,2},{6,0},{8,14},{10,12},{12,10},{14,8},{16,22},{18,... | collective-permute-start | bytes 417800 | tf_op jit(solution)/shard_map/ppermute | solution.py:548
  10.5 8.0 %collective-permute-start = (bf16[272,256]{1,0:T(8,128)(2,1)S(1)}, bf16[272,256]{1,0:T(8,128)(2,1)S(1)}, u32[]{:S(2)}, u32[]{:S(2)}) collective-permute-start(bf16[272,256]{1,0:T(8,128)(2,1)S(1)} %get-tuple-element.49), channel_id=1, source_target_pairs={{0,2},{2,0},{4,6},{6,4},{8,10},{10,8},{12,14},{14,12},{16,18},{18,... | collective-permute-start | bytes 417800 | tf_op jit(solution)/shard_map/ppermute | solution.py:548
  14.7 21.9 %collective-permute-start.3 = (bf16[3,128,256]{2,1,0:T(8,128)(2,1)S(1)}, bf16[3,128,256]{2,1,0:T(8,128)(2,1)S(1)}, u32[]{:S(2)}, u32[]{:S(2)}) collective-permute-start(bf16[3,128,256]{2,1,0:T(8,128)(2,1)S(1)} %pad_maximum_fusion.1), channel_id=1, source_target_pairs={{0,2},{2,0},{4,6},{6,4},{8,10},{10,8},{12,14},{14,12},{16,18},{18,... | collective-permute-start | bytes 589832 | tf_op jit(solution)/shard_map/ppermute | solution.py:548
  16.2 20.4 %collective-permute-start.4 = (bf16[3,128,256]{2,1,0:T(8,128)(2,1)S(1)}, bf16[3,128,256]{2,1,0:T(8,128)(2,1)S(1)}, u32[]{:S(2)}, u32[]{:S(2)}) collective-permute-start(bf16[3,128,256]{2,1,0:T(8,128)(2,1)S(1)} %pad_maximum_fusion.2), channel_id=1, source_target_pairs={{0,4},{2,6},{4,0},{6,2},{8,12},{10,14},{12,8},{14,10},{16,20},{18,... | collective-permute-start | bytes 589832 | tf_op jit(solution)/shard_map/ppermute | solution.py:548
  18.6 18.1 %collective-permute-start.5 = (bf16[3,128,256]{2,1,0:T(8,128)(2,1)S(1)}, bf16[3,128,256]{2,1,0:T(8,128)(2,1)S(1)}, u32[]{:S(2)}, u32[]{:S(2)}) collective-permute-start(bf16[3,128,256]{2,1,0:T(8,128)(2,1)S(1)} %pad_maximum_fusion.3), channel_id=1, source_target_pairs={{0,6},{2,4},{4,2},{6,0},{8,14},{10,12},{12,10},{14,8},{16,22},{18,... | collective-permute-start | bytes 589832 | tf_op jit(solution)/shard_map/ppermute | solution.py:548
  20.2 44.0 %collective-permute-start.14 = (bf16[1024,256]{1,0:T(8,128)(2,1)S(1)}, bf16[1024,256]{1,0:T(8,128)(2,1)S(1)}, u32[]{:S(2)}, u32[]{:S(2)}) collective-permute-start(bf16[1024,256]{1,0:T(8,128)(2,1)S(1)} %collective-permute-done.12.refs_4_.refs_5_), channel_id=1, source_target_pairs={{8,16},{10,18},{12,20},{14,22},{16,8},{18,10},{20,12},{22,14},{9,1... | collective-permute-start | bytes 1572872 | tf_op jit(solution)/shard_map/ppermute | solution.py:628
  28.7 35.5 %collective-permute-start.15 = (bf16[1024,256]{1,0:T(8,128)(2,1)S(1)}, bf16[1024,256]{1,0:T(8,128)(2,1)S(1)}, u32[]{:S(2)}, u32[]{:S(2)}) collective-permute-start(bf16[1024,256]{1,0:T(8,128)(2,1)S(1)} %collective-permute-done.13.refs_5_.refs_6_), channel_id=1, source_target_pairs={{8,0},{10,2},{12,4},{14,6},{16,24},{18,26},{20,28},{22,30},{9,1},{... | collective-permute-start | bytes 1572872 | tf_op jit(solution)/shard_map/ppermute | solution.py:628
  39.2 11.9 %collective-permute-start.6 = (bf16[2,128,256]{2,1,0:T(8,128)(2,1)S(1)}, bf16[2,128,256]{2,1,0:T(8,128)(2,1)S(1)}, u32[]{:S(2)}, u32[]{:S(2)}) collective-permute-start(bf16[2,128,256]{2,1,0:T(8,128)(2,1)S(1)} %get-tuple-element.30), channel_id=1, source_target_pairs={{0,8},{2,10},{4,12},{6,14},{8,16},{10,18},{12,20},{14,22},{16,24},... | collective-permute-start | bytes 393224 | tf_op jit(solution)/shard_map/ppermute | solution.py:607
  43.8 7.3 %collective-permute-start.7 = (bf16[2,128,256]{2,1,0:T(8,128)(2,1)S(1)}, bf16[2,128,256]{2,1,0:T(8,128)(2,1)S(1)}, u32[]{:S(2)}, u32[]{:S(2)}) collective-permute-start(bf16[2,128,256]{2,1,0:T(8,128)(2,1)S(1)} %get-tuple-element.30), channel_id=1, source_target_pairs={{0,16},{2,18},{4,20},{6,22},{8,24},{10,26},{12,28},{14,30},{1,17},... | collective-permute-start | bytes 393224 | tf_op jit(solution)/shard_map/ppermute | solution.py:607
  46.4 4.6 %collective-permute-start.8 = (bf16[2,128,128]{2,1,0:T(8,128)(2,1)S(1)}, bf16[2,128,128]{2,1,0:T(8,128)(2,1)S(1)}, u32[]{:S(2)}, u32[]{:S(2)}) collective-permute-start(bf16[2,128,128]{2,1,0:T(8,128)(2,1)S(1)} %get-tuple-element.31), channel_id=1, source_target_pairs={{0,24},{2,26},{4,28},{6,30},{1,25},{3,27},{5,29},{7,31}} | collective-permute-start | bytes 196616 | tf_op jit(solution)/shard_map/ppermute | solution.py:607
  51.0 10.4 %copy-start = (bf16[1024,256]{1,0:T(8,128)(2,1)S(1)}, bf16[1024,256]{1,0:T(8,128)(2,1)}, u32[]{:S(2)}) copy-start(bf16[1024,256]{1,0:T(8,128)(2,1)} %refs_4_.3) | copy-start | bytes 1572868
  51.6 9.2 %collective-permute-start.10 = (bf16[512,256]{1,0:T(8,128)(2,1)S(1)}, bf16[512,256]{1,0:T(8,128)(2,1)S(1)}, u32[]{:S(2)}, u32[]{:S(2)}) collective-permute-start(bf16[512,256]{1,0:T(8,128)(2,1)S(1)} %join.1.refs_0_), channel_id=1, source_target_pairs={{0,4},{2,6},{4,0},{6,2},{8,12},{10,14},{12,8},{14,10},{16,20},{18,... | collective-permute-start | bytes 786440 | tf_op jit(solution)/shard_map/ppermute | solution.py:548
  53.1 8.3 %collective-permute-start.9 = (bf16[512,256]{1,0:T(8,128)(2,1)S(1)}, bf16[512,256]{1,0:T(8,128)(2,1)S(1)}, u32[]{:S(2)}, u32[]{:S(2)}) collective-permute-start(bf16[512,256]{1,0:T(8,128)(2,1)S(1)} %join.1.refs_0_), channel_id=1, source_target_pairs={{0,2},{2,0},{4,6},{6,4},{8,10},{10,8},{12,14},{14,12},{16,18},{18,... | collective-permute-start | bytes 786440 | tf_op jit(solution)/shard_map/ppermute | solution.py:548
  54.6 9.5 %collective-permute-start.11 = (bf16[512,256]{1,0:T(8,128)(2,1)S(1)}, bf16[512,256]{1,0:T(8,128)(2,1)S(1)}, u32[]{:S(2)}, u32[]{:S(2)}) collective-permute-start(bf16[512,256]{1,0:T(8,128)(2,1)S(1)} %join.1.refs_0_), channel_id=1, source_target_pairs={{0,6},{2,4},{4,2},{6,0},{8,14},{10,12},{12,10},{14,8},{16,22},{18,... | collective-permute-start | bytes 786440 | tf_op jit(solution)/shard_map/ppermute | solution.py:548
  65.3 1.7 %collective-permute-start.17 = (bf16[256,512]{1,0:T(8,128)(2,1)S(1)}, bf16[256,512]{1,0:T(8,128)(2,1)S(1)}, u32[]{:S(2)}, u32[]{:S(2)}) collective-permute-start(bf16[256,512]{1,0:T(8,128)(2,1)S(1)} %get-tuple-element.43), channel_id=1, source_target_pairs={{0,1},{1,0},{2,3},{3,2},{4,5},{5,4},{6,7},{7,6},{8,9},{9,8},{10,11... | collective-permute-start | bytes 786440 | tf_op jit(solution)/shard_map/ppermute | solution.py:645
  66.4 3.7 %collective-permute-start.16 = (bf16[256,512]{1,0:T(8,128)(2,1)S(1)}, bf16[256,512]{1,0:T(8,128)(2,1)S(1)}, u32[]{:S(2)}, u32[]{:S(2)}) collective-permute-start(bf16[256,512]{1,0:T(8,128)(2,1)S(1)} %get-tuple-element.39), channel_id=1, source_target_pairs={{0,1},{1,0},{2,3},{3,2},{4,5},{5,4},{6,7},{7,6},{8,9},{9,8},{10,11... | collective-permute-start | bytes 786440 | tf_op jit(solution)/shard_map/ppermute | solution.py:645
  67.1 6.1 %collective-permute-start.18 = (bf16[128,512]{1,0:T(8,128)(2,1)S(1)}, bf16[128,512]{1,0:T(8,128)(2,1)S(1)}, u32[]{:S(2)}, u32[]{:S(2)}) collective-permute-start(bf16[128,512]{1,0:T(8,128)(2,1)S(1)} %get-tuple-element.44), channel_id=1, source_target_pairs={{0,2},{2,0},{4,6},{6,4},{8,10},{10,8},{12,14},{14,12},{16,18},{18,... | collective-permute-start | bytes 393224 | tf_op jit(solution)/shard_map/ppermute | solution.py:548
  68.6 7.8 %collective-permute-start.20 = (bf16[128,512]{1,0:T(8,128)(2,1)S(1)}, bf16[128,512]{1,0:T(8,128)(2,1)S(1)}, u32[]{:S(2)}, u32[]{:S(2)}) collective-permute-start(bf16[128,512]{1,0:T(8,128)(2,1)S(1)} %get-tuple-element.46), channel_id=1, source_target_pairs={{0,6},{2,4},{4,2},{6,0},{8,14},{10,12},{12,10},{14,8},{16,22},{18,... | collective-permute-start | bytes 393224 | tf_op jit(solution)/shard_map/ppermute | solution.py:548
  70.2 7.7 %collective-permute-start.19 = (bf16[128,512]{1,0:T(8,128)(2,1)S(1)}, bf16[128,512]{1,0:T(8,128)(2,1)S(1)}, u32[]{:S(2)}, u32[]{:S(2)}) collective-permute-start(bf16[128,512]{1,0:T(8,128)(2,1)S(1)} %get-tuple-element.45), channel_id=1, source_target_pairs={{0,4},{2,6},{4,0},{6,2},{8,12},{10,14},{12,8},{14,10},{16,20},{18,... | collective-permute-start | bytes 393224 | tf_op jit(solution)/shard_map/ppermute | solution.py:548

commit v4 on v3

--- a/solution.py
+++ b/solution.py
@@ -79,6 +79,51 @@
 
 def beta_rows(tokens, width):
     return -(-4 * max(tokens // width, 1) // 16) * 16
+
+
+def pack_kernel(group, key_ref, beta_ref, *outs):
+    _, heads, tokens = beta_ref.shape
+    mine = heads // group
+    wide = outs[0].shape[1]
+    width = wide // mine
+    pieces = max(tokens // width, 1)
+    inside = tokens // pieces
+    position, _ = where_am_i(group)
+    for offset, out_ref in enumerate(outs):
+        member = place(position, offset)
+        lanes = pl.ds(pl.multiple_of(member * wide, wide), wide)
+        for reflection in range(2):
+            out_ref[reflection * tokens : (reflection + 1) * tokens, :] = key_ref[
+                reflection, :, lanes
+            ]
+        rows = []
+        for reflection in range(2):
+            for piece in range(pieces):
+                cuts = []
+                for head in range(mine):
+                    cut = beta_ref[reflection, pl.ds(member * mine + head, 1), :]
+                    cuts.append(cut[:, piece * inside : (piece + 1) * inside])
+                    if inside < width:
+                        cuts.append(jnp.zeros((1, width - inside), F32))
+                rows.append(jnp.concatenate(cuts, axis=1) if len(cuts) > 1 else cuts[0])
+        both = jnp.concatenate(rows, axis=0)
+        high = both.astype(BF16).astype(F32)
+        spare = jnp.zeros((out_ref.shape[0] - 2 * tokens - 2 * len(rows), wide), F32)
+        out_ref[2 * tokens :, :] = jnp.concatenate([high, both - high, spare], axis=0).astype(BF16)
+
+
+def pack_keys(key_vectors, strengths, group):
+    _, tokens, wide = key_vectors.shape
+    width = wide // strengths.shape[1]
+    shape = (2 * tokens + beta_rows(tokens, width), wide // group)
+    return pl.pallas_call(
+        functools.partial(pack_kernel, group),
+        out_shape=[pltpu.VMEM(shape, BF16)] * group,
+        in_specs=[VMEM] * 2,
+        out_specs=[VMEM] * group,
+        compiler_params=PARAMS,
+        name="pack_keys",
+    )(*held(key_vectors, strengths))
 
 
 def invert_kernel(heads, tokens, *refs):
@@ -293,8 +338,8 @@
     heads, chunks, wide, _ = high_ref.shape
     chunk = wide // 2
     half = chunk // 2
-    tokens = rest_in[0].shape[1]
-    width = rest_in[0].shape[2] // heads
+    tokens = rest_in[0].shape[0]
+    width = rest_in[0].shape[1] // heads
     per_source = tokens // chunk
     token_row = iota((chunk, 2 * chunk), 0)
     token_col = iota((chunk, 2 * chunk), 1)
@@ -312,7 +357,7 @@
             lanes = lanes_of(head, width)
             source, first = index // per_source, (index % per_source) * chunk
             key = woven_key(key_in[source], tokens, first, chunk, lanes)
-            query = rest_in[source][2, first : first + chunk, lanes]
+            query = rest_in[source][first : first + chunk, lanes]
             wide_query = query.astype(F32)
             scale = lax.rsqrt(jnp.sum(wide_query * wide_query, axis=1, keepdims=True) + EPS)
             scores = jnp.where(token_col <= token_row, dot_t(query, key) * scale, 0.0)
@@ -329,7 +374,7 @@
 
 def read(keys, rests, high, low, steps):
     group = len(keys)
-    _, tokens, wide = rests[0].shape
+    tokens, wide = rests[0].shape
     return pl.pallas_call(
         functools.partial(read_kernel, group),
         out_shape=(
@@ -560,31 +605,18 @@
     planes = count // group
     position = lax.axis_index("seq") % group
     mine = heads // group
-    pieces = max(tokens // width, 1)
-    high = lax.reduce_precision(strengths, 8, 7)
-    beta = jnp.stack([high, strengths - high]).astype(BF16)
-    beta = beta.reshape(4, heads, pieces, tokens // pieces)
-    beta = jnp.pad(beta, ((0, 0), (0, 0), (0, 0), (0, width - tokens // pieces)))
-    beta = jnp.swapaxes(beta, 1, 2).reshape(4 * pieces, heads * width)
-    beta = jnp.pad(beta, ((0, beta_rows(tokens, width) - 4 * pieces), (0, 0)))
-    packed = jnp.concatenate([key_vectors[0], key_vectors[1], beta], axis=0)
-
-    keys, rests = [], []
+    keys = list(pack_keys(key_vectors, strengths, group))
+    vals, asks = [], []
     for offset in range(group):
         lane = jnp.bitwise_xor(position, offset) * mine * width
-        key = lax.dynamic_slice_in_dim(packed, lane, mine * width, 1)
-        rest = jnp.concatenate(
-            [
-                lax.dynamic_slice_in_dim(values, lane, mine * width, 2),
-                lax.dynamic_slice_in_dim(queries, lane, mine * width, 1)[None],
-            ],
-            axis=0,
-        )
+        value = lax.dynamic_slice_in_dim(values, lane, mine * width, 2)
+        ask = lax.dynamic_slice_in_dim(queries, lane, mine * width, 1)
         if offset:
-            key = swap(key, group, offset, count)
-            rest = swap(rest, group, offset, count)
-        keys.append(key)
-        rests.append(rest)
+            keys[offset] = swap(keys[offset], group, offset, count)
+            value = swap(value, group, offset, count)
+            ask = swap(ask, group, offset, count)
+        vals.append(value)
+        asks.append(ask)
 
     split_out = sides == 2 and planes in (2, 4) and group > 1
     weights = [out_weight]
@@ -599,8 +631,8 @@
         if part:
             solved.append(invert(part, mine, tokens))
     inverses, tables = zip(*solved)
-    high, low, steps, state, local_state = carry_state(keys, rests, inverses, tables)
-    local, lifted = read(keys, rests, high, low, steps)
+    high, low, steps, state, local_state = carry_state(keys, vals, inverses, tables)
+    local, lifted = read(keys, asks, high, low, steps)
 
     def from_earlier(value, distance):
         pairs = [(i, i + distance * group) for i in range(count - distance * group)]

time: 79.2 us -> 83 us (1.048)
  waiting for transfers between devices: 27 us -> 30.5 us
  starting transfers between devices: 32.8 us -> 33.7 us
    ppermute x12 -> x15, waiting for transfers between devices: 19.1 us -> 22.6 us  [swap(): return lax.ppermute(value, 'seq', pairs)]
    dynamic_slice x2, local copies, waits for them, and re-layouts: 0.15 us -> 1.24 us  [the longest x1 1.19 us: per_device(): value = lax.dynamic_slice_in_dim(values, lane, mine * width, 2)]
    squeeze x1 -> x0, local copies, waits for them, and re-layouts: 1.06 us -> none  [per_device(): packed = jnp.concatenate([key_vectors[0], key_vectors[1], beta], axis=0)]
    ppermute x12 -> x15, starting transfers between devices: 16 us -> 16.9 us  [swap(): return lax.ppermute(value, 'seq', pairs)]
  transfers between devices with their start and end apart: 21 -> 24, of which waited for: 9 -> 9; matrix products, arithmetic and copies ran while one was open for 3% -> 1% of each run, Pallas kernels for 19% -> 18%
where the time goes in v4:
time: 83 us; the launch traced here: 82.7 us
  starting transfers between devices  33.7 us (41%)
  waiting for transfers between devices  30.5 us (37%)
  Pallas kernels  16.8 us (20%)
  local copies, waits for them, and re-layouts  1.26 us (2%)
    ppermute x15, waiting for transfers between devices, swap(): return lax.ppermute(value, 'seq', pairs)  22.6 us
    ppermute x15, starting transfers between devices, swap(): return lax.ppermute(value, 'seq', pairs)  16.9 us
    ppermute x3, starting transfers between devices, from_earlier(): return lax.ppermute(value, 'seq', pairs)  8.71 us
    ppermute x2, waiting for transfers between devices, per_device(): weights.append(lax.ppermute(out_weight, 'seq', pairs))  7.96 us
    pallas_call x2, Pallas kernels, invert(): pl.pallas_call(functools.partial(invert_kernel, heads, tokens), out_shape...  6.6 us
    ppermute x2, starting transfers between devices, per_device(): weights.append(lax.ppermute(out_weight, 'seq', pairs))  5.53 us
    pallas_call x1, Pallas kernels, read(): pl.pallas_call(functools.partial(read_kernel, group), out_shape=(pltpu.VM...  3.12 us
    pallas_call x1, Pallas kernels, carry_state(): pl.pallas_call(functools.partial(state_kernel, group, parts), out_shape=(...  2.61 us
  transfers between devices with their start and end apart: 24, of which 9 were waited for; matrix products, arithmetic and copies ran while one was open for 1% of the time, Pallas kernels for 18%

profile of v4, /device:TPU:0, one launch (start us, length us, event | category | flops | bytes accessed | tf_op | source)
XLA Modules:
  0.0 82.7 jit_solution(2220596285757386331)
XLA Ops:
  0.0 3.1 %collective-permute-start.15 = (bf16[1024,256]{1,0:T(8,128)(2,1)}, bf16[1024,256]{1,0:T(8,128)(2,1)S(1)}, u32[]{:S(2)}, u32[]{:S(2)}) collective-permute-start(bf16[1024,256]{1,0:T(8,128)(2,1)} %refs_4_.3), channel_id=1, source_target_pairs={{0,8},{2,10},{4,12},{6,14},{8,0},{10,2},{12,4},{14,6},{16,24},{18,... | collective-permute-start | bytes 1572872 | tf_op jit(solution)/shard_map/ppermute | solution.py:626
  3.1 2.5 %collective-permute-start.16 = (bf16[1024,256]{1,0:T(8,128)(2,1)}, bf16[1024,256]{1,0:T(8,128)(2,1)S(1)}, u32[]{:S(2)}, u32[]{:S(2)}) collective-permute-start(bf16[1024,256]{1,0:T(8,128)(2,1)} %refs_4_.3), channel_id=1, source_target_pairs={{0,24},{2,26},{4,28},{6,30},{8,16},{10,18},{12,20},{14,22},{16,8},... | collective-permute-start | bytes 1572872 | tf_op jit(solution)/shard_map/ppermute | solution.py:626
  6.7 1.6 %collective-permute-start.3 = (bf16[2,128,256]{2,1,0:T(8,128)(2,1)S(1)}, bf16[2,128,256]{2,1,0:T(8,128)(2,1)S(1)}, u32[]{:S(2)}, u32[]{:S(2)}) collective-permute-start(bf16[2,128,256]{2,1,0:T(8,128)(2,1)S(1)} %get-tuple-element.56), channel_id=1, source_target_pairs={{0,2},{2,0},{4,6},{6,4},{8,10},{10,8},{12,14},{14,12},{16,18},{18,... | collective-permute-start | bytes 393224 | tf_op jit(solution)/shard_map/ppermute | solution.py:593
  8.3 1.5 %collective-permute-start.4 = (bf16[2,128,256]{2,1,0:T(8,128)(2,1)S(1)}, bf16[2,128,256]{2,1,0:T(8,128)(2,1)S(1)}, u32[]{:S(2)}, u32[]{:S(2)}) collective-permute-start(bf16[2,128,256]{2,1,0:T(8,128)(2,1)S(1)} %get-tuple-element.58), channel_id=1, source_target_pairs={{0,4},{2,6},{4,0},{6,2},{8,12},{10,14},{12,8},{14,10},{16,20},{18,... | collective-permute-start | bytes 393224 | tf_op jit(solution)/shard_map/ppermute | solution.py:593
  11.8 2.4 %collective-permute-start.2 = (bf16[272,256]{1,0:T(8,128)(2,1)S(1)}, bf16[272,256]{1,0:T(8,128)(2,1)S(1)}, u32[]{:S(2)}, u32[]{:S(2)}) collective-permute-start(bf16[272,256]{1,0:T(8,128)(2,1)S(1)} %get-tuple-element.33), channel_id=1, source_target_pairs={{0,6},{2,4},{4,2},{6,0},{8,14},{10,12},{12,10},{14,8},{16,22},{18,... | collective-permute-start | bytes 417800 | tf_op jit(solution)/shard_map/ppermute | solution.py:593
  14.2 1.5 %collective-permute-done.4.refs_6_ = bf16[2,128,256]{2,1,0:T(8,128)(2,1)S(1)} collective-permute-done((bf16[2,128,256]{2,1,0:T(8,128)(2,1)S(1)}, bf16[2,128,256]{2,1,0:T(8,128)(2,1)S(1)}, u32[]{:S(2)}, u32[]{:S(2)}) %collective-permute-start.4) | collective-permute-done | bytes 131104 | tf_op jit(solution)/shard_map/ppermute | solution.py:593
  15.7 4.4 %collective-permute-done.1.refs_0_.refs_2_ = bf16[272,256]{1,0:T(8,128)(2,1)S(1)} collective-permute-done((bf16[272,256]{1,0:T(8,128)(2,1)S(1)}, bf16[272,256]{1,0:T(8,128)(2,1)S(1)}, u32[]{:S(2)}, u32[]{:S(2)}) %collective-permute-start.1) | collective-permute-done | bytes 139296 | tf_op jit(solution)/shard_map/ppermute | solution.py:593
  20.8 8.0 %collective-permute-done.16.refs_5_.refs_6_ = bf16[1024,256]{1,0:T(8,128)(2,1)S(1)} collective-permute-done((bf16[1024,256]{1,0:T(8,128)(2,1)}, bf16[1024,256]{1,0:T(8,128)(2,1)S(1)}, u32[]{:S(2)}, u32[]{:S(2)}) %collective-permute-start.16) | collective-permute-done | bytes 524320 | tf_op jit(solution)/shard_map/ppermute | solution.py:626
  30.1 1.6 %collective-permute-start.10 = (bf16[128,256]{1,0:T(8,128)(2,1)S(1)}, bf16[128,256]{1,0:T(8,128)(2,1)S(1)}, u32[]{:S(2)}, u32[]{:S(2)}) collective-permute-start(bf16[128,256]{1,0:T(8,128)(2,1)S(1)} %get-tuple-element.62), channel_id=1, source_target_pairs={{0,4},{2,6},{4,0},{6,2},{8,12},{10,14},{12,8},{14,10},{16,20},{18,... | collective-permute-start | bytes 196616 | tf_op jit(solution)/shard_map/ppermute | solution.py:593
  33.1 3.3 %invert.3 = (f32[2,2,3,128,128]{4,3,2,1,0:T(8,128)S(1)}, f32[2,2,8,256]{3,2,1,0:T(8,128)S(1)}) custom-call(bf16[272,256]{1,0:T(8,128)(2,1)S(1)} %collective-permute-done.1.refs_0_.refs_2_, bf16[272,256]{1,0:T(8,128)(2,1)S(1)} %collective-permute-done.2.refs_1_.refs_3_), custom_call_target="tpu_custom_call" | custom-call | tf_op jit(solution)/shard_map/invert/pallas_call | solution.py:207
  36.4 3.3 %invert.2 = (f32[2,2,3,128,128]{4,3,2,1,0:T(8,128)S(1)}, f32[2,2,8,256]{3,2,1,0:T(8,128)S(1)}) custom-call(bf16[272,256]{1,0:T(8,128)(2,1)S(1)} %get-tuple-element.30.refs_0_, bf16[272,256]{1,0:T(8,128)(2,1)S(1)} %collective-permute-done.refs_1_), custom_call_target="tpu_custom_call" | custom-call | tf_op jit(solution)/shard_map/invert/pallas_call | solution.py:207
  40.3 2.6 %carry_state.1 = (bf16[2,4,256,256]{3,2,1,0:T(8,128)(2,1)S(1)}, bf16[2,4,256,256]{3,2,1,0:T(8,128)(2,1)S(1)}, f32[2,4,128,256]{3,2,1,0:T(8,128)S(1)}, bf16[2,128...) custom-call(bf16[272,256]{1,0:T(8,128)(2,1)S(1)} %get-tuple-element.30.refs_0_, ...), custom_call_target="tpu_custom_call" | custom-call | tf_op jit(solution)/shard_map/carry_state/pallas_call | solution.py:319
  43.0 4.6 %collective-permute-start.6 = (bf16[2,128,256]{2,1,0:T(8,128)(2,1)S(1)}, bf16[2,128,256]{2,1,0:T(8,128)(2,1)S(1)}, u32[]{:S(2)}, u32[]{:S(2)}) collective-permute-start(bf16[2,128,256]{2,1,0:T(8,128)(2,1)S(1)} %get-tuple-element.38), channel_id=1, source_target_pairs={{0,8},{2,10},{4,12},{6,14},{8,16},{10,18},{12,20},{14,22},{16,24},... | collective-permute-start | bytes 393224 | tf_op jit(solution)/shard_map/ppermute | solution.py:639
  47.6 2.6 %collective-permute-start.7 = (bf16[2,128,256]{2,1,0:T(8,128)(2,1)S(1)}, bf16[2,128,256]{2,1,0:T(8,128)(2,1)S(1)}, u32[]{:S(2)}, u32[]{:S(2)}) collective-permute-start(bf16[2,128,256]{2,1,0:T(8,128)(2,1)S(1)} %get-tuple-element.38), channel_id=1, source_target_pairs={{0,16},{2,18},{4,20},{6,22},{8,24},{10,26},{12,28},{14,30},{1,17},... | collective-permute-start | bytes 393224 | tf_op jit(solution)/shard_map/ppermute | solution.py:639
  50.2 1.5 %collective-permute-start.8 = (bf16[2,128,128]{2,1,0:T(8,128)(2,1)S(1)}, bf16[2,128,128]{2,1,0:T(8,128)(2,1)S(1)}, u32[]{:S(2)}, u32[]{:S(2)}) collective-permute-start(bf16[2,128,128]{2,1,0:T(8,128)(2,1)S(1)} %get-tuple-element.39), channel_id=1, source_target_pairs={{0,24},{2,26},{4,28},{6,30},{1,25},{3,27},{5,29},{7,31}} | collective-permute-start | bytes 196616 | tf_op jit(solution)/shard_map/ppermute | solution.py:639
  51.7 3.1 %read.1 = (f32[512,256]{1,0:T(8,128)S(1)}, bf16[512,256]{1,0:T(8,128)(2,1)S(1)}) custom-call(bf16[272,256]{1,0:T(8,128)(2,1)S(1)} %get-tuple-element.30.refs_0_, bf16[272,256]{1,0:T(8,128)(2,1)S(1)} %collective-permute-done.refs_1_, bf16[272,256]{1,0:T(8,128)(2,1)S(1)} %collective-permute-done.1.refs_0_.refs_2_, ...), custom_call_target="tpu_custom_call" | custom-call | tf_op jit(solution)/shard_map/read/pallas_call | solution.py:378
  55.4 1.6 %collective-permute-start.12 = (bf16[512,256]{1,0:T(8,128)(2,1)S(1)}, bf16[512,256]{1,0:T(8,128)(2,1)S(1)}, u32[]{:S(2)}, u32[]{:S(2)}) collective-permute-start(bf16[512,256]{1,0:T(8,128)(2,1)S(1)} %join.1.refs_0_), channel_id=1, source_target_pairs={{0,2},{2,0},{4,6},{6,4},{8,10},{10,8},{12,14},{14,12},{16,18},{18,... | collective-permute-start | bytes 786440 | tf_op jit(solution)/shard_map/ppermute | solution.py:593
  56.9 1.5 %collective-permute-start.13 = (bf16[512,256]{1,0:T(8,128)(2,1)S(1)}, bf16[512,256]{1,0:T(8,128)(2,1)S(1)}, u32[]{:S(2)}, u32[]{:S(2)}) collective-permute-start(bf16[512,256]{1,0:T(8,128)(2,1)S(1)} %join.1.refs_0_), channel_id=1, source_target_pairs={{0,4},{2,6},{4,0},{6,2},{8,12},{10,14},{12,8},{14,10},{16,20},{18,... | collective-permute-start | bytes 786440 | tf_op jit(solution)/shard_map/ppermute | solution.py:593
  58.9 4.3 %collective-permute-done.12.refs_1_ = bf16[512,256]{1,0:T(8,128)(2,1)S(1)} collective-permute-done((bf16[512,256]{1,0:T(8,128)(2,1)S(1)}, bf16[512,256]{1,0:T(8,128)(2,1)S(1)}, u32[]{:S(2)}, u32[]{:S(2)}) %collective-permute-start.12) | collective-permute-done | bytes 262176 | tf_op jit(solution)/shard_map/ppermute | solution.py:593
  63.2 4.0 %collective-permute-done.13.refs_2_ = bf16[512,256]{1,0:T(8,128)(2,1)S(1)} collective-permute-done((bf16[512,256]{1,0:T(8,128)(2,1)S(1)}, bf16[512,256]{1,0:T(8,128)(2,1)S(1)}, u32[]{:S(2)}, u32[]{:S(2)}) %collective-permute-start.13) | collective-permute-done | bytes 262176 | tf_op jit(solution)/shard_map/ppermute | solution.py:593
  71.4 2.6 %collective-permute-start.23 = (bf16[128,512]{1,0:T(8,128)(2,1)S(1)}, bf16[128,512]{1,0:T(8,128)(2,1)S(1)}, u32[]{:S(2)}, u32[]{:S(2)}) collective-permute-start(bf16[128,512]{1,0:T(8,128)(2,1)S(1)} %get-tuple-element.54), channel_id=1, source_target_pairs={{0,6},{2,4},{4,2},{6,0},{8,14},{10,12},{12,10},{14,8},{16,22},{18,... | collective-permute-start | bytes 393224 | tf_op jit(solution)/shard_map/ppermute | solution.py:593
  74.6 2.7 %collective-permute-done.21.refs_1_ = bf16[128,512]{1,0:T(8,128)(2,1)S(1)} collective-permute-done((bf16[128,512]{1,0:T(8,128)(2,1)S(1)}, bf16[128,512]{1,0:T(8,128)(2,1)S(1)}, u32[]{:S(2)}, u32[]{:S(2)}) %collective-permute-start.21) | collective-permute-done | bytes 131104 | tf_op jit(solution)/shard_map/ppermute | solution.py:593
  77.4 2.9 %collective-permute-done.23.refs_3_ = bf16[128,512]{1,0:T(8,128)(2,1)S(1)} collective-permute-done((bf16[128,512]{1,0:T(8,128)(2,1)S(1)}, bf16[128,512]{1,0:T(8,128)(2,1)S(1)}, u32[]{:S(2)}, u32[]{:S(2)}) %collective-permute-start.23) | collective-permute-done | bytes 131104 | tf_op jit(solution)/shard_map/ppermute | solution.py:593
  80.2 1.5 %collective-permute-done.22.refs_2_ = bf16[128,512]{1,0:T(8,128)(2,1)S(1)} collective-permute-done((bf16[128,512]{1,0:T(8,128)(2,1)S(1)}, bf16[128,512]{1,0:T(8,128)(2,1)S(1)}, u32[]{:S(2)}, u32[]{:S(2)}) %collective-permute-start.22) | collective-permute-done | bytes 131104 | tf_op jit(solution)/shard_map/ppermute | solution.py:593
  (46 shorter events, 13.8 us)
Async XLA Ops:
  0.0 20.1 %collective-permute-start.15 = (bf16[1024,256]{1,0:T(8,128)(2,1)}, bf16[1024,256]{1,0:T(8,128)(2,1)S(1)}, u32[]{:S(2)}, u32[]{:S(2)}) collective-permute-start(bf16[1024,256]{1,0:T(8,128)(2,1)} %refs_4_.3), channel_id=1, source_target_pairs={{0,8},{2,10},{4,12},{6,14},{8,0},{10,2},{12,4},{14,6},{16,24},{18,... | collective-permute-start | bytes 1572872 | tf_op jit(solution)/shard_map/ppermute | solution.py:626
  3.1 25.7 %collective-permute-start.16 = (bf16[1024,256]{1,0:T(8,128)(2,1)}, bf16[1024,256]{1,0:T(8,128)(2,1)S(1)}, u32[]{:S(2)}, u32[]{:S(2)}) collective-permute-start(bf16[1024,256]{1,0:T(8,128)(2,1)} %refs_4_.3), channel_id=1, source_target_pairs={{0,24},{2,26},{4,28},{6,30},{8,16},{10,18},{12,20},{14,22},{16,8},... | collective-permute-start | bytes 1572872 | tf_op jit(solution)/shard_map/ppermute | solution.py:626
  6.7 5.0 %collective-permute-start.3 = (bf16[2,128,256]{2,1,0:T(8,128)(2,1)S(1)}, bf16[2,128,256]{2,1,0:T(8,128)(2,1)S(1)}, u32[]{:S(2)}, u32[]{:S(2)}) collective-permute-start(bf16[2,128,256]{2,1,0:T(8,128)(2,1)S(1)} %get-tuple-element.56), channel_id=1, source_target_pairs={{0,2},{2,0},{4,6},{6,4},{8,10},{10,8},{12,14},{14,12},{16,18},{18,... | collective-permute-start | bytes 393224 | tf_op jit(solution)/shard_map/ppermute | solution.py:593
  8.3 7.4 %collective-permute-start.4 = (bf16[2,128,256]{2,1,0:T(8,128)(2,1)S(1)}, bf16[2,128,256]{2,1,0:T(8,128)(2,1)S(1)}, u32[]{:S(2)}, u32[]{:S(2)}) collective-permute-start(bf16[2,128,256]{2,1,0:T(8,128)(2,1)S(1)} %get-tuple-element.58), channel_id=1, source_target_pairs={{0,4},{2,6},{4,0},{6,2},{8,12},{10,14},{12,8},{14,10},{16,20},{18,... | collective-permute-start | bytes 393224 | tf_op jit(solution)/shard_map/ppermute | solution.py:593
  9.9 10.2 %collective-permute-start.1 = (bf16[272,256]{1,0:T(8,128)(2,1)S(1)}, bf16[272,256]{1,0:T(8,128)(2,1)S(1)}, u32[]{:S(2)}, u32[]{:S(2)}) collective-permute-start(bf16[272,256]{1,0:T(8,128)(2,1)S(1)} %get-tuple-element.32), channel_id=1, source_target_pairs={{0,4},{2,6},{4,0},{6,2},{8,12},{10,14},{12,8},{14,10},{16,20},{18,... | collective-permute-start | bytes 417800 | tf_op jit(solution)/shard_map/ppermute | solution.py:593
  11.8 18.3 %collective-permute-start.2 = (bf16[272,256]{1,0:T(8,128)(2,1)S(1)}, bf16[272,256]{1,0:T(8,128)(2,1)S(1)}, u32[]{:S(2)}, u32[]{:S(2)}) collective-permute-start(bf16[272,256]{1,0:T(8,128)(2,1)S(1)} %get-tuple-element.33), channel_id=1, source_target_pairs={{0,6},{2,4},{4,2},{6,0},{8,14},{10,12},{12,10},{14,8},{16,22},{18,... | collective-permute-start | bytes 417800 | tf_op jit(solution)/shard_map/ppermute | solution.py:593
  15.7 16.0 %collective-permute-start = (bf16[272,256]{1,0:T(8,128)(2,1)S(1)}, bf16[272,256]{1,0:T(8,128)(2,1)S(1)}, u32[]{:S(2)}, u32[]{:S(2)}) collective-permute-start(bf16[272,256]{1,0:T(8,128)(2,1)S(1)} %get-tuple-element.31), channel_id=1, source_target_pairs={{0,2},{2,0},{4,6},{6,4},{8,10},{10,8},{12,14},{14,12},{16,18},{18,... | collective-permute-start | bytes 417800 | tf_op jit(solution)/shard_map/ppermute | solution.py:593
  20.1 19.7 %collective-permute-start.5 = (bf16[2,128,256]{2,1,0:T(8,128)(2,1)S(1)}, bf16[2,128,256]{2,1,0:T(8,128)(2,1)S(1)}, u32[]{:S(2)}, u32[]{:S(2)}) collective-permute-start(bf16[2,128,256]{2,1,0:T(8,128)(2,1)S(1)} %get-tuple-element.55), channel_id=1, source_target_pairs={{0,6},{2,4},{4,2},{6,0},{8,14},{10,12},{12,10},{14,8},{16,22},{18,... | collective-permute-start | bytes 393224 | tf_op jit(solution)/shard_map/ppermute | solution.py:593
  20.1 48.0 %collective-permute-start.17 = (bf16[1024,256]{1,0:T(8,128)(2,1)S(1)}, bf16[1024,256]{1,0:T(8,128)(2,1)S(1)}, u32[]{:S(2)}, u32[]{:S(2)}) collective-permute-start(bf16[1024,256]{1,0:T(8,128)(2,1)S(1)} %collective-permute-done.15.refs_4_.refs_5_), channel_id=1, source_target_pairs={{8,16},{10,18},{12,20},{14,22},{16,8},{18,10},{20,12},{22,14},{9,1... | collective-permute-start | bytes 1572872 | tf_op jit(solution)/shard_map/ppermute | solution.py:660
  28.7 39.3 %collective-permute-start.18 = (bf16[1024,256]{1,0:T(8,128)(2,1)S(1)}, bf16[1024,256]{1,0:T(8,128)(2,1)S(1)}, u32[]{:S(2)}, u32[]{:S(2)}) collective-permute-start(bf16[1024,256]{1,0:T(8,128)(2,1)S(1)} %collective-permute-done.16.refs_5_.refs_6_), channel_id=1, source_target_pairs={{8,0},{10,2},{12,4},{14,6},{16,24},{18,26},{20,28},{22,30},{9,1},{... | collective-permute-start | bytes 1572872 | tf_op jit(solution)/shard_map/ppermute | solution.py:660
  30.1 12.9 %collective-permute-start.10 = (bf16[128,256]{1,0:T(8,128)(2,1)S(1)}, bf16[128,256]{1,0:T(8,128)(2,1)S(1)}, u32[]{:S(2)}, u32[]{:S(2)}) collective-permute-start(bf16[128,256]{1,0:T(8,128)(2,1)S(1)} %get-tuple-element.62), channel_id=1, source_target_pairs={{0,4},{2,6},{4,0},{6,2},{8,12},{10,14},{12,8},{14,10},{16,20},{18,... | collective-permute-start | bytes 196616 | tf_op jit(solution)/shard_map/ppermute | solution.py:593
  31.7 15.9 %collective-permute-start.11 = (bf16[128,256]{1,0:T(8,128)(2,1)S(1)}, bf16[128,256]{1,0:T(8,128)(2,1)S(1)}, u32[]{:S(2)}, u32[]{:S(2)}) collective-permute-start(bf16[128,256]{1,0:T(8,128)(2,1)S(1)} %get-tuple-element.59), channel_id=1, source_target_pairs={{0,6},{2,4},{4,2},{6,0},{8,14},{10,12},{12,10},{14,8},{16,22},{18,... | collective-permute-start | bytes 196616 | tf_op jit(solution)/shard_map/ppermute | solution.py:593
  39.7 10.5 %collective-permute-start.9 = (bf16[128,256]{1,0:T(8,128)(2,1)S(1)}, bf16[128,256]{1,0:T(8,128)(2,1)S(1)}, u32[]{:S(2)}, u32[]{:S(2)}) collective-permute-start(bf16[128,256]{1,0:T(8,128)(2,1)S(1)} %get-tuple-element.60), channel_id=1, source_target_pairs={{0,2},{2,0},{4,6},{6,4},{8,10},{10,8},{12,14},{14,12},{16,18},{18,... | collective-permute-start | bytes 196616 | tf_op jit(solution)/shard_map/ppermute | solution.py:593
  43.0 11.9 %collective-permute-start.6 = (bf16[2,128,256]{2,1,0:T(8,128)(2,1)S(1)}, bf16[2,128,256]{2,1,0:T(8,128)(2,1)S(1)}, u32[]{:S(2)}, u32[]{:S(2)}) collective-permute-start(bf16[2,128,256]{2,1,0:T(8,128)(2,1)S(1)} %get-tuple-element.38), channel_id=1, source_target_pairs={{0,8},{2,10},{4,12},{6,14},{8,16},{10,18},{12,20},{14,22},{16,24},... | collective-permute-start | bytes 393224 | tf_op jit(solution)/shard_map/ppermute | solution.py:639
  47.6 7.3 %collective-permute-start.7 = (bf16[2,128,256]{2,1,0:T(8,128)(2,1)S(1)}, bf16[2,128,256]{2,1,0:T(8,128)(2,1)S(1)}, u32[]{:S(2)}, u32[]{:S(2)}) collective-permute-start(bf16[2,128,256]{2,1,0:T(8,128)(2,1)S(1)} %get-tuple-element.38), channel_id=1, source_target_pairs={{0,16},{2,18},{4,20},{6,22},{8,24},{10,26},{12,28},{14,30},{1,17},... | collective-permute-start | bytes 393224 | tf_op jit(solution)/shard_map/ppermute | solution.py:639
  50.2 4.6 %collective-permute-start.8 = (bf16[2,128,128]{2,1,0:T(8,128)(2,1)S(1)}, bf16[2,128,128]{2,1,0:T(8,128)(2,1)S(1)}, u32[]{:S(2)}, u32[]{:S(2)}) collective-permute-start(bf16[2,128,128]{2,1,0:T(8,128)(2,1)S(1)} %get-tuple-element.39), channel_id=1, source_target_pairs={{0,24},{2,26},{4,28},{6,30},{1,25},{3,27},{5,29},{7,31}} | collective-permute-start | bytes 196616 | tf_op jit(solution)/shard_map/ppermute | solution.py:639
  55.4 7.8 %collective-permute-start.12 = (bf16[512,256]{1,0:T(8,128)(2,1)S(1)}, bf16[512,256]{1,0:T(8,128)(2,1)S(1)}, u32[]{:S(2)}, u32[]{:S(2)}) collective-permute-start(bf16[512,256]{1,0:T(8,128)(2,1)S(1)} %join.1.refs_0_), channel_id=1, source_target_pairs={{0,2},{2,0},{4,6},{6,4},{8,10},{10,8},{12,14},{14,12},{16,18},{18,... | collective-permute-start | bytes 786440 | tf_op jit(solution)/shard_map/ppermute | solution.py:593
  56.9 10.3 %collective-permute-start.13 = (bf16[512,256]{1,0:T(8,128)(2,1)S(1)}, bf16[512,256]{1,0:T(8,128)(2,1)S(1)}, u32[]{:S(2)}, u32[]{:S(2)}) collective-permute-start(bf16[512,256]{1,0:T(8,128)(2,1)S(1)} %join.1.refs_0_), channel_id=1, source_target_pairs={{0,4},{2,6},{4,0},{6,2},{8,12},{10,14},{12,8},{14,10},{16,20},{18,... | collective-permute-start | bytes 786440 | tf_op jit(solution)/shard_map/ppermute | solution.py:593
  58.5 9.6 %collective-permute-start.14 = (bf16[512,256]{1,0:T(8,128)(2,1)S(1)}, bf16[512,256]{1,0:T(8,128)(2,1)S(1)}, u32[]{:S(2)}, u32[]{:S(2)}) collective-permute-start(bf16[512,256]{1,0:T(8,128)(2,1)S(1)} %join.1.refs_0_), channel_id=1, source_target_pairs={{0,6},{2,4},{4,2},{6,0},{8,14},{10,12},{12,10},{14,8},{16,22},{18,... | collective-permute-start | bytes 786440 | tf_op jit(solution)/shard_map/ppermute | solution.py:593
  69.1 1.7 %collective-permute-start.20 = (bf16[256,512]{1,0:T(8,128)(2,1)S(1)}, bf16[256,512]{1,0:T(8,128)(2,1)S(1)}, u32[]{:S(2)}, u32[]{:S(2)}) collective-permute-start(bf16[256,512]{1,0:T(8,128)(2,1)S(1)} %get-tuple-element.51), channel_id=1, source_target_pairs={{0,1},{1,0},{2,3},{3,2},{4,5},{5,4},{6,7},{7,6},{8,9},{9,8},{10,11... | collective-permute-start | bytes 786440 | tf_op jit(solution)/shard_map/ppermute | solution.py:677
  70.3 3.6 %collective-permute-start.19 = (bf16[256,512]{1,0:T(8,128)(2,1)S(1)}, bf16[256,512]{1,0:T(8,128)(2,1)S(1)}, u32[]{:S(2)}, u32[]{:S(2)}) collective-permute-start(bf16[256,512]{1,0:T(8,128)(2,1)S(1)} %get-tuple-element.47), channel_id=1, source_target_pairs={{0,1},{1,0},{2,3},{3,2},{4,5},{5,4},{6,7},{7,6},{8,9},{9,8},{10,11... | collective-permute-start | bytes 786440 | tf_op jit(solution)/shard_map/ppermute | solution.py:677
  70.9 6.4 %collective-permute-start.21 = (bf16[128,512]{1,0:T(8,128)(2,1)S(1)}, bf16[128,512]{1,0:T(8,128)(2,1)S(1)}, u32[]{:S(2)}, u32[]{:S(2)}) collective-permute-start(bf16[128,512]{1,0:T(8,128)(2,1)S(1)} %get-tuple-element.52), channel_id=1, source_target_pairs={{0,2},{2,0},{4,6},{6,4},{8,10},{10,8},{12,14},{14,12},{16,18},{18,... | collective-permute-start | bytes 393224 | tf_op jit(solution)/shard_map/ppermute | solution.py:593
  71.4 8.9 %collective-permute-start.23 = (bf16[128,512]{1,0:T(8,128)(2,1)S(1)}, bf16[128,512]{1,0:T(8,128)(2,1)S(1)}, u32[]{:S(2)}, u32[]{:S(2)}) collective-permute-start(bf16[128,512]{1,0:T(8,128)(2,1)S(1)} %get-tuple-element.54), channel_id=1, source_target_pairs={{0,6},{2,4},{4,2},{6,0},{8,14},{10,12},{12,10},{14,8},{16,22},{18,... | collective-permute-start | bytes 393224 | tf_op jit(solution)/shard_map/ppermute | solution.py:593
  74.0 7.7 %collective-permute-start.22 = (bf16[128,512]{1,0:T(8,128)(2,1)S(1)}, bf16[128,512]{1,0:T(8,128)(2,1)S(1)}, u32[]{:S(2)}, u32[]{:S(2)}) collective-permute-start(bf16[128,512]{1,0:T(8,128)(2,1)S(1)} %get-tuple-element.53), channel_id=1, source_target_pairs={{0,4},{2,6},{4,0},{6,2},{8,12},{10,14},{12,8},{14,10},{16,20},{18,... | collective-permute-start | bytes 393224 | tf_op jit(solution)/shard_map/ppermute | solution.py:593
  (4 other events, 42.7 us)

commit v5 on v4

--- a/solution.py
+++ b/solution.py
@@ -81,21 +81,39 @@
     return -(-4 * max(tokens // width, 1) // 16) * 16
 
 
-def pack_kernel(group, key_ref, beta_ref, *outs):
+def pack_kernel(group, key_ref, value_ref, query_ref, strength_ref, *refs):
+    key_outs, rest_outs, (beta_ref, sems) = refs[:group], refs[group : 2 * group], refs[-2:]
     _, heads, tokens = beta_ref.shape
     mine = heads // group
-    wide = outs[0].shape[1]
+    wide = key_outs[0].shape[1]
     width = wide // mine
     pieces = max(tokens // width, 1)
     inside = tokens // pieces
     position, _ = where_am_i(group)
-    for offset, out_ref in enumerate(outs):
+    first_copy = pltpu.make_async_copy(strength_ref, beta_ref, sems.at[0])
+    pairs = []
+    for offset in range(group):
+        lanes = pl.ds(pl.multiple_of(place(position, offset) * wide, wide), wide)
+        for reflection in range(2):
+            rows = pl.ds(reflection * tokens, tokens)
+            pairs.append((key_ref.at[reflection, :, lanes], key_outs[offset].at[rows, :]))
+    for offset in range(group):
+        lanes = pl.ds(pl.multiple_of(place(position, offset) * wide, wide), wide)
+        for reflection in range(2):
+            pairs.append(
+                (value_ref.at[reflection, :, lanes], rest_outs[offset].at[reflection])
+            )
+        pairs.append((query_ref.at[:, lanes], rest_outs[offset].at[2]))
+    copies = [
+        pltpu.make_async_copy(source, target, sems.at[1 + number])
+        for number, (source, target) in enumerate(pairs)
+    ]
+    first_copy.start()
+    for copy in copies:
+        copy.start()
+    first_copy.wait()
+    for offset, out_ref in enumerate(key_outs):
         member = place(position, offset)
-        lanes = pl.ds(pl.multiple_of(member * wide, wide), wide)
-        for reflection in range(2):
-            out_ref[reflection * tokens : (reflection + 1) * tokens, :] = key_ref[
-                reflection, :, lanes
-            ]
         rows = []
         for reflection in range(2):
             for piece in range(pieces):
@@ -110,20 +128,33 @@
         high = both.astype(BF16).astype(F32)
         spare = jnp.zeros((out_ref.shape[0] - 2 * tokens - 2 * len(rows), wide), F32)
         out_ref[2 * tokens :, :] = jnp.concatenate([high, both - high, spare], axis=0).astype(BF16)
-
-
-def pack_keys(key_vectors, strengths, group):
+    for copy in copies:
+        copy.wait()
+
+
+def pack(queries, key_vectors, values, strengths, group):
     _, tokens, wide = key_vectors.shape
     width = wide // strengths.shape[1]
     shape = (2 * tokens + beta_rows(tokens, width), wide // group)
-    return pl.pallas_call(
+    out = pl.pallas_call(
         functools.partial(pack_kernel, group),
-        out_shape=[pltpu.VMEM(shape, BF16)] * group,
-        in_specs=[VMEM] * 2,
-        out_specs=[VMEM] * group,
-        compiler_params=PARAMS,
-        name="pack_keys",
-    )(*held(key_vectors, strengths))
+        out_shape=[pltpu.VMEM(shape, BF16)] * group
+        + [pltpu.VMEM((3, tokens, wide // group), BF16)] * group,
+        in_specs=[pl.BlockSpec(memory_space=pltpu.HBM)] * 4,
+        out_specs=[VMEM] * (2 * group),
+        scratch_shapes=[
+            pltpu.VMEM(strengths.shape, F32),
+            pltpu.SemaphoreType.DMA((1 + 5 * group,)),
+        ],
+        compiler_params=PARAMS,
+        name="pack",
+    )(
+        *(
+            pltpu.with_memory_space_constraint(array, pltpu.HBM)
+            for array in (key_vectors, values, queries, strengths)
+        )
+    )
+    return list(out[:group]), list(out[group:])
 
 
 def invert_kernel(heads, tokens, *refs):
@@ -338,8 +369,8 @@
     heads, chunks, wide, _ = high_ref.shape
     chunk = wide // 2
     half = chunk // 2
-    tokens = rest_in[0].shape[0]
-    width = rest_in[0].shape[1] // heads
+    tokens = rest_in[0].shape[1]
+    width = rest_in[0].shape[2] // heads
     per_source = tokens // chunk
     token_row = iota((chunk, 2 * chunk), 0)
     token_col = iota((chunk, 2 * chunk), 1)
@@ -357,7 +388,7 @@
             lanes = lanes_of(head, width)
             source, first = index // per_source, (index % per_source) * chunk
             key = woven_key(key_in[source], tokens, first, chunk, lanes)
-            query = rest_in[source][first : first + chunk, lanes]
+            query = rest_in[source][2, first : first + chunk, lanes]
             wide_query = query.astype(F32)
             scale = lax.rsqrt(jnp.sum(wide_query * wide_query, axis=1, keepdims=True) + EPS)
             scores = jnp.where(token_col <= token_row, dot_t(query, key) * scale, 0.0)
@@ -374,7 +405,7 @@
 
 def read(keys, rests, high, low, steps):
     group = len(keys)
-    tokens, wide = rests[0].shape
+    _, tokens, wide = rests[0].shape
     return pl.pallas_call(
         functools.partial(read_kernel, group),
         out_shape=(
@@ -427,9 +458,12 @@
 
 def weight_rows(weights, offset, inner, first, count):
     rows = pl.ds(first, count)
+    if offset < 2:
+        return weights[offset][rows, :]
     if offset == 2:
-        return jnp.where(inner, weights[3][rows, :], weights[4][rows, :])
-    return weights[{0: 0, 1: 1, 3: 2}[offset]][rows, :]
+        return jnp.where(inner, weights[5][rows, :], weights[6][rows, :])
+    far = jnp.concatenate([weights[3][rows, :], weights[4][rows, :]], axis=1)
+    return jnp.where(inner, weights[2][rows, :], far)
 
 
 def where_am_i(group):
@@ -605,25 +639,32 @@
     planes = count // group
     position = lax.axis_index("seq") % group
     mine = heads // group
-    keys = list(pack_keys(key_vectors, strengths, group))
-    vals, asks = [], []
-    for offset in range(group):
-        lane = jnp.bitwise_xor(position, offset) * mine * width
-        value = lax.dynamic_slice_in_dim(values, lane, mine * width, 2)
-        ask = lax.dynamic_slice_in_dim(queries, lane, mine * width, 1)
-        if offset:
-            keys[offset] = swap(keys[offset], group, offset, count)
-            value = swap(value, group, offset, count)
-            ask = swap(ask, group, offset, count)
-        vals.append(value)
-        asks.append(ask)
+    keys, rests = pack(queries, key_vectors, values, strengths, group)
+    for offset in range(1, group):
+        keys[offset] = swap(keys[offset], group, offset, count)
+        rests[offset] = swap(rests[offset], group, offset, count)
+
+    def between_planes(value, pairs):
+        return lax.ppermute(
+            value,
+            "seq",
+            [
+                (source * group + i, target * group + i)
+                for source, target in pairs
+                for i in range(group)
+            ],
+        )
 
     split_out = sides == 2 and planes in (2, 4) and group > 1
+    columns = out_weight.shape[1]
     weights = [out_weight]
     if split_out:
-        for offset in range(1, planes, 2):
-            pairs = [(i, ((i // group) ^ offset) * group + i % group) for i in range(count)]
-            weights.append(lax.ppermute(out_weight, "seq", pairs))
+        swapped = [(plane, plane ^ 1) for plane in range(planes)]
+        weights.append(between_planes(out_weight, swapped))
+    if split_out and planes == 4:
+        outer = ((0, 3), (3, 0))
+        weights.append(between_planes(out_weight, ((1, 2), (2, 1))))
+        weights.append(between_planes(out_weight[:, : columns // 2], outer))
 
     near = max(group // 2, 1)
     solved = []
@@ -631,8 +672,8 @@
         if part:
             solved.append(invert(part, mine, tokens))
     inverses, tables = zip(*solved)
-    high, low, steps, state, local_state = carry_state(keys, vals, inverses, tables)
-    local, lifted = read(keys, asks, high, low, steps)
+    high, low, steps, state, local_state = carry_state(keys, rests, inverses, tables)
+    local, lifted = read(keys, rests, high, low, steps)
 
     def from_earlier(value, distance):
         pairs = [(i, i + distance * group) for i in range(count - distance * group)]
@@ -651,21 +692,19 @@
             distance *= 2
         states = [total[:, :, width:]]
     if split_out and planes == 4:
-        for held_weight, hops in ((weights[1], ((1, 2), (2, 1))), (weights[2], ((1, 0), (2, 3)))):
-            pairs = [
-                (source * group + i, target * group + i)
-                for source, target in hops
-                for i in range(group)
-            ]
-            weights.append(lax.ppermute(held_weight, "seq", pairs))
+        late = between_planes(out_weight[:, columns // 2 :], outer)
+        weights += [
+            late,
+            between_planes(weights[1], ((1, 2), (2, 1))),
+            between_planes(weights[2], ((1, 0), (2, 3))),
+        ]
 
     mixed_heads = join(states, local, lifted)
 
     if split_out:
-        order = tuple(reversed(range(group)))
-        order = order[:1] + order[2:-1] + order[1:2] + order[-1:] if group > 2 else order
+        order = tuple(range(1, group)) + (0,)
         row_halves = (order[: group // 2], order[group // 2 :])
-        early = (tuple(range(group - 1)), (0, 1, 3) if planes == 4 else (0, 1))
+        early = (tuple(range(group - 1)), (0, 1))
         parts = [None] * group
         gathered = [mixed_heads]
         for offset in range(1, group):

time: 83 us -> 80 us (0.964)
  waiting for transfers between devices: 30.5 us -> 20.1 us
  starting transfers between devices: 33.7 us -> 40.5 us
  Pallas kernels: 16.8 us -> 18.6 us
  local copies, waits for them, and re-layouts: 1.26 us -> 0.04 us
    ppermute x15 -> x12, waiting for transfers between devices: 22.6 us -> 8.72 us  [swap(): return lax.ppermute(value, 'seq', pairs)]
    ppermute x4 -> x6, starting transfers between devices: 7.49 us -> 14.5 us  [between_planes(): lax.ppermute(value, 'seq', [(source * group + i, target * group + i) for...]
    ppermute x4 -> x6, waiting for transfers between devices: 7.96 us -> 11.4 us  [between_planes(): lax.ppermute(value, 'seq', [(source * group + i, target * group + i) for...]
    pallas_call x1, Pallas kernels: 0.08 us -> 1.54 us  [pack(): pl.pallas_call(functools.partial(pack_kernel, group), out_shape=[pltpu.VM...]
    dynamic_slice x2 -> x0, local copies, waits for them, and re-layouts: 1.24 us -> none  [the longest x1 1.19 us: per_device(): value = lax.dynamic_slice_in_dim(values, lane, mine * width, 2)]
    ppermute x15 -> x12, starting transfers between devices: 16.9 us -> 16.5 us  [swap(): return lax.ppermute(value, 'seq', pairs)]
  transfers between devices with their start and end apart: 24 -> 23, of which waited for: 9 -> 7; matrix products, arithmetic and copies ran while one was open for 1% -> 0% of each run, Pallas kernels for 18% -> 21%
where the time goes in v5:
time: 80 us; the launch traced here: 79.6 us
  starting transfers between devices  40.5 us (51%)
  waiting for transfers between devices  20.1 us (25%)
  Pallas kernels  18.6 us (23%)
    ppermute x12, starting transfers between devices, swap(): return lax.ppermute(value, 'seq', pairs)  16.5 us
    ppermute x6, starting transfers between devices, between_planes(): lax.ppermute(value, 'seq', [(source * group + i, target * group + i) for...  14.5 us
    ppermute x6, waiting for transfers between devices, between_planes(): lax.ppermute(value, 'seq', [(source * group + i, target * group + i) for...  11.4 us
    ppermute x3, starting transfers between devices, from_earlier(): return lax.ppermute(value, 'seq', pairs)  8.94 us
    ppermute x12, waiting for transfers between devices, swap(): return lax.ppermute(value, 'seq', pairs)  8.72 us
    pallas_call x2, Pallas kernels, invert(): pl.pallas_call(functools.partial(invert_kernel, heads, tokens), out_shape...  6.6 us
    pallas_call x1, Pallas kernels, read(): pl.pallas_call(functools.partial(read_kernel, group), out_shape=(pltpu.VM...  3.12 us
    pallas_call x2, Pallas kernels, project(): pl.pallas_call(functools.partial(project_kernel, group, targets, early, o...  2.64 us
  transfers between devices with their start and end apart: 23, of which 7 were waited for; matrix products, arithmetic and copies ran while one was open for 0% of the time, Pallas kernels for 21%

profile of v5, /device:TPU:0, one launch (start us, length us, event | category | flops | bytes accessed | tf_op | source)
XLA Modules:
  0.0 79.6 jit_solution(909096029296537450)
XLA Ops:
  0.0 3.1 %collective-permute-start.12 = (bf16[1024,256]{1,0:T(8,128)(2,1)}, bf16[1024,256]{1,0:T(8,128)(2,1)S(1)}, u32[]{:S(2)}, u32[]{:S(2)}) collective-permute-start(bf16[1024,256]{1,0:T(8,128)(2,1)} %refs_4_.3), channel_id=1, source_target_pairs={{0,8},{2,10},{4,12},{6,14},{8,0},{10,2},{12,4},{14,6},{16,24},{18,... | collective-permute-start | bytes 1572872 | tf_op jit(solution)/shard_map/ppermute | solution.py:648
  3.7 1.5 %pack.1 = (bf16[272,256]{1,0:T(8,128)(2,1)S(1)}, bf16[272,256]{1,0:T(8,128)(2,1)S(1)}, bf16[272,256]{1,0:T(8,128)(2,1)S(1)}, bf16[272,256]{1,0:T(8,128)(2,1)S(1)...) custom-call(bf16[2,128,1024]{2,1,0:T(8,128)(2,1)} %key_ref.1, ...), custom_call_target="tpu_custom_call" | custom-call | tf_op jit(solution)/shard_map/pack/pallas_call | solution.py:139
  5.3 1.6 %collective-permute-start.1 = (bf16[272,256]{1,0:T(8,128)(2,1)S(1)}, bf16[272,256]{1,0:T(8,128)(2,1)S(1)}, u32[]{:S(2)}, u32[]{:S(2)}) collective-permute-start(bf16[272,256]{1,0:T(8,128)(2,1)S(1)} %get-tuple-element.36), channel_id=1, source_target_pairs={{0,4},{2,6},{4,0},{6,2},{8,12},{10,14},{12,8},{14,10},{16,20},{18,... | collective-permute-start | bytes 417800 | tf_op jit(solution)/shard_map/ppermute | solution.py:627
  6.9 1.4 %collective-permute-start.2 = (bf16[272,256]{1,0:T(8,128)(2,1)S(1)}, bf16[272,256]{1,0:T(8,128)(2,1)S(1)}, u32[]{:S(2)}, u32[]{:S(2)}) collective-permute-start(bf16[272,256]{1,0:T(8,128)(2,1)S(1)} %get-tuple-element.37), channel_id=1, source_target_pairs={{0,6},{2,4},{4,2},{6,0},{8,14},{10,12},{12,10},{14,8},{16,22},{18,... | collective-permute-start | bytes 417800 | tf_op jit(solution)/shard_map/ppermute | solution.py:627
  8.8 3.8 %collective-permute-done.1.refs_0_.refs_2_ = bf16[272,256]{1,0:T(8,128)(2,1)S(1)} collective-permute-done((bf16[272,256]{1,0:T(8,128)(2,1)S(1)}, bf16[272,256]{1,0:T(8,128)(2,1)S(1)}, u32[]{:S(2)}, u32[]{:S(2)}) %collective-permute-start.1) | collective-permute-done | bytes 139296 | tf_op jit(solution)/shard_map/ppermute | solution.py:627
  12.6 1.5 %collective-permute-start.3 = (bf16[3,128,256]{2,1,0:T(8,128)(2,1)S(1)}, bf16[3,128,256]{2,1,0:T(8,128)(2,1)S(1)}, u32[]{:S(2)}, u32[]{:S(2)}) collective-permute-start(bf16[3,128,256]{2,1,0:T(8,128)(2,1)S(1)} %get-tuple-element.39), channel_id=1, source_target_pairs={{0,2},{2,0},{4,6},{6,4},{8,10},{10,8},{12,14},{14,12},{16,18},{18,... | collective-permute-start | bytes 589832 | tf_op jit(solution)/shard_map/ppermute | solution.py:627
  14.2 2.3 %collective-permute-start.4 = (bf16[3,128,256]{2,1,0:T(8,128)(2,1)S(1)}, bf16[3,128,256]{2,1,0:T(8,128)(2,1)S(1)}, u32[]{:S(2)}, u32[]{:S(2)}) collective-permute-start(bf16[3,128,256]{2,1,0:T(8,128)(2,1)S(1)} %get-tuple-element.40), channel_id=1, source_target_pairs={{0,4},{2,6},{4,0},{6,2},{8,12},{10,14},{12,8},{14,10},{16,20},{18,... | collective-permute-start | bytes 589832 | tf_op jit(solution)/shard_map/ppermute | solution.py:627
  16.5 1.5 %collective-permute-start.5 = (bf16[3,128,256]{2,1,0:T(8,128)(2,1)S(1)}, bf16[3,128,256]{2,1,0:T(8,128)(2,1)S(1)}, u32[]{:S(2)}, u32[]{:S(2)}) collective-permute-start(bf16[3,128,256]{2,1,0:T(8,128)(2,1)S(1)} %get-tuple-element.41), channel_id=1, source_target_pairs={{0,6},{2,4},{4,2},{6,0},{8,14},{10,12},{12,10},{14,8},{16,22},{18,... | collective-permute-start | bytes 589832 | tf_op jit(solution)/shard_map/ppermute | solution.py:627
  18.0 3.3 %invert.3 = (f32[2,2,3,128,128]{4,3,2,1,0:T(8,128)S(1)}, f32[2,2,8,256]{3,2,1,0:T(8,128)S(1)}) custom-call(bf16[272,256]{1,0:T(8,128)(2,1)S(1)} %collective-permute-done.1.refs_0_.refs_2_, bf16[272,256]{1,0:T(8,128)(2,1)S(1)} %collective-permute-done.2.refs_1_.refs_3_), custom_call_target="tpu_custom_call" | custom-call | tf_op jit(solution)/shard_map/invert/pallas_call | solution.py:238
  21.2 3.3 %invert.2 = (f32[2,2,3,128,128]{4,3,2,1,0:T(8,128)S(1)}, f32[2,2,8,256]{3,2,1,0:T(8,128)S(1)}) custom-call(bf16[272,256]{1,0:T(8,128)(2,1)S(1)} %get-tuple-element.34.refs_0_, bf16[272,256]{1,0:T(8,128)(2,1)S(1)} %collective-permute-done.refs_1_), custom_call_target="tpu_custom_call" | custom-call | tf_op jit(solution)/shard_map/invert/pallas_call | solution.py:238
  24.6 2.6 %carry_state.1 = (bf16[2,4,256,256]{3,2,1,0:T(8,128)(2,1)S(1)}, bf16[2,4,256,256]{3,2,1,0:T(8,128)(2,1)S(1)}, f32[2,4,128,256]{3,2,1,0:T(8,128)S(1)}, bf16[2,128...) custom-call(bf16[272,256]{1,0:T(8,128)(2,1)S(1)} %get-tuple-element.34.refs_0_, ...), custom_call_target="tpu_custom_call" | custom-call | tf_op jit(solution)/shard_map/carry_state/pallas_call | solution.py:350
  27.2 6.3 %collective-permute-start.6 = (bf16[2,128,256]{2,1,0:T(8,128)(2,1)S(1)}, bf16[2,128,256]{2,1,0:T(8,128)(2,1)S(1)}, u32[]{:S(2)}, u32[]{:S(2)}) collective-permute-start(bf16[2,128,256]{2,1,0:T(8,128)(2,1)S(1)} %get-tuple-element.46), channel_id=1, source_target_pairs={{0,8},{2,10},{4,12},{6,14},{8,16},{10,18},{12,20},{14,22},{16,24},... | collective-permute-start | bytes 393224 | tf_op jit(solution)/shard_map/ppermute | solution.py:680
  33.5 1.4 %collective-permute-start.7 = (bf16[2,128,256]{2,1,0:T(8,128)(2,1)S(1)}, bf16[2,128,256]{2,1,0:T(8,128)(2,1)S(1)}, u32[]{:S(2)}, u32[]{:S(2)}) collective-permute-start(bf16[2,128,256]{2,1,0:T(8,128)(2,1)S(1)} %get-tuple-element.46), channel_id=1, source_target_pairs={{0,16},{2,18},{4,20},{6,22},{8,24},{10,26},{12,28},{14,30},{1,17},... | collective-permute-start | bytes 393224 | tf_op jit(solution)/shard_map/ppermute | solution.py:680
  36.2 3.1 %read.1 = (f32[512,256]{1,0:T(8,128)S(1)}, bf16[512,256]{1,0:T(8,128)(2,1)S(1)}) custom-call(bf16[272,256]{1,0:T(8,128)(2,1)S(1)} %get-tuple-element.34.refs_0_, bf16[272,256]{1,0:T(8,128)(2,1)S(1)} %collective-permute-done.refs_1_, bf16[272,256]{1,0:T(8,128)(2,1)S(1)} %collective-permute-done.1.refs_0_.refs_2_, ...), custom_call_target="tpu_custom_call" | custom-call | tf_op jit(solution)/shard_map/read/pallas_call | solution.py:409
  39.9 1.4 %collective-permute-start.10 = (bf16[512,256]{1,0:T(8,128)(2,1)S(1)}, bf16[512,256]{1,0:T(8,128)(2,1)S(1)}, u32[]{:S(2)}, u32[]{:S(2)}) collective-permute-start(bf16[512,256]{1,0:T(8,128)(2,1)S(1)} %join.1.refs_0_), channel_id=1, source_target_pairs={{0,4},{2,6},{4,0},{6,2},{8,12},{10,14},{12,8},{14,10},{16,20},{18,... | collective-permute-start | bytes 786440 | tf_op jit(solution)/shard_map/ppermute | solution.py:627
  44.1 6.6 %collective-permute-start.14 = (bf16[1024,128]{1,0:T(8,128)(2,1)S(1)}, bf16[1024,128]{1,0:T(8,128)(2,1)S(1)}, u32[]{:S(2)}, u32[]{:S(2)}) collective-permute-start(bf16[1024,128]{1,0:T(8,128)(2,1)S(1)} %get-tuple-element.64), channel_id=1, source_target_pairs={{0,24},{2,26},{4,28},{6,30},{24,0},{26,2},{28,4},{30,6},{1,25},{3,... | collective-permute-start | bytes 786440 | tf_op jit(solution)/shard_map/ppermute | solution.py:648
  50.8 2.1 %collective-permute-start.15 = (bf16[1024,128]{1,0:T(8,128)(2,1)S(1)}, bf16[1024,128]{1,0:T(8,128)(2,1)S(1)}, u32[]{:S(2)}, u32[]{:S(2)}) collective-permute-start(bf16[1024,128]{1,0:T(8,128)(2,1)S(1)} %get-tuple-element.63), channel_id=1, source_target_pairs={{0,24},{2,26},{4,28},{6,30},{24,0},{26,2},{28,4},{30,6},{1,25},{3,... | collective-permute-start | bytes 786440 | tf_op jit(solution)/shard_map/ppermute | solution.py:648
  52.9 1.9 %collective-permute-start.11 = (bf16[512,256]{1,0:T(8,128)(2,1)S(1)}, bf16[512,256]{1,0:T(8,128)(2,1)S(1)}, u32[]{:S(2)}, u32[]{:S(2)}) collective-permute-start(bf16[512,256]{1,0:T(8,128)(2,1)S(1)} %join.1.refs_0_), channel_id=1, source_target_pairs={{0,6},{2,4},{4,2},{6,0},{8,14},{10,12},{12,10},{14,8},{16,22},{18,... | collective-permute-start | bytes 786440 | tf_op jit(solution)/shard_map/ppermute | solution.py:627
  55.3 2.1 %collective-permute-done.14.refs_7_ = bf16[1024,128]{1,0:T(8,128)(2,1)S(1)} collective-permute-done((bf16[1024,128]{1,0:T(8,128)(2,1)S(1)}, bf16[1024,128]{1,0:T(8,128)(2,1)S(1)}, u32[]{:S(2)}, u32[]{:S(2)}) %collective-permute-start.14) | collective-permute-done | bytes 262176 | tf_op jit(solution)/shard_map/ppermute | solution.py:648
  57.4 3.5 %collective-permute-done.15.refs_8_ = bf16[1024,128]{1,0:T(8,128)(2,1)S(1)} collective-permute-done((bf16[1024,128]{1,0:T(8,128)(2,1)S(1)}, bf16[1024,128]{1,0:T(8,128)(2,1)S(1)}, u32[]{:S(2)}, u32[]{:S(2)}) %collective-permute-start.15) | collective-permute-done | bytes 262176 | tf_op jit(solution)/shard_map/ppermute | solution.py:648
  60.9 5.8 %collective-permute-done.17.refs_10_ = bf16[1024,256]{1,0:T(8,128)(2,1)S(1)} collective-permute-done((bf16[1024,256]{1,0:T(8,128)(2,1)S(1)}, bf16[1024,256]{1,0:T(8,128)(2,1)S(1)}, u32[]{:S(2)}, u32[]{:S(2)}) %collective-permute-start.17) | collective-permute-done | bytes 524320 | tf_op jit(solution)/shard_map/ppermute | solution.py:648
  71.7 2.1 %collective-permute-start.22 = (bf16[128,512]{1,0:T(8,128)(2,1)S(1)}, bf16[128,512]{1,0:T(8,128)(2,1)S(1)}, u32[]{:S(2)}, u32[]{:S(2)}) collective-permute-start(bf16[128,512]{1,0:T(8,128)(2,1)S(1)} %get-tuple-element.62), channel_id=1, source_target_pairs={{0,6},{2,4},{4,2},{6,0},{8,14},{10,12},{12,10},{14,8},{16,22},{18,... | collective-permute-start | bytes 393224 | tf_op jit(solution)/shard_map/ppermute | solution.py:627
  73.7 2.7 %collective-permute-done.20.refs_1_ = bf16[128,512]{1,0:T(8,128)(2,1)S(1)} collective-permute-done((bf16[128,512]{1,0:T(8,128)(2,1)S(1)}, bf16[128,512]{1,0:T(8,128)(2,1)S(1)}, u32[]{:S(2)}, u32[]{:S(2)}) %collective-permute-start.20) | collective-permute-done | bytes 131104 | tf_op jit(solution)/shard_map/ppermute | solution.py:627
  76.5 2.1 %collective-permute-done.21.refs_2_ = bf16[128,512]{1,0:T(8,128)(2,1)S(1)} collective-permute-done((bf16[128,512]{1,0:T(8,128)(2,1)S(1)}, bf16[128,512]{1,0:T(8,128)(2,1)S(1)}, u32[]{:S(2)}, u32[]{:S(2)}) %collective-permute-start.21) | collective-permute-done | bytes 131104 | tf_op jit(solution)/shard_map/ppermute | solution.py:627
  (37 shorter events, 12.2 us)
Async XLA Ops:
  0.0 42.1 %collective-permute-start.12 = (bf16[1024,256]{1,0:T(8,128)(2,1)}, bf16[1024,256]{1,0:T(8,128)(2,1)S(1)}, u32[]{:S(2)}, u32[]{:S(2)}) collective-permute-start(bf16[1024,256]{1,0:T(8,128)(2,1)} %refs_4_.3), channel_id=1, source_target_pairs={{0,8},{2,10},{4,12},{6,14},{8,0},{10,2},{12,4},{14,6},{16,24},{18,... | collective-permute-start | bytes 1572872 | tf_op jit(solution)/shard_map/ppermute | solution.py:648
  3.1 39.7 %collective-permute-start.13 = (bf16[1024,256]{1,0:T(8,128)(2,1)}, bf16[1024,256]{1,0:T(8,128)(2,1)S(1)}, u32[]{:S(2)}, u32[]{:S(2)}) collective-permute-start(bf16[1024,256]{1,0:T(8,128)(2,1)} %refs_4_.3), channel_id=1, source_target_pairs={{8,16},{10,18},{12,20},{14,22},{16,8},{18,10},{20,12},{22,14},{9,1... | collective-permute-start | bytes 1572872 | tf_op jit(solution)/shard_map/ppermute | solution.py:648
  5.3 7.3 %collective-permute-start.1 = (bf16[272,256]{1,0:T(8,128)(2,1)S(1)}, bf16[272,256]{1,0:T(8,128)(2,1)S(1)}, u32[]{:S(2)}, u32[]{:S(2)}) collective-permute-start(bf16[272,256]{1,0:T(8,128)(2,1)S(1)} %get-tuple-element.36), channel_id=1, source_target_pairs={{0,4},{2,6},{4,0},{6,2},{8,12},{10,14},{12,8},{14,10},{16,20},{18,... | collective-permute-start | bytes 417800 | tf_op jit(solution)/shard_map/ppermute | solution.py:627
  6.9 7.3 %collective-permute-start.2 = (bf16[272,256]{1,0:T(8,128)(2,1)S(1)}, bf16[272,256]{1,0:T(8,128)(2,1)S(1)}, u32[]{:S(2)}, u32[]{:S(2)}) collective-permute-start(bf16[272,256]{1,0:T(8,128)(2,1)S(1)} %get-tuple-element.37), channel_id=1, source_target_pairs={{0,6},{2,4},{4,2},{6,0},{8,14},{10,12},{12,10},{14,8},{16,22},{18,... | collective-permute-start | bytes 417800 | tf_op jit(solution)/shard_map/ppermute | solution.py:627
  8.3 8.2 %collective-permute-start = (bf16[272,256]{1,0:T(8,128)(2,1)S(1)}, bf16[272,256]{1,0:T(8,128)(2,1)S(1)}, u32[]{:S(2)}, u32[]{:S(2)}) collective-permute-start(bf16[272,256]{1,0:T(8,128)(2,1)S(1)} %get-tuple-element.35), channel_id=1, source_target_pairs={{0,2},{2,0},{4,6},{6,4},{8,10},{10,8},{12,14},{14,12},{16,18},{18,... | collective-permute-start | bytes 417800 | tf_op jit(solution)/shard_map/ppermute | solution.py:627
  12.6 12.0 %collective-permute-start.3 = (bf16[3,128,256]{2,1,0:T(8,128)(2,1)S(1)}, bf16[3,128,256]{2,1,0:T(8,128)(2,1)S(1)}, u32[]{:S(2)}, u32[]{:S(2)}) collective-permute-start(bf16[3,128,256]{2,1,0:T(8,128)(2,1)S(1)} %get-tuple-element.39), channel_id=1, source_target_pairs={{0,2},{2,0},{4,6},{6,4},{8,10},{10,8},{12,14},{14,12},{16,18},{18,... | collective-permute-start | bytes 589832 | tf_op jit(solution)/shard_map/ppermute | solution.py:627
  14.2 10.4 %collective-permute-start.4 = (bf16[3,128,256]{2,1,0:T(8,128)(2,1)S(1)}, bf16[3,128,256]{2,1,0:T(8,128)(2,1)S(1)}, u32[]{:S(2)}, u32[]{:S(2)}) collective-permute-start(bf16[3,128,256]{2,1,0:T(8,128)(2,1)S(1)} %get-tuple-element.40), channel_id=1, source_target_pairs={{0,4},{2,6},{4,0},{6,2},{8,12},{10,14},{12,8},{14,10},{16,20},{18,... | collective-permute-start | bytes 589832 | tf_op jit(solution)/shard_map/ppermute | solution.py:627
  16.5 8.1 %collective-permute-start.5 = (bf16[3,128,256]{2,1,0:T(8,128)(2,1)S(1)}, bf16[3,128,256]{2,1,0:T(8,128)(2,1)S(1)}, u32[]{:S(2)}, u32[]{:S(2)}) collective-permute-start(bf16[3,128,256]{2,1,0:T(8,128)(2,1)S(1)} %get-tuple-element.41), channel_id=1, source_target_pairs={{0,6},{2,4},{4,2},{6,0},{8,14},{10,12},{12,10},{14,8},{16,22},{18,... | collective-permute-start | bytes 589832 | tf_op jit(solution)/shard_map/ppermute | solution.py:627
  27.2 12.1 %collective-permute-start.6 = (bf16[2,128,256]{2,1,0:T(8,128)(2,1)S(1)}, bf16[2,128,256]{2,1,0:T(8,128)(2,1)S(1)}, u32[]{:S(2)}, u32[]{:S(2)}) collective-permute-start(bf16[2,128,256]{2,1,0:T(8,128)(2,1)S(1)} %get-tuple-element.46), channel_id=1, source_target_pairs={{0,8},{2,10},{4,12},{6,14},{8,16},{10,18},{12,20},{14,22},{16,24},... | collective-permute-start | bytes 393224 | tf_op jit(solution)/shard_map/ppermute | solution.py:680
  33.5 5.8 %collective-permute-start.7 = (bf16[2,128,256]{2,1,0:T(8,128)(2,1)S(1)}, bf16[2,128,256]{2,1,0:T(8,128)(2,1)S(1)}, u32[]{:S(2)}, u32[]{:S(2)}) collective-permute-start(bf16[2,128,256]{2,1,0:T(8,128)(2,1)S(1)} %get-tuple-element.46), channel_id=1, source_target_pairs={{0,16},{2,18},{4,20},{6,22},{8,24},{10,26},{12,28},{14,30},{1,17},... | collective-permute-start | bytes 393224 | tf_op jit(solution)/shard_map/ppermute | solution.py:680
  34.9 4.4 %collective-permute-start.8 = (bf16[2,128,128]{2,1,0:T(8,128)(2,1)S(1)}, bf16[2,128,128]{2,1,0:T(8,128)(2,1)S(1)}, u32[]{:S(2)}, u32[]{:S(2)}) collective-permute-start(bf16[2,128,128]{2,1,0:T(8,128)(2,1)S(1)} %get-tuple-element.47), channel_id=1, source_target_pairs={{0,24},{2,26},{4,28},{6,30},{1,25},{3,27},{5,29},{7,31}} | collective-permute-start | bytes 196616 | tf_op jit(solution)/shard_map/ppermute | solution.py:680
  39.4 4.7 %copy-start = (bf16[1024,256]{1,0:T(8,128)(2,1)S(1)}, bf16[1024,256]{1,0:T(8,128)(2,1)}, u32[]{:S(2)}) copy-start(bf16[1024,256]{1,0:T(8,128)(2,1)} %refs_4_.3) | copy-start | bytes 1572868
  39.9 10.9 %collective-permute-start.10 = (bf16[512,256]{1,0:T(8,128)(2,1)S(1)}, bf16[512,256]{1,0:T(8,128)(2,1)S(1)}, u32[]{:S(2)}, u32[]{:S(2)}) collective-permute-start(bf16[512,256]{1,0:T(8,128)(2,1)S(1)} %join.1.refs_0_), channel_id=1, source_target_pairs={{0,4},{2,6},{4,0},{6,2},{8,12},{10,14},{12,8},{14,10},{16,20},{18,... | collective-permute-start | bytes 786440 | tf_op jit(solution)/shard_map/ppermute | solution.py:627
  41.3 11.6 %collective-permute-start.9 = (bf16[512,256]{1,0:T(8,128)(2,1)S(1)}, bf16[512,256]{1,0:T(8,128)(2,1)S(1)}, u32[]{:S(2)}, u32[]{:S(2)}) collective-permute-start(bf16[512,256]{1,0:T(8,128)(2,1)S(1)} %join.1.refs_0_), channel_id=1, source_target_pairs={{0,2},{2,0},{4,6},{6,4},{8,10},{10,8},{12,14},{14,12},{16,18},{18,... | collective-permute-start | bytes 786440 | tf_op jit(solution)/shard_map/ppermute | solution.py:627
  42.1 18.9 %collective-permute-start.16 = (bf16[1024,256]{1,0:T(8,128)(2,1)S(1)}, bf16[1024,256]{1,0:T(8,128)(2,1)S(1)}, u32[]{:S(2)}, u32[]{:S(2)}) collective-permute-start(bf16[1024,256]{1,0:T(8,128)(2,1)S(1)} %collective-permute-done.12.refs_4_.refs_5_), channel_id=1, source_target_pairs={{8,16},{10,18},{12,20},{14,22},{16,8},{18,10},{20,12},{22,14},{9,1... | collective-permute-start | bytes 1572872 | tf_op jit(solution)/shard_map/ppermute | solution.py:648
  42.8 23.9 %collective-permute-start.17 = (bf16[1024,256]{1,0:T(8,128)(2,1)S(1)}, bf16[1024,256]{1,0:T(8,128)(2,1)S(1)}, u32[]{:S(2)}, u32[]{:S(2)}) collective-permute-start(bf16[1024,256]{1,0:T(8,128)(2,1)S(1)} %collective-permute-done.13.refs_6_), channel_id=1, source_target_pairs={{8,0},{10,2},{12,4},{14,6},{16,24},{18,26},{20,28},{22,30},{9,1},{... | collective-permute-start | bytes 1572872 | tf_op jit(solution)/shard_map/ppermute | solution.py:648
  44.1 13.3 %collective-permute-start.14 = (bf16[1024,128]{1,0:T(8,128)(2,1)S(1)}, bf16[1024,128]{1,0:T(8,128)(2,1)S(1)}, u32[]{:S(2)}, u32[]{:S(2)}) collective-permute-start(bf16[1024,128]{1,0:T(8,128)(2,1)S(1)} %get-tuple-element.64), channel_id=1, source_target_pairs={{0,24},{2,26},{4,28},{6,30},{24,0},{26,2},{28,4},{30,6},{1,25},{3,... | collective-permute-start | bytes 786440 | tf_op jit(solution)/shard_map/ppermute | solution.py:648
  50.8 10.2 %collective-permute-start.15 = (bf16[1024,128]{1,0:T(8,128)(2,1)S(1)}, bf16[1024,128]{1,0:T(8,128)(2,1)S(1)}, u32[]{:S(2)}, u32[]{:S(2)}) collective-permute-start(bf16[1024,128]{1,0:T(8,128)(2,1)S(1)} %get-tuple-element.63), channel_id=1, source_target_pairs={{0,24},{2,26},{4,28},{6,30},{24,0},{26,2},{28,4},{30,6},{1,25},{3,... | collective-permute-start | bytes 786440 | tf_op jit(solution)/shard_map/ppermute | solution.py:648
  52.9 8.0 %collective-permute-start.11 = (bf16[512,256]{1,0:T(8,128)(2,1)S(1)}, bf16[512,256]{1,0:T(8,128)(2,1)S(1)}, u32[]{:S(2)}, u32[]{:S(2)}) collective-permute-start(bf16[512,256]{1,0:T(8,128)(2,1)S(1)} %join.1.refs_0_), channel_id=1, source_target_pairs={{0,6},{2,4},{4,2},{6,0},{8,14},{10,12},{12,10},{14,8},{16,22},{18,... | collective-permute-start | bytes 786440 | tf_op jit(solution)/shard_map/ppermute | solution.py:627
  68.0 2.0 %collective-permute-start.19 = (bf16[256,512]{1,0:T(8,128)(2,1)S(1)}, bf16[256,512]{1,0:T(8,128)(2,1)S(1)}, u32[]{:S(2)}, u32[]{:S(2)}) collective-permute-start(bf16[256,512]{1,0:T(8,128)(2,1)S(1)} %get-tuple-element.59), channel_id=1, source_target_pairs={{0,1},{1,0},{2,3},{3,2},{4,5},{5,4},{6,7},{7,6},{8,9},{9,8},{10,11... | collective-permute-start | bytes 786440 | tf_op jit(solution)/shard_map/ppermute | solution.py:716
  69.4 2.2 %collective-permute-start.18 = (bf16[256,512]{1,0:T(8,128)(2,1)S(1)}, bf16[256,512]{1,0:T(8,128)(2,1)S(1)}, u32[]{:S(2)}, u32[]{:S(2)}) collective-permute-start(bf16[256,512]{1,0:T(8,128)(2,1)S(1)} %get-tuple-element.55), channel_id=1, source_target_pairs={{0,1},{1,0},{2,3},{3,2},{4,5},{5,4},{6,7},{7,6},{8,9},{9,8},{10,11... | collective-permute-start | bytes 786440 | tf_op jit(solution)/shard_map/ppermute | solution.py:716
  70.1 6.4 %collective-permute-start.20 = (bf16[128,512]{1,0:T(8,128)(2,1)S(1)}, bf16[128,512]{1,0:T(8,128)(2,1)S(1)}, u32[]{:S(2)}, u32[]{:S(2)}) collective-permute-start(bf16[128,512]{1,0:T(8,128)(2,1)S(1)} %get-tuple-element.60), channel_id=1, source_target_pairs={{0,2},{2,0},{4,6},{6,4},{8,10},{10,8},{12,14},{14,12},{16,18},{18,... | collective-permute-start | bytes 393224 | tf_op jit(solution)/shard_map/ppermute | solution.py:627
  70.6 8.0 %collective-permute-start.21 = (bf16[128,512]{1,0:T(8,128)(2,1)S(1)}, bf16[128,512]{1,0:T(8,128)(2,1)S(1)}, u32[]{:S(2)}, u32[]{:S(2)}) collective-permute-start(bf16[128,512]{1,0:T(8,128)(2,1)S(1)} %get-tuple-element.61), channel_id=1, source_target_pairs={{0,4},{2,6},{4,0},{6,2},{8,12},{10,14},{12,8},{14,10},{16,20},{18,... | collective-permute-start | bytes 393224 | tf_op jit(solution)/shard_map/ppermute | solution.py:627
  71.7 6.9 %collective-permute-start.22 = (bf16[128,512]{1,0:T(8,128)(2,1)S(1)}, bf16[128,512]{1,0:T(8,128)(2,1)S(1)}, u32[]{:S(2)}, u32[]{:S(2)}) collective-permute-start(bf16[128,512]{1,0:T(8,128)(2,1)S(1)} %get-tuple-element.62), channel_id=1, source_target_pairs={{0,6},{2,4},{4,2},{6,0},{8,14},{10,12},{12,10},{14,8},{16,22},{18,... | collective-permute-start | bytes 393224 | tf_op jit(solution)/shard_map/ppermute | solution.py:627

commit v6 on v5

--- a/solution.py
+++ b/solution.py
@@ -365,7 +365,8 @@
 
 def read_kernel(group, *refs):
     key_in, rest_in = refs[:group], refs[group : 2 * group]
-    high_ref, low_ref, step_ref, out_ref, lift_ref, before_buf = refs[2 * group :]
+    high_ref, low_ref, step_ref, out_ref, lift_ref = refs[2 * group : -3]
+    before_buf, local_buf, lift_buf = refs[-3:]
     heads, chunks, wide, _ = high_ref.shape
     chunk = wide // 2
     half = chunk // 2
@@ -375,13 +376,6 @@
     token_row = iota((chunk, 2 * chunk), 0)
     token_col = iota((chunk, 2 * chunk), 1)
     token_col = (token_col // chunk) * half + lax.rem(token_col, half)
-    totals = [step_ref[head, 0] for head in range(heads)]
-    for head in range(heads):
-        before_buf[head, 0] = jnp.zeros((width, 2 * width), BF16)
-    for slot in range(1, chunks):
-        for head in range(heads):
-            before_buf[head, slot] = totals[head].astype(BF16)
-        totals = [after(totals[head], step_ref[head, slot]) for head in range(heads)]
 
     def answer(units):
         for head, index in units:
@@ -393,19 +387,36 @@
             scale = lax.rsqrt(jnp.sum(wide_query * wide_query, axis=1, keepdims=True) + EPS)
             scores = jnp.where(token_col <= token_row, dot_t(query, key) * scale, 0.0)
             applied = dot3(scores, high_ref[head, index], low_ref[head, index])
-            lifted = scale * wide_query - applied[:, :width]
+            local_buf[head, index] = applied[:, width:]
+            lift_buf[head, index] = scale * wide_query - applied[:, :width]
+
+    every_unit(heads, chunks, answer)
+    totals = [step_ref[head, 0] for head in range(heads)]
+    for head in range(heads):
+        before_buf[head, 0] = jnp.zeros((width, 2 * width), BF16)
+    for slot in range(1, chunks):
+        for head in range(heads):
+            before_buf[head, slot] = totals[head].astype(BF16)
+        if slot + 1 < chunks:
+            totals = [after(totals[head], step_ref[head, slot]) for head in range(heads)]
+
+    def correct(units):
+        for head, index in units:
+            lanes = lanes_of(head, width)
             slot = slot_of(group, index, per_source)
+            lifted = lift_buf[head, index]
             moved = dot(lifted.astype(BF16), before_buf[head, slot])
             rows = pl.ds(pl.multiple_of(slot * chunk, chunk), chunk)
-            out_ref[rows, lanes] = applied[:, width:] + moved[:, width:]
+            out_ref[rows, lanes] = local_buf[head, index] + moved[:, width:]
             lift_ref[rows, lanes] = (lifted - moved[:, :width]).astype(BF16)
 
-    every_unit(heads, chunks, answer)
+    every_unit(heads, chunks, correct)
 
 
 def read(keys, rests, high, low, steps):
     group = len(keys)
     _, tokens, wide = rests[0].shape
+    chunk, width = high.shape[2] // 2, steps.shape[2]
     return pl.pallas_call(
         functools.partial(read_kernel, group),
         out_shape=(
@@ -414,7 +425,11 @@
         ),
         in_specs=[VMEM] * (2 * group + 3),
         out_specs=(VMEM, VMEM),
-        scratch_shapes=[pltpu.VMEM(steps.shape, BF16)],
+        scratch_shapes=[
+            pltpu.VMEM(steps.shape, BF16),
+            pltpu.VMEM(steps.shape[:2] + (chunk, width), F32),
+            pltpu.VMEM(steps.shape[:2] + (chunk, width), F32),
+        ],
         compiler_params=PARAMS,
         name="read",
     )(*held(*keys, *rests, high, low, steps))
@@ -458,12 +473,9 @@
 
 def weight_rows(weights, offset, inner, first, count):
     rows = pl.ds(first, count)
-    if offset < 2:
-        return weights[offset][rows, :]
     if offset == 2:
-        return jnp.where(inner, weights[5][rows, :], weights[6][rows, :])
-    far = jnp.concatenate([weights[3][rows, :], weights[4][rows, :]], axis=1)
-    return jnp.where(inner, weights[2][rows, :], far)
+        return jnp.where(inner, weights[3][rows, :], weights[4][rows, :])
+    return weights[{0: 0, 1: 1, 3: 2}[offset]][rows, :]
 
 
 def where_am_i(group):
@@ -656,15 +668,11 @@
         )
 
     split_out = sides == 2 and planes in (2, 4) and group > 1
-    columns = out_weight.shape[1]
     weights = [out_weight]
     if split_out:
-        swapped = [(plane, plane ^ 1) for plane in range(planes)]
-        weights.append(between_planes(out_weight, swapped))
-    if split_out and planes == 4:
-        outer = ((0, 3), (3, 0))
-        weights.append(between_planes(out_weight, ((1, 2), (2, 1))))
-        weights.append(between_planes(out_weight[:, : columns // 2], outer))
+        for offset in range(1, planes, 2):
+            swapped = [(plane, plane ^ offset) for plane in range(planes)]
+            weights.append(between_planes(out_weight, swapped))
 
     near = max(group // 2, 1)
     solved = []
@@ -692,9 +700,7 @@
             distance *= 2
         states = [total[:, :, width:]]
     if split_out and planes == 4:
-        late = between_planes(out_weight[:, columns // 2 :], outer)
         weights += [
-            late,
             between_planes(weights[1], ((1, 2), (2, 1))),
             between_planes(weights[2], ((1, 0), (2, 3))),
         ]
@@ -704,7 +710,7 @@
     if split_out:
         order = tuple(range(1, group)) + (0,)
         row_halves = (order[: group // 2], order[group // 2 :])
-        early = (tuple(range(group - 1)), (0, 1))
+        early = (tuple(range(group - 1)), (0, 1, 3) if planes == 4 else (0, 1))
         parts = [None] * group
         gathered = [mixed_heads]
         for offset in range(1, group):

time: 80 us -> 77.3 us (0.966)
  starting transfers between devices: 40.5 us -> 32.6 us
  waiting for transfers between devices: 20.1 us -> 27.5 us
  Pallas kernels: 18.6 us -> 16.8 us
    ppermute x12, waiting for transfers between devices: 8.72 us -> 18.6 us  [swap(): return lax.ppermute(value, 'seq', pairs)]
    ppermute x6 -> x4, starting transfers between devices: 14.5 us -> 7.49 us  [between_planes(): lax.ppermute(value, 'seq', [(source * group + i, target * group + i) for...]
    ppermute x6 -> x4, waiting for transfers between devices: 11.4 us -> 8.29 us  [between_planes(): lax.ppermute(value, 'seq', [(source * group + i, target * group + i) for...]
    pallas_call x1, Pallas kernels: 3.12 us -> 1.66 us  [read(): pl.pallas_call(functools.partial(read_kernel, group), out_shape=(pltpu.VM...]
  transfers between devices with their start and end apart: 23 -> 21, of which waited for: 7 -> 9; matrix products, arithmetic and copies ran while one was open for 0% -> 0% of each run, Pallas kernels for 21% -> 19%
where the time goes in v6:
time: 77.3 us; the launch traced here: 77 us
  starting transfers between devices  32.6 us (42%)
  waiting for transfers between devices  27.5 us (36%)
  Pallas kernels  16.8 us (22%)
    ppermute x12, waiting for transfers between devices, swap(): return lax.ppermute(value, 'seq', pairs)  18.6 us
    ppermute x12, starting transfers between devices, swap(): return lax.ppermute(value, 'seq', pairs)  16 us
    ppermute x3, starting transfers between devices, from_earlier(): return lax.ppermute(value, 'seq', pairs)  8.52 us
    ppermute x4, waiting for transfers between devices, between_planes(): lax.ppermute(value, 'seq', [(source * group + i, target * group + i) for...  8.29 us
    ppermute x4, starting transfers between devices, between_planes(): lax.ppermute(value, 'seq', [(source * group + i, target * group + i) for...  7.49 us
    pallas_call x2, Pallas kernels, invert(): pl.pallas_call(functools.partial(invert_kernel, heads, tokens), out_shape...  6.6 us
    pallas_call x1, Pallas kernels, carry_state(): pl.pallas_call(functools.partial(state_kernel, group, parts), out_shape=(...  2.63 us
    pallas_call x2, Pallas kernels, project(): pl.pallas_call(functools.partial(project_kernel, group, targets, early, o...  2.16 us
  transfers between devices with their start and end apart: 21, of which 9 were waited for; matrix products, arithmetic and copies ran while one was open for 0% of the time, Pallas kernels for 19%

profile of v6, /device:TPU:0, one launch (start us, length us, event | category | flops | bytes accessed | tf_op | source)
XLA Modules:
  0.0 77.0 jit_solution(9047171130955697390)
XLA Ops:
  0.0 3.1 %collective-permute-start.12 = (bf16[1024,256]{1,0:T(8,128)(2,1)}, bf16[1024,256]{1,0:T(8,128)(2,1)S(1)}, u32[]{:S(2)}, u32[]{:S(2)}) collective-permute-start(bf16[1024,256]{1,0:T(8,128)(2,1)} %refs_4_.3), channel_id=1, source_target_pairs={{0,8},{2,10},{4,12},{6,14},{8,0},{10,2},{12,4},{14,6},{16,24},{18,... | collective-permute-start | bytes 1572872 | tf_op jit(solution)/shard_map/ppermute | solution.py:660
  3.1 2.5 %collective-permute-start.13 = (bf16[1024,256]{1,0:T(8,128)(2,1)}, bf16[1024,256]{1,0:T(8,128)(2,1)S(1)}, u32[]{:S(2)}, u32[]{:S(2)}) collective-permute-start(bf16[1024,256]{1,0:T(8,128)(2,1)} %refs_4_.3), channel_id=1, source_target_pairs={{0,24},{2,26},{4,28},{6,30},{8,16},{10,18},{12,20},{14,22},{16,8},... | collective-permute-start | bytes 1572872 | tf_op jit(solution)/shard_map/ppermute | solution.py:660
  5.5 1.5 %pack.1 = (bf16[272,256]{1,0:T(8,128)(2,1)S(1)}, bf16[272,256]{1,0:T(8,128)(2,1)S(1)}, bf16[272,256]{1,0:T(8,128)(2,1)S(1)}, bf16[272,256]{1,0:T(8,128)(2,1)S(1)...) custom-call(bf16[2,128,1024]{2,1,0:T(8,128)(2,1)} %key_ref.1, ...), custom_call_target="tpu_custom_call" | custom-call | tf_op jit(solution)/shard_map/pack/pallas_call | solution.py:139
  7.1 1.6 %collective-permute-start.1 = (bf16[272,256]{1,0:T(8,128)(2,1)S(1)}, bf16[272,256]{1,0:T(8,128)(2,1)S(1)}, u32[]{:S(2)}, u32[]{:S(2)}) collective-permute-start(bf16[272,256]{1,0:T(8,128)(2,1)S(1)} %get-tuple-element.36), channel_id=1, source_target_pairs={{0,4},{2,6},{4,0},{6,2},{8,12},{10,14},{12,8},{14,10},{16,20},{18,... | collective-permute-start | bytes 417800 | tf_op jit(solution)/shard_map/ppermute | solution.py:639
  10.6 3.6 %collective-permute-done.1.refs_0_.refs_2_ = bf16[272,256]{1,0:T(8,128)(2,1)S(1)} collective-permute-done((bf16[272,256]{1,0:T(8,128)(2,1)S(1)}, bf16[272,256]{1,0:T(8,128)(2,1)S(1)}, u32[]{:S(2)}, u32[]{:S(2)}) %collective-permute-start.1) | collective-permute-done | bytes 139296 | tf_op jit(solution)/shard_map/ppermute | solution.py:639
  14.2 1.5 %collective-permute-start.3 = (bf16[3,128,256]{2,1,0:T(8,128)(2,1)S(1)}, bf16[3,128,256]{2,1,0:T(8,128)(2,1)S(1)}, u32[]{:S(2)}, u32[]{:S(2)}) collective-permute-start(bf16[3,128,256]{2,1,0:T(8,128)(2,1)S(1)} %get-tuple-element.39), channel_id=1, source_target_pairs={{0,2},{2,0},{4,6},{6,4},{8,10},{10,8},{12,14},{14,12},{16,18},{18,... | collective-permute-start | bytes 589832 | tf_op jit(solution)/shard_map/ppermute | solution.py:639
  15.7 2.1 %collective-permute-start.4 = (bf16[3,128,256]{2,1,0:T(8,128)(2,1)S(1)}, bf16[3,128,256]{2,1,0:T(8,128)(2,1)S(1)}, u32[]{:S(2)}, u32[]{:S(2)}) collective-permute-start(bf16[3,128,256]{2,1,0:T(8,128)(2,1)S(1)} %get-tuple-element.40), channel_id=1, source_target_pairs={{0,4},{2,6},{4,0},{6,2},{8,12},{10,14},{12,8},{14,10},{16,20},{18,... | collective-permute-start | bytes 589832 | tf_op jit(solution)/shard_map/ppermute | solution.py:639
  18.1 1.6 %collective-permute-start.5 = (bf16[3,128,256]{2,1,0:T(8,128)(2,1)S(1)}, bf16[3,128,256]{2,1,0:T(8,128)(2,1)S(1)}, u32[]{:S(2)}, u32[]{:S(2)}) collective-permute-start(bf16[3,128,256]{2,1,0:T(8,128)(2,1)S(1)} %get-tuple-element.41), channel_id=1, source_target_pairs={{0,6},{2,4},{4,2},{6,0},{8,14},{10,12},{12,10},{14,8},{16,22},{18,... | collective-permute-start | bytes 589832 | tf_op jit(solution)/shard_map/ppermute | solution.py:639
  20.4 8.3 %collective-permute-done.13.refs_5_.refs_6_ = bf16[1024,256]{1,0:T(8,128)(2,1)S(1)} collective-permute-done((bf16[1024,256]{1,0:T(8,128)(2,1)}, bf16[1024,256]{1,0:T(8,128)(2,1)S(1)}, u32[]{:S(2)}, u32[]{:S(2)}) %collective-permute-start.13) | collective-permute-done | bytes 524320 | tf_op jit(solution)/shard_map/ppermute | solution.py:660
  30.0 3.3 %invert.3 = (f32[2,2,3,128,128]{4,3,2,1,0:T(8,128)S(1)}, f32[2,2,8,256]{3,2,1,0:T(8,128)S(1)}) custom-call(bf16[272,256]{1,0:T(8,128)(2,1)S(1)} %collective-permute-done.1.refs_0_.refs_2_, bf16[272,256]{1,0:T(8,128)(2,1)S(1)} %collective-permute-done.2.refs_1_.refs_3_), custom_call_target="tpu_custom_call" | custom-call | tf_op jit(solution)/shard_map/invert/pallas_call | solution.py:238
  33.3 3.3 %invert.2 = (f32[2,2,3,128,128]{4,3,2,1,0:T(8,128)S(1)}, f32[2,2,8,256]{3,2,1,0:T(8,128)S(1)}) custom-call(bf16[272,256]{1,0:T(8,128)(2,1)S(1)} %get-tuple-element.34.refs_0_, bf16[272,256]{1,0:T(8,128)(2,1)S(1)} %collective-permute-done.refs_1_), custom_call_target="tpu_custom_call" | custom-call | tf_op jit(solution)/shard_map/invert/pallas_call | solution.py:238
  36.7 2.6 %carry_state.1 = (bf16[2,4,256,256]{3,2,1,0:T(8,128)(2,1)S(1)}, bf16[2,4,256,256]{3,2,1,0:T(8,128)(2,1)S(1)}, f32[2,4,128,256]{3,2,1,0:T(8,128)S(1)}, bf16[2,128...) custom-call(bf16[272,256]{1,0:T(8,128)(2,1)S(1)} %get-tuple-element.34.refs_0_, ...), custom_call_target="tpu_custom_call" | custom-call | tf_op jit(solution)/shard_map/carry_state/pallas_call | solution.py:350
  39.3 4.6 %collective-permute-start.6 = (bf16[2,128,256]{2,1,0:T(8,128)(2,1)S(1)}, bf16[2,128,256]{2,1,0:T(8,128)(2,1)S(1)}, u32[]{:S(2)}, u32[]{:S(2)}) collective-permute-start(bf16[2,128,256]{2,1,0:T(8,128)(2,1)S(1)} %get-tuple-element.46), channel_id=1, source_target_pairs={{0,8},{2,10},{4,12},{6,14},{8,16},{10,18},{12,20},{14,22},{16,24},... | collective-permute-start | bytes 393224 | tf_op jit(solution)/shard_map/ppermute | solution.py:688
  43.9 2.6 %collective-permute-start.7 = (bf16[2,128,256]{2,1,0:T(8,128)(2,1)S(1)}, bf16[2,128,256]{2,1,0:T(8,128)(2,1)S(1)}, u32[]{:S(2)}, u32[]{:S(2)}) collective-permute-start(bf16[2,128,256]{2,1,0:T(8,128)(2,1)S(1)} %get-tuple-element.46), channel_id=1, source_target_pairs={{0,16},{2,18},{4,20},{6,22},{8,24},{10,26},{12,28},{14,30},{1,17},... | collective-permute-start | bytes 393224 | tf_op jit(solution)/shard_map/ppermute | solution.py:688
  47.8 1.7 %read.1 = (f32[512,256]{1,0:T(8,128)S(1)}, bf16[512,256]{1,0:T(8,128)(2,1)S(1)}) custom-call(bf16[272,256]{1,0:T(8,128)(2,1)S(1)} %get-tuple-element.34.refs_0_, bf16[272,256]{1,0:T(8,128)(2,1)S(1)} %collective-permute-done.refs_1_, bf16[272,256]{1,0:T(8,128)(2,1)S(1)} %collective-permute-done.1.refs_0_.refs_2_, ...), custom_call_target="tpu_custom_call" | custom-call | tf_op jit(solution)/shard_map/read/pallas_call | solution.py:420
  50.5 1.6 %collective-permute-start.10 = (bf16[512,256]{1,0:T(8,128)(2,1)S(1)}, bf16[512,256]{1,0:T(8,128)(2,1)S(1)}, u32[]{:S(2)}, u32[]{:S(2)}) collective-permute-start(bf16[512,256]{1,0:T(8,128)(2,1)S(1)} %join.1.refs_0_), channel_id=1, source_target_pairs={{0,4},{2,6},{4,0},{6,2},{8,12},{10,14},{12,8},{14,10},{16,20},{18,... | collective-permute-start | bytes 786440 | tf_op jit(solution)/shard_map/ppermute | solution.py:639
  52.1 1.5 %collective-permute-start.9 = (bf16[512,256]{1,0:T(8,128)(2,1)S(1)}, bf16[512,256]{1,0:T(8,128)(2,1)S(1)}, u32[]{:S(2)}, u32[]{:S(2)}) collective-permute-start(bf16[512,256]{1,0:T(8,128)(2,1)S(1)} %join.1.refs_0_), channel_id=1, source_target_pairs={{0,2},{2,0},{4,6},{6,4},{8,10},{10,8},{12,14},{14,12},{16,18},{18,... | collective-permute-start | bytes 786440 | tf_op jit(solution)/shard_map/ppermute | solution.py:639
  54.1 4.8 %collective-permute-done.10.refs_2_ = bf16[512,256]{1,0:T(8,128)(2,1)S(1)} collective-permute-done((bf16[512,256]{1,0:T(8,128)(2,1)S(1)}, bf16[512,256]{1,0:T(8,128)(2,1)S(1)}, u32[]{:S(2)}, u32[]{:S(2)}) %collective-permute-start.10) | collective-permute-done | bytes 262176 | tf_op jit(solution)/shard_map/ppermute | solution.py:639
  58.9 2.2 %collective-permute-done.9.refs_1_ = bf16[512,256]{1,0:T(8,128)(2,1)S(1)} collective-permute-done((bf16[512,256]{1,0:T(8,128)(2,1)S(1)}, bf16[512,256]{1,0:T(8,128)(2,1)S(1)}, u32[]{:S(2)}, u32[]{:S(2)}) %collective-permute-start.9) | collective-permute-done | bytes 262176 | tf_op jit(solution)/shard_map/ppermute | solution.py:639
  61.9 2.0 %collective-permute-done.11.refs_3_ = bf16[512,256]{1,0:T(8,128)(2,1)S(1)} collective-permute-done((bf16[512,256]{1,0:T(8,128)(2,1)S(1)}, bf16[512,256]{1,0:T(8,128)(2,1)S(1)}, u32[]{:S(2)}, u32[]{:S(2)}) %collective-permute-start.11) | collective-permute-done | bytes 262176 | tf_op jit(solution)/shard_map/ppermute | solution.py:639
  66.7 1.5 %collective-permute-start.18 = (bf16[128,512]{1,0:T(8,128)(2,1)S(1)}, bf16[128,512]{1,0:T(8,128)(2,1)S(1)}, u32[]{:S(2)}, u32[]{:S(2)}) collective-permute-start(bf16[128,512]{1,0:T(8,128)(2,1)S(1)} %get-tuple-element.60), channel_id=1, source_target_pairs={{0,2},{2,0},{4,6},{6,4},{8,10},{10,8},{12,14},{14,12},{16,18},{18,... | collective-permute-start | bytes 393224 | tf_op jit(solution)/shard_map/ppermute | solution.py:639
  68.2 1.6 %collective-permute-start.19 = (bf16[128,512]{1,0:T(8,128)(2,1)S(1)}, bf16[128,512]{1,0:T(8,128)(2,1)S(1)}, u32[]{:S(2)}, u32[]{:S(2)}) collective-permute-start(bf16[128,512]{1,0:T(8,128)(2,1)S(1)} %get-tuple-element.61), channel_id=1, source_target_pairs={{0,4},{2,6},{4,0},{6,2},{8,12},{10,14},{12,8},{14,10},{16,20},{18,... | collective-permute-start | bytes 393224 | tf_op jit(solution)/shard_map/ppermute | solution.py:639
  70.4 2.1 %collective-permute-done.18.refs_1_ = bf16[128,512]{1,0:T(8,128)(2,1)S(1)} collective-permute-done((bf16[128,512]{1,0:T(8,128)(2,1)S(1)}, bf16[128,512]{1,0:T(8,128)(2,1)S(1)}, u32[]{:S(2)}, u32[]{:S(2)}) %collective-permute-start.18) | collective-permute-done | bytes 131104 | tf_op jit(solution)/shard_map/ppermute | solution.py:639
  72.5 3.7 %collective-permute-done.19.refs_2_ = bf16[128,512]{1,0:T(8,128)(2,1)S(1)} collective-permute-done((bf16[128,512]{1,0:T(8,128)(2,1)S(1)}, bf16[128,512]{1,0:T(8,128)(2,1)S(1)}, u32[]{:S(2)}, u32[]{:S(2)}) %collective-permute-start.19) | collective-permute-done | bytes 131104 | tf_op jit(solution)/shard_map/ppermute | solution.py:639
  (32 shorter events, 12.1 us)
Async XLA Ops:
  0.0 19.7 %collective-permute-start.12 = (bf16[1024,256]{1,0:T(8,128)(2,1)}, bf16[1024,256]{1,0:T(8,128)(2,1)S(1)}, u32[]{:S(2)}, u32[]{:S(2)}) collective-permute-start(bf16[1024,256]{1,0:T(8,128)(2,1)} %refs_4_.3), channel_id=1, source_target_pairs={{0,8},{2,10},{4,12},{6,14},{8,0},{10,2},{12,4},{14,6},{16,24},{18,... | collective-permute-start | bytes 1572872 | tf_op jit(solution)/shard_map/ppermute | solution.py:660
  3.1 25.7 %collective-permute-start.13 = (bf16[1024,256]{1,0:T(8,128)(2,1)}, bf16[1024,256]{1,0:T(8,128)(2,1)S(1)}, u32[]{:S(2)}, u32[]{:S(2)}) collective-permute-start(bf16[1024,256]{1,0:T(8,128)(2,1)} %refs_4_.3), channel_id=1, source_target_pairs={{0,24},{2,26},{4,28},{6,30},{8,16},{10,18},{12,20},{14,22},{16,8},... | collective-permute-start | bytes 1572872 | tf_op jit(solution)/shard_map/ppermute | solution.py:660
  7.1 7.2 %collective-permute-start.1 = (bf16[272,256]{1,0:T(8,128)(2,1)S(1)}, bf16[272,256]{1,0:T(8,128)(2,1)S(1)}, u32[]{:S(2)}, u32[]{:S(2)}) collective-permute-start(bf16[272,256]{1,0:T(8,128)(2,1)S(1)} %get-tuple-element.36), channel_id=1, source_target_pairs={{0,4},{2,6},{4,0},{6,2},{8,12},{10,14},{12,8},{14,10},{16,20},{18,... | collective-permute-start | bytes 417800 | tf_op jit(solution)/shard_map/ppermute | solution.py:639
  8.6 7.1 %collective-permute-start.2 = (bf16[272,256]{1,0:T(8,128)(2,1)S(1)}, bf16[272,256]{1,0:T(8,128)(2,1)S(1)}, u32[]{:S(2)}, u32[]{:S(2)}) collective-permute-start(bf16[272,256]{1,0:T(8,128)(2,1)S(1)} %get-tuple-element.37), channel_id=1, source_target_pairs={{0,6},{2,4},{4,2},{6,0},{8,14},{10,12},{12,10},{14,8},{16,22},{18,... | collective-permute-start | bytes 417800 | tf_op jit(solution)/shard_map/ppermute | solution.py:639
  10.1 8.0 %collective-permute-start = (bf16[272,256]{1,0:T(8,128)(2,1)S(1)}, bf16[272,256]{1,0:T(8,128)(2,1)S(1)}, u32[]{:S(2)}, u32[]{:S(2)}) collective-permute-start(bf16[272,256]{1,0:T(8,128)(2,1)S(1)} %get-tuple-element.35), channel_id=1, source_target_pairs={{0,2},{2,0},{4,6},{6,4},{8,10},{10,8},{12,14},{14,12},{16,18},{18,... | collective-permute-start | bytes 417800 | tf_op jit(solution)/shard_map/ppermute | solution.py:639
  14.2 22.4 %collective-permute-start.3 = (bf16[3,128,256]{2,1,0:T(8,128)(2,1)S(1)}, bf16[3,128,256]{2,1,0:T(8,128)(2,1)S(1)}, u32[]{:S(2)}, u32[]{:S(2)}) collective-permute-start(bf16[3,128,256]{2,1,0:T(8,128)(2,1)S(1)} %get-tuple-element.39), channel_id=1, source_target_pairs={{0,2},{2,0},{4,6},{6,4},{8,10},{10,8},{12,14},{14,12},{16,18},{18,... | collective-permute-start | bytes 589832 | tf_op jit(solution)/shard_map/ppermute | solution.py:639
  15.7 20.9 %collective-permute-start.4 = (bf16[3,128,256]{2,1,0:T(8,128)(2,1)S(1)}, bf16[3,128,256]{2,1,0:T(8,128)(2,1)S(1)}, u32[]{:S(2)}, u32[]{:S(2)}) collective-permute-start(bf16[3,128,256]{2,1,0:T(8,128)(2,1)S(1)} %get-tuple-element.40), channel_id=1, source_target_pairs={{0,4},{2,6},{4,0},{6,2},{8,12},{10,14},{12,8},{14,10},{16,20},{18,... | collective-permute-start | bytes 589832 | tf_op jit(solution)/shard_map/ppermute | solution.py:639
  18.1 18.5 %collective-permute-start.5 = (bf16[3,128,256]{2,1,0:T(8,128)(2,1)S(1)}, bf16[3,128,256]{2,1,0:T(8,128)(2,1)S(1)}, u32[]{:S(2)}, u32[]{:S(2)}) collective-permute-start(bf16[3,128,256]{2,1,0:T(8,128)(2,1)S(1)} %get-tuple-element.41), channel_id=1, source_target_pairs={{0,6},{2,4},{4,2},{6,0},{8,14},{10,12},{12,10},{14,8},{16,22},{18,... | collective-permute-start | bytes 589832 | tf_op jit(solution)/shard_map/ppermute | solution.py:639
  19.7 44.1 %collective-permute-start.14 = (bf16[1024,256]{1,0:T(8,128)(2,1)S(1)}, bf16[1024,256]{1,0:T(8,128)(2,1)S(1)}, u32[]{:S(2)}, u32[]{:S(2)}) collective-permute-start(bf16[1024,256]{1,0:T(8,128)(2,1)S(1)} %collective-permute-done.12.refs_4_.refs_5_), channel_id=1, source_target_pairs={{8,16},{10,18},{12,20},{14,22},{16,8},{18,10},{20,12},{22,14},{9,1... | collective-permute-start | bytes 1572872 | tf_op jit(solution)/shard_map/ppermute | solution.py:660
  28.7 35.1 %collective-permute-start.15 = (bf16[1024,256]{1,0:T(8,128)(2,1)S(1)}, bf16[1024,256]{1,0:T(8,128)(2,1)S(1)}, u32[]{:S(2)}, u32[]{:S(2)}) collective-permute-start(bf16[1024,256]{1,0:T(8,128)(2,1)S(1)} %collective-permute-done.13.refs_5_.refs_6_), channel_id=1, source_target_pairs={{8,0},{10,2},{12,4},{14,6},{16,24},{18,26},{20,28},{22,30},{9,1},{... | collective-permute-start | bytes 1572872 | tf_op jit(solution)/shard_map/ppermute | solution.py:660
  39.3 10.8 %collective-permute-start.6 = (bf16[2,128,256]{2,1,0:T(8,128)(2,1)S(1)}, bf16[2,128,256]{2,1,0:T(8,128)(2,1)S(1)}, u32[]{:S(2)}, u32[]{:S(2)}) collective-permute-start(bf16[2,128,256]{2,1,0:T(8,128)(2,1)S(1)} %get-tuple-element.46), channel_id=1, source_target_pairs={{0,8},{2,10},{4,12},{6,14},{8,16},{10,18},{12,20},{14,22},{16,24},... | collective-permute-start | bytes 393224 | tf_op jit(solution)/shard_map/ppermute | solution.py:688
  43.9 6.2 %collective-permute-start.7 = (bf16[2,128,256]{2,1,0:T(8,128)(2,1)S(1)}, bf16[2,128,256]{2,1,0:T(8,128)(2,1)S(1)}, u32[]{:S(2)}, u32[]{:S(2)}) collective-permute-start(bf16[2,128,256]{2,1,0:T(8,128)(2,1)S(1)} %get-tuple-element.46), channel_id=1, source_target_pairs={{0,16},{2,18},{4,20},{6,22},{8,24},{10,26},{12,28},{14,30},{1,17},... | collective-permute-start | bytes 393224 | tf_op jit(solution)/shard_map/ppermute | solution.py:688
  46.5 3.5 %collective-permute-start.8 = (bf16[2,128,128]{2,1,0:T(8,128)(2,1)S(1)}, bf16[2,128,128]{2,1,0:T(8,128)(2,1)S(1)}, u32[]{:S(2)}, u32[]{:S(2)}) collective-permute-start(bf16[2,128,128]{2,1,0:T(8,128)(2,1)S(1)} %get-tuple-element.47), channel_id=1, source_target_pairs={{0,24},{2,26},{4,28},{6,30},{1,25},{3,27},{5,29},{7,31}} | collective-permute-start | bytes 196616 | tf_op jit(solution)/shard_map/ppermute | solution.py:688
  50.0 11.0 %copy-start = (bf16[1024,256]{1,0:T(8,128)(2,1)S(1)}, bf16[1024,256]{1,0:T(8,128)(2,1)}, u32[]{:S(2)}) copy-start(bf16[1024,256]{1,0:T(8,128)(2,1)} %refs_4_.3) | copy-start | bytes 1572868
  50.5 8.3 %collective-permute-start.10 = (bf16[512,256]{1,0:T(8,128)(2,1)S(1)}, bf16[512,256]{1,0:T(8,128)(2,1)S(1)}, u32[]{:S(2)}, u32[]{:S(2)}) collective-permute-start(bf16[512,256]{1,0:T(8,128)(2,1)S(1)} %join.1.refs_0_), channel_id=1, source_target_pairs={{0,4},{2,6},{4,0},{6,2},{8,12},{10,14},{12,8},{14,10},{16,20},{18,... | collective-permute-start | bytes 786440 | tf_op jit(solution)/shard_map/ppermute | solution.py:639
  52.1 8.9 %collective-permute-start.9 = (bf16[512,256]{1,0:T(8,128)(2,1)S(1)}, bf16[512,256]{1,0:T(8,128)(2,1)S(1)}, u32[]{:S(2)}, u32[]{:S(2)}) collective-permute-start(bf16[512,256]{1,0:T(8,128)(2,1)S(1)} %join.1.refs_0_), channel_id=1, source_target_pairs={{0,2},{2,0},{4,6},{6,4},{8,10},{10,8},{12,14},{14,12},{16,18},{18,... | collective-permute-start | bytes 786440 | tf_op jit(solution)/shard_map/ppermute | solution.py:639
  53.6 10.2 %collective-permute-start.11 = (bf16[512,256]{1,0:T(8,128)(2,1)S(1)}, bf16[512,256]{1,0:T(8,128)(2,1)S(1)}, u32[]{:S(2)}, u32[]{:S(2)}) collective-permute-start(bf16[512,256]{1,0:T(8,128)(2,1)S(1)} %join.1.refs_0_), channel_id=1, source_target_pairs={{0,6},{2,4},{4,2},{6,0},{8,14},{10,12},{12,10},{14,8},{16,22},{18,... | collective-permute-start | bytes 786440 | tf_op jit(solution)/shard_map/ppermute | solution.py:639
  64.9 1.7 %collective-permute-start.17 = (bf16[256,512]{1,0:T(8,128)(2,1)S(1)}, bf16[256,512]{1,0:T(8,128)(2,1)S(1)}, u32[]{:S(2)}, u32[]{:S(2)}) collective-permute-start(bf16[256,512]{1,0:T(8,128)(2,1)S(1)} %get-tuple-element.59), channel_id=1, source_target_pairs={{0,1},{1,0},{2,3},{3,2},{4,5},{5,4},{6,7},{7,6},{8,9},{9,8},{10,11... | collective-permute-start | bytes 786440 | tf_op jit(solution)/shard_map/ppermute | solution.py:722
  66.1 3.7 %collective-permute-start.16 = (bf16[256,512]{1,0:T(8,128)(2,1)S(1)}, bf16[256,512]{1,0:T(8,128)(2,1)S(1)}, u32[]{:S(2)}, u32[]{:S(2)}) collective-permute-start(bf16[256,512]{1,0:T(8,128)(2,1)S(1)} %get-tuple-element.55), channel_id=1, source_target_pairs={{0,1},{1,0},{2,3},{3,2},{4,5},{5,4},{6,7},{7,6},{8,9},{9,8},{10,11... | collective-permute-start | bytes 786440 | tf_op jit(solution)/shard_map/ppermute | solution.py:722
  66.7 5.8 %collective-permute-start.18 = (bf16[128,512]{1,0:T(8,128)(2,1)S(1)}, bf16[128,512]{1,0:T(8,128)(2,1)S(1)}, u32[]{:S(2)}, u32[]{:S(2)}) collective-permute-start(bf16[128,512]{1,0:T(8,128)(2,1)S(1)} %get-tuple-element.60), channel_id=1, source_target_pairs={{0,2},{2,0},{4,6},{6,4},{8,10},{10,8},{12,14},{14,12},{16,18},{18,... | collective-permute-start | bytes 393224 | tf_op jit(solution)/shard_map/ppermute | solution.py:639
  68.2 8.0 %collective-permute-start.19 = (bf16[128,512]{1,0:T(8,128)(2,1)S(1)}, bf16[128,512]{1,0:T(8,128)(2,1)S(1)}, u32[]{:S(2)}, u32[]{:S(2)}) collective-permute-start(bf16[128,512]{1,0:T(8,128)(2,1)S(1)} %get-tuple-element.61), channel_id=1, source_target_pairs={{0,4},{2,6},{4,0},{6,2},{8,12},{10,14},{12,8},{14,10},{16,20},{18,... | collective-permute-start | bytes 393224 | tf_op jit(solution)/shard_map/ppermute | solution.py:639
  69.9 6.3 %collective-permute-start.20 = (bf16[128,512]{1,0:T(8,128)(2,1)S(1)}, bf16[128,512]{1,0:T(8,128)(2,1)S(1)}, u32[]{:S(2)}, u32[]{:S(2)}) collective-permute-start(bf16[128,512]{1,0:T(8,128)(2,1)S(1)} %get-tuple-element.62), channel_id=1, source_target_pairs={{0,6},{2,4},{4,2},{6,0},{8,14},{10,12},{12,10},{14,8},{16,22},{18,... | collective-permute-start | bytes 393224 | tf_op jit(solution)/shard_map/ppermute | solution.py:639

commit v7 on v6

--- a/solution.py
+++ b/solution.py
@@ -435,9 +435,12 @@
     )(*held(*keys, *rests, high, low, steps))
 
 
-def join_kernel(count, *refs):
-    states, (local_ref, lift_ref, out_ref) = refs[:count], refs[count:]
+def join_kernel(count, splits, *refs):
+    states, (local_ref, lift_ref), outs = refs[:count], refs[count : count + 2], refs[count + 2 :]
     heads, width, _ = states[0].shape
+    group = sum(len(split) for split in splits)
+    tokens = local_ref.shape[0] // group
+    position, _ = where_am_i(group)
     for head in range(heads):
         lanes = slice(head * width, (head + 1) * width)
         total = None
@@ -449,17 +452,23 @@
                 total = (
                     total + step[:, width:] - dot(state[head, :, :width], total.astype(BF16))
                 )
-        out_ref[:, lanes] = (
-            local_ref[:, lanes] + dot(lift_ref[:, lanes], total.astype(BF16))
-        ).astype(BF16)
-
-
-def join(states, local, lifted):
+        total = total.astype(BF16)
+        for split_of, out_ref in zip(splits, outs):
+            for number, offset in enumerate(split_of):
+                rows = pl.ds(pl.multiple_of(place(position, offset) * tokens, tokens), tokens)
+                out_ref[number * tokens : (number + 1) * tokens, lanes] = (
+                    local_ref[rows, lanes] + dot(lift_ref[rows, lanes], total)
+                ).astype(BF16)
+
+
+def join(states, local, lifted, splits):
+    group = sum(len(split) for split in splits)
+    rows, wide = local.shape
     return pl.pallas_call(
-        functools.partial(join_kernel, len(states)),
-        out_shape=pltpu.VMEM(local.shape, BF16),
+        functools.partial(join_kernel, len(states), splits),
+        out_shape=[pltpu.VMEM((rows // group * len(split), wide), BF16) for split in splits],
         in_specs=[VMEM] * (len(states) + 2),
-        out_specs=VMEM,
+        out_specs=[VMEM] * len(splits),
         compiler_params=PARAMS,
         name="join",
     )(*held(*states, local, lifted))
@@ -483,56 +492,28 @@
     return lax.rem(device, group), device // group
 
 
-def target_rows(source, group, targets):
-    position, _ = where_am_i(group)
-    tokens = source.shape[0] // group
-    firsts = [pl.multiple_of(place(position, t) * tokens, tokens) for t in targets]
-    return jnp.concatenate([source[pl.ds(first, tokens), :] for first in firsts], axis=0)
-
-
-def begin_kernel(group, halves, early, *refs):
-    heads_in, weight_in, totals = refs[: len(early[0])], refs[len(early[0]) : -2], refs[-2:]
-    position, _ = where_am_i(group)
-    wide = heads_in[0].shape[1]
-    columns = weight_in[0].shape[1]
-    for targets, total_ref in zip(halves, totals):
-        for number, offset in enumerate(early[1]):
-            total = None
-            for member, source in zip(early[0], heads_in):
-                first = pl.multiple_of(place(position, member) * wide, wide)
-                part = dot(
-                    target_rows(source, group, targets),
-                    weight_rows(weight_in, offset, None, first, wide),
-                )
-                total = part if total is None else total + part
-            total_ref[:, number * columns : (number + 1) * columns] = total
-
-
-def project_kernel(group, targets, early, offsets, *refs):
-    heads_in, weight_in = refs[:group], refs[group:-3]
-    total_ref, send_ref, keep_ref = refs[-3:]
+def project_kernel(group, orders, offsets, *refs):
+    heads_in, weight_in, (send_ref, keep_ref) = refs[:group], refs[group:-2], refs[-2:]
     core = lax.axis_index("head")
     position, plane = where_am_i(group)
-    wide = heads_in[0].shape[1]
+    rows, wide = heads_in[0].shape
+    tokens = rows // len(orders[0])
     columns = weight_in[0].shape[1]
     side = keep_ref.shape[1] // columns
     inner = (plane == 1) | (plane == 2)
     for offset in offsets:
         owner = jnp.bitwise_xor(plane, offset)
         total = None
-        members = range(group)
-        if offset in early[1]:
-            number = early[1].index(offset)
-            members = [member for member in members if member not in early[0]]
-        for member in members:
+        for member in range(group):
             first = pl.multiple_of(place(position, member) * wide, wide)
+            blocks = [
+                heads_in[member][at * tokens : (at + 1) * tokens, :] for at in orders[member]
+            ]
             part = dot(
-                target_rows(heads_in[member], group, targets),
+                jnp.concatenate(blocks, axis=0),
                 weight_rows(weight_in, offset, inner, first, wide),
             )
             total = part if total is None else total + part
-        if offset in early[1]:
-            total = total + total_ref[:, number * columns : (number + 1) * columns]
         result = total.astype(BF16)
         lanes = pl.ds(pl.multiple_of(lax.rem(owner, side) * columns, columns), columns)
 
@@ -545,38 +526,20 @@
             send_ref[:, lanes] = result
 
 
-def begin_projection(heads, weights, halves, early):
+def project(heads, weights, planes, orders):
     group = len(heads)
-    tokens = heads[0].shape[0] // group
-    columns = weights[0].shape[1]
-    here = [heads[member] for member in early[0]] + list(weights[: len(early[1])])
-    return pl.pallas_call(
-        functools.partial(begin_kernel, group, halves, early),
-        out_shape=[
-            pltpu.VMEM((tokens * len(targets), columns * len(early[1])), F32)
-            for targets in halves
-        ],
-        in_specs=[VMEM] * len(here),
-        out_specs=[VMEM] * 2,
-        compiler_params=PARAMS,
-        name="begin_projection",
-    )(*held(*here))
-
-
-def project(heads, weights, planes, targets, early, total):
-    group = len(heads)
-    rows = heads[0].shape[0] // group * len(targets)
+    rows = heads[0].shape[0]
     columns = weights[0].shape[1]
     offsets = (0, 1, 3, 2) if planes == 4 else (0, 1)
     shape = pltpu.VMEM((rows, columns * planes // 2), BF16)
     return pl.pallas_call(
-        functools.partial(project_kernel, group, targets, early, offsets),
+        functools.partial(project_kernel, group, orders, offsets),
         out_shape=(shape, shape),
-        in_specs=[VMEM] * (group + len(weights) + 1),
+        in_specs=[VMEM] * (group + len(weights)),
         out_specs=(VMEM, VMEM),
         compiler_params=PARAMS,
         name="project",
-    )(*held(*heads, *weights, total))
+    )(*held(*heads, *weights))
 
 
 def sum_kernel(keep_ref, other_ref, *outs):
@@ -705,32 +668,37 @@
             between_planes(weights[2], ((1, 0), (2, 3))),
         ]
 
-    mixed_heads = join(states, local, lifted)
-
     if split_out:
-        order = tuple(range(1, group)) + (0,)
-        row_halves = (order[: group // 2], order[group // 2 :])
-        early = (tuple(range(group - 1)), (0, 1, 3) if planes == 4 else (0, 1))
+        row_halves = ((3, 1), (2, 0)) if group == 4 else ((1,), (0,))
+        ready = join(states, local, lifted, row_halves)
         parts = [None] * group
-        gathered = [mixed_heads]
-        for offset in range(1, group):
-            gathered.append(swap(mixed_heads, group, offset, count))
-        totals = begin_projection(gathered, weights, row_halves, early)
-        halves = []
-        for targets, total in zip(row_halves, totals):
-            send, keep = project(gathered, weights, planes, targets, early, total)
+        gathered, orders = [], []
+        for targets in row_halves:
+            arrays, order = [], []
+            for offset in range(group):
+                seen = [target ^ offset for target in targets]
+                source = row_halves.index(
+                    next(half for half in row_halves if set(half) == set(seen))
+                )
+                order.append(tuple(row_halves[source].index(block) for block in seen))
+                array = ready[source]
+                if offset:
+                    array = swap(array, group, offset, count)
+                arrays.append(array)
+            gathered.append(arrays)
+            orders.append(tuple(order))
+        for number, targets in enumerate(row_halves):
+            send, keep = project(gathered[number], weights, planes, orders[number])
             other = lax.ppermute(send, "head", [(0, 1), (1, 0)])
-            halves.append((targets, keep, other))
-        for targets, keep, other in halves:
             for offset, part in zip(targets, sum_parts(keep, other, len(targets))):
                 parts[offset] = swap(part, group, offset, count) if offset else part
         return lay_out(parts, out_weight.shape[1])
 
+    (mixed_heads,) = join(states, local, lifted, (tuple(range(group)),))
     if group > 1:
         position_rows = []
         for offset in range(group):
-            first = jnp.bitwise_xor(position, offset) * tokens
-            part = lax.dynamic_slice_in_dim(mixed_heads, first, tokens, 0)
+            part = lax.dynamic_slice_in_dim(mixed_heads, offset * tokens, tokens, 0)
             position_rows.append(swap(part, group, offset, count) if offset else part)
         stacked = jnp.stack(position_rows)
         order = jnp.bitwise_xor(position, jnp.arange(group))

time: 77.3 us -> 82.7 us (1.070)
  starting transfers between devices: 32.6 us -> 36.1 us
  waiting for transfers between devices: 27.5 us -> 28.6 us
    ppermute x12 -> x15, starting transfers between devices: 16 us -> 19.9 us  [swap(): return lax.ppermute(value, 'seq', pairs)]
    ppermute x12 -> x15, waiting for transfers between devices: 18.6 us -> 19.7 us  [swap(): return lax.ppermute(value, 'seq', pairs)]
    pallas_call x4 -> x3, Pallas kernels: 3.43 us -> 4.2 us  [the longest x2 3.43 us: project(): pl.pallas_call(functools.partial(project_kernel, group, orders, offsets),...]
  transfers between devices with their start and end apart: 21 -> 24, of which waited for: 9 -> 11; matrix products, arithmetic and copies ran while one was open for 0% -> 0% of each run, Pallas kernels for 19% -> 20%
where the time goes in v7:
time: 82.7 us; the launch traced here: 82.5 us
  starting transfers between devices  36.1 us (44%)
  waiting for transfers between devices  28.6 us (35%)
  Pallas kernels  17.6 us (21%)
    ppermute x15, starting transfers between devices, swap(): return lax.ppermute(value, 'seq', pairs)  19.9 us
    ppermute x15, waiting for transfers between devices, swap(): return lax.ppermute(value, 'seq', pairs)  19.7 us
    ppermute x3, starting transfers between devices, from_earlier(): return lax.ppermute(value, 'seq', pairs)  8.52 us
    ppermute x4, waiting for transfers between devices, between_planes(): lax.ppermute(value, 'seq', [(source * group + i, target * group + i) for...  8.29 us
    ppermute x4, starting transfers between devices, between_planes(): lax.ppermute(value, 'seq', [(source * group + i, target * group + i) for...  7.49 us
    pallas_call x2, Pallas kernels, invert(): pl.pallas_call(functools.partial(invert_kernel, heads, tokens), out_shape...  6.6 us
    pallas_call x2, Pallas kernels, project(): pl.pallas_call(functools.partial(project_kernel, group, orders, offsets),...  3.43 us
    pallas_call x1, Pallas kernels, carry_state(): pl.pallas_call(functools.partial(state_kernel, group, parts), out_shape=(...  2.63 us
  transfers between devices with their start and end apart: 24, of which 11 were waited for; matrix products, arithmetic and copies ran while one was open for 0% of the time, Pallas kernels for 20%

profile of v7, /device:TPU:0, one launch (start us, length us, event | category | flops | bytes accessed | tf_op | source)
XLA Modules:
  0.0 82.5 jit_solution(4639619715783790663)
XLA Ops:
  0.0 3.1 %collective-permute-start.12 = (bf16[1024,256]{1,0:T(8,128)(2,1)}, bf16[1024,256]{1,0:T(8,128)(2,1)S(1)}, u32[]{:S(2)}, u32[]{:S(2)}) collective-permute-start(bf16[1024,256]{1,0:T(8,128)(2,1)} %refs_4_.3), channel_id=1, source_target_pairs={{0,8},{2,10},{4,12},{6,14},{8,0},{10,2},{12,4},{14,6},{16,24},{18,... | collective-permute-start | bytes 1572872 | tf_op jit(solution)/shard_map/ppermute | solution.py:623
  3.1 2.5 %collective-permute-start.13 = (bf16[1024,256]{1,0:T(8,128)(2,1)}, bf16[1024,256]{1,0:T(8,128)(2,1)S(1)}, u32[]{:S(2)}, u32[]{:S(2)}) collective-permute-start(bf16[1024,256]{1,0:T(8,128)(2,1)} %refs_4_.3), channel_id=1, source_target_pairs={{0,24},{2,26},{4,28},{6,30},{8,16},{10,18},{12,20},{14,22},{16,8},... | collective-permute-start | bytes 1572872 | tf_op jit(solution)/shard_map/ppermute | solution.py:623
  7.1 1.6 %collective-permute-start.1 = (bf16[272,256]{1,0:T(8,128)(2,1)S(1)}, bf16[272,256]{1,0:T(8,128)(2,1)S(1)}, u32[]{:S(2)}, u32[]{:S(2)}) collective-permute-start(bf16[272,256]{1,0:T(8,128)(2,1)S(1)} %get-tuple-element.36), channel_id=1, source_target_pairs={{0,4},{2,6},{4,0},{6,2},{8,12},{10,14},{12,8},{14,10},{16,20},{18,... | collective-permute-start | bytes 417800 | tf_op jit(solution)/shard_map/ppermute | solution.py:602
  10.6 3.6 %collective-permute-done.1.refs_0_.refs_2_ = bf16[272,256]{1,0:T(8,128)(2,1)S(1)} collective-permute-done((bf16[272,256]{1,0:T(8,128)(2,1)S(1)}, bf16[272,256]{1,0:T(8,128)(2,1)S(1)}, u32[]{:S(2)}, u32[]{:S(2)}) %collective-permute-start.1) | collective-permute-done | bytes 139296 | tf_op jit(solution)/shard_map/ppermute | solution.py:602
  15.7 2.1 %collective-permute-start.4 = (bf16[3,128,256]{2,1,0:T(8,128)(2,1)S(1)}, bf16[3,128,256]{2,1,0:T(8,128)(2,1)S(1)}, u32[]{:S(2)}, u32[]{:S(2)}) collective-permute-start(bf16[3,128,256]{2,1,0:T(8,128)(2,1)S(1)} %get-tuple-element.40), channel_id=1, source_target_pairs={{0,4},{2,6},{4,0},{6,2},{8,12},{10,14},{12,8},{14,10},{16,20},{18,... | collective-permute-start | bytes 589832 | tf_op jit(solution)/shard_map/ppermute | solution.py:602
  18.1 1.6 %collective-permute-start.5 = (bf16[3,128,256]{2,1,0:T(8,128)(2,1)S(1)}, bf16[3,128,256]{2,1,0:T(8,128)(2,1)S(1)}, u32[]{:S(2)}, u32[]{:S(2)}) collective-permute-start(bf16[3,128,256]{2,1,0:T(8,128)(2,1)S(1)} %get-tuple-element.41), channel_id=1, source_target_pairs={{0,6},{2,4},{4,2},{6,0},{8,14},{10,12},{12,10},{14,8},{16,22},{18,... | collective-permute-start | bytes 589832 | tf_op jit(solution)/shard_map/ppermute | solution.py:602
  20.4 8.3 %collective-permute-done.13.refs_6_ = bf16[1024,256]{1,0:T(8,128)(2,1)S(1)} collective-permute-done((bf16[1024,256]{1,0:T(8,128)(2,1)}, bf16[1024,256]{1,0:T(8,128)(2,1)S(1)}, u32[]{:S(2)}, u32[]{:S(2)}) %collective-permute-start.13) | collective-permute-done | bytes 524320 | tf_op jit(solution)/shard_map/ppermute | solution.py:623
  30.0 3.3 %invert.3 = (f32[2,2,3,128,128]{4,3,2,1,0:T(8,128)S(1)}, f32[2,2,8,256]{3,2,1,0:T(8,128)S(1)}) custom-call(bf16[272,256]{1,0:T(8,128)(2,1)S(1)} %collective-permute-done.1.refs_0_.refs_2_, bf16[272,256]{1,0:T(8,128)(2,1)S(1)} %collective-permute-done.2.refs_1_.refs_3_), custom_call_target="tpu_custom_call" | custom-call | tf_op jit(solution)/shard_map/invert/pallas_call | solution.py:238
  33.3 3.3 %invert.2 = (f32[2,2,3,128,128]{4,3,2,1,0:T(8,128)S(1)}, f32[2,2,8,256]{3,2,1,0:T(8,128)S(1)}) custom-call(bf16[272,256]{1,0:T(8,128)(2,1)S(1)} %get-tuple-element.34.refs_0_, bf16[272,256]{1,0:T(8,128)(2,1)S(1)} %collective-permute-done.refs_1_), custom_call_target="tpu_custom_call" | custom-call | tf_op jit(solution)/shard_map/invert/pallas_call | solution.py:238
  36.7 2.6 %carry_state.1 = (bf16[2,4,256,256]{3,2,1,0:T(8,128)(2,1)S(1)}, bf16[2,4,256,256]{3,2,1,0:T(8,128)(2,1)S(1)}, f32[2,4,128,256]{3,2,1,0:T(8,128)S(1)}, bf16[2,128...) custom-call(bf16[272,256]{1,0:T(8,128)(2,1)S(1)} %get-tuple-element.34.refs_0_, ...), custom_call_target="tpu_custom_call" | custom-call | tf_op jit(solution)/shard_map/carry_state/pallas_call | solution.py:350
  39.3 4.6 %collective-permute-start.6 = (bf16[2,128,256]{2,1,0:T(8,128)(2,1)S(1)}, bf16[2,128,256]{2,1,0:T(8,128)(2,1)S(1)}, u32[]{:S(2)}, u32[]{:S(2)}) collective-permute-start(bf16[2,128,256]{2,1,0:T(8,128)(2,1)S(1)} %get-tuple-element.46), channel_id=1, source_target_pairs={{0,8},{2,10},{4,12},{6,14},{8,16},{10,18},{12,20},{14,22},{16,24},... | collective-permute-start | bytes 393224 | tf_op jit(solution)/shard_map/ppermute | solution.py:651
  43.9 2.6 %collective-permute-start.7 = (bf16[2,128,256]{2,1,0:T(8,128)(2,1)S(1)}, bf16[2,128,256]{2,1,0:T(8,128)(2,1)S(1)}, u32[]{:S(2)}, u32[]{:S(2)}) collective-permute-start(bf16[2,128,256]{2,1,0:T(8,128)(2,1)S(1)} %get-tuple-element.46), channel_id=1, source_target_pairs={{0,16},{2,18},{4,20},{6,22},{8,24},{10,26},{12,28},{14,30},{1,17},... | collective-permute-start | bytes 393224 | tf_op jit(solution)/shard_map/ppermute | solution.py:651
  47.8 1.7 %read.1 = (f32[512,256]{1,0:T(8,128)S(1)}, bf16[512,256]{1,0:T(8,128)(2,1)S(1)}) custom-call(bf16[272,256]{1,0:T(8,128)(2,1)S(1)} %get-tuple-element.34.refs_0_, bf16[272,256]{1,0:T(8,128)(2,1)S(1)} %collective-permute-done.refs_1_, bf16[272,256]{1,0:T(8,128)(2,1)S(1)} %collective-permute-done.1.refs_0_.refs_2_, ...), custom_call_target="tpu_custom_call" | custom-call | tf_op jit(solution)/shard_map/read/pallas_call | solution.py:420
  50.8 1.5 %collective-permute-start.17 = (bf16[256,256]{1,0:T(8,128)(2,1)S(1)}, bf16[256,256]{1,0:T(8,128)(2,1)S(1)}, u32[]{:S(2)}, u32[]{:S(2)}) collective-permute-start(bf16[256,256]{1,0:T(8,128)(2,1)S(1)} %get-tuple-element.53.refs_0_), channel_id=1, source_target_pairs={{0,2},{2,0},{4,6},{6,4},{8,10},{10,8},{12,14},{14,12},{16,18},{18,... | collective-permute-start | bytes 393224 | tf_op jit(solution)/shard_map/ppermute | solution.py:602
  54.4 2.5 %collective-permute-done.17.refs_1_ = bf16[256,256]{1,0:T(8,128)(2,1)S(1)} collective-permute-done((bf16[256,256]{1,0:T(8,128)(2,1)S(1)}, bf16[256,256]{1,0:T(8,128)(2,1)S(1)}, u32[]{:S(2)}, u32[]{:S(2)}) %collective-permute-start.17) | collective-permute-done | bytes 131104 | tf_op jit(solution)/shard_map/ppermute | solution.py:602
  56.9 1.6 %collective-permute-start.10 = (bf16[256,256]{1,0:T(8,128)(2,1)S(1)}, bf16[256,256]{1,0:T(8,128)(2,1)S(1)}, u32[]{:S(2)}, u32[]{:S(2)}) collective-permute-start(bf16[256,256]{1,0:T(8,128)(2,1)S(1)} %get-tuple-element.53.refs_0_), channel_id=1, source_target_pairs={{0,4},{2,6},{4,0},{6,2},{8,12},{10,14},{12,8},{14,10},{16,20},{18,... | collective-permute-start | bytes 393224 | tf_op jit(solution)/shard_map/ppermute | solution.py:602
  58.4 3.7 %collective-permute-done.18.refs_2_ = bf16[256,256]{1,0:T(8,128)(2,1)S(1)} collective-permute-done((bf16[256,256]{1,0:T(8,128)(2,1)S(1)}, bf16[256,256]{1,0:T(8,128)(2,1)S(1)}, u32[]{:S(2)}, u32[]{:S(2)}) %collective-permute-start.18) | collective-permute-done | bytes 131104 | tf_op jit(solution)/shard_map/ppermute | solution.py:602
  62.5 2.0 %collective-permute-start.9 = (bf16[256,256]{1,0:T(8,128)(2,1)S(1)}, bf16[256,256]{1,0:T(8,128)(2,1)S(1)}, u32[]{:S(2)}, u32[]{:S(2)}) collective-permute-start(bf16[256,256]{1,0:T(8,128)(2,1)S(1)} %get-tuple-element.54.refs_0_), channel_id=1, source_target_pairs={{0,2},{2,0},{4,6},{6,4},{8,10},{10,8},{12,14},{14,12},{16,18},{18,... | collective-permute-start | bytes 393224 | tf_op jit(solution)/shard_map/ppermute | solution.py:602
  64.6 1.7 %project.3 = (bf16[256,512]{1,0:T(8,128)(2,1)S(1)}, bf16[256,512]{1,0:T(8,128)(2,1)S(1)}) custom-call(bf16[256,256]{1,0:T(8,128)(2,1)S(1)} %get-tuple-element.54.refs_0_, bf16[256,256]{1,0:T(8,128)(2,1)S(1)} %collective-permute-done.17.refs_1_, bf16[256,256]{1,0:T(8,128)(2,1)S(1)} %collective-permute-done.18.refs_2_, ...), custom_call_target="tpu_custom_call" | custom-call | tf_op jit(solution)/shard_map/project/pallas_call | solution.py:535
  66.4 1.6 %collective-permute-done.11.refs_3_ = bf16[256,256]{1,0:T(8,128)(2,1)S(1)} collective-permute-done((bf16[256,256]{1,0:T(8,128)(2,1)S(1)}, bf16[256,256]{1,0:T(8,128)(2,1)S(1)}, u32[]{:S(2)}, u32[]{:S(2)}) %collective-permute-start.11) | collective-permute-done | bytes 131104 | tf_op jit(solution)/shard_map/ppermute | solution.py:602
  68.9 1.7 %project.2 = (bf16[256,512]{1,0:T(8,128)(2,1)S(1)}, bf16[256,512]{1,0:T(8,128)(2,1)S(1)}) custom-call(bf16[256,256]{1,0:T(8,128)(2,1)S(1)} %get-tuple-element.53.refs_0_, bf16[256,256]{1,0:T(8,128)(2,1)S(1)} %collective-permute-done.9.refs_1_, bf16[256,256]{1,0:T(8,128)(2,1)S(1)} %collective-permute-done.10.refs_2_, ...), custom_call_target="tpu_custom_call" | custom-call | tf_op jit(solution)/shard_map/project/pallas_call | solution.py:535
  71.5 1.9 %collective-permute-start.23 = (bf16[128,512]{1,0:T(8,128)(2,1)S(1)}, bf16[128,512]{1,0:T(8,128)(2,1)S(1)}, u32[]{:S(2)}, u32[]{:S(2)}) collective-permute-start(bf16[128,512]{1,0:T(8,128)(2,1)S(1)} %get-tuple-element.62), channel_id=1, source_target_pairs={{0,6},{2,4},{4,2},{6,0},{8,14},{10,12},{12,10},{14,8},{16,22},{18,... | collective-permute-start | bytes 393224 | tf_op jit(solution)/shard_map/ppermute | solution.py:602
  74.5 2.7 %collective-permute-done.21.refs_1_ = bf16[128,512]{1,0:T(8,128)(2,1)S(1)} collective-permute-done((bf16[128,512]{1,0:T(8,128)(2,1)S(1)}, bf16[128,512]{1,0:T(8,128)(2,1)S(1)}, u32[]{:S(2)}, u32[]{:S(2)}) %collective-permute-start.21) | collective-permute-done | bytes 131104 | tf_op jit(solution)/shard_map/ppermute | solution.py:602
  77.2 2.9 %collective-permute-done.23.refs_3_ = bf16[128,512]{1,0:T(8,128)(2,1)S(1)} collective-permute-done((bf16[128,512]{1,0:T(8,128)(2,1)S(1)}, bf16[128,512]{1,0:T(8,128)(2,1)S(1)}, u32[]{:S(2)}, u32[]{:S(2)}) %collective-permute-start.23) | collective-permute-done | bytes 131104 | tf_op jit(solution)/shard_map/ppermute | solution.py:602
  (37 shorter events, 17.5 us)
Async XLA Ops:
  0.0 19.7 %collective-permute-start.12 = (bf16[1024,256]{1,0:T(8,128)(2,1)}, bf16[1024,256]{1,0:T(8,128)(2,1)S(1)}, u32[]{:S(2)}, u32[]{:S(2)}) collective-permute-start(bf16[1024,256]{1,0:T(8,128)(2,1)} %refs_4_.3), channel_id=1, source_target_pairs={{0,8},{2,10},{4,12},{6,14},{8,0},{10,2},{12,4},{14,6},{16,24},{18,... | collective-permute-start | bytes 1572872 | tf_op jit(solution)/shard_map/ppermute | solution.py:623
  3.1 25.7 %collective-permute-start.13 = (bf16[1024,256]{1,0:T(8,128)(2,1)}, bf16[1024,256]{1,0:T(8,128)(2,1)S(1)}, u32[]{:S(2)}, u32[]{:S(2)}) collective-permute-start(bf16[1024,256]{1,0:T(8,128)(2,1)} %refs_4_.3), channel_id=1, source_target_pairs={{0,24},{2,26},{4,28},{6,30},{8,16},{10,18},{12,20},{14,22},{16,8},... | collective-permute-start | bytes 1572872 | tf_op jit(solution)/shard_map/ppermute | solution.py:623
  7.1 7.2 %collective-permute-start.1 = (bf16[272,256]{1,0:T(8,128)(2,1)S(1)}, bf16[272,256]{1,0:T(8,128)(2,1)S(1)}, u32[]{:S(2)}, u32[]{:S(2)}) collective-permute-start(bf16[272,256]{1,0:T(8,128)(2,1)S(1)} %get-tuple-element.36), channel_id=1, source_target_pairs={{0,4},{2,6},{4,0},{6,2},{8,12},{10,14},{12,8},{14,10},{16,20},{18,... | collective-permute-start | bytes 417800 | tf_op jit(solution)/shard_map/ppermute | solution.py:602
  8.6 7.1 %collective-permute-start.2 = (bf16[272,256]{1,0:T(8,128)(2,1)S(1)}, bf16[272,256]{1,0:T(8,128)(2,1)S(1)}, u32[]{:S(2)}, u32[]{:S(2)}) collective-permute-start(bf16[272,256]{1,0:T(8,128)(2,1)S(1)} %get-tuple-element.37), channel_id=1, source_target_pairs={{0,6},{2,4},{4,2},{6,0},{8,14},{10,12},{12,10},{14,8},{16,22},{18,... | collective-permute-start | bytes 417800 | tf_op jit(solution)/shard_map/ppermute | solution.py:602
  10.1 8.0 %collective-permute-start = (bf16[272,256]{1,0:T(8,128)(2,1)S(1)}, bf16[272,256]{1,0:T(8,128)(2,1)S(1)}, u32[]{:S(2)}, u32[]{:S(2)}) collective-permute-start(bf16[272,256]{1,0:T(8,128)(2,1)S(1)} %get-tuple-element.35), channel_id=1, source_target_pairs={{0,2},{2,0},{4,6},{6,4},{8,10},{10,8},{12,14},{14,12},{16,18},{18,... | collective-permute-start | bytes 417800 | tf_op jit(solution)/shard_map/ppermute | solution.py:602
  14.2 22.4 %collective-permute-start.3 = (bf16[3,128,256]{2,1,0:T(8,128)(2,1)S(1)}, bf16[3,128,256]{2,1,0:T(8,128)(2,1)S(1)}, u32[]{:S(2)}, u32[]{:S(2)}) collective-permute-start(bf16[3,128,256]{2,1,0:T(8,128)(2,1)S(1)} %get-tuple-element.39), channel_id=1, source_target_pairs={{0,2},{2,0},{4,6},{6,4},{8,10},{10,8},{12,14},{14,12},{16,18},{18,... | collective-permute-start | bytes 589832 | tf_op jit(solution)/shard_map/ppermute | solution.py:602
  15.7 20.9 %collective-permute-start.4 = (bf16[3,128,256]{2,1,0:T(8,128)(2,1)S(1)}, bf16[3,128,256]{2,1,0:T(8,128)(2,1)S(1)}, u32[]{:S(2)}, u32[]{:S(2)}) collective-permute-start(bf16[3,128,256]{2,1,0:T(8,128)(2,1)S(1)} %get-tuple-element.40), channel_id=1, source_target_pairs={{0,4},{2,6},{4,0},{6,2},{8,12},{10,14},{12,8},{14,10},{16,20},{18,... | collective-permute-start | bytes 589832 | tf_op jit(solution)/shard_map/ppermute | solution.py:602
  18.1 18.5 %collective-permute-start.5 = (bf16[3,128,256]{2,1,0:T(8,128)(2,1)S(1)}, bf16[3,128,256]{2,1,0:T(8,128)(2,1)S(1)}, u32[]{:S(2)}, u32[]{:S(2)}) collective-permute-start(bf16[3,128,256]{2,1,0:T(8,128)(2,1)S(1)} %get-tuple-element.41), channel_id=1, source_target_pairs={{0,6},{2,4},{4,2},{6,0},{8,14},{10,12},{12,10},{14,8},{16,22},{18,... | collective-permute-start | bytes 589832 | tf_op jit(solution)/shard_map/ppermute | solution.py:602
  19.7 44.8 %collective-permute-start.14 = (bf16[1024,256]{1,0:T(8,128)(2,1)S(1)}, bf16[1024,256]{1,0:T(8,128)(2,1)S(1)}, u32[]{:S(2)}, u32[]{:S(2)}) collective-permute-start(bf16[1024,256]{1,0:T(8,128)(2,1)S(1)} %collective-permute-done.12.refs_5_), channel_id=1, source_target_pairs={{8,16},{10,18},{12,20},{14,22},{16,8},{18,10},{20,12},{22,14},{9,1... | collective-permute-start | bytes 1572872 | tf_op jit(solution)/shard_map/ppermute | solution.py:623
  28.7 35.8 %collective-permute-start.15 = (bf16[1024,256]{1,0:T(8,128)(2,1)S(1)}, bf16[1024,256]{1,0:T(8,128)(2,1)S(1)}, u32[]{:S(2)}, u32[]{:S(2)}) collective-permute-start(bf16[1024,256]{1,0:T(8,128)(2,1)S(1)} %collective-permute-done.13.refs_6_), channel_id=1, source_target_pairs={{8,0},{10,2},{12,4},{14,6},{16,24},{18,26},{20,28},{22,30},{9,1},{... | collective-permute-start | bytes 1572872 | tf_op jit(solution)/shard_map/ppermute | solution.py:623
  39.3 10.8 %collective-permute-start.6 = (bf16[2,128,256]{2,1,0:T(8,128)(2,1)S(1)}, bf16[2,128,256]{2,1,0:T(8,128)(2,1)S(1)}, u32[]{:S(2)}, u32[]{:S(2)}) collective-permute-start(bf16[2,128,256]{2,1,0:T(8,128)(2,1)S(1)} %get-tuple-element.46), channel_id=1, source_target_pairs={{0,8},{2,10},{4,12},{6,14},{8,16},{10,18},{12,20},{14,22},{16,24},... | collective-permute-start | bytes 393224 | tf_op jit(solution)/shard_map/ppermute | solution.py:651
  43.9 6.2 %collective-permute-start.7 = (bf16[2,128,256]{2,1,0:T(8,128)(2,1)S(1)}, bf16[2,128,256]{2,1,0:T(8,128)(2,1)S(1)}, u32[]{:S(2)}, u32[]{:S(2)}) collective-permute-start(bf16[2,128,256]{2,1,0:T(8,128)(2,1)S(1)} %get-tuple-element.46), channel_id=1, source_target_pairs={{0,16},{2,18},{4,20},{6,22},{8,24},{10,26},{12,28},{14,30},{1,17},... | collective-permute-start | bytes 393224 | tf_op jit(solution)/shard_map/ppermute | solution.py:651
  46.5 3.5 %collective-permute-start.8 = (bf16[2,128,128]{2,1,0:T(8,128)(2,1)S(1)}, bf16[2,128,128]{2,1,0:T(8,128)(2,1)S(1)}, u32[]{:S(2)}, u32[]{:S(2)}) collective-permute-start(bf16[2,128,128]{2,1,0:T(8,128)(2,1)S(1)} %get-tuple-element.47), channel_id=1, source_target_pairs={{0,24},{2,26},{4,28},{6,30},{1,25},{3,27},{5,29},{7,31}} | collective-permute-start | bytes 196616 | tf_op jit(solution)/shard_map/ppermute | solution.py:651
  50.8 6.0 %collective-permute-start.17 = (bf16[256,256]{1,0:T(8,128)(2,1)S(1)}, bf16[256,256]{1,0:T(8,128)(2,1)S(1)}, u32[]{:S(2)}, u32[]{:S(2)}) collective-permute-start(bf16[256,256]{1,0:T(8,128)(2,1)S(1)} %get-tuple-element.53.refs_0_), channel_id=1, source_target_pairs={{0,2},{2,0},{4,6},{6,4},{8,10},{10,8},{12,14},{14,12},{16,18},{18,... | collective-permute-start | bytes 393224 | tf_op jit(solution)/shard_map/ppermute | solution.py:602
  52.4 9.7 %collective-permute-start.18 = (bf16[256,256]{1,0:T(8,128)(2,1)S(1)}, bf16[256,256]{1,0:T(8,128)(2,1)S(1)}, u32[]{:S(2)}, u32[]{:S(2)}) collective-permute-start(bf16[256,256]{1,0:T(8,128)(2,1)S(1)} %get-tuple-element.54.refs_0_), channel_id=1, source_target_pairs={{0,4},{2,6},{4,0},{6,2},{8,12},{10,14},{12,8},{14,10},{16,20},{18,... | collective-permute-start | bytes 393224 | tf_op jit(solution)/shard_map/ppermute | solution.py:602
  53.9 8.6 %collective-permute-start.19 = (bf16[256,256]{1,0:T(8,128)(2,1)S(1)}, bf16[256,256]{1,0:T(8,128)(2,1)S(1)}, u32[]{:S(2)}, u32[]{:S(2)}) collective-permute-start(bf16[256,256]{1,0:T(8,128)(2,1)S(1)} %get-tuple-element.53.refs_0_), channel_id=1, source_target_pairs={{0,6},{2,4},{4,2},{6,0},{8,14},{10,12},{12,10},{14,8},{16,22},{18,... | collective-permute-start | bytes 393224 | tf_op jit(solution)/shard_map/ppermute | solution.py:602
  56.9 9.5 %collective-permute-start.10 = (bf16[256,256]{1,0:T(8,128)(2,1)S(1)}, bf16[256,256]{1,0:T(8,128)(2,1)S(1)}, u32[]{:S(2)}, u32[]{:S(2)}) collective-permute-start(bf16[256,256]{1,0:T(8,128)(2,1)S(1)} %get-tuple-element.53.refs_0_), channel_id=1, source_target_pairs={{0,4},{2,6},{4,0},{6,2},{8,12},{10,14},{12,8},{14,10},{16,20},{18,... | collective-permute-start | bytes 393224 | tf_op jit(solution)/shard_map/ppermute | solution.py:602
  62.1 5.9 %collective-permute-start.11 = (bf16[256,256]{1,0:T(8,128)(2,1)S(1)}, bf16[256,256]{1,0:T(8,128)(2,1)S(1)}, u32[]{:S(2)}, u32[]{:S(2)}) collective-permute-start(bf16[256,256]{1,0:T(8,128)(2,1)S(1)} %get-tuple-element.54.refs_0_), channel_id=1, source_target_pairs={{0,6},{2,4},{4,2},{6,0},{8,14},{10,12},{12,10},{14,8},{16,22},{18,... | collective-permute-start | bytes 393224 | tf_op jit(solution)/shard_map/ppermute | solution.py:602
  62.5 6.4 %collective-permute-start.9 = (bf16[256,256]{1,0:T(8,128)(2,1)S(1)}, bf16[256,256]{1,0:T(8,128)(2,1)S(1)}, u32[]{:S(2)}, u32[]{:S(2)}) collective-permute-start(bf16[256,256]{1,0:T(8,128)(2,1)S(1)} %get-tuple-element.54.refs_0_), channel_id=1, source_target_pairs={{0,2},{2,0},{4,6},{6,4},{8,10},{10,8},{12,14},{14,12},{16,18},{18,... | collective-permute-start | bytes 393224 | tf_op jit(solution)/shard_map/ppermute | solution.py:602
  66.3 4.4 %collective-permute-start.20 = (bf16[256,512]{1,0:T(8,128)(2,1)S(1)}, bf16[256,512]{1,0:T(8,128)(2,1)S(1)}, u32[]{:S(2)}, u32[]{:S(2)}) collective-permute-start(bf16[256,512]{1,0:T(8,128)(2,1)S(1)} %get-tuple-element.59), channel_id=1, source_target_pairs={{0,1},{1,0},{2,3},{3,2},{4,5},{5,4},{6,7},{7,6},{8,9},{9,8},{10,11... | collective-permute-start | bytes 786440 | tf_op jit(solution)/shard_map/ppermute | solution.py:692
  70.6 2.7 %collective-permute-start.16 = (bf16[256,512]{1,0:T(8,128)(2,1)S(1)}, bf16[256,512]{1,0:T(8,128)(2,1)S(1)}, u32[]{:S(2)}, u32[]{:S(2)}) collective-permute-start(bf16[256,512]{1,0:T(8,128)(2,1)S(1)} %get-tuple-element.56), channel_id=1, source_target_pairs={{0,1},{1,0},{2,3},{3,2},{4,5},{5,4},{6,7},{7,6},{8,9},{9,8},{10,11... | collective-permute-start | bytes 786440 | tf_op jit(solution)/shard_map/ppermute | solution.py:692
  70.8 6.4 %collective-permute-start.21 = (bf16[128,512]{1,0:T(8,128)(2,1)S(1)}, bf16[128,512]{1,0:T(8,128)(2,1)S(1)}, u32[]{:S(2)}, u32[]{:S(2)}) collective-permute-start(bf16[128,512]{1,0:T(8,128)(2,1)S(1)} %get-tuple-element.60), channel_id=1, source_target_pairs={{0,2},{2,0},{4,6},{6,4},{8,10},{10,8},{12,14},{14,12},{16,18},{18,... | collective-permute-start | bytes 393224 | tf_op jit(solution)/shard_map/ppermute | solution.py:602
  71.5 8.7 %collective-permute-start.23 = (bf16[128,512]{1,0:T(8,128)(2,1)S(1)}, bf16[128,512]{1,0:T(8,128)(2,1)S(1)}, u32[]{:S(2)}, u32[]{:S(2)}) collective-permute-start(bf16[128,512]{1,0:T(8,128)(2,1)S(1)} %get-tuple-element.62), channel_id=1, source_target_pairs={{0,6},{2,4},{4,2},{6,0},{8,14},{10,12},{12,10},{14,8},{16,22},{18,... | collective-permute-start | bytes 393224 | tf_op jit(solution)/shard_map/ppermute | solution.py:602
  73.4 8.2 %collective-permute-start.22 = (bf16[128,512]{1,0:T(8,128)(2,1)S(1)}, bf16[128,512]{1,0:T(8,128)(2,1)S(1)}, u32[]{:S(2)}, u32[]{:S(2)}) collective-permute-start(bf16[128,512]{1,0:T(8,128)(2,1)S(1)} %get-tuple-element.61), channel_id=1, source_target_pairs={{0,4},{2,6},{4,0},{6,2},{8,12},{10,14},{12,8},{14,10},{16,20},{18,... | collective-permute-start | bytes 393224 | tf_op jit(solution)/shard_map/ppermute | solution.py:602
  (1 other events, 14.5 us)

commit v8 on v7

--- a/solution.py
+++ b/solution.py
@@ -315,8 +315,9 @@
             source, first = index // per_source, (index % per_source) * chunk
             turned = woven_key(key_in[source], tokens, first, chunk, lanes_of(head, width)).T
             step_ref[head, slot_of(group, index, per_source)] = dot(
-                turned, high_ref[head, index]
-            ) + dot(turned, low_ref[head, index])
+                jnp.concatenate([turned, turned], axis=1),
+                jnp.concatenate([high_ref[head, index], low_ref[head, index]], axis=0),
+            )
 
     every_unit(heads, chunks, solve)
     totals = [[step_ref[head, slot] for slot in range(chunks)] for head in range(heads)]
@@ -338,7 +339,10 @@
 
 def dot3(left, high, low):
     left_high, left_low = split(left)
-    return dot(left_high, high) + dot(left_low, high) + dot(left_high, low)
+    return dot(
+        jnp.concatenate([left_high, left_low, left_high], axis=1),
+        jnp.concatenate([high, high, low], axis=0),
+    )
 
 
 def carry_state(keys, rests, inverses, tables):
@@ -482,9 +486,10 @@
 
 def weight_rows(weights, offset, inner, first, count):
     rows = pl.ds(first, count)
-    if offset == 2:
-        return jnp.where(inner, weights[3][rows, :], weights[4][rows, :])
-    return weights[{0: 0, 1: 1, 3: 2}[offset]][rows, :]
+    if offset < 2:
+        return weights[offset][rows, :]
+    near, far = (4, 5) if offset == 2 else (2, 3)
+    return jnp.where(inner, weights[near][rows, :], weights[far][rows, :])
 
 
 def where_am_i(group):
@@ -501,20 +506,25 @@
     columns = weight_in[0].shape[1]
     side = keep_ref.shape[1] // columns
     inner = (plane == 1) | (plane == 2)
+    left = jnp.concatenate(
+        [
+            jnp.concatenate(
+                [heads_in[member][at * tokens : (at + 1) * tokens, :] for at in orders[member]],
+                axis=0,
+            )
+            for member in range(group)
+        ],
+        axis=1,
+    )
+    firsts = [
+        pl.multiple_of(place(position, member) * wide, wide) for member in range(group)
+    ]
     for offset in offsets:
         owner = jnp.bitwise_xor(plane, offset)
-        total = None
-        for member in range(group):
-            first = pl.multiple_of(place(position, member) * wide, wide)
-            blocks = [
-                heads_in[member][at * tokens : (at + 1) * tokens, :] for at in orders[member]
-            ]
-            part = dot(
-                jnp.concatenate(blocks, axis=0),
-                weight_rows(weight_in, offset, inner, first, wide),
-            )
-            total = part if total is None else total + part
-        result = total.astype(BF16)
+        right = jnp.concatenate(
+            [weight_rows(weight_in, offset, inner, first, wide) for first in firsts], axis=0
+        )
+        result = dot(left, right).astype(BF16)
         lanes = pl.ds(pl.multiple_of(lax.rem(owner, side) * columns, columns), columns)
 
         @pl.when(owner // side == core)
@@ -633,9 +643,11 @@
     split_out = sides == 2 and planes in (2, 4) and group > 1
     weights = [out_weight]
     if split_out:
-        for offset in range(1, planes, 2):
-            swapped = [(plane, plane ^ offset) for plane in range(planes)]
-            weights.append(between_planes(out_weight, swapped))
+        swapped = [(plane, plane ^ 1) for plane in range(planes)]
+        weights.append(between_planes(out_weight, swapped))
+    if split_out and planes == 4:
+        for pairs in (((1, 2), (2, 1)), ((0, 3), (3, 0))):
+            weights.append(between_planes(out_weight, pairs))
 
     near = max(group // 2, 1)
     solved = []

time: 82.7 us -> 81.6 us (0.987)
  the two profiles are of different devices: /device:TPU:0 before, /device:TPU:16 now
where the time goes in v8:
time: 81.6 us; the launch traced here: 81.3 us
  starting transfers between devices  43.9 us (54%)
  waiting for transfers between devices  19.6 us (24%)
  Pallas kernels  17.6 us (22%)
    ppermute x15, starting transfers between devices, swap(): return lax.ppermute(value, 'seq', pairs)  22.6 us
    ppermute x15, waiting for transfers between devices, swap(): return lax.ppermute(value, 'seq', pairs)  19.5 us
    ppermute x5, starting transfers between devices, between_planes(): lax.ppermute(value, 'seq', [(source * group + i, target * group + i) for...  14.9 us
    pallas_call x2, Pallas kernels, invert(): pl.pallas_call(functools.partial(invert_kernel, heads, tokens), out_shape...  6.6 us
    ppermute x3, starting transfers between devices, from_earlier(): return lax.ppermute(value, 'seq', pairs)  6.28 us
    pallas_call x2, Pallas kernels, project(): pl.pallas_call(functools.partial(project_kernel, group, orders, offsets),...  3.44 us
    pallas_call x1, Pallas kernels, carry_state(): pl.pallas_call(functools.partial(state_kernel, group, parts), out_shape=(...  2.63 us
    pallas_call x1, Pallas kernels, read(): pl.pallas_call(functools.partial(read_kernel, group), out_shape=(pltpu.VM...  1.66 us
  transfers between devices with their start and end apart: 25, of which 10 were waited for; matrix products, arithmetic and copies ran while one was open for 0% of the time, Pallas kernels for 21%

profile of v8, /device:TPU:16, one launch (start us, length us, event | category | flops | bytes accessed | tf_op | source)
XLA Modules:
  0.0 81.3 jit_solution(12976789331709307794)
XLA Ops:
  0.0 1.6 %collective-permute-start.12 = (bf16[1024,256]{1,0:T(8,128)(2,1)}, bf16[1024,256]{1,0:T(8,128)(2,1)S(1)}, u32[]{:S(2)}, u32[]{:S(2)}) collective-permute-start(bf16[1024,256]{1,0:T(8,128)(2,1)} %refs_4_.3), channel_id=1, source_target_pairs={{0,8},{2,10},{4,12},{6,14},{8,0},{10,2},{12,4},{14,6},{16,24},{18,... | collective-permute-start | bytes 1572872 | tf_op jit(solution)/shard_map/ppermute | solution.py:633
  1.6 1.9 %collective-permute-start.13 = (bf16[1024,256]{1,0:T(8,128)(2,1)}, bf16[1024,256]{1,0:T(8,128)(2,1)S(1)}, u32[]{:S(2)}, u32[]{:S(2)}) collective-permute-start(bf16[1024,256]{1,0:T(8,128)(2,1)} %refs_4_.3), channel_id=1, source_target_pairs={{8,16},{10,18},{12,20},{14,22},{16,8},{18,10},{20,12},{22,14},{9,1... | collective-permute-start | bytes 1572872 | tf_op jit(solution)/shard_map/ppermute | solution.py:633
  3.5 1.5 %pack.1 = (bf16[272,256]{1,0:T(8,128)(2,1)S(1)}, bf16[272,256]{1,0:T(8,128)(2,1)S(1)}, bf16[272,256]{1,0:T(8,128)(2,1)S(1)}, bf16[272,256]{1,0:T(8,128)(2,1)S(1)...) custom-call(bf16[2,128,1024]{2,1,0:T(8,128)(2,1)} %key_ref.1, ...), custom_call_target="tpu_custom_call" | custom-call | tf_op jit(solution)/shard_map/pack/pallas_call | solution.py:139
  5.0 1.6 %collective-permute-start.1 = (bf16[272,256]{1,0:T(8,128)(2,1)S(1)}, bf16[272,256]{1,0:T(8,128)(2,1)S(1)}, u32[]{:S(2)}, u32[]{:S(2)}) collective-permute-start(bf16[272,256]{1,0:T(8,128)(2,1)S(1)} %get-tuple-element.36), channel_id=1, source_target_pairs={{0,4},{2,6},{4,0},{6,2},{8,12},{10,14},{12,8},{14,10},{16,20},{18,... | collective-permute-start | bytes 417800 | tf_op jit(solution)/shard_map/ppermute | solution.py:612
  8.6 3.8 %collective-permute-done.1.refs_0_.refs_2_ = bf16[272,256]{1,0:T(8,128)(2,1)S(1)} collective-permute-done((bf16[272,256]{1,0:T(8,128)(2,1)S(1)}, bf16[272,256]{1,0:T(8,128)(2,1)S(1)}, u32[]{:S(2)}, u32[]{:S(2)}) %collective-permute-start.1) | collective-permute-done | bytes 139296 | tf_op jit(solution)/shard_map/ppermute | solution.py:612
  13.9 2.3 %collective-permute-start.4 = (bf16[3,128,256]{2,1,0:T(8,128)(2,1)S(1)}, bf16[3,128,256]{2,1,0:T(8,128)(2,1)S(1)}, u32[]{:S(2)}, u32[]{:S(2)}) collective-permute-start(bf16[3,128,256]{2,1,0:T(8,128)(2,1)S(1)} %get-tuple-element.40), channel_id=1, source_target_pairs={{0,4},{2,6},{4,0},{6,2},{8,12},{10,14},{12,8},{14,10},{16,20},{18,... | collective-permute-start | bytes 589832 | tf_op jit(solution)/shard_map/ppermute | solution.py:612
  17.7 2.6 %collective-permute-done.3.refs_5_ = bf16[3,128,256]{2,1,0:T(8,128)(2,1)S(1)} collective-permute-done((bf16[3,128,256]{2,1,0:T(8,128)(2,1)S(1)}, bf16[3,128,256]{2,1,0:T(8,128)(2,1)S(1)}, u32[]{:S(2)}, u32[]{:S(2)}) %collective-permute-start.3) | collective-permute-done | bytes 196640 | tf_op jit(solution)/shard_map/ppermute | solution.py:612
  21.0 3.3 %invert.3 = (f32[2,2,3,128,128]{4,3,2,1,0:T(8,128)S(1)}, f32[2,2,8,256]{3,2,1,0:T(8,128)S(1)}) custom-call(bf16[272,256]{1,0:T(8,128)(2,1)S(1)} %collective-permute-done.1.refs_0_.refs_2_, bf16[272,256]{1,0:T(8,128)(2,1)S(1)} %collective-permute-done.2.refs_1_.refs_3_), custom_call_target="tpu_custom_call" | custom-call | tf_op jit(solution)/shard_map/invert/pallas_call | solution.py:238
  24.3 3.3 %invert.2 = (f32[2,2,3,128,128]{4,3,2,1,0:T(8,128)S(1)}, f32[2,2,8,256]{3,2,1,0:T(8,128)S(1)}) custom-call(bf16[272,256]{1,0:T(8,128)(2,1)S(1)} %get-tuple-element.34.refs_0_, bf16[272,256]{1,0:T(8,128)(2,1)S(1)} %collective-permute-done.refs_1_), custom_call_target="tpu_custom_call" | custom-call | tf_op jit(solution)/shard_map/invert/pallas_call | solution.py:238
  27.6 2.6 %carry_state.1 = (bf16[2,4,256,256]{3,2,1,0:T(8,128)(2,1)S(1)}, bf16[2,4,256,256]{3,2,1,0:T(8,128)(2,1)S(1)}, f32[2,4,128,256]{3,2,1,0:T(8,128)S(1)}, bf16[2,128...) custom-call(bf16[272,256]{1,0:T(8,128)(2,1)S(1)} %get-tuple-element.34.refs_0_, ...), custom_call_target="tpu_custom_call" | custom-call | tf_op jit(solution)/shard_map/carry_state/pallas_call | solution.py:354
  31.0 4.3 %collective-permute-start.6 = (bf16[2,128,256]{2,1,0:T(8,128)(2,1)S(1)}, bf16[2,128,256]{2,1,0:T(8,128)(2,1)S(1)}, u32[]{:S(2)}, u32[]{:S(2)}) collective-permute-start(bf16[2,128,256]{2,1,0:T(8,128)(2,1)S(1)} %get-tuple-element.46), channel_id=1, source_target_pairs={{0,8},{2,10},{4,12},{6,14},{8,16},{10,18},{12,20},{14,22},{16,24},... | collective-permute-start | bytes 393224 | tf_op jit(solution)/shard_map/ppermute | solution.py:663
  36.6 9.4 %collective-permute-start.15 = (bf16[1024,256]{1,0:T(8,128)(2,1)S(1)}, bf16[1024,256]{1,0:T(8,128)(2,1)S(1)}, u32[]{:S(2)}, u32[]{:S(2)}) collective-permute-start(bf16[1024,256]{1,0:T(8,128)(2,1)S(1)} %collective-permute-done.12.refs_5_), channel_id=1, source_target_pairs={{8,16},{10,18},{12,20},{14,22},{16,8},{18,10},{20,12},{22,14},{9,1... | collective-permute-start | bytes 1572872 | tf_op jit(solution)/shard_map/ppermute | solution.py:633
  47.3 1.7 %read.1 = (f32[512,256]{1,0:T(8,128)S(1)}, bf16[512,256]{1,0:T(8,128)(2,1)S(1)}) custom-call(bf16[272,256]{1,0:T(8,128)(2,1)S(1)} %get-tuple-element.34.refs_0_, bf16[272,256]{1,0:T(8,128)(2,1)S(1)} %collective-permute-done.refs_1_, bf16[272,256]{1,0:T(8,128)(2,1)S(1)} %collective-permute-done.1.refs_0_.refs_2_, ...), custom_call_target="tpu_custom_call" | custom-call | tf_op jit(solution)/shard_map/read/pallas_call | solution.py:424
  49.8 1.6 %collective-permute-start.18 = (bf16[256,256]{1,0:T(8,128)(2,1)S(1)}, bf16[256,256]{1,0:T(8,128)(2,1)S(1)}, u32[]{:S(2)}, u32[]{:S(2)}) collective-permute-start(bf16[256,256]{1,0:T(8,128)(2,1)S(1)} %get-tuple-element.53.refs_0_), channel_id=1, source_target_pairs={{0,2},{2,0},{4,6},{6,4},{8,10},{10,8},{12,14},{14,12},{16,18},{18,... | collective-permute-start | bytes 393224 | tf_op jit(solution)/shard_map/ppermute | solution.py:612
  52.8 2.1 %collective-permute-done.18.refs_1_ = bf16[256,256]{1,0:T(8,128)(2,1)S(1)} collective-permute-done((bf16[256,256]{1,0:T(8,128)(2,1)S(1)}, bf16[256,256]{1,0:T(8,128)(2,1)S(1)}, u32[]{:S(2)}, u32[]{:S(2)}) %collective-permute-start.18) | collective-permute-done | bytes 131104 | tf_op jit(solution)/shard_map/ppermute | solution.py:612
  54.8 2.3 %collective-permute-start.20 = (bf16[256,256]{1,0:T(8,128)(2,1)S(1)}, bf16[256,256]{1,0:T(8,128)(2,1)S(1)}, u32[]{:S(2)}, u32[]{:S(2)}) collective-permute-start(bf16[256,256]{1,0:T(8,128)(2,1)S(1)} %get-tuple-element.53.refs_0_), channel_id=1, source_target_pairs={{0,6},{2,4},{4,2},{6,0},{8,14},{10,12},{12,10},{14,8},{16,22},{18,... | collective-permute-start | bytes 393224 | tf_op jit(solution)/shard_map/ppermute | solution.py:612
  57.2 2.0 %collective-permute-start.10 = (bf16[256,256]{1,0:T(8,128)(2,1)S(1)}, bf16[256,256]{1,0:T(8,128)(2,1)S(1)}, u32[]{:S(2)}, u32[]{:S(2)}) collective-permute-start(bf16[256,256]{1,0:T(8,128)(2,1)S(1)} %get-tuple-element.53.refs_0_), channel_id=1, source_target_pairs={{0,4},{2,6},{4,0},{6,2},{8,12},{10,14},{12,8},{14,10},{16,20},{18,... | collective-permute-start | bytes 393224 | tf_op jit(solution)/shard_map/ppermute | solution.py:612
  59.1 1.6 %collective-permute-done.20.refs_3_ = bf16[256,256]{1,0:T(8,128)(2,1)S(1)} collective-permute-done((bf16[256,256]{1,0:T(8,128)(2,1)S(1)}, bf16[256,256]{1,0:T(8,128)(2,1)S(1)}, u32[]{:S(2)}, u32[]{:S(2)}) %collective-permute-start.20) | collective-permute-done | bytes 131104 | tf_op jit(solution)/shard_map/ppermute | solution.py:612
  60.7 2.4 %collective-permute-start.11 = (bf16[256,256]{1,0:T(8,128)(2,1)S(1)}, bf16[256,256]{1,0:T(8,128)(2,1)S(1)}, u32[]{:S(2)}, u32[]{:S(2)}) collective-permute-start(bf16[256,256]{1,0:T(8,128)(2,1)S(1)} %get-tuple-element.54.refs_0_), channel_id=1, source_target_pairs={{0,6},{2,4},{4,2},{6,0},{8,14},{10,12},{12,10},{14,8},{16,22},{18,... | collective-permute-start | bytes 393224 | tf_op jit(solution)/shard_map/ppermute | solution.py:612
  63.6 1.7 %project.3 = (bf16[256,512]{1,0:T(8,128)(2,1)S(1)}, bf16[256,512]{1,0:T(8,128)(2,1)S(1)}) custom-call(bf16[256,256]{1,0:T(8,128)(2,1)S(1)} %get-tuple-element.54.refs_0_, bf16[256,256]{1,0:T(8,128)(2,1)S(1)} %collective-permute-done.18.refs_1_, bf16[256,256]{1,0:T(8,128)(2,1)S(1)} %collective-permute-done.19.refs_2_, ...), custom_call_target="tpu_custom_call" | custom-call | tf_op jit(solution)/shard_map/project/pallas_call | solution.py:545
  66.6 1.5 %collective-permute-done.9.refs_1_ = bf16[256,256]{1,0:T(8,128)(2,1)S(1)} collective-permute-done((bf16[256,256]{1,0:T(8,128)(2,1)S(1)}, bf16[256,256]{1,0:T(8,128)(2,1)S(1)}, u32[]{:S(2)}, u32[]{:S(2)}) %collective-permute-start.9) | collective-permute-done | bytes 131104 | tf_op jit(solution)/shard_map/ppermute | solution.py:612
  68.1 1.7 %project.2 = (bf16[256,512]{1,0:T(8,128)(2,1)S(1)}, bf16[256,512]{1,0:T(8,128)(2,1)S(1)}) custom-call(bf16[256,256]{1,0:T(8,128)(2,1)S(1)} %get-tuple-element.53.refs_0_, bf16[256,256]{1,0:T(8,128)(2,1)S(1)} %collective-permute-done.9.refs_1_, bf16[256,256]{1,0:T(8,128)(2,1)S(1)} %collective-permute-done.10.refs_2_, ...), custom_call_target="tpu_custom_call" | custom-call | tf_op jit(solution)/shard_map/project/pallas_call | solution.py:545
  73.7 2.7 %collective-permute-done.22.refs_1_ = bf16[128,512]{1,0:T(8,128)(2,1)S(1)} collective-permute-done((bf16[128,512]{1,0:T(8,128)(2,1)S(1)}, bf16[128,512]{1,0:T(8,128)(2,1)S(1)}, u32[]{:S(2)}, u32[]{:S(2)}) %collective-permute-start.22) | collective-permute-done | bytes 131104 | tf_op jit(solution)/shard_map/ppermute | solution.py:612
  76.4 2.5 %collective-permute-done.24.refs_3_ = bf16[128,512]{1,0:T(8,128)(2,1)S(1)} collective-permute-done((bf16[128,512]{1,0:T(8,128)(2,1)S(1)}, bf16[128,512]{1,0:T(8,128)(2,1)S(1)}, u32[]{:S(2)}, u32[]{:S(2)}) %collective-permute-start.24) | collective-permute-done | bytes 131104 | tf_op jit(solution)/shard_map/ppermute | solution.py:612
  (39 shorter events, 19.0 us)
Async XLA Ops:
  0.0 36.6 %collective-permute-start.12 = (bf16[1024,256]{1,0:T(8,128)(2,1)}, bf16[1024,256]{1,0:T(8,128)(2,1)S(1)}, u32[]{:S(2)}, u32[]{:S(2)}) collective-permute-start(bf16[1024,256]{1,0:T(8,128)(2,1)} %refs_4_.3), channel_id=1, source_target_pairs={{0,8},{2,10},{4,12},{6,14},{8,0},{10,2},{12,4},{14,6},{16,24},{18,... | collective-permute-start | bytes 1572872 | tf_op jit(solution)/shard_map/ppermute | solution.py:633
  1.6 44.4 %collective-permute-start.13 = (bf16[1024,256]{1,0:T(8,128)(2,1)}, bf16[1024,256]{1,0:T(8,128)(2,1)S(1)}, u32[]{:S(2)}, u32[]{:S(2)}) collective-permute-start(bf16[1024,256]{1,0:T(8,128)(2,1)} %refs_4_.3), channel_id=1, source_target_pairs={{8,16},{10,18},{12,20},{14,22},{16,8},{18,10},{20,12},{22,14},{9,1... | collective-permute-start | bytes 1572872 | tf_op jit(solution)/shard_map/ppermute | solution.py:633
  5.0 7.3 %collective-permute-start.1 = (bf16[272,256]{1,0:T(8,128)(2,1)S(1)}, bf16[272,256]{1,0:T(8,128)(2,1)S(1)}, u32[]{:S(2)}, u32[]{:S(2)}) collective-permute-start(bf16[272,256]{1,0:T(8,128)(2,1)S(1)} %get-tuple-element.36), channel_id=1, source_target_pairs={{0,4},{2,6},{4,0},{6,2},{8,12},{10,14},{12,8},{14,10},{16,20},{18,... | collective-permute-start | bytes 417800 | tf_op jit(solution)/shard_map/ppermute | solution.py:612
  6.6 7.3 %collective-permute-start.2 = (bf16[272,256]{1,0:T(8,128)(2,1)S(1)}, bf16[272,256]{1,0:T(8,128)(2,1)S(1)}, u32[]{:S(2)}, u32[]{:S(2)}) collective-permute-start(bf16[272,256]{1,0:T(8,128)(2,1)S(1)} %get-tuple-element.37), channel_id=1, source_target_pairs={{0,6},{2,4},{4,2},{6,0},{8,14},{10,12},{12,10},{14,8},{16,22},{18,... | collective-permute-start | bytes 417800 | tf_op jit(solution)/shard_map/ppermute | solution.py:612
  8.1 8.2 %collective-permute-start = (bf16[272,256]{1,0:T(8,128)(2,1)S(1)}, bf16[272,256]{1,0:T(8,128)(2,1)S(1)}, u32[]{:S(2)}, u32[]{:S(2)}) collective-permute-start(bf16[272,256]{1,0:T(8,128)(2,1)S(1)} %get-tuple-element.35), channel_id=1, source_target_pairs={{0,2},{2,0},{4,6},{6,4},{8,10},{10,8},{12,14},{14,12},{16,18},{18,... | collective-permute-start | bytes 417800 | tf_op jit(solution)/shard_map/ppermute | solution.py:612
  12.4 7.9 %collective-permute-start.3 = (bf16[3,128,256]{2,1,0:T(8,128)(2,1)S(1)}, bf16[3,128,256]{2,1,0:T(8,128)(2,1)S(1)}, u32[]{:S(2)}, u32[]{:S(2)}) collective-permute-start(bf16[3,128,256]{2,1,0:T(8,128)(2,1)S(1)} %get-tuple-element.39), channel_id=1, source_target_pairs={{0,2},{2,0},{4,6},{6,4},{8,10},{10,8},{12,14},{14,12},{16,18},{18,... | collective-permute-start | bytes 589832 | tf_op jit(solution)/shard_map/ppermute | solution.py:612
  13.9 13.7 %collective-permute-start.4 = (bf16[3,128,256]{2,1,0:T(8,128)(2,1)S(1)}, bf16[3,128,256]{2,1,0:T(8,128)(2,1)S(1)}, u32[]{:S(2)}, u32[]{:S(2)}) collective-permute-start(bf16[3,128,256]{2,1,0:T(8,128)(2,1)S(1)} %get-tuple-element.40), channel_id=1, source_target_pairs={{0,4},{2,6},{4,0},{6,2},{8,12},{10,14},{12,8},{14,10},{16,20},{18,... | collective-permute-start | bytes 589832 | tf_op jit(solution)/shard_map/ppermute | solution.py:612
  16.2 11.4 %collective-permute-start.5 = (bf16[3,128,256]{2,1,0:T(8,128)(2,1)S(1)}, bf16[3,128,256]{2,1,0:T(8,128)(2,1)S(1)}, u32[]{:S(2)}, u32[]{:S(2)}) collective-permute-start(bf16[3,128,256]{2,1,0:T(8,128)(2,1)S(1)} %get-tuple-element.41), channel_id=1, source_target_pairs={{0,6},{2,4},{4,2},{6,0},{8,14},{10,12},{12,10},{14,8},{16,22},{18,... | collective-permute-start | bytes 589832 | tf_op jit(solution)/shard_map/ppermute | solution.py:612
  20.3 42.8 %collective-permute-start.14 = (bf16[1024,256]{1,0:T(8,128)(2,1)S(1)}, bf16[1024,256]{1,0:T(8,128)(2,1)S(1)}, u32[]{:S(2)}, u32[]{:S(2)}) collective-permute-start(bf16[1024,256]{1,0:T(8,128)(2,1)S(1)} %copy-done), channel_id=1, source_target_pairs={{0,24},{2,26},{4,28},{6,30},{24,0},{26,2},{28,4},{30,6},{1,25},{3,... | collective-permute-start | bytes 1572872 | tf_op jit(solution)/shard_map/ppermute | solution.py:633
  30.3 5.0 %collective-permute-start.8 = (bf16[2,128,128]{2,1,0:T(8,128)(2,1)S(1)}, bf16[2,128,128]{2,1,0:T(8,128)(2,1)S(1)}, u32[]{:S(2)}, u32[]{:S(2)}) collective-permute-start(bf16[2,128,128]{2,1,0:T(8,128)(2,1)S(1)} %get-tuple-element.47), channel_id=1, source_target_pairs={{0,24},{2,26},{4,28},{6,30},{1,25},{3,27},{5,29},{7,31}} | collective-permute-start | bytes 196616 | tf_op jit(solution)/shard_map/ppermute | solution.py:663
  31.0 18.1 %collective-permute-start.6 = (bf16[2,128,256]{2,1,0:T(8,128)(2,1)S(1)}, bf16[2,128,256]{2,1,0:T(8,128)(2,1)S(1)}, u32[]{:S(2)}, u32[]{:S(2)}) collective-permute-start(bf16[2,128,256]{2,1,0:T(8,128)(2,1)S(1)} %get-tuple-element.46), channel_id=1, source_target_pairs={{0,8},{2,10},{4,12},{6,14},{8,16},{10,18},{12,20},{14,22},{16,24},... | collective-permute-start | bytes 393224 | tf_op jit(solution)/shard_map/ppermute | solution.py:663
  35.3 13.7 %collective-permute-start.7 = (bf16[2,128,256]{2,1,0:T(8,128)(2,1)S(1)}, bf16[2,128,256]{2,1,0:T(8,128)(2,1)S(1)}, u32[]{:S(2)}, u32[]{:S(2)}) collective-permute-start(bf16[2,128,256]{2,1,0:T(8,128)(2,1)S(1)} %get-tuple-element.46), channel_id=1, source_target_pairs={{0,16},{2,18},{4,20},{6,22},{8,24},{10,26},{12,28},{14,30},{1,17},... | collective-permute-start | bytes 393224 | tf_op jit(solution)/shard_map/ppermute | solution.py:663
  36.6 27.0 %collective-permute-start.15 = (bf16[1024,256]{1,0:T(8,128)(2,1)S(1)}, bf16[1024,256]{1,0:T(8,128)(2,1)S(1)}, u32[]{:S(2)}, u32[]{:S(2)}) collective-permute-start(bf16[1024,256]{1,0:T(8,128)(2,1)S(1)} %collective-permute-done.12.refs_5_), channel_id=1, source_target_pairs={{8,16},{10,18},{12,20},{14,22},{16,8},{18,10},{20,12},{22,14},{9,1... | collective-permute-start | bytes 1572872 | tf_op jit(solution)/shard_map/ppermute | solution.py:633
  46.0 17.6 %collective-permute-start.16 = (bf16[1024,256]{1,0:T(8,128)(2,1)S(1)}, bf16[1024,256]{1,0:T(8,128)(2,1)S(1)}, u32[]{:S(2)}, u32[]{:S(2)}) collective-permute-start(bf16[1024,256]{1,0:T(8,128)(2,1)S(1)} %collective-permute-done.13.refs_6_), channel_id=1, source_target_pairs={{8,0},{10,2},{12,4},{14,6},{16,24},{18,26},{20,28},{22,30},{9,1},{... | collective-permute-start | bytes 1572872 | tf_op jit(solution)/shard_map/ppermute | solution.py:633
  49.8 5.0 %collective-permute-start.18 = (bf16[256,256]{1,0:T(8,128)(2,1)S(1)}, bf16[256,256]{1,0:T(8,128)(2,1)S(1)}, u32[]{:S(2)}, u32[]{:S(2)}) collective-permute-start(bf16[256,256]{1,0:T(8,128)(2,1)S(1)} %get-tuple-element.53.refs_0_), channel_id=1, source_target_pairs={{0,2},{2,0},{4,6},{6,4},{8,10},{10,8},{12,14},{14,12},{16,18},{18,... | collective-permute-start | bytes 393224 | tf_op jit(solution)/shard_map/ppermute | solution.py:612
  51.4 5.8 %collective-permute-start.19 = (bf16[256,256]{1,0:T(8,128)(2,1)S(1)}, bf16[256,256]{1,0:T(8,128)(2,1)S(1)}, u32[]{:S(2)}, u32[]{:S(2)}) collective-permute-start(bf16[256,256]{1,0:T(8,128)(2,1)S(1)} %get-tuple-element.54.refs_0_), channel_id=1, source_target_pairs={{0,4},{2,6},{4,0},{6,2},{8,12},{10,14},{12,8},{14,10},{16,20},{18,... | collective-permute-start | bytes 393224 | tf_op jit(solution)/shard_map/ppermute | solution.py:612
  54.8 5.9 %collective-permute-start.20 = (bf16[256,256]{1,0:T(8,128)(2,1)S(1)}, bf16[256,256]{1,0:T(8,128)(2,1)S(1)}, u32[]{:S(2)}, u32[]{:S(2)}) collective-permute-start(bf16[256,256]{1,0:T(8,128)(2,1)S(1)} %get-tuple-element.53.refs_0_), channel_id=1, source_target_pairs={{0,6},{2,4},{4,2},{6,0},{8,14},{10,12},{12,10},{14,8},{16,22},{18,... | collective-permute-start | bytes 393224 | tf_op jit(solution)/shard_map/ppermute | solution.py:612
  57.2 8.2 %collective-permute-start.10 = (bf16[256,256]{1,0:T(8,128)(2,1)S(1)}, bf16[256,256]{1,0:T(8,128)(2,1)S(1)}, u32[]{:S(2)}, u32[]{:S(2)}) collective-permute-start(bf16[256,256]{1,0:T(8,128)(2,1)S(1)} %get-tuple-element.53.refs_0_), channel_id=1, source_target_pairs={{0,4},{2,6},{4,0},{6,2},{8,12},{10,14},{12,8},{14,10},{16,20},{18,... | collective-permute-start | bytes 393224 | tf_op jit(solution)/shard_map/ppermute | solution.py:612
  60.7 5.9 %collective-permute-start.11 = (bf16[256,256]{1,0:T(8,128)(2,1)S(1)}, bf16[256,256]{1,0:T(8,128)(2,1)S(1)}, u32[]{:S(2)}, u32[]{:S(2)}) collective-permute-start(bf16[256,256]{1,0:T(8,128)(2,1)S(1)} %get-tuple-element.54.refs_0_), channel_id=1, source_target_pairs={{0,6},{2,4},{4,2},{6,0},{8,14},{10,12},{12,10},{14,8},{16,22},{18,... | collective-permute-start | bytes 393224 | tf_op jit(solution)/shard_map/ppermute | solution.py:612
  63.1 5.0 %collective-permute-start.9 = (bf16[256,256]{1,0:T(8,128)(2,1)S(1)}, bf16[256,256]{1,0:T(8,128)(2,1)S(1)}, u32[]{:S(2)}, u32[]{:S(2)}) collective-permute-start(bf16[256,256]{1,0:T(8,128)(2,1)S(1)} %get-tuple-element.54.refs_0_), channel_id=1, source_target_pairs={{0,2},{2,0},{4,6},{6,4},{8,10},{10,8},{12,14},{14,12},{16,18},{18,... | collective-permute-start | bytes 393224 | tf_op jit(solution)/shard_map/ppermute | solution.py:612
  65.3 4.6 %collective-permute-start.21 = (bf16[256,512]{1,0:T(8,128)(2,1)S(1)}, bf16[256,512]{1,0:T(8,128)(2,1)S(1)}, u32[]{:S(2)}, u32[]{:S(2)}) collective-permute-start(bf16[256,512]{1,0:T(8,128)(2,1)S(1)} %get-tuple-element.59), channel_id=1, source_target_pairs={{0,1},{1,0},{2,3},{3,2},{4,5},{5,4},{6,7},{7,6},{8,9},{9,8},{10,11... | collective-permute-start | bytes 786440 | tf_op jit(solution)/shard_map/ppermute | solution.py:704
  70.0 6.4 %collective-permute-start.22 = (bf16[128,512]{1,0:T(8,128)(2,1)S(1)}, bf16[128,512]{1,0:T(8,128)(2,1)S(1)}, u32[]{:S(2)}, u32[]{:S(2)}) collective-permute-start(bf16[128,512]{1,0:T(8,128)(2,1)S(1)} %get-tuple-element.60), channel_id=1, source_target_pairs={{0,2},{2,0},{4,6},{6,4},{8,10},{10,8},{12,14},{14,12},{16,18},{18,... | collective-permute-start | bytes 393224 | tf_op jit(solution)/shard_map/ppermute | solution.py:612
  71.5 7.5 %collective-permute-start.24 = (bf16[128,512]{1,0:T(8,128)(2,1)S(1)}, bf16[128,512]{1,0:T(8,128)(2,1)S(1)}, u32[]{:S(2)}, u32[]{:S(2)}) collective-permute-start(bf16[128,512]{1,0:T(8,128)(2,1)S(1)} %get-tuple-element.62), channel_id=1, source_target_pairs={{0,6},{2,4},{4,2},{6,0},{8,14},{10,12},{12,10},{14,8},{16,22},{18,... | collective-permute-start | bytes 393224 | tf_op jit(solution)/shard_map/ppermute | solution.py:612
  72.2 8.2 %collective-permute-start.23 = (bf16[128,512]{1,0:T(8,128)(2,1)S(1)}, bf16[128,512]{1,0:T(8,128)(2,1)S(1)}, u32[]{:S(2)}, u32[]{:S(2)}) collective-permute-start(bf16[128,512]{1,0:T(8,128)(2,1)S(1)} %get-tuple-element.61), channel_id=1, source_target_pairs={{0,4},{2,6},{4,0},{6,2},{8,12},{10,14},{12,8},{14,10},{16,20},{18,... | collective-permute-start | bytes 393224 | tf_op jit(solution)/shard_map/ppermute | solution.py:612
  (2 other events, 22.6 us)

commit v9 on v7

--- a/solution.py
+++ b/solution.py
@@ -480,63 +480,60 @@
     return (earlier.astype(F32) + later.astype(F32) - moved).astype(BF16)
 
 
-def weight_rows(weights, offset, inner, first, count):
-    rows = pl.ds(first, count)
-    if offset == 2:
-        return jnp.where(inner, weights[3][rows, :], weights[4][rows, :])
-    return weights[{0: 0, 1: 1, 3: 2}[offset]][rows, :]
-
-
 def where_am_i(group):
     device = lax.axis_index("seq")
     return lax.rem(device, group), device // group
 
 
-def project_kernel(group, orders, offsets, *refs):
-    heads_in, weight_in, (send_ref, keep_ref) = refs[:group], refs[group:-2], refs[-2:]
+def project_kernel(group, orders, *refs):
+    heads_in, weight_in, (send_ref, keep_ref, left_buf) = refs[:group], refs[group:-3], refs[-3:]
     core = lax.axis_index("head")
     position, plane = where_am_i(group)
     rows, wide = heads_in[0].shape
     tokens = rows // len(orders[0])
     columns = weight_in[0].shape[1]
     side = keep_ref.shape[1] // columns
-    inner = (plane == 1) | (plane == 2)
-    for offset in offsets:
+    for member in range(group):
+        lanes = pl.ds(pl.multiple_of(place(position, member) * wide, wide), wide)
+        for to, at in enumerate(orders[member]):
+            left_buf[to * tokens : (to + 1) * tokens, lanes] = heads_in[member][
+                at * tokens : (at + 1) * tokens, :
+            ]
+    offsets = (0, 1, 3, 2) if len(weight_in) > 2 else (0, 1)
+    for number, offset in enumerate(offsets):
+        if offset == 2:
+            inner = (plane == 1) | (plane == 2)
+            right = jnp.where(inner, weight_in[3][...], weight_in[4][...])
+        else:
+            right = weight_in[number][...]
+        result = dot(left_buf[...], right).astype(BF16)
         owner = jnp.bitwise_xor(plane, offset)
-        total = None
-        for member in range(group):
-            first = pl.multiple_of(place(position, member) * wide, wide)
-            blocks = [
-                heads_in[member][at * tokens : (at + 1) * tokens, :] for at in orders[member]
-            ]
-            part = dot(
-                jnp.concatenate(blocks, axis=0),
-                weight_rows(weight_in, offset, inner, first, wide),
-            )
-            total = part if total is None else total + part
-        result = total.astype(BF16)
-        lanes = pl.ds(pl.multiple_of(lax.rem(owner, side) * columns, columns), columns)
-
-        @pl.when(owner // side == core)
-        def _():
-            keep_ref[:, lanes] = result
-
-        @pl.when(owner // side != core)
-        def _():
-            send_ref[:, lanes] = result
+        even = lax.rem(owner, side) == 0
+        mine = owner // side == core
+        for slot in range(side):
+            here = (even if slot == 0 else ~even) if side == 2 else owner == owner
+            lanes = slice(slot * columns, (slot + 1) * columns)
+
+            @pl.when(mine & here)
+            def _():
+                keep_ref[:, lanes] = result
+
+            @pl.when(~mine & here)
+            def _():
+                send_ref[:, lanes] = result
 
 
 def project(heads, weights, planes, orders):
     group = len(heads)
     rows = heads[0].shape[0]
     columns = weights[0].shape[1]
-    offsets = (0, 1, 3, 2) if planes == 4 else (0, 1)
     shape = pltpu.VMEM((rows, columns * planes // 2), BF16)
     return pl.pallas_call(
-        functools.partial(project_kernel, group, orders, offsets),
+        functools.partial(project_kernel, group, orders),
         out_shape=(shape, shape),
         in_specs=[VMEM] * (group + len(weights)),
         out_specs=(VMEM, VMEM),
+        scratch_shapes=[pltpu.VMEM((rows, weights[0].shape[0]), BF16)],
         compiler_params=PARAMS,
         name="project",
     )(*held(*heads, *weights))

time: 82.7 us -> 82.8 us (level)
  no operation moved by 1% of the time
where the time goes in v9:
time: 82.8 us; the launch traced here: 82.5 us
  starting transfers between devices  36.1 us (44%)
  waiting for transfers between devices  28.5 us (34%)
  Pallas kernels  17.7 us (21%)
    ppermute x15, starting transfers between devices, swap(): return lax.ppermute(value, 'seq', pairs)  19.9 us
    ppermute x15, waiting for transfers between devices, swap(): return lax.ppermute(value, 'seq', pairs)  19.7 us
    ppermute x3, starting transfers between devices, from_earlier(): return lax.ppermute(value, 'seq', pairs)  8.52 us
    ppermute x4, waiting for transfers between devices, between_planes(): lax.ppermute(value, 'seq', [(source * group + i, target * group + i) for...  8.29 us
    ppermute x4, starting transfers between devices, between_planes(): lax.ppermute(value, 'seq', [(source * group + i, target * group + i) for...  7.49 us
    pallas_call x2, Pallas kernels, invert(): pl.pallas_call(functools.partial(invert_kernel, heads, tokens), out_shape...  6.6 us
    pallas_call x2, Pallas kernels, project(): pl.pallas_call(functools.partial(project_kernel, group, orders), out_shap...  3.58 us
    pallas_call x1, Pallas kernels, carry_state(): pl.pallas_call(functools.partial(state_kernel, group, parts), out_shape=(...  2.63 us
  transfers between devices with their start and end apart: 24, of which 11 were waited for; matrix products, arithmetic and copies ran while one was open for 0% of the time, Pallas kernels for 20%

profile of v9, /device:TPU:0, one launch (start us, length us, event | category | flops | bytes accessed | tf_op | source)
XLA Modules:
  0.0 82.5 jit_solution(7914999446633291525)
XLA Ops:
  0.0 3.1 %collective-permute-start.12 = (bf16[1024,256]{1,0:T(8,128)(2,1)}, bf16[1024,256]{1,0:T(8,128)(2,1)S(1)}, u32[]{:S(2)}, u32[]{:S(2)}) collective-permute-start(bf16[1024,256]{1,0:T(8,128)(2,1)} %refs_4_.3), channel_id=1, source_target_pairs={{0,8},{2,10},{4,12},{6,14},{8,0},{10,2},{12,4},{14,6},{16,24},{18,... | collective-permute-start | bytes 1572872 | tf_op jit(solution)/shard_map/ppermute | solution.py:620
  3.1 2.5 %collective-permute-start.13 = (bf16[1024,256]{1,0:T(8,128)(2,1)}, bf16[1024,256]{1,0:T(8,128)(2,1)S(1)}, u32[]{:S(2)}, u32[]{:S(2)}) collective-permute-start(bf16[1024,256]{1,0:T(8,128)(2,1)} %refs_4_.3), channel_id=1, source_target_pairs={{0,24},{2,26},{4,28},{6,30},{8,16},{10,18},{12,20},{14,22},{16,8},... | collective-permute-start | bytes 1572872 | tf_op jit(solution)/shard_map/ppermute | solution.py:620
  7.1 1.6 %collective-permute-start.1 = (bf16[272,256]{1,0:T(8,128)(2,1)S(1)}, bf16[272,256]{1,0:T(8,128)(2,1)S(1)}, u32[]{:S(2)}, u32[]{:S(2)}) collective-permute-start(bf16[272,256]{1,0:T(8,128)(2,1)S(1)} %get-tuple-element.36), channel_id=1, source_target_pairs={{0,4},{2,6},{4,0},{6,2},{8,12},{10,14},{12,8},{14,10},{16,20},{18,... | collective-permute-start | bytes 417800 | tf_op jit(solution)/shard_map/ppermute | solution.py:599
  10.6 3.6 %collective-permute-done.1.refs_0_.refs_2_ = bf16[272,256]{1,0:T(8,128)(2,1)S(1)} collective-permute-done((bf16[272,256]{1,0:T(8,128)(2,1)S(1)}, bf16[272,256]{1,0:T(8,128)(2,1)S(1)}, u32[]{:S(2)}, u32[]{:S(2)}) %collective-permute-start.1) | collective-permute-done | bytes 139296 | tf_op jit(solution)/shard_map/ppermute | solution.py:599
  15.7 2.1 %collective-permute-start.4 = (bf16[3,128,256]{2,1,0:T(8,128)(2,1)S(1)}, bf16[3,128,256]{2,1,0:T(8,128)(2,1)S(1)}, u32[]{:S(2)}, u32[]{:S(2)}) collective-permute-start(bf16[3,128,256]{2,1,0:T(8,128)(2,1)S(1)} %get-tuple-element.40), channel_id=1, source_target_pairs={{0,4},{2,6},{4,0},{6,2},{8,12},{10,14},{12,8},{14,10},{16,20},{18,... | collective-permute-start | bytes 589832 | tf_op jit(solution)/shard_map/ppermute | solution.py:599
  18.1 1.6 %collective-permute-start.5 = (bf16[3,128,256]{2,1,0:T(8,128)(2,1)S(1)}, bf16[3,128,256]{2,1,0:T(8,128)(2,1)S(1)}, u32[]{:S(2)}, u32[]{:S(2)}) collective-permute-start(bf16[3,128,256]{2,1,0:T(8,128)(2,1)S(1)} %get-tuple-element.41), channel_id=1, source_target_pairs={{0,6},{2,4},{4,2},{6,0},{8,14},{10,12},{12,10},{14,8},{16,22},{18,... | collective-permute-start | bytes 589832 | tf_op jit(solution)/shard_map/ppermute | solution.py:599
  20.4 8.3 %collective-permute-done.13.refs_6_ = bf16[1024,256]{1,0:T(8,128)(2,1)S(1)} collective-permute-done((bf16[1024,256]{1,0:T(8,128)(2,1)}, bf16[1024,256]{1,0:T(8,128)(2,1)S(1)}, u32[]{:S(2)}, u32[]{:S(2)}) %collective-permute-start.13) | collective-permute-done | bytes 524320 | tf_op jit(solution)/shard_map/ppermute | solution.py:620
  30.0 3.3 %invert.3 = (f32[2,2,3,128,128]{4,3,2,1,0:T(8,128)S(1)}, f32[2,2,8,256]{3,2,1,0:T(8,128)S(1)}) custom-call(bf16[272,256]{1,0:T(8,128)(2,1)S(1)} %collective-permute-done.1.refs_0_.refs_2_, bf16[272,256]{1,0:T(8,128)(2,1)S(1)} %collective-permute-done.2.refs_1_.refs_3_), custom_call_target="tpu_custom_call" | custom-call | tf_op jit(solution)/shard_map/invert/pallas_call | solution.py:238
  33.3 3.3 %invert.2 = (f32[2,2,3,128,128]{4,3,2,1,0:T(8,128)S(1)}, f32[2,2,8,256]{3,2,1,0:T(8,128)S(1)}) custom-call(bf16[272,256]{1,0:T(8,128)(2,1)S(1)} %get-tuple-element.34.refs_0_, bf16[272,256]{1,0:T(8,128)(2,1)S(1)} %collective-permute-done.refs_1_), custom_call_target="tpu_custom_call" | custom-call | tf_op jit(solution)/shard_map/invert/pallas_call | solution.py:238
  36.7 2.6 %carry_state.1 = (bf16[2,4,256,256]{3,2,1,0:T(8,128)(2,1)S(1)}, bf16[2,4,256,256]{3,2,1,0:T(8,128)(2,1)S(1)}, f32[2,4,128,256]{3,2,1,0:T(8,128)S(1)}, bf16[2,128...) custom-call(bf16[272,256]{1,0:T(8,128)(2,1)S(1)} %get-tuple-element.34.refs_0_, ...), custom_call_target="tpu_custom_call" | custom-call | tf_op jit(solution)/shard_map/carry_state/pallas_call | solution.py:350
  39.3 4.6 %collective-permute-start.6 = (bf16[2,128,256]{2,1,0:T(8,128)(2,1)S(1)}, bf16[2,128,256]{2,1,0:T(8,128)(2,1)S(1)}, u32[]{:S(2)}, u32[]{:S(2)}) collective-permute-start(bf16[2,128,256]{2,1,0:T(8,128)(2,1)S(1)} %get-tuple-element.46), channel_id=1, source_target_pairs={{0,8},{2,10},{4,12},{6,14},{8,16},{10,18},{12,20},{14,22},{16,24},... | collective-permute-start | bytes 393224 | tf_op jit(solution)/shard_map/ppermute | solution.py:648
  43.9 2.6 %collective-permute-start.7 = (bf16[2,128,256]{2,1,0:T(8,128)(2,1)S(1)}, bf16[2,128,256]{2,1,0:T(8,128)(2,1)S(1)}, u32[]{:S(2)}, u32[]{:S(2)}) collective-permute-start(bf16[2,128,256]{2,1,0:T(8,128)(2,1)S(1)} %get-tuple-element.46), channel_id=1, source_target_pairs={{0,16},{2,18},{4,20},{6,22},{8,24},{10,26},{12,28},{14,30},{1,17},... | collective-permute-start | bytes 393224 | tf_op jit(solution)/shard_map/ppermute | solution.py:648
  47.8 1.7 %read.1 = (f32[512,256]{1,0:T(8,128)S(1)}, bf16[512,256]{1,0:T(8,128)(2,1)S(1)}) custom-call(bf16[272,256]{1,0:T(8,128)(2,1)S(1)} %get-tuple-element.34.refs_0_, bf16[272,256]{1,0:T(8,128)(2,1)S(1)} %collective-permute-done.refs_1_, bf16[272,256]{1,0:T(8,128)(2,1)S(1)} %collective-permute-done.1.refs_0_.refs_2_, ...), custom_call_target="tpu_custom_call" | custom-call | tf_op jit(solution)/shard_map/read/pallas_call | solution.py:420
  50.8 1.5 %collective-permute-start.17 = (bf16[256,256]{1,0:T(8,128)(2,1)S(1)}, bf16[256,256]{1,0:T(8,128)(2,1)S(1)}, u32[]{:S(2)}, u32[]{:S(2)}) collective-permute-start(bf16[256,256]{1,0:T(8,128)(2,1)S(1)} %get-tuple-element.53.refs_0_), channel_id=1, source_target_pairs={{0,2},{2,0},{4,6},{6,4},{8,10},{10,8},{12,14},{14,12},{16,18},{18,... | collective-permute-start | bytes 393224 | tf_op jit(solution)/shard_map/ppermute | solution.py:599
  52.4 1.5 %collective-permute-start.18 = (bf16[256,256]{1,0:T(8,128)(2,1)S(1)}, bf16[256,256]{1,0:T(8,128)(2,1)S(1)}, u32[]{:S(2)}, u32[]{:S(2)}) collective-permute-start(bf16[256,256]{1,0:T(8,128)(2,1)S(1)} %get-tuple-element.54.refs_0_), channel_id=1, source_target_pairs={{0,4},{2,6},{4,0},{6,2},{8,12},{10,14},{12,8},{14,10},{16,20},{18,... | collective-permute-start | bytes 393224 | tf_op jit(solution)/shard_map/ppermute | solution.py:599
  54.4 2.5 %collective-permute-done.17.refs_1_ = bf16[256,256]{1,0:T(8,128)(2,1)S(1)} collective-permute-done((bf16[256,256]{1,0:T(8,128)(2,1)S(1)}, bf16[256,256]{1,0:T(8,128)(2,1)S(1)}, u32[]{:S(2)}, u32[]{:S(2)}) %collective-permute-start.17) | collective-permute-done | bytes 131104 | tf_op jit(solution)/shard_map/ppermute | solution.py:599
  56.9 1.6 %collective-permute-start.10 = (bf16[256,256]{1,0:T(8,128)(2,1)S(1)}, bf16[256,256]{1,0:T(8,128)(2,1)S(1)}, u32[]{:S(2)}, u32[]{:S(2)}) collective-permute-start(bf16[256,256]{1,0:T(8,128)(2,1)S(1)} %get-tuple-element.53.refs_0_), channel_id=1, source_target_pairs={{0,4},{2,6},{4,0},{6,2},{8,12},{10,14},{12,8},{14,10},{16,20},{18,... | collective-permute-start | bytes 393224 | tf_op jit(solution)/shard_map/ppermute | solution.py:599
  58.4 3.7 %collective-permute-done.18.refs_2_ = bf16[256,256]{1,0:T(8,128)(2,1)S(1)} collective-permute-done((bf16[256,256]{1,0:T(8,128)(2,1)S(1)}, bf16[256,256]{1,0:T(8,128)(2,1)S(1)}, u32[]{:S(2)}, u32[]{:S(2)}) %collective-permute-start.18) | collective-permute-done | bytes 131104 | tf_op jit(solution)/shard_map/ppermute | solution.py:599
  62.5 2.0 %collective-permute-start.9 = (bf16[256,256]{1,0:T(8,128)(2,1)S(1)}, bf16[256,256]{1,0:T(8,128)(2,1)S(1)}, u32[]{:S(2)}, u32[]{:S(2)}) collective-permute-start(bf16[256,256]{1,0:T(8,128)(2,1)S(1)} %get-tuple-element.54.refs_0_), channel_id=1, source_target_pairs={{0,2},{2,0},{4,6},{6,4},{8,10},{10,8},{12,14},{14,12},{16,18},{18,... | collective-permute-start | bytes 393224 | tf_op jit(solution)/shard_map/ppermute | solution.py:599
  64.6 1.8 %project.3 = (bf16[256,512]{1,0:T(8,128)(2,1)S(1)}, bf16[256,512]{1,0:T(8,128)(2,1)S(1)}) custom-call(bf16[256,256]{1,0:T(8,128)(2,1)S(1)} %get-tuple-element.54.refs_0_, bf16[256,256]{1,0:T(8,128)(2,1)S(1)} %collective-permute-done.17.refs_1_, bf16[256,256]{1,0:T(8,128)(2,1)S(1)} %collective-permute-done.18.refs_2_, ...), custom_call_target="tpu_custom_call" | custom-call | tf_op jit(solution)/shard_map/project/pallas_call | solution.py:531
  68.9 1.8 %project.2 = (bf16[256,512]{1,0:T(8,128)(2,1)S(1)}, bf16[256,512]{1,0:T(8,128)(2,1)S(1)}) custom-call(bf16[256,256]{1,0:T(8,128)(2,1)S(1)} %get-tuple-element.53.refs_0_, bf16[256,256]{1,0:T(8,128)(2,1)S(1)} %collective-permute-done.9.refs_1_, bf16[256,256]{1,0:T(8,128)(2,1)S(1)} %collective-permute-done.10.refs_2_, ...), custom_call_target="tpu_custom_call" | custom-call | tf_op jit(solution)/shard_map/project/pallas_call | solution.py:531
  71.5 1.9 %collective-permute-start.23 = (bf16[128,512]{1,0:T(8,128)(2,1)S(1)}, bf16[128,512]{1,0:T(8,128)(2,1)S(1)}, u32[]{:S(2)}, u32[]{:S(2)}) collective-permute-start(bf16[128,512]{1,0:T(8,128)(2,1)S(1)} %get-tuple-element.62), channel_id=1, source_target_pairs={{0,6},{2,4},{4,2},{6,0},{8,14},{10,12},{12,10},{14,8},{16,22},{18,... | collective-permute-start | bytes 393224 | tf_op jit(solution)/shard_map/ppermute | solution.py:599
  74.5 2.7 %collective-permute-done.21.refs_1_ = bf16[128,512]{1,0:T(8,128)(2,1)S(1)} collective-permute-done((bf16[128,512]{1,0:T(8,128)(2,1)S(1)}, bf16[128,512]{1,0:T(8,128)(2,1)S(1)}, u32[]{:S(2)}, u32[]{:S(2)}) %collective-permute-start.21) | collective-permute-done | bytes 131104 | tf_op jit(solution)/shard_map/ppermute | solution.py:599
  77.3 2.9 %collective-permute-done.23.refs_3_ = bf16[128,512]{1,0:T(8,128)(2,1)S(1)} collective-permute-done((bf16[128,512]{1,0:T(8,128)(2,1)S(1)}, bf16[128,512]{1,0:T(8,128)(2,1)S(1)}, u32[]{:S(2)}, u32[]{:S(2)}) %collective-permute-start.23) | collective-permute-done | bytes 131104 | tf_op jit(solution)/shard_map/ppermute | solution.py:599
  (37 shorter events, 17.5 us)
Async XLA Ops:
  0.0 19.7 %collective-permute-start.12 = (bf16[1024,256]{1,0:T(8,128)(2,1)}, bf16[1024,256]{1,0:T(8,128)(2,1)S(1)}, u32[]{:S(2)}, u32[]{:S(2)}) collective-permute-start(bf16[1024,256]{1,0:T(8,128)(2,1)} %refs_4_.3), channel_id=1, source_target_pairs={{0,8},{2,10},{4,12},{6,14},{8,0},{10,2},{12,4},{14,6},{16,24},{18,... | collective-permute-start | bytes 1572872 | tf_op jit(solution)/shard_map/ppermute | solution.py:620
  3.1 25.7 %collective-permute-start.13 = (bf16[1024,256]{1,0:T(8,128)(2,1)}, bf16[1024,256]{1,0:T(8,128)(2,1)S(1)}, u32[]{:S(2)}, u32[]{:S(2)}) collective-permute-start(bf16[1024,256]{1,0:T(8,128)(2,1)} %refs_4_.3), channel_id=1, source_target_pairs={{0,24},{2,26},{4,28},{6,30},{8,16},{10,18},{12,20},{14,22},{16,8},... | collective-permute-start | bytes 1572872 | tf_op jit(solution)/shard_map/ppermute | solution.py:620
  7.1 7.2 %collective-permute-start.1 = (bf16[272,256]{1,0:T(8,128)(2,1)S(1)}, bf16[272,256]{1,0:T(8,128)(2,1)S(1)}, u32[]{:S(2)}, u32[]{:S(2)}) collective-permute-start(bf16[272,256]{1,0:T(8,128)(2,1)S(1)} %get-tuple-element.36), channel_id=1, source_target_pairs={{0,4},{2,6},{4,0},{6,2},{8,12},{10,14},{12,8},{14,10},{16,20},{18,... | collective-permute-start | bytes 417800 | tf_op jit(solution)/shard_map/ppermute | solution.py:599
  8.6 7.1 %collective-permute-start.2 = (bf16[272,256]{1,0:T(8,128)(2,1)S(1)}, bf16[272,256]{1,0:T(8,128)(2,1)S(1)}, u32[]{:S(2)}, u32[]{:S(2)}) collective-permute-start(bf16[272,256]{1,0:T(8,128)(2,1)S(1)} %get-tuple-element.37), channel_id=1, source_target_pairs={{0,6},{2,4},{4,2},{6,0},{8,14},{10,12},{12,10},{14,8},{16,22},{18,... | collective-permute-start | bytes 417800 | tf_op jit(solution)/shard_map/ppermute | solution.py:599
  10.1 8.0 %collective-permute-start = (bf16[272,256]{1,0:T(8,128)(2,1)S(1)}, bf16[272,256]{1,0:T(8,128)(2,1)S(1)}, u32[]{:S(2)}, u32[]{:S(2)}) collective-permute-start(bf16[272,256]{1,0:T(8,128)(2,1)S(1)} %get-tuple-element.35), channel_id=1, source_target_pairs={{0,2},{2,0},{4,6},{6,4},{8,10},{10,8},{12,14},{14,12},{16,18},{18,... | collective-permute-start | bytes 417800 | tf_op jit(solution)/shard_map/ppermute | solution.py:599
  14.2 22.4 %collective-permute-start.3 = (bf16[3,128,256]{2,1,0:T(8,128)(2,1)S(1)}, bf16[3,128,256]{2,1,0:T(8,128)(2,1)S(1)}, u32[]{:S(2)}, u32[]{:S(2)}) collective-permute-start(bf16[3,128,256]{2,1,0:T(8,128)(2,1)S(1)} %get-tuple-element.39), channel_id=1, source_target_pairs={{0,2},{2,0},{4,6},{6,4},{8,10},{10,8},{12,14},{14,12},{16,18},{18,... | collective-permute-start | bytes 589832 | tf_op jit(solution)/shard_map/ppermute | solution.py:599
  15.7 20.9 %collective-permute-start.4 = (bf16[3,128,256]{2,1,0:T(8,128)(2,1)S(1)}, bf16[3,128,256]{2,1,0:T(8,128)(2,1)S(1)}, u32[]{:S(2)}, u32[]{:S(2)}) collective-permute-start(bf16[3,128,256]{2,1,0:T(8,128)(2,1)S(1)} %get-tuple-element.40), channel_id=1, source_target_pairs={{0,4},{2,6},{4,0},{6,2},{8,12},{10,14},{12,8},{14,10},{16,20},{18,... | collective-permute-start | bytes 589832 | tf_op jit(solution)/shard_map/ppermute | solution.py:599
  18.1 18.5 %collective-permute-start.5 = (bf16[3,128,256]{2,1,0:T(8,128)(2,1)S(1)}, bf16[3,128,256]{2,1,0:T(8,128)(2,1)S(1)}, u32[]{:S(2)}, u32[]{:S(2)}) collective-permute-start(bf16[3,128,256]{2,1,0:T(8,128)(2,1)S(1)} %get-tuple-element.41), channel_id=1, source_target_pairs={{0,6},{2,4},{4,2},{6,0},{8,14},{10,12},{12,10},{14,8},{16,22},{18,... | collective-permute-start | bytes 589832 | tf_op jit(solution)/shard_map/ppermute | solution.py:599
  19.7 44.8 %collective-permute-start.14 = (bf16[1024,256]{1,0:T(8,128)(2,1)S(1)}, bf16[1024,256]{1,0:T(8,128)(2,1)S(1)}, u32[]{:S(2)}, u32[]{:S(2)}) collective-permute-start(bf16[1024,256]{1,0:T(8,128)(2,1)S(1)} %collective-permute-done.12.refs_5_), channel_id=1, source_target_pairs={{8,16},{10,18},{12,20},{14,22},{16,8},{18,10},{20,12},{22,14},{9,1... | collective-permute-start | bytes 1572872 | tf_op jit(solution)/shard_map/ppermute | solution.py:620
  28.7 35.8 %collective-permute-start.15 = (bf16[1024,256]{1,0:T(8,128)(2,1)S(1)}, bf16[1024,256]{1,0:T(8,128)(2,1)S(1)}, u32[]{:S(2)}, u32[]{:S(2)}) collective-permute-start(bf16[1024,256]{1,0:T(8,128)(2,1)S(1)} %collective-permute-done.13.refs_6_), channel_id=1, source_target_pairs={{8,0},{10,2},{12,4},{14,6},{16,24},{18,26},{20,28},{22,30},{9,1},{... | collective-permute-start | bytes 1572872 | tf_op jit(solution)/shard_map/ppermute | solution.py:620
  39.3 10.8 %collective-permute-start.6 = (bf16[2,128,256]{2,1,0:T(8,128)(2,1)S(1)}, bf16[2,128,256]{2,1,0:T(8,128)(2,1)S(1)}, u32[]{:S(2)}, u32[]{:S(2)}) collective-permute-start(bf16[2,128,256]{2,1,0:T(8,128)(2,1)S(1)} %get-tuple-element.46), channel_id=1, source_target_pairs={{0,8},{2,10},{4,12},{6,14},{8,16},{10,18},{12,20},{14,22},{16,24},... | collective-permute-start | bytes 393224 | tf_op jit(solution)/shard_map/ppermute | solution.py:648
  43.9 6.2 %collective-permute-start.7 = (bf16[2,128,256]{2,1,0:T(8,128)(2,1)S(1)}, bf16[2,128,256]{2,1,0:T(8,128)(2,1)S(1)}, u32[]{:S(2)}, u32[]{:S(2)}) collective-permute-start(bf16[2,128,256]{2,1,0:T(8,128)(2,1)S(1)} %get-tuple-element.46), channel_id=1, source_target_pairs={{0,16},{2,18},{4,20},{6,22},{8,24},{10,26},{12,28},{14,30},{1,17},... | collective-permute-start | bytes 393224 | tf_op jit(solution)/shard_map/ppermute | solution.py:648
  46.5 3.5 %collective-permute-start.8 = (bf16[2,128,128]{2,1,0:T(8,128)(2,1)S(1)}, bf16[2,128,128]{2,1,0:T(8,128)(2,1)S(1)}, u32[]{:S(2)}, u32[]{:S(2)}) collective-permute-start(bf16[2,128,128]{2,1,0:T(8,128)(2,1)S(1)} %get-tuple-element.47), channel_id=1, source_target_pairs={{0,24},{2,26},{4,28},{6,30},{1,25},{3,27},{5,29},{7,31}} | collective-permute-start | bytes 196616 | tf_op jit(solution)/shard_map/ppermute | solution.py:648
  50.8 6.0 %collective-permute-start.17 = (bf16[256,256]{1,0:T(8,128)(2,1)S(1)}, bf16[256,256]{1,0:T(8,128)(2,1)S(1)}, u32[]{:S(2)}, u32[]{:S(2)}) collective-permute-start(bf16[256,256]{1,0:T(8,128)(2,1)S(1)} %get-tuple-element.53.refs_0_), channel_id=1, source_target_pairs={{0,2},{2,0},{4,6},{6,4},{8,10},{10,8},{12,14},{14,12},{16,18},{18,... | collective-permute-start | bytes 393224 | tf_op jit(solution)/shard_map/ppermute | solution.py:599
  52.4 9.7 %collective-permute-start.18 = (bf16[256,256]{1,0:T(8,128)(2,1)S(1)}, bf16[256,256]{1,0:T(8,128)(2,1)S(1)}, u32[]{:S(2)}, u32[]{:S(2)}) collective-permute-start(bf16[256,256]{1,0:T(8,128)(2,1)S(1)} %get-tuple-element.54.refs_0_), channel_id=1, source_target_pairs={{0,4},{2,6},{4,0},{6,2},{8,12},{10,14},{12,8},{14,10},{16,20},{18,... | collective-permute-start | bytes 393224 | tf_op jit(solution)/shard_map/ppermute | solution.py:599
  53.9 8.6 %collective-permute-start.19 = (bf16[256,256]{1,0:T(8,128)(2,1)S(1)}, bf16[256,256]{1,0:T(8,128)(2,1)S(1)}, u32[]{:S(2)}, u32[]{:S(2)}) collective-permute-start(bf16[256,256]{1,0:T(8,128)(2,1)S(1)} %get-tuple-element.53.refs_0_), channel_id=1, source_target_pairs={{0,6},{2,4},{4,2},{6,0},{8,14},{10,12},{12,10},{14,8},{16,22},{18,... | collective-permute-start | bytes 393224 | tf_op jit(solution)/shard_map/ppermute | solution.py:599
  56.9 9.6 %collective-permute-start.10 = (bf16[256,256]{1,0:T(8,128)(2,1)S(1)}, bf16[256,256]{1,0:T(8,128)(2,1)S(1)}, u32[]{:S(2)}, u32[]{:S(2)}) collective-permute-start(bf16[256,256]{1,0:T(8,128)(2,1)S(1)} %get-tuple-element.53.refs_0_), channel_id=1, source_target_pairs={{0,4},{2,6},{4,0},{6,2},{8,12},{10,14},{12,8},{14,10},{16,20},{18,... | collective-permute-start | bytes 393224 | tf_op jit(solution)/shard_map/ppermute | solution.py:599
  62.1 5.9 %collective-permute-start.11 = (bf16[256,256]{1,0:T(8,128)(2,1)S(1)}, bf16[256,256]{1,0:T(8,128)(2,1)S(1)}, u32[]{:S(2)}, u32[]{:S(2)}) collective-permute-start(bf16[256,256]{1,0:T(8,128)(2,1)S(1)} %get-tuple-element.54.refs_0_), channel_id=1, source_target_pairs={{0,6},{2,4},{4,2},{6,0},{8,14},{10,12},{12,10},{14,8},{16,22},{18,... | collective-permute-start | bytes 393224 | tf_op jit(solution)/shard_map/ppermute | solution.py:599
  62.5 6.4 %collective-permute-start.9 = (bf16[256,256]{1,0:T(8,128)(2,1)S(1)}, bf16[256,256]{1,0:T(8,128)(2,1)S(1)}, u32[]{:S(2)}, u32[]{:S(2)}) collective-permute-start(bf16[256,256]{1,0:T(8,128)(2,1)S(1)} %get-tuple-element.54.refs_0_), channel_id=1, source_target_pairs={{0,2},{2,0},{4,6},{6,4},{8,10},{10,8},{12,14},{14,12},{16,18},{18,... | collective-permute-start | bytes 393224 | tf_op jit(solution)/shard_map/ppermute | solution.py:599
  66.4 4.4 %collective-permute-start.20 = (bf16[256,512]{1,0:T(8,128)(2,1)S(1)}, bf16[256,512]{1,0:T(8,128)(2,1)S(1)}, u32[]{:S(2)}, u32[]{:S(2)}) collective-permute-start(bf16[256,512]{1,0:T(8,128)(2,1)S(1)} %get-tuple-element.59), channel_id=1, source_target_pairs={{0,1},{1,0},{2,3},{3,2},{4,5},{5,4},{6,7},{7,6},{8,9},{9,8},{10,11... | collective-permute-start | bytes 786440 | tf_op jit(solution)/shard_map/ppermute | solution.py:689
  70.7 2.7 %collective-permute-start.16 = (bf16[256,512]{1,0:T(8,128)(2,1)S(1)}, bf16[256,512]{1,0:T(8,128)(2,1)S(1)}, u32[]{:S(2)}, u32[]{:S(2)}) collective-permute-start(bf16[256,512]{1,0:T(8,128)(2,1)S(1)} %get-tuple-element.56), channel_id=1, source_target_pairs={{0,1},{1,0},{2,3},{3,2},{4,5},{5,4},{6,7},{7,6},{8,9},{9,8},{10,11... | collective-permute-start | bytes 786440 | tf_op jit(solution)/shard_map/ppermute | solution.py:689
  70.8 6.4 %collective-permute-start.21 = (bf16[128,512]{1,0:T(8,128)(2,1)S(1)}, bf16[128,512]{1,0:T(8,128)(2,1)S(1)}, u32[]{:S(2)}, u32[]{:S(2)}) collective-permute-start(bf16[128,512]{1,0:T(8,128)(2,1)S(1)} %get-tuple-element.60), channel_id=1, source_target_pairs={{0,2},{2,0},{4,6},{6,4},{8,10},{10,8},{12,14},{14,12},{16,18},{18,... | collective-permute-start | bytes 393224 | tf_op jit(solution)/shard_map/ppermute | solution.py:599
  71.5 8.7 %collective-permute-start.23 = (bf16[128,512]{1,0:T(8,128)(2,1)S(1)}, bf16[128,512]{1,0:T(8,128)(2,1)S(1)}, u32[]{:S(2)}, u32[]{:S(2)}) collective-permute-start(bf16[128,512]{1,0:T(8,128)(2,1)S(1)} %get-tuple-element.62), channel_id=1, source_target_pairs={{0,6},{2,4},{4,2},{6,0},{8,14},{10,12},{12,10},{14,8},{16,22},{18,... | collective-permute-start | bytes 393224 | tf_op jit(solution)/shard_map/ppermute | solution.py:599
  73.5 8.2 %collective-permute-start.22 = (bf16[128,512]{1,0:T(8,128)(2,1)S(1)}, bf16[128,512]{1,0:T(8,128)(2,1)S(1)}, u32[]{:S(2)}, u32[]{:S(2)}) collective-permute-start(bf16[128,512]{1,0:T(8,128)(2,1)S(1)} %get-tuple-element.61), channel_id=1, source_target_pairs={{0,4},{2,6},{4,0},{6,2},{8,12},{10,14},{12,8},{14,10},{16,20},{18,... | collective-permute-start | bytes 393224 | tf_op jit(solution)/shard_map/ppermute | solution.py:599
  (1 other events, 14.5 us)

commit v10 on v9

--- a/solution.py
+++ b/solution.py
@@ -443,12 +443,12 @@
     position, _ = where_am_i(group)
     for head in range(heads):
         lanes = slice(head * width, (head + 1) * width)
-        total = None
+        total = jnp.zeros((width, width), F32)
         for state in reversed(states):
-            if total is None:
-                total = state[head].astype(F32)
+            step = state[head].astype(F32)
+            if step.shape[1] == width:
+                total = total + step
             else:
-                step = state[head].astype(F32)
                 total = (
                     total + step[:, width:] - dot(state[head, :, :width], total.astype(BF16))
                 )
@@ -486,7 +486,8 @@
 
 
 def project_kernel(group, orders, *refs):
-    heads_in, weight_in, (send_ref, keep_ref, left_buf) = refs[:group], refs[group:-3], refs[-3:]
+    heads_in, weight_in = refs[:group], refs[group:-4]
+    send_ref, keep_ref, left_buf, all_buf = refs[-4:]
     core = lax.axis_index("head")
     position, plane = where_am_i(group)
     rows, wide = heads_in[0].shape
@@ -506,21 +507,16 @@
             right = jnp.where(inner, weight_in[3][...], weight_in[4][...])
         else:
             right = weight_in[number][...]
-        result = dot(left_buf[...], right).astype(BF16)
-        owner = jnp.bitwise_xor(plane, offset)
-        even = lax.rem(owner, side) == 0
-        mine = owner // side == core
+        all_buf[:, number * columns : (number + 1) * columns] = dot(left_buf[...], right).astype(
+            BF16
+        )
+    for target, owner in ((send_ref, 1 - core), (keep_ref, core)):
         for slot in range(side):
-            here = (even if slot == 0 else ~even) if side == 2 else owner == owner
-            lanes = slice(slot * columns, (slot + 1) * columns)
-
-            @pl.when(mine & here)
-            def _():
-                keep_ref[:, lanes] = result
-
-            @pl.when(~mine & here)
-            def _():
-                send_ref[:, lanes] = result
+            offset = jnp.bitwise_xor(plane, owner * side + slot)
+            number = jnp.bitwise_xor(offset, offset // 2)
+            target[:, slot * columns : (slot + 1) * columns] = all_buf[
+                :, pl.ds(pl.multiple_of(number * columns, columns), columns)
+            ]
 
 
 def project(heads, weights, planes, orders):
@@ -533,7 +529,10 @@
         out_shape=(shape, shape),
         in_specs=[VMEM] * (group + len(weights)),
         out_specs=(VMEM, VMEM),
-        scratch_shapes=[pltpu.VMEM((rows, weights[0].shape[0]), BF16)],
+        scratch_shapes=[
+            pltpu.VMEM((rows, weights[0].shape[0]), BF16),
+            pltpu.VMEM((rows, columns * planes), BF16),
+        ],
         compiler_params=PARAMS,
         name="project",
     )(*held(*heads, *weights))
@@ -648,10 +647,16 @@
         return lax.ppermute(value, "seq", pairs)
 
     if planes <= 4:
-        states = []
+        states, firsts = [], []
         for distance in range(1, planes):
-            sent = state if distance + 1 < planes else local_state
-            states.append(from_earlier(sent, distance))
+            pairs = [(plane, plane + distance) for plane in range(planes - distance)]
+            if distance == 1:
+                states.append(between_planes(state, pairs))
+                continue
+            firsts.append(between_planes(local_state, pairs[:1]))
+            if pairs[1:]:
+                states.append(between_planes(state, pairs[1:]))
+        states += firsts
     else:
         total = from_earlier(state, 1)
         distance = 1

time: 82.8 us -> 81.1 us (0.979)
  the two profiles are of different devices: /device:TPU:0 before, /device:TPU:28 now
where the time goes in v10:
time: 81.1 us; the launch traced here: 80.8 us
  waiting for transfers between devices  38 us (47%)
  starting transfers between devices  26.6 us (33%)
  Pallas kernels  15.8 us (19%)
    ppermute x15, waiting for transfers between devices, swap(): return lax.ppermute(value, 'seq', pairs)  21.4 us
    ppermute x15, starting transfers between devices, swap(): return lax.ppermute(value, 'seq', pairs)  18 us
    ppermute x8, waiting for transfers between devices, between_planes(): lax.ppermute(value, 'seq', [(source * group + i, target * group + i) for...  16.6 us
    ppermute x8, starting transfers between devices, between_planes(): lax.ppermute(value, 'seq', [(source * group + i, target * group + i) for...  8.49 us
    pallas_call x2, Pallas kernels, invert(): pl.pallas_call(functools.partial(invert_kernel, heads, tokens), out_shape...  6.6 us
    pallas_call x1, Pallas kernels, carry_state(): pl.pallas_call(functools.partial(state_kernel, group, parts), out_shape=(...  2.63 us
    pallas_call x1, Pallas kernels, read(): pl.pallas_call(functools.partial(read_kernel, group), out_shape=(pltpu.VM...  1.66 us
    pallas_call x2, Pallas kernels, project(): pl.pallas_call(functools.partial(project_kernel, group, orders), out_shap...  1.66 us
  transfers between devices with their start and end apart: 25, of which 11 were waited for; matrix products, arithmetic and copies ran while one was open for 0% of the time, Pallas kernels for 19%

profile of v10, /device:TPU:28, one launch (start us, length us, event | category | flops | bytes accessed | tf_op | source)
XLA Modules:
  0.0 80.8 jit_solution(2165402031025878803)
XLA Ops:
  0.5 1.3 %collective-permute-start.14 = (bf16[1024,256]{1,0:T(8,128)(2,1)}, bf16[1024,256]{1,0:T(8,128)(2,1)S(1)}, u32[]{:S(2)}, u32[]{:S(2)}) collective-permute-start(bf16[1024,256]{1,0:T(8,128)(2,1)} %refs_4_.3), channel_id=1, source_target_pairs={{0,24},{2,26},{4,28},{6,30},{8,16},{10,18},{12,20},{14,22},{16,8},... | collective-permute-start | bytes 1572872 | tf_op jit(solution)/shard_map/ppermute | solution.py:619
  1.8 1.5 %pack.1 = (bf16[272,256]{1,0:T(8,128)(2,1)S(1)}, bf16[272,256]{1,0:T(8,128)(2,1)S(1)}, bf16[272,256]{1,0:T(8,128)(2,1)S(1)}, bf16[272,256]{1,0:T(8,128)(2,1)S(1)...) custom-call(bf16[2,128,1024]{2,1,0:T(8,128)(2,1)} %key_ref.1, ...), custom_call_target="tpu_custom_call" | custom-call | tf_op jit(solution)/shard_map/pack/pallas_call | solution.py:139
  3.9 2.4 %collective-permute-start.2 = (bf16[272,256]{1,0:T(8,128)(2,1)S(1)}, bf16[272,256]{1,0:T(8,128)(2,1)S(1)}, u32[]{:S(2)}, u32[]{:S(2)}) collective-permute-start(bf16[272,256]{1,0:T(8,128)(2,1)S(1)} %get-tuple-element.37), channel_id=1, source_target_pairs={{0,6},{2,4},{4,2},{6,0},{8,14},{10,12},{12,10},{14,8},{16,22},{18,... | collective-permute-start | bytes 417800 | tf_op jit(solution)/shard_map/ppermute | solution.py:598
  6.9 4.2 %collective-permute-done.1.refs_0_.refs_2_ = bf16[272,256]{1,0:T(8,128)(2,1)S(1)} collective-permute-done((bf16[272,256]{1,0:T(8,128)(2,1)S(1)}, bf16[272,256]{1,0:T(8,128)(2,1)S(1)}, u32[]{:S(2)}, u32[]{:S(2)}) %collective-permute-start.1) | collective-permute-done | bytes 139296 | tf_op jit(solution)/shard_map/ppermute | solution.py:598
  11.1 1.5 %collective-permute-start.3 = (bf16[3,128,256]{2,1,0:T(8,128)(2,1)S(1)}, bf16[3,128,256]{2,1,0:T(8,128)(2,1)S(1)}, u32[]{:S(2)}, u32[]{:S(2)}) collective-permute-start(bf16[3,128,256]{2,1,0:T(8,128)(2,1)S(1)} %get-tuple-element.39), channel_id=1, source_target_pairs={{0,2},{2,0},{4,6},{6,4},{8,10},{10,8},{12,14},{14,12},{16,18},{18,... | collective-permute-start | bytes 589832 | tf_op jit(solution)/shard_map/ppermute | solution.py:598
  13.6 2.3 %collective-permute-start.5 = (bf16[3,128,256]{2,1,0:T(8,128)(2,1)S(1)}, bf16[3,128,256]{2,1,0:T(8,128)(2,1)S(1)}, u32[]{:S(2)}, u32[]{:S(2)}) collective-permute-start(bf16[3,128,256]{2,1,0:T(8,128)(2,1)S(1)} %get-tuple-element.41), channel_id=1, source_target_pairs={{0,6},{2,4},{4,2},{6,0},{8,14},{10,12},{12,10},{14,8},{16,22},{18,... | collective-permute-start | bytes 589832 | tf_op jit(solution)/shard_map/ppermute | solution.py:598
  15.8 9.3 %collective-permute-done.13.refs_5_ = bf16[1024,256]{1,0:T(8,128)(2,1)S(1)} collective-permute-done((bf16[1024,256]{1,0:T(8,128)(2,1)}, bf16[1024,256]{1,0:T(8,128)(2,1)S(1)}, u32[]{:S(2)}, u32[]{:S(2)}) %collective-permute-start.13) | collective-permute-done | bytes 524320 | tf_op jit(solution)/shard_map/ppermute | solution.py:619
  27.1 3.3 %invert.3 = (f32[2,2,3,128,128]{4,3,2,1,0:T(8,128)S(1)}, f32[2,2,8,256]{3,2,1,0:T(8,128)S(1)}) custom-call(bf16[272,256]{1,0:T(8,128)(2,1)S(1)} %collective-permute-done.1.refs_0_.refs_2_, bf16[272,256]{1,0:T(8,128)(2,1)S(1)} %collective-permute-done.2.refs_1_.refs_3_), custom_call_target="tpu_custom_call" | custom-call | tf_op jit(solution)/shard_map/invert/pallas_call | solution.py:238
  30.4 3.3 %invert.2 = (f32[2,2,3,128,128]{4,3,2,1,0:T(8,128)S(1)}, f32[2,2,8,256]{3,2,1,0:T(8,128)S(1)}) custom-call(bf16[272,256]{1,0:T(8,128)(2,1)S(1)} %get-tuple-element.34.refs_0_, bf16[272,256]{1,0:T(8,128)(2,1)S(1)} %collective-permute-done.refs_1_), custom_call_target="tpu_custom_call" | custom-call | tf_op jit(solution)/shard_map/invert/pallas_call | solution.py:238
  33.8 2.6 %carry_state.1 = (bf16[2,4,256,256]{3,2,1,0:T(8,128)(2,1)S(1)}, bf16[2,4,256,256]{3,2,1,0:T(8,128)(2,1)S(1)}, f32[2,4,128,256]{3,2,1,0:T(8,128)S(1)}, bf16[2,128...) custom-call(bf16[272,256]{1,0:T(8,128)(2,1)S(1)} %get-tuple-element.34.refs_0_, ...), custom_call_target="tpu_custom_call" | custom-call | tf_op jit(solution)/shard_map/carry_state/pallas_call | solution.py:350
  39.7 1.5 %collective-permute-start.9 = (bf16[2,128,128]{2,1,0:T(8,128)(2,1)S(1)}, bf16[2,128,128]{2,1,0:T(8,128)(2,1)S(1)}, u32[]{:S(2)}, u32[]{:S(2)}) collective-permute-start(bf16[2,128,128]{2,1,0:T(8,128)(2,1)S(1)} %get-tuple-element.47), channel_id=1, source_target_pairs={{0,24},{2,26},{4,28},{6,30},{1,25},{3,27},{5,29},{7,31}} | collective-permute-start | bytes 196616 | tf_op jit(solution)/shard_map/ppermute | solution.py:619
  41.2 1.7 %read.1 = (f32[512,256]{1,0:T(8,128)S(1)}, bf16[512,256]{1,0:T(8,128)(2,1)S(1)}) custom-call(bf16[272,256]{1,0:T(8,128)(2,1)S(1)} %get-tuple-element.34.refs_0_, bf16[272,256]{1,0:T(8,128)(2,1)S(1)} %collective-permute-done.refs_1_, bf16[272,256]{1,0:T(8,128)(2,1)S(1)} %collective-permute-done.1.refs_0_.refs_2_, ...), custom_call_target="tpu_custom_call" | custom-call | tf_op jit(solution)/shard_map/read/pallas_call | solution.py:420
  42.8 6.5 %collective-permute-done.9.refs_3_ = bf16[2,128,128]{2,1,0:T(8,128)(2,1)S(1)} collective-permute-done((bf16[2,128,128]{2,1,0:T(8,128)(2,1)S(1)}, bf16[2,128,128]{2,1,0:T(8,128)(2,1)S(1)}, u32[]{:S(2)}, u32[]{:S(2)}) %collective-permute-start.9) | collective-permute-done | bytes 65568 | tf_op jit(solution)/shard_map/ppermute | solution.py:619
  50.9 1.6 %collective-permute-start.18 = (bf16[256,256]{1,0:T(8,128)(2,1)S(1)}, bf16[256,256]{1,0:T(8,128)(2,1)S(1)}, u32[]{:S(2)}, u32[]{:S(2)}) collective-permute-start(bf16[256,256]{1,0:T(8,128)(2,1)S(1)} %get-tuple-element.53.refs_0_), channel_id=1, source_target_pairs={{0,2},{2,0},{4,6},{6,4},{8,10},{10,8},{12,14},{14,12},{16,18},{18,... | collective-permute-start | bytes 393224 | tf_op jit(solution)/shard_map/ppermute | solution.py:598
  53.0 1.5 %collective-permute-start.20 = (bf16[256,256]{1,0:T(8,128)(2,1)S(1)}, bf16[256,256]{1,0:T(8,128)(2,1)S(1)}, u32[]{:S(2)}, u32[]{:S(2)}) collective-permute-start(bf16[256,256]{1,0:T(8,128)(2,1)S(1)} %get-tuple-element.53.refs_0_), channel_id=1, source_target_pairs={{0,6},{2,4},{4,2},{6,0},{8,14},{10,12},{12,10},{14,8},{16,22},{18,... | collective-permute-start | bytes 393224 | tf_op jit(solution)/shard_map/ppermute | solution.py:598
  54.4 2.3 %collective-permute-done.18.refs_1_ = bf16[256,256]{1,0:T(8,128)(2,1)S(1)} collective-permute-done((bf16[256,256]{1,0:T(8,128)(2,1)S(1)}, bf16[256,256]{1,0:T(8,128)(2,1)S(1)}, u32[]{:S(2)}, u32[]{:S(2)}) %collective-permute-start.18) | collective-permute-done | bytes 131104 | tf_op jit(solution)/shard_map/ppermute | solution.py:598
  56.7 1.5 %collective-permute-start.10 = (bf16[256,256]{1,0:T(8,128)(2,1)S(1)}, bf16[256,256]{1,0:T(8,128)(2,1)S(1)}, u32[]{:S(2)}, u32[]{:S(2)}) collective-permute-start(bf16[256,256]{1,0:T(8,128)(2,1)S(1)} %get-tuple-element.54.refs_0_), channel_id=1, source_target_pairs={{0,2},{2,0},{4,6},{6,4},{8,10},{10,8},{12,14},{14,12},{16,18},{18,... | collective-permute-start | bytes 393224 | tf_op jit(solution)/shard_map/ppermute | solution.py:598
  58.2 2.9 %collective-permute-done.19.refs_2_ = bf16[256,256]{1,0:T(8,128)(2,1)S(1)} collective-permute-done((bf16[256,256]{1,0:T(8,128)(2,1)S(1)}, bf16[256,256]{1,0:T(8,128)(2,1)S(1)}, u32[]{:S(2)}, u32[]{:S(2)}) %collective-permute-start.19) | collective-permute-done | bytes 131104 | tf_op jit(solution)/shard_map/ppermute | solution.py:598
  61.1 2.0 %collective-permute-start.12 = (bf16[256,256]{1,0:T(8,128)(2,1)S(1)}, bf16[256,256]{1,0:T(8,128)(2,1)S(1)}, u32[]{:S(2)}, u32[]{:S(2)}) collective-permute-start(bf16[256,256]{1,0:T(8,128)(2,1)S(1)} %get-tuple-element.54.refs_0_), channel_id=1, source_target_pairs={{0,6},{2,4},{4,2},{6,0},{8,14},{10,12},{12,10},{14,8},{16,22},{18,... | collective-permute-start | bytes 393224 | tf_op jit(solution)/shard_map/ppermute | solution.py:598
  64.0 3.4 %collective-permute-done.11.refs_2_ = bf16[256,256]{1,0:T(8,128)(2,1)S(1)} collective-permute-done((bf16[256,256]{1,0:T(8,128)(2,1)S(1)}, bf16[256,256]{1,0:T(8,128)(2,1)S(1)}, u32[]{:S(2)}, u32[]{:S(2)}) %collective-permute-start.11) | collective-permute-done | bytes 131104 | tf_op jit(solution)/shard_map/ppermute | solution.py:598
  69.1 2.4 %collective-permute-start.24 = (bf16[128,512]{1,0:T(8,128)(2,1)S(1)}, bf16[128,512]{1,0:T(8,128)(2,1)S(1)}, u32[]{:S(2)}, u32[]{:S(2)}) collective-permute-start(bf16[128,512]{1,0:T(8,128)(2,1)S(1)} %get-tuple-element.62), channel_id=1, source_target_pairs={{0,6},{2,4},{4,2},{6,0},{8,14},{10,12},{12,10},{14,8},{16,22},{18,... | collective-permute-start | bytes 393224 | tf_op jit(solution)/shard_map/ppermute | solution.py:598
  72.2 2.7 %collective-permute-done.22.refs_1_ = bf16[128,512]{1,0:T(8,128)(2,1)S(1)} collective-permute-done((bf16[128,512]{1,0:T(8,128)(2,1)S(1)}, bf16[128,512]{1,0:T(8,128)(2,1)S(1)}, u32[]{:S(2)}, u32[]{:S(2)}) %collective-permute-start.22) | collective-permute-done | bytes 131104 | tf_op jit(solution)/shard_map/ppermute | solution.py:598
  74.9 3.4 %collective-permute-done.24.refs_3_ = bf16[128,512]{1,0:T(8,128)(2,1)S(1)} collective-permute-done((bf16[128,512]{1,0:T(8,128)(2,1)S(1)}, bf16[128,512]{1,0:T(8,128)(2,1)S(1)}, u32[]{:S(2)}, u32[]{:S(2)}) %collective-permute-start.24) | collective-permute-done | bytes 131104 | tf_op jit(solution)/shard_map/ppermute | solution.py:598
  78.3 1.5 %collective-permute-done.23.refs_2_ = bf16[128,512]{1,0:T(8,128)(2,1)S(1)} collective-permute-done((bf16[128,512]{1,0:T(8,128)(2,1)S(1)}, bf16[128,512]{1,0:T(8,128)(2,1)S(1)}, u32[]{:S(2)}, u32[]{:S(2)}) %collective-permute-start.23) | collective-permute-done | bytes 131104 | tf_op jit(solution)/shard_map/ppermute | solution.py:598
  (39 shorter events, 13.8 us)
Async XLA Ops:
  0.0 25.1 %collective-permute-start.13 = (bf16[1024,256]{1,0:T(8,128)(2,1)}, bf16[1024,256]{1,0:T(8,128)(2,1)S(1)}, u32[]{:S(2)}, u32[]{:S(2)}) collective-permute-start(bf16[1024,256]{1,0:T(8,128)(2,1)} %refs_4_.3), channel_id=1, source_target_pairs={{0,8},{2,10},{4,12},{6,14},{8,0},{10,2},{12,4},{14,6},{16,24},{18,... | collective-permute-start | bytes 1572872 | tf_op jit(solution)/shard_map/ppermute | solution.py:619
  0.5 25.4 %collective-permute-start.14 = (bf16[1024,256]{1,0:T(8,128)(2,1)}, bf16[1024,256]{1,0:T(8,128)(2,1)S(1)}, u32[]{:S(2)}, u32[]{:S(2)}) collective-permute-start(bf16[1024,256]{1,0:T(8,128)(2,1)} %refs_4_.3), channel_id=1, source_target_pairs={{0,24},{2,26},{4,28},{6,30},{8,16},{10,18},{12,20},{14,22},{16,8},... | collective-permute-start | bytes 1572872 | tf_op jit(solution)/shard_map/ppermute | solution.py:619
  3.3 7.8 %collective-permute-start.1 = (bf16[272,256]{1,0:T(8,128)(2,1)S(1)}, bf16[272,256]{1,0:T(8,128)(2,1)S(1)}, u32[]{:S(2)}, u32[]{:S(2)}) collective-permute-start(bf16[272,256]{1,0:T(8,128)(2,1)S(1)} %get-tuple-element.36), channel_id=1, source_target_pairs={{0,4},{2,6},{4,0},{6,2},{8,12},{10,14},{12,8},{14,10},{16,20},{18,... | collective-permute-start | bytes 417800 | tf_op jit(solution)/shard_map/ppermute | solution.py:598
  3.9 8.7 %collective-permute-start.2 = (bf16[272,256]{1,0:T(8,128)(2,1)S(1)}, bf16[272,256]{1,0:T(8,128)(2,1)S(1)}, u32[]{:S(2)}, u32[]{:S(2)}) collective-permute-start(bf16[272,256]{1,0:T(8,128)(2,1)S(1)} %get-tuple-element.37), channel_id=1, source_target_pairs={{0,6},{2,4},{4,2},{6,0},{8,14},{10,12},{12,10},{14,8},{16,22},{18,... | collective-permute-start | bytes 417800 | tf_op jit(solution)/shard_map/ppermute | solution.py:598
  6.4 7.2 %collective-permute-start = (bf16[272,256]{1,0:T(8,128)(2,1)S(1)}, bf16[272,256]{1,0:T(8,128)(2,1)S(1)}, u32[]{:S(2)}, u32[]{:S(2)}) collective-permute-start(bf16[272,256]{1,0:T(8,128)(2,1)S(1)} %get-tuple-element.35), channel_id=1, source_target_pairs={{0,2},{2,0},{4,6},{6,4},{8,10},{10,8},{12,14},{14,12},{16,18},{18,... | collective-permute-start | bytes 417800 | tf_op jit(solution)/shard_map/ppermute | solution.py:598
  11.1 22.6 %collective-permute-start.3 = (bf16[3,128,256]{2,1,0:T(8,128)(2,1)S(1)}, bf16[3,128,256]{2,1,0:T(8,128)(2,1)S(1)}, u32[]{:S(2)}, u32[]{:S(2)}) collective-permute-start(bf16[3,128,256]{2,1,0:T(8,128)(2,1)S(1)} %get-tuple-element.39), channel_id=1, source_target_pairs={{0,2},{2,0},{4,6},{6,4},{8,10},{10,8},{12,14},{14,12},{16,18},{18,... | collective-permute-start | bytes 589832 | tf_op jit(solution)/shard_map/ppermute | solution.py:598
  12.6 21.1 %collective-permute-start.4 = (bf16[3,128,256]{2,1,0:T(8,128)(2,1)S(1)}, bf16[3,128,256]{2,1,0:T(8,128)(2,1)S(1)}, u32[]{:S(2)}, u32[]{:S(2)}) collective-permute-start(bf16[3,128,256]{2,1,0:T(8,128)(2,1)S(1)} %get-tuple-element.40), channel_id=1, source_target_pairs={{0,4},{2,6},{4,0},{6,2},{8,12},{10,14},{12,8},{14,10},{16,20},{18,... | collective-permute-start | bytes 589832 | tf_op jit(solution)/shard_map/ppermute | solution.py:598
  13.6 20.2 %collective-permute-start.5 = (bf16[3,128,256]{2,1,0:T(8,128)(2,1)S(1)}, bf16[3,128,256]{2,1,0:T(8,128)(2,1)S(1)}, u32[]{:S(2)}, u32[]{:S(2)}) collective-permute-start(bf16[3,128,256]{2,1,0:T(8,128)(2,1)S(1)} %get-tuple-element.41), channel_id=1, source_target_pairs={{0,6},{2,4},{4,2},{6,0},{8,14},{10,12},{12,10},{14,8},{16,22},{18,... | collective-permute-start | bytes 589832 | tf_op jit(solution)/shard_map/ppermute | solution.py:598
  25.1 38.0 %collective-permute-start.15 = (bf16[1024,256]{1,0:T(8,128)(2,1)S(1)}, bf16[1024,256]{1,0:T(8,128)(2,1)S(1)}, u32[]{:S(2)}, u32[]{:S(2)}) collective-permute-start(bf16[1024,256]{1,0:T(8,128)(2,1)S(1)} %collective-permute-done.13.refs_5_), channel_id=1, source_target_pairs={{8,16},{10,18},{12,20},{14,22},{16,8},{18,10},{20,12},{22,14},{9,1... | collective-permute-start | bytes 1572872 | tf_op jit(solution)/shard_map/ppermute | solution.py:619
  25.8 37.3 %collective-permute-start.16 = (bf16[1024,256]{1,0:T(8,128)(2,1)S(1)}, bf16[1024,256]{1,0:T(8,128)(2,1)S(1)}, u32[]{:S(2)}, u32[]{:S(2)}) collective-permute-start(bf16[1024,256]{1,0:T(8,128)(2,1)S(1)} %collective-permute-done.14.refs_6_), channel_id=1, source_target_pairs={{8,0},{10,2},{12,4},{14,6},{16,24},{18,26},{20,28},{22,30},{9,1},{... | collective-permute-start | bytes 1572872 | tf_op jit(solution)/shard_map/ppermute | solution.py:619
  36.4 3.3 %collective-permute-start.8 = (bf16[2,128,128]{2,1,0:T(8,128)(2,1)S(1)}, bf16[2,128,128]{2,1,0:T(8,128)(2,1)S(1)}, u32[]{:S(2)}, u32[]{:S(2)}) collective-permute-start(bf16[2,128,128]{2,1,0:T(8,128)(2,1)S(1)} %get-tuple-element.47), channel_id=1, source_target_pairs={{0,16},{2,18},{4,20},{6,22},{1,17},{3,19},{5,21},{7,23}} | collective-permute-start | bytes 196616 | tf_op jit(solution)/shard_map/ppermute | solution.py:619
  37.1 12.3 %collective-permute-start.6 = (bf16[2,128,256]{2,1,0:T(8,128)(2,1)S(1)}, bf16[2,128,256]{2,1,0:T(8,128)(2,1)S(1)}, u32[]{:S(2)}, u32[]{:S(2)}) collective-permute-start(bf16[2,128,256]{2,1,0:T(8,128)(2,1)S(1)} %get-tuple-element.46), channel_id=1, source_target_pairs={{0,8},{2,10},{4,12},{6,14},{8,16},{10,18},{12,20},{14,22},{16,24},... | collective-permute-start | bytes 393224 | tf_op jit(solution)/shard_map/ppermute | solution.py:619
  38.4 11.8 %collective-permute-start.7 = (bf16[2,128,256]{2,1,0:T(8,128)(2,1)S(1)}, bf16[2,128,256]{2,1,0:T(8,128)(2,1)S(1)}, u32[]{:S(2)}, u32[]{:S(2)}) collective-permute-start(bf16[2,128,256]{2,1,0:T(8,128)(2,1)S(1)} %get-tuple-element.46), channel_id=1, source_target_pairs={{8,24},{10,26},{12,28},{14,30},{9,25},{11,27},{13,29},{15,31}} | collective-permute-start | bytes 393224 | tf_op jit(solution)/shard_map/ppermute | solution.py:619
  39.7 9.7 %collective-permute-start.9 = (bf16[2,128,128]{2,1,0:T(8,128)(2,1)S(1)}, bf16[2,128,128]{2,1,0:T(8,128)(2,1)S(1)}, u32[]{:S(2)}, u32[]{:S(2)}) collective-permute-start(bf16[2,128,128]{2,1,0:T(8,128)(2,1)S(1)} %get-tuple-element.47), channel_id=1, source_target_pairs={{0,24},{2,26},{4,28},{6,30},{1,25},{3,27},{5,29},{7,31}} | collective-permute-start | bytes 196616 | tf_op jit(solution)/shard_map/ppermute | solution.py:619
  50.9 5.8 %collective-permute-start.18 = (bf16[256,256]{1,0:T(8,128)(2,1)S(1)}, bf16[256,256]{1,0:T(8,128)(2,1)S(1)}, u32[]{:S(2)}, u32[]{:S(2)}) collective-permute-start(bf16[256,256]{1,0:T(8,128)(2,1)S(1)} %get-tuple-element.53.refs_0_), channel_id=1, source_target_pairs={{0,2},{2,0},{4,6},{6,4},{8,10},{10,8},{12,14},{14,12},{16,18},{18,... | collective-permute-start | bytes 393224 | tf_op jit(solution)/shard_map/ppermute | solution.py:598
  52.4 8.6 %collective-permute-start.19 = (bf16[256,256]{1,0:T(8,128)(2,1)S(1)}, bf16[256,256]{1,0:T(8,128)(2,1)S(1)}, u32[]{:S(2)}, u32[]{:S(2)}) collective-permute-start(bf16[256,256]{1,0:T(8,128)(2,1)S(1)} %get-tuple-element.54.refs_0_), channel_id=1, source_target_pairs={{0,4},{2,6},{4,0},{6,2},{8,12},{10,14},{12,8},{14,10},{16,20},{18,... | collective-permute-start | bytes 393224 | tf_op jit(solution)/shard_map/ppermute | solution.py:598
  53.0 8.1 %collective-permute-start.20 = (bf16[256,256]{1,0:T(8,128)(2,1)S(1)}, bf16[256,256]{1,0:T(8,128)(2,1)S(1)}, u32[]{:S(2)}, u32[]{:S(2)}) collective-permute-start(bf16[256,256]{1,0:T(8,128)(2,1)S(1)} %get-tuple-element.53.refs_0_), channel_id=1, source_target_pairs={{0,6},{2,4},{4,2},{6,0},{8,14},{10,12},{12,10},{14,8},{16,22},{18,... | collective-permute-start | bytes 393224 | tf_op jit(solution)/shard_map/ppermute | solution.py:598
  56.7 7.3 %collective-permute-start.10 = (bf16[256,256]{1,0:T(8,128)(2,1)S(1)}, bf16[256,256]{1,0:T(8,128)(2,1)S(1)}, u32[]{:S(2)}, u32[]{:S(2)}) collective-permute-start(bf16[256,256]{1,0:T(8,128)(2,1)S(1)} %get-tuple-element.54.refs_0_), channel_id=1, source_target_pairs={{0,2},{2,0},{4,6},{6,4},{8,10},{10,8},{12,14},{14,12},{16,18},{18,... | collective-permute-start | bytes 393224 | tf_op jit(solution)/shard_map/ppermute | solution.py:598
  61.1 6.4 %collective-permute-start.11 = (bf16[256,256]{1,0:T(8,128)(2,1)S(1)}, bf16[256,256]{1,0:T(8,128)(2,1)S(1)}, u32[]{:S(2)}, u32[]{:S(2)}) collective-permute-start(bf16[256,256]{1,0:T(8,128)(2,1)S(1)} %get-tuple-element.53.refs_0_), channel_id=1, source_target_pairs={{0,4},{2,6},{4,0},{6,2},{8,12},{10,14},{12,8},{14,10},{16,20},{18,... | collective-permute-start | bytes 393224 | tf_op jit(solution)/shard_map/ppermute | solution.py:598
  61.1 6.4 %collective-permute-start.12 = (bf16[256,256]{1,0:T(8,128)(2,1)S(1)}, bf16[256,256]{1,0:T(8,128)(2,1)S(1)}, u32[]{:S(2)}, u32[]{:S(2)}) collective-permute-start(bf16[256,256]{1,0:T(8,128)(2,1)S(1)} %get-tuple-element.54.refs_0_), channel_id=1, source_target_pairs={{0,6},{2,4},{4,2},{6,0},{8,14},{10,12},{12,10},{14,8},{16,22},{18,... | collective-permute-start | bytes 393224 | tf_op jit(solution)/shard_map/ppermute | solution.py:598
  63.9 4.4 %collective-permute-start.21 = (bf16[256,512]{1,0:T(8,128)(2,1)S(1)}, bf16[256,512]{1,0:T(8,128)(2,1)S(1)}, u32[]{:S(2)}, u32[]{:S(2)}) collective-permute-start(bf16[256,512]{1,0:T(8,128)(2,1)S(1)} %get-tuple-element.59), channel_id=1, source_target_pairs={{0,1},{1,0},{2,3},{3,2},{4,5},{5,4},{6,7},{7,6},{8,9},{9,8},{10,11... | collective-permute-start | bytes 786440 | tf_op jit(solution)/shard_map/ppermute | solution.py:694
  68.5 6.4 %collective-permute-start.22 = (bf16[128,512]{1,0:T(8,128)(2,1)S(1)}, bf16[128,512]{1,0:T(8,128)(2,1)S(1)}, u32[]{:S(2)}, u32[]{:S(2)}) collective-permute-start(bf16[128,512]{1,0:T(8,128)(2,1)S(1)} %get-tuple-element.60), channel_id=1, source_target_pairs={{0,2},{2,0},{4,6},{6,4},{8,10},{10,8},{12,14},{14,12},{16,18},{18,... | collective-permute-start | bytes 393224 | tf_op jit(solution)/shard_map/ppermute | solution.py:598
  69.1 9.2 %collective-permute-start.24 = (bf16[128,512]{1,0:T(8,128)(2,1)S(1)}, bf16[128,512]{1,0:T(8,128)(2,1)S(1)}, u32[]{:S(2)}, u32[]{:S(2)}) collective-permute-start(bf16[128,512]{1,0:T(8,128)(2,1)S(1)} %get-tuple-element.62), channel_id=1, source_target_pairs={{0,6},{2,4},{4,2},{6,0},{8,14},{10,12},{12,10},{14,8},{16,22},{18,... | collective-permute-start | bytes 393224 | tf_op jit(solution)/shard_map/ppermute | solution.py:598
  71.6 8.2 %collective-permute-start.23 = (bf16[128,512]{1,0:T(8,128)(2,1)S(1)}, bf16[128,512]{1,0:T(8,128)(2,1)S(1)}, u32[]{:S(2)}, u32[]{:S(2)}) collective-permute-start(bf16[128,512]{1,0:T(8,128)(2,1)S(1)} %get-tuple-element.61), channel_id=1, source_target_pairs={{0,4},{2,6},{4,0},{6,2},{8,12},{10,14},{12,8},{14,10},{16,20},{18,... | collective-permute-start | bytes 393224 | tf_op jit(solution)/shard_map/ppermute | solution.py:598
  (2 other events, 16.2 us)

commit v11 on v10

--- a/solution.py
+++ b/solution.py
@@ -443,12 +443,12 @@
     position, _ = where_am_i(group)
     for head in range(heads):
         lanes = slice(head * width, (head + 1) * width)
-        total = jnp.zeros((width, width), F32)
+        total = None
         for state in reversed(states):
-            step = state[head].astype(F32)
-            if step.shape[1] == width:
-                total = total + step
+            if total is None:
+                total = state[head].astype(F32)
             else:
+                step = state[head].astype(F32)
                 total = (
                     total + step[:, width:] - dot(state[head, :, :width], total.astype(BF16))
                 )
@@ -647,16 +647,10 @@
         return lax.ppermute(value, "seq", pairs)
 
     if planes <= 4:
-        states, firsts = [], []
+        states = []
         for distance in range(1, planes):
-            pairs = [(plane, plane + distance) for plane in range(planes - distance)]
-            if distance == 1:
-                states.append(between_planes(state, pairs))
-                continue
-            firsts.append(between_planes(local_state, pairs[:1]))
-            if pairs[1:]:
-                states.append(between_planes(state, pairs[1:]))
-        states += firsts
+            sent = state if distance + 1 < planes else local_state
+            states.append(from_earlier(sent, distance))
     else:
         total = from_earlier(state, 1)
         distance = 1

time: 81.1 us -> 82 us (1.011)
  the two profiles are of different devices: /device:TPU:28 before, /device:TPU:0 now
where the time goes in v11:
time: 82 us; the launch traced here: 81.7 us
  starting transfers between devices  36.3 us (44%)
  waiting for transfers between devices  29.3 us (36%)
  Pallas kernels  15.8 us (19%)
    ppermute x15, waiting for transfers between devices, swap(): return lax.ppermute(value, 'seq', pairs)  20.6 us
    ppermute x15, starting transfers between devices, swap(): return lax.ppermute(value, 'seq', pairs)  20 us
    ppermute x3, starting transfers between devices, from_earlier(): return lax.ppermute(value, 'seq', pairs)  8.71 us
    ppermute x4, waiting for transfers between devices, between_planes(): lax.ppermute(value, 'seq', [(source * group + i, target * group + i) for...  8.29 us
    ppermute x4, starting transfers between devices, between_planes(): lax.ppermute(value, 'seq', [(source * group + i, target * group + i) for...  7.49 us
    pallas_call x2, Pallas kernels, invert(): pl.pallas_call(functools.partial(invert_kernel, heads, tokens), out_shape...  6.6 us
    pallas_call x1, Pallas kernels, carry_state(): pl.pallas_call(functools.partial(state_kernel, group, parts), out_shape=(...  2.63 us
    pallas_call x1, Pallas kernels, read(): pl.pallas_call(functools.partial(read_kernel, group), out_shape=(pltpu.VM...  1.66 us
  transfers between devices with their start and end apart: 24, of which 11 were waited for; matrix products, arithmetic and copies ran while one was open for 0% of the time, Pallas kernels for 18%

profile of v11, /device:TPU:0, one launch (start us, length us, event | category | flops | bytes accessed | tf_op | source)
XLA Modules:
  0.0 81.7 jit_solution(14578651560645049033)
XLA Ops:
  0.0 3.1 %collective-permute-start.12 = (bf16[1024,256]{1,0:T(8,128)(2,1)}, bf16[1024,256]{1,0:T(8,128)(2,1)S(1)}, u32[]{:S(2)}, u32[]{:S(2)}) collective-permute-start(bf16[1024,256]{1,0:T(8,128)(2,1)} %refs_4_.3), channel_id=1, source_target_pairs={{0,8},{2,10},{4,12},{6,14},{8,0},{10,2},{12,4},{14,6},{16,24},{18,... | collective-permute-start | bytes 1572872 | tf_op jit(solution)/shard_map/ppermute | solution.py:619
  3.1 2.5 %collective-permute-start.13 = (bf16[1024,256]{1,0:T(8,128)(2,1)}, bf16[1024,256]{1,0:T(8,128)(2,1)S(1)}, u32[]{:S(2)}, u32[]{:S(2)}) collective-permute-start(bf16[1024,256]{1,0:T(8,128)(2,1)} %refs_4_.3), channel_id=1, source_target_pairs={{0,24},{2,26},{4,28},{6,30},{8,16},{10,18},{12,20},{14,22},{16,8},... | collective-permute-start | bytes 1572872 | tf_op jit(solution)/shard_map/ppermute | solution.py:619
  5.5 1.5 %pack.1 = (bf16[272,256]{1,0:T(8,128)(2,1)S(1)}, bf16[272,256]{1,0:T(8,128)(2,1)S(1)}, bf16[272,256]{1,0:T(8,128)(2,1)S(1)}, bf16[272,256]{1,0:T(8,128)(2,1)S(1)...) custom-call(bf16[2,128,1024]{2,1,0:T(8,128)(2,1)} %key_ref.1, ...), custom_call_target="tpu_custom_call" | custom-call | tf_op jit(solution)/shard_map/pack/pallas_call | solution.py:139
  7.1 1.6 %collective-permute-start.1 = (bf16[272,256]{1,0:T(8,128)(2,1)S(1)}, bf16[272,256]{1,0:T(8,128)(2,1)S(1)}, u32[]{:S(2)}, u32[]{:S(2)}) collective-permute-start(bf16[272,256]{1,0:T(8,128)(2,1)S(1)} %get-tuple-element.36), channel_id=1, source_target_pairs={{0,4},{2,6},{4,0},{6,2},{8,12},{10,14},{12,8},{14,10},{16,20},{18,... | collective-permute-start | bytes 417800 | tf_op jit(solution)/shard_map/ppermute | solution.py:598
  10.6 3.6 %collective-permute-done.1.refs_0_.refs_2_ = bf16[272,256]{1,0:T(8,128)(2,1)S(1)} collective-permute-done((bf16[272,256]{1,0:T(8,128)(2,1)S(1)}, bf16[272,256]{1,0:T(8,128)(2,1)S(1)}, u32[]{:S(2)}, u32[]{:S(2)}) %collective-permute-start.1) | collective-permute-done | bytes 139296 | tf_op jit(solution)/shard_map/ppermute | solution.py:598
  15.7 2.1 %collective-permute-start.4 = (bf16[3,128,256]{2,1,0:T(8,128)(2,1)S(1)}, bf16[3,128,256]{2,1,0:T(8,128)(2,1)S(1)}, u32[]{:S(2)}, u32[]{:S(2)}) collective-permute-start(bf16[3,128,256]{2,1,0:T(8,128)(2,1)S(1)} %get-tuple-element.40), channel_id=1, source_target_pairs={{0,4},{2,6},{4,0},{6,2},{8,12},{10,14},{12,8},{14,10},{16,20},{18,... | collective-permute-start | bytes 589832 | tf_op jit(solution)/shard_map/ppermute | solution.py:598
  18.1 1.6 %collective-permute-start.5 = (bf16[3,128,256]{2,1,0:T(8,128)(2,1)S(1)}, bf16[3,128,256]{2,1,0:T(8,128)(2,1)S(1)}, u32[]{:S(2)}, u32[]{:S(2)}) collective-permute-start(bf16[3,128,256]{2,1,0:T(8,128)(2,1)S(1)} %get-tuple-element.41), channel_id=1, source_target_pairs={{0,6},{2,4},{4,2},{6,0},{8,14},{10,12},{12,10},{14,8},{16,22},{18,... | collective-permute-start | bytes 589832 | tf_op jit(solution)/shard_map/ppermute | solution.py:598
  20.4 8.3 %collective-permute-done.13.refs_6_ = bf16[1024,256]{1,0:T(8,128)(2,1)S(1)} collective-permute-done((bf16[1024,256]{1,0:T(8,128)(2,1)}, bf16[1024,256]{1,0:T(8,128)(2,1)S(1)}, u32[]{:S(2)}, u32[]{:S(2)}) %collective-permute-start.13) | collective-permute-done | bytes 524320 | tf_op jit(solution)/shard_map/ppermute | solution.py:619
  30.0 3.3 %invert.3 = (f32[2,2,3,128,128]{4,3,2,1,0:T(8,128)S(1)}, f32[2,2,8,256]{3,2,1,0:T(8,128)S(1)}) custom-call(bf16[272,256]{1,0:T(8,128)(2,1)S(1)} %collective-permute-done.1.refs_0_.refs_2_, bf16[272,256]{1,0:T(8,128)(2,1)S(1)} %collective-permute-done.2.refs_1_.refs_3_), custom_call_target="tpu_custom_call" | custom-call | tf_op jit(solution)/shard_map/invert/pallas_call | solution.py:238
  33.3 3.3 %invert.2 = (f32[2,2,3,128,128]{4,3,2,1,0:T(8,128)S(1)}, f32[2,2,8,256]{3,2,1,0:T(8,128)S(1)}) custom-call(bf16[272,256]{1,0:T(8,128)(2,1)S(1)} %get-tuple-element.34.refs_0_, bf16[272,256]{1,0:T(8,128)(2,1)S(1)} %collective-permute-done.refs_1_), custom_call_target="tpu_custom_call" | custom-call | tf_op jit(solution)/shard_map/invert/pallas_call | solution.py:238
  36.6 2.6 %carry_state.1 = (bf16[2,4,256,256]{3,2,1,0:T(8,128)(2,1)S(1)}, bf16[2,4,256,256]{3,2,1,0:T(8,128)(2,1)S(1)}, f32[2,4,128,256]{3,2,1,0:T(8,128)S(1)}, bf16[2,128...) custom-call(bf16[272,256]{1,0:T(8,128)(2,1)S(1)} %get-tuple-element.34.refs_0_, ...), custom_call_target="tpu_custom_call" | custom-call | tf_op jit(solution)/shard_map/carry_state/pallas_call | solution.py:350
  39.3 4.6 %collective-permute-start.6 = (bf16[2,128,256]{2,1,0:T(8,128)(2,1)S(1)}, bf16[2,128,256]{2,1,0:T(8,128)(2,1)S(1)}, u32[]{:S(2)}, u32[]{:S(2)}) collective-permute-start(bf16[2,128,256]{2,1,0:T(8,128)(2,1)S(1)} %get-tuple-element.46), channel_id=1, source_target_pairs={{0,8},{2,10},{4,12},{6,14},{8,16},{10,18},{12,20},{14,22},{16,24},... | collective-permute-start | bytes 393224 | tf_op jit(solution)/shard_map/ppermute | solution.py:647
  43.9 2.6 %collective-permute-start.7 = (bf16[2,128,256]{2,1,0:T(8,128)(2,1)S(1)}, bf16[2,128,256]{2,1,0:T(8,128)(2,1)S(1)}, u32[]{:S(2)}, u32[]{:S(2)}) collective-permute-start(bf16[2,128,256]{2,1,0:T(8,128)(2,1)S(1)} %get-tuple-element.46), channel_id=1, source_target_pairs={{0,16},{2,18},{4,20},{6,22},{8,24},{10,26},{12,28},{14,30},{1,17},... | collective-permute-start | bytes 393224 | tf_op jit(solution)/shard_map/ppermute | solution.py:647
  48.0 1.7 %read.1 = (f32[512,256]{1,0:T(8,128)S(1)}, bf16[512,256]{1,0:T(8,128)(2,1)S(1)}) custom-call(bf16[272,256]{1,0:T(8,128)(2,1)S(1)} %get-tuple-element.34.refs_0_, bf16[272,256]{1,0:T(8,128)(2,1)S(1)} %collective-permute-done.refs_1_, bf16[272,256]{1,0:T(8,128)(2,1)S(1)} %collective-permute-done.1.refs_0_.refs_2_, ...), custom_call_target="tpu_custom_call" | custom-call | tf_op jit(solution)/shard_map/read/pallas_call | solution.py:420
  50.8 1.6 %collective-permute-start.17 = (bf16[256,256]{1,0:T(8,128)(2,1)S(1)}, bf16[256,256]{1,0:T(8,128)(2,1)S(1)}, u32[]{:S(2)}, u32[]{:S(2)}) collective-permute-start(bf16[256,256]{1,0:T(8,128)(2,1)S(1)} %get-tuple-element.53.refs_0_), channel_id=1, source_target_pairs={{0,2},{2,0},{4,6},{6,4},{8,10},{10,8},{12,14},{14,12},{16,18},{18,... | collective-permute-start | bytes 393224 | tf_op jit(solution)/shard_map/ppermute | solution.py:598
  52.4 1.5 %collective-permute-start.18 = (bf16[256,256]{1,0:T(8,128)(2,1)S(1)}, bf16[256,256]{1,0:T(8,128)(2,1)S(1)}, u32[]{:S(2)}, u32[]{:S(2)}) collective-permute-start(bf16[256,256]{1,0:T(8,128)(2,1)S(1)} %get-tuple-element.54.refs_0_), channel_id=1, source_target_pairs={{0,4},{2,6},{4,0},{6,2},{8,12},{10,14},{12,8},{14,10},{16,20},{18,... | collective-permute-start | bytes 393224 | tf_op jit(solution)/shard_map/ppermute | solution.py:598
  54.4 2.5 %collective-permute-done.17.refs_1_ = bf16[256,256]{1,0:T(8,128)(2,1)S(1)} collective-permute-done((bf16[256,256]{1,0:T(8,128)(2,1)S(1)}, bf16[256,256]{1,0:T(8,128)(2,1)S(1)}, u32[]{:S(2)}, u32[]{:S(2)}) %collective-permute-start.17) | collective-permute-done | bytes 131104 | tf_op jit(solution)/shard_map/ppermute | solution.py:598
  56.9 1.5 %collective-permute-start.10 = (bf16[256,256]{1,0:T(8,128)(2,1)S(1)}, bf16[256,256]{1,0:T(8,128)(2,1)S(1)}, u32[]{:S(2)}, u32[]{:S(2)}) collective-permute-start(bf16[256,256]{1,0:T(8,128)(2,1)S(1)} %get-tuple-element.53.refs_0_), channel_id=1, source_target_pairs={{0,4},{2,6},{4,0},{6,2},{8,12},{10,14},{12,8},{14,10},{16,20},{18,... | collective-permute-start | bytes 393224 | tf_op jit(solution)/shard_map/ppermute | solution.py:598
  58.4 3.7 %collective-permute-done.18.refs_2_ = bf16[256,256]{1,0:T(8,128)(2,1)S(1)} collective-permute-done((bf16[256,256]{1,0:T(8,128)(2,1)S(1)}, bf16[256,256]{1,0:T(8,128)(2,1)S(1)}, u32[]{:S(2)}, u32[]{:S(2)}) %collective-permute-start.18) | collective-permute-done | bytes 131104 | tf_op jit(solution)/shard_map/ppermute | solution.py:598
  62.5 2.1 %collective-permute-start.9 = (bf16[256,256]{1,0:T(8,128)(2,1)S(1)}, bf16[256,256]{1,0:T(8,128)(2,1)S(1)}, u32[]{:S(2)}, u32[]{:S(2)}) collective-permute-start(bf16[256,256]{1,0:T(8,128)(2,1)S(1)} %get-tuple-element.54.refs_0_), channel_id=1, source_target_pairs={{0,2},{2,0},{4,6},{6,4},{8,10},{10,8},{12,14},{14,12},{16,18},{18,... | collective-permute-start | bytes 393224 | tf_op jit(solution)/shard_map/ppermute | solution.py:598
  65.5 2.4 %collective-permute-done.11.refs_3_ = bf16[256,256]{1,0:T(8,128)(2,1)S(1)} collective-permute-done((bf16[256,256]{1,0:T(8,128)(2,1)S(1)}, bf16[256,256]{1,0:T(8,128)(2,1)S(1)}, u32[]{:S(2)}, u32[]{:S(2)}) %collective-permute-start.11) | collective-permute-done | bytes 131104 | tf_op jit(solution)/shard_map/ppermute | solution.py:598
  70.6 1.8 %collective-permute-start.23 = (bf16[128,512]{1,0:T(8,128)(2,1)S(1)}, bf16[128,512]{1,0:T(8,128)(2,1)S(1)}, u32[]{:S(2)}, u32[]{:S(2)}) collective-permute-start(bf16[128,512]{1,0:T(8,128)(2,1)S(1)} %get-tuple-element.62), channel_id=1, source_target_pairs={{0,6},{2,4},{4,2},{6,0},{8,14},{10,12},{12,10},{14,8},{16,22},{18,... | collective-permute-start | bytes 393224 | tf_op jit(solution)/shard_map/ppermute | solution.py:598
  73.6 2.7 %collective-permute-done.21.refs_1_ = bf16[128,512]{1,0:T(8,128)(2,1)S(1)} collective-permute-done((bf16[128,512]{1,0:T(8,128)(2,1)S(1)}, bf16[128,512]{1,0:T(8,128)(2,1)S(1)}, u32[]{:S(2)}, u32[]{:S(2)}) %collective-permute-start.21) | collective-permute-done | bytes 131104 | tf_op jit(solution)/shard_map/ppermute | solution.py:598
  76.4 2.9 %collective-permute-done.23.refs_3_ = bf16[128,512]{1,0:T(8,128)(2,1)S(1)} collective-permute-done((bf16[128,512]{1,0:T(8,128)(2,1)S(1)}, bf16[128,512]{1,0:T(8,128)(2,1)S(1)}, u32[]{:S(2)}, u32[]{:S(2)}) %collective-permute-start.23) | collective-permute-done | bytes 131104 | tf_op jit(solution)/shard_map/ppermute | solution.py:598
  (37 shorter events, 16.2 us)
Async XLA Ops:
  0.0 19.7 %collective-permute-start.12 = (bf16[1024,256]{1,0:T(8,128)(2,1)}, bf16[1024,256]{1,0:T(8,128)(2,1)S(1)}, u32[]{:S(2)}, u32[]{:S(2)}) collective-permute-start(bf16[1024,256]{1,0:T(8,128)(2,1)} %refs_4_.3), channel_id=1, source_target_pairs={{0,8},{2,10},{4,12},{6,14},{8,0},{10,2},{12,4},{14,6},{16,24},{18,... | collective-permute-start | bytes 1572872 | tf_op jit(solution)/shard_map/ppermute | solution.py:619
  3.1 25.7 %collective-permute-start.13 = (bf16[1024,256]{1,0:T(8,128)(2,1)}, bf16[1024,256]{1,0:T(8,128)(2,1)S(1)}, u32[]{:S(2)}, u32[]{:S(2)}) collective-permute-start(bf16[1024,256]{1,0:T(8,128)(2,1)} %refs_4_.3), channel_id=1, source_target_pairs={{0,24},{2,26},{4,28},{6,30},{8,16},{10,18},{12,20},{14,22},{16,8},... | collective-permute-start | bytes 1572872 | tf_op jit(solution)/shard_map/ppermute | solution.py:619
  7.1 7.2 %collective-permute-start.1 = (bf16[272,256]{1,0:T(8,128)(2,1)S(1)}, bf16[272,256]{1,0:T(8,128)(2,1)S(1)}, u32[]{:S(2)}, u32[]{:S(2)}) collective-permute-start(bf16[272,256]{1,0:T(8,128)(2,1)S(1)} %get-tuple-element.36), channel_id=1, source_target_pairs={{0,4},{2,6},{4,0},{6,2},{8,12},{10,14},{12,8},{14,10},{16,20},{18,... | collective-permute-start | bytes 417800 | tf_op jit(solution)/shard_map/ppermute | solution.py:598
  8.6 7.1 %collective-permute-start.2 = (bf16[272,256]{1,0:T(8,128)(2,1)S(1)}, bf16[272,256]{1,0:T(8,128)(2,1)S(1)}, u32[]{:S(2)}, u32[]{:S(2)}) collective-permute-start(bf16[272,256]{1,0:T(8,128)(2,1)S(1)} %get-tuple-element.37), channel_id=1, source_target_pairs={{0,6},{2,4},{4,2},{6,0},{8,14},{10,12},{12,10},{14,8},{16,22},{18,... | collective-permute-start | bytes 417800 | tf_op jit(solution)/shard_map/ppermute | solution.py:598
  10.1 8.0 %collective-permute-start = (bf16[272,256]{1,0:T(8,128)(2,1)S(1)}, bf16[272,256]{1,0:T(8,128)(2,1)S(1)}, u32[]{:S(2)}, u32[]{:S(2)}) collective-permute-start(bf16[272,256]{1,0:T(8,128)(2,1)S(1)} %get-tuple-element.35), channel_id=1, source_target_pairs={{0,2},{2,0},{4,6},{6,4},{8,10},{10,8},{12,14},{14,12},{16,18},{18,... | collective-permute-start | bytes 417800 | tf_op jit(solution)/shard_map/ppermute | solution.py:598
  14.2 22.4 %collective-permute-start.3 = (bf16[3,128,256]{2,1,0:T(8,128)(2,1)S(1)}, bf16[3,128,256]{2,1,0:T(8,128)(2,1)S(1)}, u32[]{:S(2)}, u32[]{:S(2)}) collective-permute-start(bf16[3,128,256]{2,1,0:T(8,128)(2,1)S(1)} %get-tuple-element.39), channel_id=1, source_target_pairs={{0,2},{2,0},{4,6},{6,4},{8,10},{10,8},{12,14},{14,12},{16,18},{18,... | collective-permute-start | bytes 589832 | tf_op jit(solution)/shard_map/ppermute | solution.py:598
  15.7 20.9 %collective-permute-start.4 = (bf16[3,128,256]{2,1,0:T(8,128)(2,1)S(1)}, bf16[3,128,256]{2,1,0:T(8,128)(2,1)S(1)}, u32[]{:S(2)}, u32[]{:S(2)}) collective-permute-start(bf16[3,128,256]{2,1,0:T(8,128)(2,1)S(1)} %get-tuple-element.40), channel_id=1, source_target_pairs={{0,4},{2,6},{4,0},{6,2},{8,12},{10,14},{12,8},{14,10},{16,20},{18,... | collective-permute-start | bytes 589832 | tf_op jit(solution)/shard_map/ppermute | solution.py:598
  18.1 18.5 %collective-permute-start.5 = (bf16[3,128,256]{2,1,0:T(8,128)(2,1)S(1)}, bf16[3,128,256]{2,1,0:T(8,128)(2,1)S(1)}, u32[]{:S(2)}, u32[]{:S(2)}) collective-permute-start(bf16[3,128,256]{2,1,0:T(8,128)(2,1)S(1)} %get-tuple-element.41), channel_id=1, source_target_pairs={{0,6},{2,4},{4,2},{6,0},{8,14},{10,12},{12,10},{14,8},{16,22},{18,... | collective-permute-start | bytes 589832 | tf_op jit(solution)/shard_map/ppermute | solution.py:598
  19.7 44.9 %collective-permute-start.14 = (bf16[1024,256]{1,0:T(8,128)(2,1)S(1)}, bf16[1024,256]{1,0:T(8,128)(2,1)S(1)}, u32[]{:S(2)}, u32[]{:S(2)}) collective-permute-start(bf16[1024,256]{1,0:T(8,128)(2,1)S(1)} %collective-permute-done.12.refs_5_), channel_id=1, source_target_pairs={{8,16},{10,18},{12,20},{14,22},{16,8},{18,10},{20,12},{22,14},{9,1... | collective-permute-start | bytes 1572872 | tf_op jit(solution)/shard_map/ppermute | solution.py:619
  28.7 35.9 %collective-permute-start.15 = (bf16[1024,256]{1,0:T(8,128)(2,1)S(1)}, bf16[1024,256]{1,0:T(8,128)(2,1)S(1)}, u32[]{:S(2)}, u32[]{:S(2)}) collective-permute-start(bf16[1024,256]{1,0:T(8,128)(2,1)S(1)} %collective-permute-done.13.refs_6_), channel_id=1, source_target_pairs={{8,0},{10,2},{12,4},{14,6},{16,24},{18,26},{20,28},{22,30},{9,1},{... | collective-permute-start | bytes 1572872 | tf_op jit(solution)/shard_map/ppermute | solution.py:619
  39.3 10.7 %collective-permute-start.6 = (bf16[2,128,256]{2,1,0:T(8,128)(2,1)S(1)}, bf16[2,128,256]{2,1,0:T(8,128)(2,1)S(1)}, u32[]{:S(2)}, u32[]{:S(2)}) collective-permute-start(bf16[2,128,256]{2,1,0:T(8,128)(2,1)S(1)} %get-tuple-element.46), channel_id=1, source_target_pairs={{0,8},{2,10},{4,12},{6,14},{8,16},{10,18},{12,20},{14,22},{16,24},... | collective-permute-start | bytes 393224 | tf_op jit(solution)/shard_map/ppermute | solution.py:647
  43.9 6.2 %collective-permute-start.7 = (bf16[2,128,256]{2,1,0:T(8,128)(2,1)S(1)}, bf16[2,128,256]{2,1,0:T(8,128)(2,1)S(1)}, u32[]{:S(2)}, u32[]{:S(2)}) collective-permute-start(bf16[2,128,256]{2,1,0:T(8,128)(2,1)S(1)} %get-tuple-element.46), channel_id=1, source_target_pairs={{0,16},{2,18},{4,20},{6,22},{8,24},{10,26},{12,28},{14,30},{1,17},... | collective-permute-start | bytes 393224 | tf_op jit(solution)/shard_map/ppermute | solution.py:647
  46.5 3.5 %collective-permute-start.8 = (bf16[2,128,128]{2,1,0:T(8,128)(2,1)S(1)}, bf16[2,128,128]{2,1,0:T(8,128)(2,1)S(1)}, u32[]{:S(2)}, u32[]{:S(2)}) collective-permute-start(bf16[2,128,128]{2,1,0:T(8,128)(2,1)S(1)} %get-tuple-element.47), channel_id=1, source_target_pairs={{0,24},{2,26},{4,28},{6,30},{1,25},{3,27},{5,29},{7,31}} | collective-permute-start | bytes 196616 | tf_op jit(solution)/shard_map/ppermute | solution.py:647
  50.8 6.1 %collective-permute-start.17 = (bf16[256,256]{1,0:T(8,128)(2,1)S(1)}, bf16[256,256]{1,0:T(8,128)(2,1)S(1)}, u32[]{:S(2)}, u32[]{:S(2)}) collective-permute-start(bf16[256,256]{1,0:T(8,128)(2,1)S(1)} %get-tuple-element.53.refs_0_), channel_id=1, source_target_pairs={{0,2},{2,0},{4,6},{6,4},{8,10},{10,8},{12,14},{14,12},{16,18},{18,... | collective-permute-start | bytes 393224 | tf_op jit(solution)/shard_map/ppermute | solution.py:598
  52.4 9.7 %collective-permute-start.18 = (bf16[256,256]{1,0:T(8,128)(2,1)S(1)}, bf16[256,256]{1,0:T(8,128)(2,1)S(1)}, u32[]{:S(2)}, u32[]{:S(2)}) collective-permute-start(bf16[256,256]{1,0:T(8,128)(2,1)S(1)} %get-tuple-element.54.refs_0_), channel_id=1, source_target_pairs={{0,4},{2,6},{4,0},{6,2},{8,12},{10,14},{12,8},{14,10},{16,20},{18,... | collective-permute-start | bytes 393224 | tf_op jit(solution)/shard_map/ppermute | solution.py:598
  53.9 8.6 %collective-permute-start.19 = (bf16[256,256]{1,0:T(8,128)(2,1)S(1)}, bf16[256,256]{1,0:T(8,128)(2,1)S(1)}, u32[]{:S(2)}, u32[]{:S(2)}) collective-permute-start(bf16[256,256]{1,0:T(8,128)(2,1)S(1)} %get-tuple-element.53.refs_0_), channel_id=1, source_target_pairs={{0,6},{2,4},{4,2},{6,0},{8,14},{10,12},{12,10},{14,8},{16,22},{18,... | collective-permute-start | bytes 393224 | tf_op jit(solution)/shard_map/ppermute | solution.py:598
  56.9 8.6 %collective-permute-start.10 = (bf16[256,256]{1,0:T(8,128)(2,1)S(1)}, bf16[256,256]{1,0:T(8,128)(2,1)S(1)}, u32[]{:S(2)}, u32[]{:S(2)}) collective-permute-start(bf16[256,256]{1,0:T(8,128)(2,1)S(1)} %get-tuple-element.53.refs_0_), channel_id=1, source_target_pairs={{0,4},{2,6},{4,0},{6,2},{8,12},{10,14},{12,8},{14,10},{16,20},{18,... | collective-permute-start | bytes 393224 | tf_op jit(solution)/shard_map/ppermute | solution.py:598
  62.1 5.9 %collective-permute-start.11 = (bf16[256,256]{1,0:T(8,128)(2,1)S(1)}, bf16[256,256]{1,0:T(8,128)(2,1)S(1)}, u32[]{:S(2)}, u32[]{:S(2)}) collective-permute-start(bf16[256,256]{1,0:T(8,128)(2,1)S(1)} %get-tuple-element.54.refs_0_), channel_id=1, source_target_pairs={{0,6},{2,4},{4,2},{6,0},{8,14},{10,12},{12,10},{14,8},{16,22},{18,... | collective-permute-start | bytes 393224 | tf_op jit(solution)/shard_map/ppermute | solution.py:598
  62.5 6.4 %collective-permute-start.9 = (bf16[256,256]{1,0:T(8,128)(2,1)S(1)}, bf16[256,256]{1,0:T(8,128)(2,1)S(1)}, u32[]{:S(2)}, u32[]{:S(2)}) collective-permute-start(bf16[256,256]{1,0:T(8,128)(2,1)S(1)} %get-tuple-element.54.refs_0_), channel_id=1, source_target_pairs={{0,2},{2,0},{4,6},{6,4},{8,10},{10,8},{12,14},{14,12},{16,18},{18,... | collective-permute-start | bytes 393224 | tf_op jit(solution)/shard_map/ppermute | solution.py:598
  65.4 4.4 %collective-permute-start.20 = (bf16[256,512]{1,0:T(8,128)(2,1)S(1)}, bf16[256,512]{1,0:T(8,128)(2,1)S(1)}, u32[]{:S(2)}, u32[]{:S(2)}) collective-permute-start(bf16[256,512]{1,0:T(8,128)(2,1)S(1)} %get-tuple-element.59), channel_id=1, source_target_pairs={{0,1},{1,0},{2,3},{3,2},{4,5},{5,4},{6,7},{7,6},{8,9},{9,8},{10,11... | collective-permute-start | bytes 786440 | tf_op jit(solution)/shard_map/ppermute | solution.py:688
  69.8 2.7 %collective-permute-start.16 = (bf16[256,512]{1,0:T(8,128)(2,1)S(1)}, bf16[256,512]{1,0:T(8,128)(2,1)S(1)}, u32[]{:S(2)}, u32[]{:S(2)}) collective-permute-start(bf16[256,512]{1,0:T(8,128)(2,1)S(1)} %get-tuple-element.56), channel_id=1, source_target_pairs={{0,1},{1,0},{2,3},{3,2},{4,5},{5,4},{6,7},{7,6},{8,9},{9,8},{10,11... | collective-permute-start | bytes 786440 | tf_op jit(solution)/shard_map/ppermute | solution.py:688
  69.9 6.4 %collective-permute-start.21 = (bf16[128,512]{1,0:T(8,128)(2,1)S(1)}, bf16[128,512]{1,0:T(8,128)(2,1)S(1)}, u32[]{:S(2)}, u32[]{:S(2)}) collective-permute-start(bf16[128,512]{1,0:T(8,128)(2,1)S(1)} %get-tuple-element.60), channel_id=1, source_target_pairs={{0,2},{2,0},{4,6},{6,4},{8,10},{10,8},{12,14},{14,12},{16,18},{18,... | collective-permute-start | bytes 393224 | tf_op jit(solution)/shard_map/ppermute | solution.py:598
  70.6 8.6 %collective-permute-start.23 = (bf16[128,512]{1,0:T(8,128)(2,1)S(1)}, bf16[128,512]{1,0:T(8,128)(2,1)S(1)}, u32[]{:S(2)}, u32[]{:S(2)}) collective-permute-start(bf16[128,512]{1,0:T(8,128)(2,1)S(1)} %get-tuple-element.62), channel_id=1, source_target_pairs={{0,6},{2,4},{4,2},{6,0},{8,14},{10,12},{12,10},{14,8},{16,22},{18,... | collective-permute-start | bytes 393224 | tf_op jit(solution)/shard_map/ppermute | solution.py:598
  72.5 8.2 %collective-permute-start.22 = (bf16[128,512]{1,0:T(8,128)(2,1)S(1)}, bf16[128,512]{1,0:T(8,128)(2,1)S(1)}, u32[]{:S(2)}, u32[]{:S(2)}) collective-permute-start(bf16[128,512]{1,0:T(8,128)(2,1)S(1)} %get-tuple-element.61), channel_id=1, source_target_pairs={{0,4},{2,6},{4,0},{6,2},{8,12},{10,14},{12,8},{14,10},{16,20},{18,... | collective-permute-start | bytes 393224 | tf_op jit(solution)/shard_map/ppermute | solution.py:598
  (1 other events, 14.6 us)
